TPU v7x, 32 devices: a whole 2x2x4 slice. The times are simulated.
32 devices in a mesh: sample: 2 (over x), sy: 4 (over y, core), sz: 4 (over z).
Axes of the slice: x: 2, y: 2, z: 4, core: 2. Of those that a mesh axis runs over, the one named last changes fastest.
Arguments:
- volume: bfloat16 [2, 32, 16, 32, 128], P('sample', None, 'sz', 'sy'), may hold values from -22.5 to 22.5
- amax_history: float32 [4, 16], replicated, may hold values from 0.48 to 2.5
- conv_first: bfloat16 [27, 32, 32], replicated, may hold values from -0.21875 to 0.21875
- conv_second: bfloat16 [27, 32, 32], replicated, may hold values from -0.21875 to 0.21875
- conv_third: bfloat16 [27, 64, 32], P(None, 'sy'), may hold values from -0.21875 to 0.21875
- conv_fourth: bfloat16 [27, 64, 64], P(None, 'sy'), may hold values from -0.15625 to 0.15625
- gain_fine: float32 [2, 32], replicated, may hold values from 0.5 to 1.5
- shift_fine: float32 [2, 32], replicated, may hold values from -0.5 to 0.5
- gain_coarse: float32 [2, 64], P(None, 'sy'), may hold values from 0.5 to 1.5
- shift_coarse: float32 [2, 64], P(None, 'sy'), may hold values from -0.5 to 0.5
Outputs:
- skip_features: bfloat16 [2, 32, 16, 32, 128], P('sample', None, 'sz', 'sy')
- coarse_features: bfloat16 [2, 64, 8, 1024], P('sample', 'sy', 'sz')
- amax_now: float32 [4], replicated
All inputs are finite; a program needn't handle non-finite values.
Results may differ from a plain program's by a relative error of at most 0.012.
Values may be sent and summed in bfloat16 or wider, within the bound.
No kernel may reach another device: no remote copies, remote signals or barrier semaphores. Data moves between devices by JAX's collectives and lax.ppermute only.
A program may use at most 128 MiB of HBM per device.

v0:
```python
import jax
import jax.numpy as jnp
from jax import lax
from jax.sharding import PartitionSpec as P

norm_eps = 1e-05
leak_slope = 0.01


def padded_2(cells, sides, width):
    for axis, dim in sides:
        count = lax.axis_size(axis)
        ends = count - 1
        head = lax.slice_in_dim(cells, 0, width, axis=dim)
        tail = lax.slice_in_dim(cells, cells.shape[dim] - width, cells.shape[dim], axis=dim)
        cells = jnp.concatenate(
            [
                lax.ppermute(tail, axis, [(i, (i + 1) % count) for i in range(ends)]),
                cells,
                lax.ppermute(head, axis, [((i + 1) % count, i) for i in range(ends)]),
            ],
            axis=dim,
        )
    return cells


def limited(values, bound):
    return jnp.clip(values.astype(jnp.float32), -bound, bound).astype(jnp.bfloat16)


def fine_faces(values):
    return padded_2(values, (("sy", 2), ("sz", 1)), 1)


def coarse_faces(values):
    return padded_2(values, (("sz", 1),), 1)


def fine_stats(values):
    flat_rows = values.reshape(values.shape[0], -1)
    return lax.psum(
        (jnp.sum(flat_rows, axis=1), jnp.sum(flat_rows * flat_rows, axis=1)), ("sy", "sz")
    )


def coarse_stats(values):
    flat_rows = values.reshape(values.shape[0], -1)
    return lax.psum((jnp.sum(flat_rows, axis=1), jnp.sum(flat_rows * flat_rows, axis=1)), "sz")


def apply_norm(values, moments, cell_count, gains, offset):
    chan_mean = moments[0] / cell_count
    spread = moments[1] / cell_count - chan_mean * chan_mean
    scaling = lax.rsqrt(spread + norm_eps) * gains
    shaped = (-1,) + (1,) * (values.ndim - 1)
    normed = (values - chan_mean.reshape(shaped)) * scaling.reshape(shaped) + offset.reshape(shaped)
    return jnp.where(normed >= 0, normed, leak_slope * normed).astype(jnp.bfloat16)


def level_one_conv(padded, weight):
    channels, depth_cells, height_cells, width_cells = padded.shape
    out_depth = depth_cells - 2
    out_height = height_cells - 2
    out_chan = weight.shape[1]
    widened = jnp.pad(padded, ((0, 0), (0, 0), (0, 0), (1, 1)))
    stacked = jnp.concatenate(
        [widened[:, :, :, x_tap : x_tap + width_cells] for x_tap in range(3)], axis=0
    )
    summed = jnp.zeros((out_chan, out_depth * out_height * width_cells), jnp.float32)
    for z_tap in range(3):
        for y_tap in range(3):
            first_tap = z_tap * 9 + y_tap * 3
            taps = weight[first_tap : first_tap + 3]
            matrix = jnp.transpose(taps, (1, 0, 2)).reshape(out_chan, 3 * channels)
            window = stacked[:, z_tap : z_tap + out_depth, y_tap : y_tap + out_height, :].reshape(
                3 * channels, -1
            )
            summed = summed + jnp.dot(matrix, window, preferred_element_type=jnp.float32)
    return summed.reshape(out_chan, out_depth, out_height, width_cells)


def level_two_conv(padded, weight, row_len):
    channels, depth_cells, flat_len = padded.shape
    out_depth = depth_cells - 2
    out_chan = weight.shape[1]
    column = lax.broadcasted_iota(jnp.int32, (1, 1, flat_len), 2) % row_len
    blank = jnp.zeros((), padded.dtype)
    sources = (
        jnp.where(column == row_len - 1, blank, padded),
        padded,
        jnp.where(column == 0, blank, padded),
    )
    wide_len = flat_len + 2 * row_len
    stacked = jnp.concatenate(
        [
            jnp.pad(sources[x_tap], ((0, 0), (0, 0), (row_len + 1, row_len + 1)))[
                :, :, x_tap : x_tap + wide_len
            ]
            for x_tap in range(3)
        ],
        axis=0,
    )
    summed = jnp.zeros((out_chan, out_depth * flat_len), jnp.float32)
    for z_tap in range(3):
        for y_tap in range(3):
            first_tap = z_tap * 9 + y_tap * 3
            taps = weight[first_tap : first_tap + 3]
            matrix = jnp.transpose(taps, (1, 0, 2)).reshape(out_chan, 3 * channels)
            window = stacked[
                :, z_tap : z_tap + out_depth, y_tap * row_len : y_tap * row_len + flat_len
            ].reshape(3 * channels, -1)
            summed = summed + jnp.dot(matrix, window, preferred_element_type=jnp.float32)
    return summed.reshape(out_chan, out_depth, flat_len)


def magnitude(values):
    return jnp.max(jnp.abs(values.astype(jnp.float32)))


def per_device(
    volume,
    amax_history,
    conv_first,
    conv_second,
    conv_third,
    conv_fourth,
    gain_fine,
    shift_fine,
    gain_coarse,
    shift_coarse,
):
    bounds = jnp.max(amax_history, axis=1)
    sample_count, channels, z_cells, y_cells, x_cells = volume.shape
    z_groups = lax.axis_size("sz")
    y_groups = lax.axis_size("sy")
    half_x = x_cells // 2
    half_z = z_cells // 2
    fine_cells = float(z_cells * z_groups * y_cells * y_groups * x_cells)
    coarse_cells = float(half_z * z_groups * (y_cells // 2) * y_groups * half_x)
    source = volume[0]
    layer_peaks = [magnitude(source)]
    first_in = limited(source, bounds[0])
    first_out = level_one_conv(fine_faces(first_in), conv_first)
    hidden = apply_norm(first_out, fine_stats(first_out), fine_cells, gain_fine[0], shift_fine[0])
    layer_peaks.append(magnitude(hidden))
    second_out = level_one_conv(fine_faces(limited(hidden, bounds[1])), conv_second)
    skip_out = apply_norm(
        second_out, fine_stats(second_out), fine_cells, gain_fine[1], shift_fine[1]
    )
    skip_list = [skip_out]
    blocks = skip_out.reshape(channels, half_z, 2, y_cells // 2, 2, half_x, 2)
    pooled = jnp.max(blocks, axis=(2, 4, 6))
    layer_peaks.append(magnitude(pooled))
    gathered = lax.all_gather(limited(pooled, bounds[2]), "sy", axis=2, tiled=True)
    flat_in = gathered.reshape(channels, half_z, -1)
    third_out = level_two_conv(coarse_faces(flat_in), conv_third, half_x)
    coarse_hidden = apply_norm(
        third_out, coarse_stats(third_out), coarse_cells, gain_coarse[0], shift_coarse[0]
    )
    layer_peaks.append(magnitude(coarse_hidden))
    edged = coarse_faces(limited(coarse_hidden, bounds[3]))
    fourth_out = level_two_conv(
        lax.all_gather(edged, "sy", axis=0, tiled=True), conv_fourth, half_x
    )
    coarse_list = [
        apply_norm(
            fourth_out, coarse_stats(fourth_out), coarse_cells, gain_coarse[1], shift_coarse[1]
        )
    ]
    peak_rows = [jnp.stack(layer_peaks)]
    peaks = jnp.max(jnp.stack(peak_rows), axis=0)
    peaks = lax.pmax(peaks, ("sample", "sy", "sz"))
    return (jnp.stack(skip_list), jnp.stack(coarse_list), peaks)


def solution(mesh):
    return jax.shard_map(
        per_device,
        mesh=mesh,
        in_specs=(
            P("sample", None, "sz", "sy", None),
            P(),
            P(),
            P(),
            P(None, "sy", None),
            P(None, "sy", None),
            P(),
            P(),
            P(None, "sy"),
            P(None, "sy"),
        ),
        out_specs=(P("sample", None, "sz", "sy", None), P("sample", "sy", "sz", None), P()),
        check_vma=False,
    )
```

profile of v0, /device:TPU:0, one launch (start us, length us, event | category | flops | bytes accessed | tf_op | source)
XLA Modules:
  0.0 249.3 jit_solution(14499063451682183801)
XLA Ops:
  0.6 0.8 reduce_max.58
  1.4 0.6 fusion.85
  2.7 1.7 fusion.64
  4.5 2.4 collective-permute-start
  6.9 1.3 collective-permute-start.1
  8.2 0.8 slice_bitcast_fusion.47
  8.9 0.8 slice_bitcast_fusion.45
  9.7 0.9 slice_bitcast_fusion.36
  10.5 0.9 slice_bitcast_fusion.27
  11.4 0.9 slice_bitcast_fusion.18
  12.3 0.9 slice_bitcast_fusion.9
  13.2 1.7 fusion.57
  16.6 4.3 %collective-permute-start.2 = (bf16[32,1,10,128]{3,2,1,0:T(8,128)(2,1)S(1)}, bf16[32,1,10,128]{3,2,1,0:T(8,128)(2,1)S(1)}, u32[]{:S(2)}, u32[]{:S(2)}) collective-permute-start(bf16[32,1,10,128]{3,2,1,0:T(8,128)(2,1)S(1)} %get-tuple-element.55), channel_id=1, source_target_pairs={{0,1},{1,2},{2,3},{4,5},{5,6},{6,7},{8,9},{9,10},{10,11},{12,13},{... | collective-permute-start | bytes 245768 | tf_op jit(solution)/shard_map/ppermute | solution.py:18
  20.9 1.3 collective-permute-start.3
  22.3 1.2 collective-permute-done.2
  23.4 4.6 %collective-permute-done.3 = bf16[32,1,10,128]{3,2,1,0:T(8,128)(2,1)S(1)} collective-permute-done((bf16[32,1,10,128]{3,2,1,0:T(8,128)(2,1)S(1)}, bf16[32,1,10,128]{3,2,1,0:T(8,128)(2,1)S(1)}, u32[]{:S(2)}, u32[]{:S(2)}) %collective-permute-start.3) | collective-permute-done | bytes 81952 | tf_op jit(solution)/shard_map/ppermute | solution.py:20
  28.0 1.8 fusion.11
  30.2 1.2 pad_maximum_fusion
  31.4 1.5 fusion.77
  33.3 0.4 convolution_add_fusion.15
  33.8 0.4 convolution_add_fusion.14
  34.2 0.4 convolution_add_fusion.13
  34.6 0.4 convolution_add_fusion.12
  36.2 0.5 fusion.61
  37.0 31.8 %all-reduce.9 = (f32[32]{0:T(128)S(1)}, f32[32]{0:T(128)S(1)}) all-reduce(f32[32]{0:T(128)S(1)} %get-tuple-element.119, f32[32]{0:T(128)S(1)} %reduce_sum.72), channel_id=1, replica_groups=mesh['sample'=2,'sy'=4,'sz'=4] {'sy','sz'}, use_global_device_ids=true, to_apply=%region_4.5 | all-reduce | flops 64 | bytes 512 | tf_op jit(solution)/shard_map/psum | solution.py:41
  68.8 0.8 minimum_convert_fusion
  69.7 1.3 collective-permute-start.4
  71.0 1.3 collective-permute-start.5
  76.4 1.2 collective-permute-done.5
  77.8 2.6 %collective-permute-start.6 = (bf16[32,1,10,128]{3,2,1,0:T(8,128)(2,1)S(1)}, bf16[32,1,10,128]{3,2,1,0:T(8,128)(2,1)S(1)}, u32[]{:S(2)}, u32[]{:S(2)}) collective-permute-start(bf16[32,1,10,128]{3,2,1,0:T(8,128)(2,1)S(1)} %get-tuple-element.53), channel_id=1, source_target_pairs={{0,1},{1,2},{2,3},{4,5},{5,6},{6,7},{8,9},{9,10},{10,11},{12,13},{... | collective-permute-start | bytes 245768 | tf_op jit(solution)/shard_map/ppermute | solution.py:18
  80.4 1.5 collective-permute-start.7
  81.9 0.8 abs_reduce_fusion
  82.9 4.4 %collective-permute-done.7 = bf16[32,1,10,128]{3,2,1,0:T(8,128)(2,1)S(1)} collective-permute-done((bf16[32,1,10,128]{3,2,1,0:T(8,128)(2,1)S(1)}, bf16[32,1,10,128]{3,2,1,0:T(8,128)(2,1)S(1)}, u32[]{:S(2)}, u32[]{:S(2)}) %collective-permute-start.7) | collective-permute-done | bytes 81952 | tf_op jit(solution)/shard_map/ppermute | solution.py:20
  87.3 1.8 select_maximum_fusion
  89.5 1.2 pad_maximum_fusion.1
  90.7 1.5 fusion.76
  92.6 0.4 convolution_add_fusion.7
  95.5 0.5 multiply_reduce_fusion
  96.3 0.6 copy.193
  96.9 30.0 %all-reduce.8 = (f32[32]{0:T(128)S(1)}, f32[32]{0:T(128)S(1)}) all-reduce(f32[32]{0:T(128)S(1)} %get-tuple-element.121, f32[32]{0:T(128)S(1)} %reduce_sum.74), channel_id=1, replica_groups=mesh['sample'=2,'sy'=4,'sz'=4] {'sy','sz'}, use_global_device_ids=true, to_apply=%region_8.9 | all-reduce | flops 64 | bytes 512 | tf_op jit(solution)/shard_map/psum | solution.py:41
  126.9 2.9 %fusion.16 = bf16[32,2,4,64]{0,3,2,1:T(8,128)(2,1)S(1)} fusion(f32[32]{0:T(128)S(1)} %get-tuple-element.105, f32[32]{0:T(128)S(1)} %get-tuple-element.116, f32[32,2,2,4,2,64,2]{0,6,5,4,3,2,1:T(2,128)S(1)} %bitcast.322, f32[32]{0:T(128)S(1)} %get-tuple-element.115), kind=kLoop, calls=%fused_computation.59 | loop fusion | flops 1032192 | bytes 557440 | tf_op jit(solution)/shard_map/reduce_max | solution.py:152
  130.0 0.7 fusion.66
  130.7 8.9 %all_gather.6 = bf16[32,2,16,64]{3,0,1,2:T(8,128)(2,1)S(1)} all-gather(bf16[32,2,4,64]{3,0,1,2:T(8,128)(2,1)S(1)} %copy.195), channel_id=1, replica_groups=mesh['sample'=2,'sy'=4,'sz'=4] {'sy'}, dimensions={2}, use_global_device_ids=true | all-gather | bytes 163840 | tf_op jit(solution)/shard_map/all_gather | solution.py:154
  140.0 1.3 collective-permute-start.9
  141.3 4.8 %collective-permute-start.8 = (bf16[32,1,1024]{2,0,1:T(8,128)(2,1)S(1)}, bf16[32,1,1024]{2,0,1:T(8,128)(2,1)S(1)}, u32[]{:S(2)}, u32[]{:S(2)}) collective-permute-start(bf16[32,1,1024]{2,0,1:T(8,128)(2,1)S(1)} %get-tuple-element.82), channel_id=1, source_target_pairs={{0,1},{1,2},{2,3},{4,5},{5,6},{6,7},{8,9},{9,10},{10,11},{12,13},{... | collective-permute-start | bytes 196616 | tf_op jit(solution)/shard_map/ppermute | solution.py:18
  146.1 0.6 fusion.67
  146.7 1.2 collective-permute-done.8
  148.6 0.6 slice_bitcast_fusion
  151.5 11.7 %all-reduce.11 = (f32[16]{0:T(128)S(1)}, f32[16]{0:T(128)S(1)}) all-reduce(f32[16]{0:T(128)S(1)} %get-tuple-element.123, f32[16]{0:T(128)S(1)} %reduce_sum.76), channel_id=1, replica_groups=mesh['sample'=2,'sy'=4,'sz'=4] {'sz'}, use_global_device_ids=true, to_apply=%region_13.14 | all-reduce | flops 32 | bytes 256 | tf_op jit(solution)/shard_map/psum | solution.py:48
  163.2 0.7 abs_reduce_fusion.1
  163.9 0.9 minimum_convert_fusion.1
  164.9 2.0 collective-permute-start.10
  166.9 1.3 collective-permute-start.11
  168.2 2.6 %pad_maximum_fusion.11 = f32[4]{0:T(128)S(1)} fusion(f32[1]{0:T(128)} %bitcast.57, f32[1]{0:T(128)} %bitcast.56, f32[1]{0:T(128)} %bitcast.55, f32[1]{0:T(128)} %bitcast.54), kind=kLoop, calls=%fused_computation.203 | loop fusion | flops 12 | bytes 32 | tf_op jit(solution)/shard_map/stack | solution.py:170
  170.9 0.9 fusion.59
  171.8 41.5 %pmax.7 = f32[4]{0:T(128)} all-reduce(f32[4]{0:T(128)S(1)} %pad_maximum_fusion.11), channel_id=1, replica_groups=mesh['sample'=2,'sy'=4,'sz'=4] {'sample','sy','sz'}, use_global_device_ids=true, to_apply=%region_22.23 | all-reduce | flops 4 | bytes 32 | tf_op jit(solution)/shard_map/pmax | solution.py:172
  213.5 8.1 %all_gather.7 = bf16[64,4,1024]{2,1,0:T(4,128)(2,1)S(1)} all-gather(bf16[16,4,1024]{2,1,0:T(4,128)(2,1)S(1)} %pad_maximum_fusion.10), channel_id=1, replica_groups=mesh['sample'=2,'sy'=4,'sz'=4] {'sy'}, dimensions={0}, use_global_device_ids=true | all-gather | bytes 655360 | tf_op jit(solution)/shard_map/all_gather | solution.py:163
  221.6 0.4 pad_slice_fusion.1
  222.5 0.4 pad_slice_fusion.2
  222.9 0.4 pad_slice_fusion
  223.3 3.0 %pad_maximum_fusion.2 = bf16[192,4,1152]{2,1,0:T(4,128)(2,1)S(1)} fusion(bf16[64,4,1152]{2,1,0:T(4,128)(2,1)S(1)} %pad_slice_fusion, bf16[64,4,1152]{2,1,0:T(4,128)(2,1)S(1)} %pad_slice_fusion.1, bf16[64,4,1152]{2,1,0:T(4,128)(2,1)S(1)} %pad_slice_fusion.2), kind=kLoop, calls=%fused_computation.39 | loop fusion | flops 1769472 | bytes 3538944 | tf_op jit(solution)/shard_map/concatenate | solution.py:94
  226.3 8.0 %fusion.78 = (bf16[192,2,1024]{2,1,0:T(2,128)(2,1)S(1)}, bf16[192,2,1024]{2,1,0:T(2,128)(2,1)S(1)}, bf16[192,2,1024]{2,1,0:T(2,128)(2,1)S(1)}, bf16[192,2,1024]{...) fusion(bf16[192,4,1152]{2,1,0:T(4,128)(2,1)S(1)} %pad_maximum_f, ...), kind=kLoop, calls=%fused_computation.218 | loop fusion | bytes 14155776 | tf_op jit(solution)/shard_map/slice | solution.py:109
  238.6 9.9 %all-reduce.10 = (f32[16]{0:T(128)S(1)}, f32[16]{0:T(128)S(1)}) all-reduce(f32[16]{0:T(128)S(1)} %get-tuple-element.125, f32[16]{0:T(128)S(1)} %reduce_sum.78), channel_id=1, replica_groups=mesh['sample'=2,'sy'=4,'sz'=4] {'sz'}, use_global_device_ids=true, to_apply=%region_17.18 | all-reduce | flops 32 | bytes 256 | tf_op jit(solution)/shard_map/psum | solution.py:48
  248.5 0.9 fusion.70
  (165 shorter events, 18.2 us)
Async XLA Ops:
  4.5 12.0 %collective-permute-start = (bf16[32,4,1,128]{3,2,1,0:T(2,128)(2,1)S(1)}, bf16[32,4,1,128]{3,2,1,0:T(2,128)(2,1)S(1)}, u32[]{:S(2)}, u32[]{:S(2)}) collective-permute-start(bf16[32,4,1,128]{3,2,1,0:T(2,128)(2,1)S(1)} %get-tuple-element.61), channel_id=1, source_target_pairs={{0,4},{4,8},{8,12},{1,5},{5,9},{9,13},{2,6},{6,10},{10,14},{3,7},{... | collective-permute-start | bytes 98312 | tf_op jit(solution)/shard_map/ppermute | solution.py:18
  6.9 9.6 %collective-permute-start.1 = (bf16[32,4,1,128]{3,2,1,0:T(2,128)(2,1)S(1)}, bf16[32,4,1,128]{3,2,1,0:T(2,128)(2,1)S(1)}, u32[]{:S(2)}, u32[]{:S(2)}) collective-permute-start(bf16[32,4,1,128]{3,2,1,0:T(2,128)(2,1)S(1)} %get-tuple-element.62), channel_id=1, source_target_pairs={{4,0},{8,4},{12,8},{5,1},{9,5},{13,9},{6,2},{10,6},{14,10},{7,3},{... | collective-permute-start | bytes 98312 | tf_op jit(solution)/shard_map/ppermute | solution.py:20
  16.6 6.8 %collective-permute-start.2 = (bf16[32,1,10,128]{3,2,1,0:T(8,128)(2,1)S(1)}, bf16[32,1,10,128]{3,2,1,0:T(8,128)(2,1)S(1)}, u32[]{:S(2)}, u32[]{:S(2)}) collective-permute-start(bf16[32,1,10,128]{3,2,1,0:T(8,128)(2,1)S(1)} %get-tuple-element.55), channel_id=1, source_target_pairs={{0,1},{1,2},{2,3},{4,5},{5,6},{6,7},{8,9},{9,10},{10,11},{12,13},{... | collective-permute-start | bytes 245768 | tf_op jit(solution)/shard_map/ppermute | solution.py:18
  20.9 7.1 %collective-permute-start.3 = (bf16[32,1,10,128]{3,2,1,0:T(8,128)(2,1)S(1)}, bf16[32,1,10,128]{3,2,1,0:T(8,128)(2,1)S(1)}, u32[]{:S(2)}, u32[]{:S(2)}) collective-permute-start(bf16[32,1,10,128]{3,2,1,0:T(8,128)(2,1)S(1)} %get-tuple-element.56), channel_id=1, source_target_pairs={{1,0},{2,1},{3,2},{5,4},{6,5},{7,6},{9,8},{10,9},{11,10},{13,12},{... | collective-permute-start | bytes 245768 | tf_op jit(solution)/shard_map/ppermute | solution.py:20
  35.8 33.0 %copy-start = (f32[2,32]{1,0:T(2,128)S(1)}, f32[2,32]{1,0:T(2,128)}, u32[]{:S(2)}) copy-start(f32[2,32]{1,0:T(2,128)} %param.16) | copy-start | bytes 772
  69.7 6.7 %collective-permute-start.4 = (bf16[32,4,1,128]{3,2,1,0:T(2,128)(2,1)S(1)}, bf16[32,4,1,128]{3,2,1,0:T(2,128)(2,1)S(1)}, u32[]{:S(2)}, u32[]{:S(2)}) collective-permute-start(bf16[32,4,1,128]{3,2,1,0:T(2,128)(2,1)S(1)} %get-tuple-element.59), channel_id=1, source_target_pairs={{0,4},{4,8},{8,12},{1,5},{5,9},{9,13},{2,6},{6,10},{10,14},{3,7},{... | collective-permute-start | bytes 98312 | tf_op jit(solution)/shard_map/ppermute | solution.py:18
  71.0 6.7 %collective-permute-start.5 = (bf16[32,4,1,128]{3,2,1,0:T(2,128)(2,1)S(1)}, bf16[32,4,1,128]{3,2,1,0:T(2,128)(2,1)S(1)}, u32[]{:S(2)}, u32[]{:S(2)}) collective-permute-start(bf16[32,4,1,128]{3,2,1,0:T(2,128)(2,1)S(1)} %get-tuple-element.60), channel_id=1, source_target_pairs={{4,0},{8,4},{12,8},{5,1},{9,5},{13,9},{6,2},{10,6},{14,10},{7,3},{... | collective-permute-start | bytes 98312 | tf_op jit(solution)/shard_map/ppermute | solution.py:20
  77.8 5.1 %collective-permute-start.6 = (bf16[32,1,10,128]{3,2,1,0:T(8,128)(2,1)S(1)}, bf16[32,1,10,128]{3,2,1,0:T(8,128)(2,1)S(1)}, u32[]{:S(2)}, u32[]{:S(2)}) collective-permute-start(bf16[32,1,10,128]{3,2,1,0:T(8,128)(2,1)S(1)} %get-tuple-element.53), channel_id=1, source_target_pairs={{0,1},{1,2},{2,3},{4,5},{5,6},{6,7},{8,9},{9,10},{10,11},{12,13},{... | collective-permute-start | bytes 245768 | tf_op jit(solution)/shard_map/ppermute | solution.py:18
  80.4 6.9 %collective-permute-start.7 = (bf16[32,1,10,128]{3,2,1,0:T(8,128)(2,1)S(1)}, bf16[32,1,10,128]{3,2,1,0:T(8,128)(2,1)S(1)}, u32[]{:S(2)}, u32[]{:S(2)}) collective-permute-start(bf16[32,1,10,128]{3,2,1,0:T(8,128)(2,1)S(1)} %get-tuple-element.54), channel_id=1, source_target_pairs={{1,0},{2,1},{3,2},{5,4},{6,5},{7,6},{9,8},{10,9},{11,10},{13,12},{... | collective-permute-start | bytes 245768 | tf_op jit(solution)/shard_map/ppermute | solution.py:20
  140.0 8.0 %collective-permute-start.9 = (bf16[32,1,1024]{2,0,1:T(8,128)(2,1)S(1)}, bf16[32,1,1024]{2,0,1:T(8,128)(2,1)S(1)}, u32[]{:S(2)}, u32[]{:S(2)}) collective-permute-start(bf16[32,1,1024]{2,0,1:T(8,128)(2,1)S(1)} %get-tuple-element.81), channel_id=1, source_target_pairs={{1,0},{2,1},{3,2},{5,4},{6,5},{7,6},{9,8},{10,9},{11,10},{13,12},{... | collective-permute-start | bytes 196616 | tf_op jit(solution)/shard_map/ppermute | solution.py:20
  141.3 6.7 %collective-permute-start.8 = (bf16[32,1,1024]{2,0,1:T(8,128)(2,1)S(1)}, bf16[32,1,1024]{2,0,1:T(8,128)(2,1)S(1)}, u32[]{:S(2)}, u32[]{:S(2)}) collective-permute-start(bf16[32,1,1024]{2,0,1:T(8,128)(2,1)S(1)} %get-tuple-element.82), channel_id=1, source_target_pairs={{0,1},{1,2},{2,3},{4,5},{5,6},{6,7},{8,9},{9,10},{10,11},{12,13},{... | collective-permute-start | bytes 196616 | tf_op jit(solution)/shard_map/ppermute | solution.py:18
  149.9 13.3 %copy-start.1 = (f32[2,16]{1,0:T(2,128)S(1)}, f32[2,16]{1,0:T(2,128)}, u32[]{:S(2)}) copy-start(f32[2,16]{1,0:T(2,128)} %param.18) | copy-start | bytes 388
  164.9 48.3 %collective-permute-start.10 = (bf16[16,1,1024]{2,1,0:T(2,128)(2,1)S(1)}, bf16[16,1,1024]{2,1,0:T(2,128)(2,1)S(1)}, u32[]{:S(2)}, u32[]{:S(2)}) collective-permute-start(bf16[16,1,1024]{2,1,0:T(2,128)(2,1)S(1)} %get-tuple-element.101), channel_id=1, source_target_pairs={{0,1},{1,2},{2,3},{4,5},{5,6},{6,7},{8,9},{9,10},{10,11},{12,13},{... | collective-permute-start | bytes 98312 | tf_op jit(solution)/shard_map/ppermute | solution.py:18
  166.9 46.3 %collective-permute-start.11 = (bf16[16,1,1024]{2,1,0:T(2,128)(2,1)S(1)}, bf16[16,1,1024]{2,1,0:T(2,128)(2,1)S(1)}, u32[]{:S(2)}, u32[]{:S(2)}) collective-permute-start(bf16[16,1,1024]{2,1,0:T(2,128)(2,1)S(1)} %get-tuple-element.102), channel_id=1, source_target_pairs={{1,0},{2,1},{3,2},{5,4},{6,5},{7,6},{9,8},{10,9},{11,10},{13,12},{... | collective-permute-start | bytes 98312 | tf_op jit(solution)/shard_map/ppermute | solution.py:20
where the time goes:
time: 250 us; the launch traced here: 249 us
  blocking collectives  142 us (57%)
  local copies, waits for them, and re-layouts  27.2 us (11%)
  other arithmetic  26.6 us (11%)
  starting transfers between devices  25.3 us (10%)
  waiting for transfers between devices  12.9 us (5%)
  matrix products  11.3 us (5%)
  between operations  3.99 us (2%)
    psum x2, blocking collectives, fine_stats(): lax.psum((jnp.sum(flat_rows, axis=1), jnp.sum(flat_rows * flat_rows, axis...  61.8 us
    pmax x1, blocking collectives, per_device(): peaks = lax.pmax(peaks, ('sample', 'sy', 'sz'))  41.5 us
    psum x2, blocking collectives, coarse_stats(): lax.psum((jnp.sum(flat_rows, axis=1), jnp.sum(flat_rows * flat_rows, axis...  21.6 us
    ppermute x6, starting transfers between devices, padded_2(): lax.ppermute(tail, axis, [(i, (i + 1) % count) for i in range(ends)])  17.4 us
    ppermute x6, waiting for transfers between devices, padded_2(): lax.ppermute(head, axis, [((i + 1) % count, i) for i in range(ends)])  10.2 us
    all_gather x1, blocking collectives, per_device(): lax.all_gather(limited(pooled, bounds[2]), 'sy', axis=2, tiled=True)  8.94 us
    all_gather x1, blocking collectives, per_device(): lax.all_gather(edged, 'sy', axis=0, tiled=True)  8.15 us
    slice x1, local copies, waits for them, and re-layouts, level_two_conv(): stacked[:, z_tap:z_tap + out_depth, y_tap * row_len:y_tap * row_len + fla...  8.01 us
  transfers between devices with their start and end apart: 12, of which 6 were waited for; matrix products, arithmetic and copies ran while one was open for 6% of the time, Pallas kernels for 0%

commit v1 on v0

v1 whole, which is shorter than its diff:
```python
import jax
import jax.numpy as jnp
from jax import lax
from jax.experimental import pallas as pl
from jax.experimental.pallas import tpu as pltpu
from jax.sharding import PartitionSpec as P

norm_eps = 1e-05
leak_slope = 0.01
f32 = jnp.float32
bf16 = jnp.bfloat16
LANES = 128
HALO = 2
PEAK_AT = 64
GAIN_AT = 80
SHIFT_AT = 96


def near(axis):
    count = lax.axis_size(axis)
    first = [(i, i ^ 1) for i in range(count)]
    second = [(i, min(max(((i + 1) ^ 1) - 1, 0), count - 1)) for i in range(count)]
    return first, second


def column(row, channels, start):
    lanes = lax.broadcasted_iota(jnp.int32, (channels, row.shape[1]), 1)
    chans = lax.broadcasted_iota(jnp.int32, (channels, row.shape[1]), 0)
    return jnp.sum(jnp.where(lanes == chans + start, row, 0.0), axis=1, keepdims=True)


def as_row(col, start):
    channels = col.shape[0]
    lanes = lax.broadcasted_iota(jnp.int32, (channels, LANES), 1)
    chans = lax.broadcasted_iota(jnp.int32, (channels, LANES), 0)
    return jnp.sum(jnp.where(lanes == chans + start, col, 0.0), axis=0, keepdims=True)


def at_lane(value, lane):
    lanes = lax.broadcasted_iota(jnp.int32, (1, LANES), 1)
    return jnp.where(lanes == lane, value, 0.0)


def affine(total, square, cells, gains, offset):
    mean = total / cells
    spread = square / cells - mean * mean
    scale = lax.rsqrt(spread + norm_eps) * gains
    return scale, offset - mean * scale


def activated(values, scale, offset):
    normed = values * scale + offset
    return jnp.where(normed >= 0, normed, leak_slope * normed).astype(bf16)


def peak_of(values):
    return jnp.max(jnp.max(values, axis=1, keepdims=True), axis=0, keepdims=True)


def bounded(values, bound):
    return jnp.minimum(jnp.maximum(values.astype(f32), -bound), bound).astype(bf16)


def bound_of(hist_ref, level):
    return jnp.max(hist_ref[level : level + 1, :], axis=1, keepdims=True)


def tap_sum(left, middle, right, period):
    lane = lax.broadcasted_iota(jnp.int32, middle.shape, 1) % period
    up = pltpu.roll(left, 1, 1)
    down = pltpu.roll(right, LANES - 1, 1)
    return middle + jnp.where(lane == 0, 0.0, up) + jnp.where(lane == period - 1, 0.0, down)


def prep_kernel(vol_ref, hist_ref, cells_ref, first_ref, second_ref, peak_ref, wide_ref):
    channels, depth, height, width = vol_ref.shape[1:]
    rows = depth * height
    wide = vol_ref[0].astype(f32).reshape(channels * rows, width)
    wide_ref[...] = wide
    peak_ref[...] = jnp.broadcast_to(peak_of(jnp.abs(wide)), (1, LANES))
    bound = bound_of(hist_ref, 0)
    for r in range(rows):
        cells_ref[r // height, r % height] = bounded(
            wide_ref[pl.ds(r, channels, stride=rows), :], bound
        )
    even = lax.axis_index("sz") % 2 == 0
    start_first = jnp.where(even, depth - HALO, 0)
    start_second = jnp.where(even, 0, depth - HALO)
    first_ref[...] = cells_ref[pl.ds(start_first, HALO)]
    second_ref[...] = cells_ref[pl.ds(start_second, HALO)]


def sides(axis, first, second):
    at = lax.axis_index(axis)
    count = lax.axis_size(axis)
    even = at % 2 == 0
    blank = jnp.zeros_like(first)
    below = jnp.where(at == 0, blank, jnp.where(even, second, first))
    above = jnp.where(at == count - 1, blank, jnp.where(even, first, second))
    return below, above


def deep_kernel(cells_ref, got_first_ref, got_second_ref, deep_ref, first_ref, second_ref):
    depth, height = cells_ref.shape[:2]
    below, above = sides("sz", got_first_ref[...], got_second_ref[...])
    deep_ref[0:HALO] = below
    deep_ref[HALO : HALO + depth] = cells_ref[...]
    deep_ref[HALO + depth :] = above
    even = lax.axis_index("sy") % 2 == 0
    start_first = jnp.where(even, height - HALO, 0)
    start_second = jnp.where(even, 0, height - HALO)
    first_ref[...] = deep_ref[:, pl.ds(start_first, HALO)]
    second_ref[...] = deep_ref[:, pl.ds(start_second, HALO)]


def conv_rows(cells_ref, weight, z, y, out_chan):
    window = jnp.concatenate(
        [
            jnp.concatenate(
                [cells_ref[z + dz, y + dy], cells_ref[z + dz, y + 1 + dy]], axis=1
            )
            for dz in range(3)
            for dy in range(3)
        ],
        axis=0,
    )
    taps = jnp.dot(weight, window, preferred_element_type=f32)
    outs = []
    for half in range(2):
        part = taps[:, half * LANES : (half + 1) * LANES]
        outs.append(
            tap_sum(
                part[:out_chan], part[out_chan : 2 * out_chan], part[2 * out_chan :], LANES
            )
        )
    return outs


def first_kernel(
    deep_ref, got_first_ref, got_second_ref, weight_ref, peak_ref, raw_ref, row_ref, cells_ref
):
    depth, height = raw_ref.shape[:2]
    channels = raw_ref.shape[2]
    inner = deep_ref.shape[1]
    below, above = sides("sy", got_first_ref[...], got_second_ref[...])
    cells_ref[:, 0:HALO] = below
    cells_ref[:, HALO : HALO + inner] = deep_ref[...]
    cells_ref[:, HALO + inner :] = above
    weight = weight_ref[...]

    def plane(z, sums):
        total, square = sums
        own = jnp.where((z >= 1) & (z < depth - 1), 1.0, 0.0).astype(f32)
        for y in range(0, height, 2):
            outs = conv_rows(cells_ref, weight, z, y, channels)
            for half in range(2):
                raw_ref[z, y + half] = outs[half]
                if 1 <= y + half < height - 1:
                    mine = outs[half] * own
                    total = total + mine
                    square = square + mine * mine
        return total, square

    blank = jnp.zeros((channels, LANES), f32)
    total, square = lax.fori_loop(0, depth, plane, (blank, blank))
    row = as_row(jnp.sum(total, axis=1, keepdims=True), 0)
    row = row + as_row(jnp.sum(square, axis=1, keepdims=True), channels)
    row = row + at_lane(peak_ref[...], PEAK_AT)
    row_ref[...] = jnp.broadcast_to(row[None], row_ref.shape)


def second_kernel(cell_count):
    def kernel(
        raw_ref,
        rows_ref,
        weight_ref,
        hist_ref,
        gain_ref,
        shift_ref,
        gain_coarse_ref,
        shift_coarse_ref,
        out_ref,
        load_ref,
        hidden_ref,
        pool_ref,
    ):
        wide_depth, wide_height, channels, width = raw_ref.shape
        depth, height = out_ref.shape[:2]
        rows = rows_ref[...]
        merged = jnp.sum(rows, axis=0)
        peak_vol = jnp.max(rows, axis=0)
        scale, offset = affine(
            column(merged, channels, 0),
            column(merged, channels, channels),
            cell_count,
            column(gain_ref[0:1, :], channels, 0),
            column(shift_ref[0:1, :], channels, 0),
        )
        bound = bound_of(hist_ref, 1)
        at_z = lax.axis_index("sz")
        at_y = lax.axis_index("sy")
        last_z = lax.axis_size("sz") - 1
        last_y = lax.axis_size("sy") - 1

        def plane(z, peak):
            inside_z = ((z > 0) | (at_z > 0)) & ((z < wide_depth - 1) | (at_z < last_z))
            own = jnp.where((z >= 1) & (z < wide_depth - 1), 1.0, 0.0).astype(f32)
            for y in range(wide_height):
                inside = inside_z
                if y == 0:
                    inside = inside & (at_y > 0)
                if y == wide_height - 1:
                    inside = inside & (at_y < last_y)
                hidden = activated(raw_ref[z, y], scale, offset).astype(f32)
                if 1 <= y < wide_height - 1:
                    peak = jnp.maximum(peak, jnp.abs(hidden) * own)
                clipped = jnp.minimum(jnp.maximum(hidden, -bound), bound)
                hidden_ref[z, y] = jnp.where(inside, clipped, 0.0).astype(bf16)
            return peak

        blank = jnp.zeros((channels, width), f32)
        peak = lax.fori_loop(0, wide_depth, plane, blank)
        weight = weight_ref[...]
        sign = jnp.where(column(gain_ref[1:2, :], channels, 0) >= 0, 1.0, -1.0).astype(f32)
        half_height = height // 2

        def pair(zp, sums):
            total, square = sums
            for yp in range(half_height):
                best = None
                for dz in range(2):
                    outs = conv_rows(hidden_ref, weight, 2 * zp + dz, 2 * yp, channels)
                    for half in range(2):
                        out_ref[2 * zp + dz, 2 * yp + half] = outs[half]
                        total = total + outs[half]
                        square = square + outs[half] * outs[half]
                        signed = outs[half] * sign
                        best = signed if best is None else jnp.maximum(best, signed)
                best = jnp.maximum(best, pltpu.roll(best, LANES - 1, 1)) * sign
                pool_ref[zp, yp] = best.astype(bf16)
            return total, square

        total, square = lax.fori_loop(0, depth // 2, pair, (blank, blank))
        pick = jnp.where(
            lax.broadcasted_iota(jnp.int32, (2 * LANES, LANES), 0)
            == 2 * lax.broadcasted_iota(jnp.int32, (2 * LANES, LANES), 1),
            1.0,
            0.0,
        ).astype(bf16)
        for zp in range(depth // 2):
            for yq in range(half_height // 2):
                both = jnp.concatenate([pool_ref[zp, 2 * yq], pool_ref[zp, 2 * yq + 1]], axis=1)
                load_ref[
                    zp * channels : (zp + 1) * channels, yq * LANES : (yq + 1) * LANES
                ] = jnp.dot(both, pick, preferred_element_type=f32).astype(bf16)
        mine = gain_coarse_ref.shape[1]
        row = as_row(jnp.sum(total, axis=1, keepdims=True), 0)
        row = row + as_row(jnp.sum(square, axis=1, keepdims=True), channels)
        row = row + at_lane(peak_vol, PEAK_AT)
        row = row + at_lane(peak_of(peak), PEAK_AT + 1)
        row = row + as_row(column(gain_coarse_ref[0:1, :], mine, 0), GAIN_AT)
        row = row + as_row(column(shift_coarse_ref[0:1, :], mine, 0), SHIFT_AT)
        high = row.astype(bf16).astype(f32)
        middle = (row - high).astype(bf16).astype(f32)
        low = row - high - middle
        level = lax.broadcasted_iota(jnp.int32, (16, LANES), 0)
        parts = jnp.where(
            level == 0, high, jnp.where(level == 1, middle, jnp.where(level == 2, low, 0.0))
        )
        body = (depth // 2) * channels
        load_ref[body:, 0:LANES] = parts.astype(bf16)
        load_ref[body:, LANES:] = jnp.zeros((16, load_ref.shape[1] - LANES), bf16)

    return kernel


def spread_rows(cells, store):
    count = cells.shape[1] // LANES
    parts = [cells[:, j * LANES : (j + 1) * LANES] for j in range(count)]
    turned = [pltpu.roll(part, LANES // 2, 1) for part in parts]
    lower = lax.broadcasted_iota(jnp.int32, parts[0].shape, 1) < LANES // 2
    blank = jnp.zeros_like(parts[0])
    for j in range(count):
        before = turned[j - 1] if j > 0 else blank
        after = turned[j + 1] if j + 1 < count else blank
        store(0, j, jnp.where(lower, before, turned[j]))
        store(1, j, parts[j])
        store(2, j, jnp.where(lower, turned[j], after))


def coarse_kernel(fine_cells, coarse_cells, load_rows, piece):
    def kernel(
        all_ref,
        hist_ref,
        gain_ref,
        shift_ref,
        gain_coarse_ref,
        shift_coarse_ref,
        weight_ref,
        out_ref,
        peak_ref,
        affine_ref,
        cells_ref,
        raw_ref,
        hidden_ref,
        last_ref,
    ):
        y_groups = all_ref.shape[0]
        z_groups = lax.axis_size("sz")
        span = all_ref.shape[2]
        planes = raw_ref.shape[0]
        channels = gain_ref.shape[1]
        chan_own = gain_coarse_ref.shape[1]
        chan_all = raw_ref.shape[1]
        flat = raw_ref.shape[2]
        row_len = LANES // 2
        body = load_rows - 16
        z_own = body // channels
        at_z = lax.axis_index("sz")
        totals = jnp.zeros((16, LANES), f32)
        tops = jnp.zeros((1, LANES), f32)
        gain_rows = []
        for s in range(y_groups):
            for k in range(z_groups):
                parts = all_ref[s, k * load_rows + body : (k + 1) * load_rows, 0:LANES].astype(f32)
                one = jnp.sum(parts, axis=0, keepdims=True)
                totals = totals + parts
                tops = jnp.maximum(tops, one)
                if k == 0:
                    gain_rows.append(one)
        merged = jnp.sum(totals, axis=0, keepdims=True)
        scale, offset = affine(
            column(merged, channels, 0),
            column(merged, channels, channels),
            fine_cells,
            column(gain_ref[1:2, :], channels, 0),
            column(shift_ref[1:2, :], channels, 0),
        )
        lanes = lax.broadcasted_iota(jnp.int32, (channels, LANES), 1)
        affine_ref[...] = jnp.where(lanes == 0, scale, jnp.where(lanes == 1, offset, 0.0))
        bound = bound_of(hist_ref, 2)
        peak_pool = jnp.zeros((channels, span), f32)
        for s in range(y_groups):
            for k in range(z_groups):
                for zp in range(z_own):
                    at = k * load_rows + zp * channels
                    value = activated(all_ref[s, at : at + channels, :].astype(f32), scale, offset)
                    value = value.astype(f32)
                    peak_pool = jnp.maximum(peak_pool, jnp.abs(value))
                    clipped = jnp.minimum(jnp.maximum(value, -bound), bound)
                    raw_ref[(at_z ^ k) * z_own + zp, 0:channels, s * span : (s + 1) * span] = clipped
        cells_ref[0] = jnp.zeros(cells_ref.shape[1:], bf16)
        cells_ref[planes + 1] = jnp.zeros(cells_ref.shape[1:], bf16)

        def spread_pool(z, carry):
            def store(dy, j, value):
                cells_ref[
                    z + 1, dy * channels : (dy + 1) * channels, j * LANES : (j + 1) * LANES
                ] = value.astype(bf16)

            spread_rows(raw_ref[z, 0:channels, :], store)
            return carry

        lax.fori_loop(0, planes, spread_pool, 0)
        near_weight = jnp.concatenate(
            [
                all_ref[s, z_groups * load_rows : z_groups * load_rows + piece, :]
                for s in range(y_groups)
            ],
            axis=0,
        )
        far_weight = jnp.concatenate(
            [
                all_ref[s, z_groups * load_rows + piece :, 0 : 9 * channels - span]
                for s in range(y_groups)
            ],
            axis=0,
        )

        def third(z, sums):
            totals, squares = list(sums[0]), list(sums[1])
            for t in range(flat // span):
                window = jnp.concatenate(
                    [cells_ref[z + dz, :, t * span : (t + 1) * span] for dz in range(3)], axis=0
                )
                taps = jnp.dot(near_weight, window[:span], preferred_element_type=f32)
                taps = taps + jnp.dot(far_weight, window[span:], preferred_element_type=f32)
                for s in range(y_groups):
                    for half in range(span // LANES):
                        at = s * piece
                        part = taps[at : at + piece, half * LANES : (half + 1) * LANES]
                        out = tap_sum(
                            part[:chan_own],
                            part[chan_own : 2 * chan_own],
                            part[2 * chan_own :],
                            row_len,
                        )
                        start = t * span + half * LANES
                        raw_ref[
                            z, s * chan_own : (s + 1) * chan_own, start : start + LANES
                        ] = out
                        totals[s] = totals[s] + out
                        squares[s] = squares[s] + out * out
            return tuple(totals), tuple(squares)

        blank = jnp.zeros((chan_own, LANES), f32)
        zero = tuple(blank for _ in range(y_groups))
        totals, squares = lax.fori_loop(0, planes, third, (zero, zero))
        pairs = [
            affine(
                jnp.sum(totals[s], axis=1, keepdims=True),
                jnp.sum(squares[s], axis=1, keepdims=True),
                coarse_cells,
                column(gain_rows[s], chan_own, GAIN_AT),
                column(gain_rows[s], chan_own, SHIFT_AT),
            )
            for s in range(y_groups)
        ]
        scale = jnp.concatenate([one[0] for one in pairs], axis=0)
        offset = jnp.concatenate([one[1] for one in pairs], axis=0)
        bound = bound_of(hist_ref, 3)
        hidden_ref[0] = jnp.zeros(hidden_ref.shape[1:], bf16)
        hidden_ref[planes + 1] = jnp.zeros(hidden_ref.shape[1:], bf16)

        def spread_hidden(z, peak):
            value = activated(raw_ref[z], scale, offset).astype(f32)
            for j in range(flat // LANES):
                peak = jnp.maximum(peak, jnp.abs(value[:, j * LANES : (j + 1) * LANES]))
            clipped = jnp.minimum(jnp.maximum(value, -bound), bound)

            def store(dy, j, part):
                hidden_ref[
                    z + 1, dy * chan_all : (dy + 1) * chan_all, j * LANES : (j + 1) * LANES
                ] = part.astype(bf16)

            spread_rows(clipped, store)
            return peak

        peak_coarse = lax.fori_loop(
            0, planes, spread_hidden, jnp.zeros((chan_all, LANES), f32)
        )
        weight = weight_ref[...]

        def fourth(z, sums):
            total, square = sums
            for t in range(flat // span):
                window = jnp.concatenate(
                    [hidden_ref[z + dz, :, t * span : (t + 1) * span] for dz in range(3)], axis=0
                )
                taps = jnp.dot(weight, window, preferred_element_type=f32)
                for half in range(span // LANES):
                    part = taps[:, half * LANES : (half + 1) * LANES]
                    out = tap_sum(
                        part[:chan_own],
                        part[chan_own : 2 * chan_own],
                        part[2 * chan_own :],
                        row_len,
                    )
                    start = t * span + half * LANES
                    last_ref[z, :, start : start + LANES] = out
                    total = total + out
                    square = square + out * out
            return total, square

        total, square = lax.fori_loop(0, planes, fourth, (blank, blank))
        scale, offset = affine(
            jnp.sum(total, axis=1, keepdims=True),
            jnp.sum(square, axis=1, keepdims=True),
            coarse_cells,
            column(gain_coarse_ref[1:2, :], chan_own, 0),
            column(shift_coarse_ref[1:2, :], chan_own, 0),
        )
        for i in range(z_own):
            out_ref[i] = activated(last_ref[at_z * z_own + i], scale, offset)
        row = at_lane(jnp.max(tops[:, PEAK_AT : PEAK_AT + 1], axis=1, keepdims=True), 0)
        row = row + at_lane(jnp.max(tops[:, PEAK_AT + 1 : PEAK_AT + 2], axis=1, keepdims=True), 1)
        row = row + at_lane(peak_of(peak_pool), 2)
        row = row + at_lane(peak_of(peak_coarse), 3)
        peak_ref[...] = row

    return kernel


def skip_kernel(raw_ref, affine_ref, out_ref, wide_ref):
    depth, height, channels, width = raw_ref.shape
    rows = depth * height
    scale = affine_ref[:, 0:1]
    offset = affine_ref[:, 1:2]
    for r in range(rows):
        wide_ref[pl.ds(r, channels, stride=rows), :] = activated(
            raw_ref[r // height, r % height], scale, offset
        ).astype(f32)
    out_ref[0] = wide_ref[...].reshape(channels, depth, height, width).astype(bf16)


def tap_matrix(weight):
    taps, out_chan, in_chan = weight.shape
    split = weight.reshape(taps // 3, 3, out_chan, in_chan)
    return jnp.transpose(split, (1, 2, 0, 3)).reshape(3 * out_chan, (taps // 3) * in_chan)


def shape(dims, dtype):
    return jax.ShapeDtypeStruct(dims, dtype)


def per_device(
    volume,
    amax_history,
    conv_first,
    conv_second,
    conv_third,
    conv_fourth,
    gain_fine,
    shift_fine,
    gain_coarse,
    shift_coarse,
):
    channels, depth, height, width = volume.shape[1:]
    z_groups = lax.axis_size("sz")
    y_groups = lax.axis_size("sy")
    samples = lax.axis_size("sample")
    fine_cells = float(depth * z_groups * height * y_groups * width)
    coarse_cells = fine_cells / 8
    chan_own = conv_third.shape[1]
    chan_all = conv_fourth.shape[2]
    span = (height // 2) * (width // 2)
    planes = (depth // 2) * z_groups
    flat = span * y_groups
    group = z_groups * y_groups
    load_rows = (depth // 2) * channels + 16

    cells, first, second, peak = pl.pallas_call(
        prep_kernel,
        out_shape=(
            shape((depth, height, channels, width), bf16),
            shape((HALO, height, channels, width), bf16),
            shape((HALO, height, channels, width), bf16),
            shape((1, LANES), f32),
        ),
        scratch_shapes=[pltpu.VMEM((channels * depth * height, width), f32)],
        name="prep",
    )(volume, amax_history)
    pair_first, pair_second = near("sz")
    first = lax.ppermute(first, "sz", pair_first)
    second = lax.ppermute(second, "sz", pair_second)
    deep_depth = depth + 2 * HALO
    deep, first, second = pl.pallas_call(
        deep_kernel,
        out_shape=(
            shape((deep_depth, height, channels, width), bf16),
            shape((deep_depth, HALO, channels, width), bf16),
            shape((deep_depth, HALO, channels, width), bf16),
        ),
        name="deep",
    )(cells, first, second)
    pair_first, pair_second = near("sy")
    first = lax.ppermute(first, "sy", pair_first)
    second = lax.ppermute(second, "sy", pair_second)
    raw_first, row = pl.pallas_call(
        first_kernel,
        out_shape=(
            shape((depth + 2, height + 2, channels, width), f32),
            shape((group, 1, LANES), f32),
        ),
        scratch_shapes=[pltpu.VMEM((deep_depth, height + 2 * HALO, channels, width), bf16)],
        name="first",
    )(deep, first, second, tap_matrix(conv_first), peak)
    rows = lax.all_to_all(row, ("sy", "sz"), 0, 0, tiled=True)
    raw_second, load = pl.pallas_call(
        second_kernel(fine_cells),
        out_shape=(
            shape((depth, height, channels, width), f32),
            shape((load_rows, span), bf16),
        ),
        scratch_shapes=[
            pltpu.VMEM((depth + 2, height + 2, channels, width), bf16),
            pltpu.VMEM((depth // 2, height // 2, channels, width), bf16),
        ],
        name="second",
    )(
        raw_first,
        rows,
        tap_matrix(conv_second),
        amax_history,
        gain_fine,
        shift_fine,
        gain_coarse,
        shift_coarse,
    )
    loads = [load]
    for k in range(1, z_groups):
        loads.append(lax.ppermute(load, "sz", [(i, i ^ k) for i in range(z_groups)]))
    third = tap_matrix(conv_third)
    piece = third.shape[0]
    loads.append(third[:, :span])
    loads.append(jnp.pad(third[:, span:], ((0, 0), (0, 2 * span - third.shape[1]))))
    gathered = lax.all_gather(jnp.concatenate(loads, axis=0), "sy", axis=0)
    coarse, peaks, fine_affine = pl.pallas_call(
        coarse_kernel(fine_cells, coarse_cells, load_rows, piece),
        out_shape=(
            shape((depth // 2, chan_own, flat), bf16),
            shape((1, LANES), f32),
            shape((channels, LANES), f32),
        ),
        scratch_shapes=[
            pltpu.VMEM((planes + 2, 3 * channels, flat), bf16),
            pltpu.VMEM((planes, chan_all, flat), f32),
            pltpu.VMEM((planes + 2, 3 * chan_all, flat), bf16),
            pltpu.VMEM((planes, chan_own, flat), f32),
        ],
        name="coarse",
    )(
        gathered,
        amax_history,
        gain_fine,
        shift_fine,
        gain_coarse,
        shift_coarse,
        tap_matrix(conv_fourth),
    )
    if samples <= 4:
        others = [
            lax.ppermute(peaks, "sample", [(i, (i + k) % samples) for i in range(samples)])
            for k in range(1, samples)
        ]
        for other in others:
            peaks = jnp.maximum(peaks, other)
    else:
        peaks = lax.pmax(peaks, "sample")
    skip = pl.pallas_call(
        skip_kernel,
        out_shape=shape((1, channels, depth, height, width), bf16),
        scratch_shapes=[pltpu.VMEM((channels * depth * height, width), f32)],
        name="skip",
    )(raw_second, fine_affine)
    levels = amax_history.shape[0]
    return skip, jnp.transpose(coarse, (1, 0, 2))[None], peaks[0, :levels]


def solution(mesh):
    return jax.shard_map(
        per_device,
        mesh=mesh,
        in_specs=(
            P("sample", None, "sz", "sy", None),
            P(),
            P(),
            P(),
            P(None, "sy", None),
            P(None, "sy", None),
            P(),
            P(),
            P(None, "sy"),
            P(None, "sy"),
        ),
        out_specs=(P("sample", None, "sz", "sy", None), P("sample", "sy", "sz", None), P()),
        check_vma=False,
    )
```

time: 250 us -> 79.3 us (0.32)
  blocking collectives: 142 us -> 9.2 us
  Pallas kernels: 0 us -> 27.1 us
  other arithmetic: 26.6 us -> 0.01 us
  local copies, waits for them, and re-layouts: 27.2 us -> 9.66 us
  matrix products: 11.3 us -> 0 us
  waiting for transfers between devices: 12.9 us -> 8.03 us
  between operations: 3.99 us -> 0.75 us
    psum x4 -> x0, blocking collectives: 83.4 us -> none  [the longest x2 61.8 us: fine_stats(): lax.psum((jnp.sum(flat_rows, axis=1), jnp.sum(flat_rows * flat_rows, axis...]
    pmax x1 -> x0, blocking collectives: 41.5 us -> none  [per_device(): peaks = lax.pmax(peaks, ('sample', 'sy', 'sz'))]
    pallas_call x0 -> x6, Pallas kernels: none -> 27.1 us  [the longest x1 12.1 us: per_device(): pl.pallas_call(coarse_kernel(fine_cells, coarse_cells, load_rows, piece),...]
    slice x15 -> x1, local copies, waits for them, and re-layouts: 14.3 us -> 0.01 us  [per_device(): third[:, span:]]
    ppermute x12 -> x8, starting transfers between devices: 25.3 us -> 12 us  [the longest x3 4.39 us: per_device(): lax.ppermute(load, 'sz', [(i, i ^ k) for i in range(z_groups)])]
    all_to_all x0 -> x1, starting transfers between devices: none -> 12 us  [per_device(): rows = lax.all_to_all(row, ('sy', 'sz'), 0, 0, tiled=True)]
    dot_general x36 -> x0, matrix products: 11.3 us -> none  [the longest x18 7.54 us: level_one_conv(): jnp.dot(matrix, window, preferred_element_type=jnp.float32)]
    concatenate x7 -> x0, other arithmetic: 9.29 us -> none  [the longest x3 3.83 us: padded_2(): jnp.concatenate([lax.ppermute(tail, axis, [(i, (i + 1) % count) for i in...]
  transfers between devices with their start and end apart: 12 -> 9, of which waited for: 6 -> 4; matrix products, arithmetic and copies ran while one was open for 6% -> 7% of each run, Pallas kernels for 0% -> 3%
where the time goes in v1:
time: 79.3 us; the launch traced here: 78.8 us
  Pallas kernels  27.1 us (34%)
  starting transfers between devices  24 us (30%)
  local copies, waits for them, and re-layouts  9.66 us (12%)
  blocking collectives  9.2 us (12%)
  waiting for transfers between devices  8.03 us (10%)
    pallas_call x1, Pallas kernels, per_device(): pl.pallas_call(coarse_kernel(fine_cells, coarse_cells, load_rows, piece),...  12.1 us
    all_to_all x1, starting transfers between devices, per_device(): rows = lax.all_to_all(row, ('sy', 'sz'), 0, 0, tiled=True)  12 us
    all_gather x1, blocking collectives, per_device(): gathered = lax.all_gather(jnp.concatenate(loads, axis=0), 'sy', axis=0)  9.2 us
    unnamed x28, local copies, waits for them, and re-layouts  5.9 us
    pallas_call x1, Pallas kernels, per_device(): pl.pallas_call(first_kernel, out_shape=(shape((depth + 2, height + 2, cha...  4.51 us
    ppermute x3, starting transfers between devices, per_device(): lax.ppermute(load, 'sz', [(i, i ^ k) for i in range(z_groups)])  4.39 us
    pallas_call x1, Pallas kernels, per_device(): pl.pallas_call(second_kernel(fine_cells), out_shape=(shape((depth, height...  3.83 us
    all_to_all x1, waiting for transfers between devices, per_device(): rows = lax.all_to_all(row, ('sy', 'sz'), 0, 0, tiled=True)  3.32 us
  transfers between devices with their start and end apart: 9, of which 4 were waited for; matrix products, arithmetic and copies ran while one was open for 7% of the time, Pallas kernels for 3%

profile of v1, /device:TPU:0, one launch (start us, length us, event | category | flops | bytes accessed | tf_op | source)
XLA Modules:
  0.0 78.8 jit_solution(1587097212659598712)
XLA Ops:
  0.6 2.3 %prep.1 = (bf16[4,8,32,128]{3,2,1,0:T(8,128)(2,1)}, bf16[2,8,32,128]{3,2,1,0:T(8,128)(2,1)}, bf16[2,8,32,128]{3,2,1,0:T(8,128)(2,1)}, f32[1,128]{1,0:T(1,128)}) custom-call(bf16[1,32,4,8,128]{4,3,2,1,0:T(8,128)(2,1)} %vol_ref.1, f32[4,16]{1,0:T(4,128)} %hist_ref.5), custom_call_target="tpu_custom_call" | custom-call | tf_op jit(solution)/shard_map/prep/pallas_call | solution.py:532
  2.9 3.1 %collective-permute-start = (bf16[2,8,32,128]{3,2,1,0:T(8,128)(2,1)}, bf16[2,8,32,128]{3,2,1,0:T(8,128)(2,1)S(1)}, u32[]{:S(2)}, u32[]{:S(2)}) collective-permute-start(bf16[2,8,32,128]{3,2,1,0:T(8,128)(2,1)} %get-tuple-element.18), channel_id=1, source_target_pairs={{0,1},{1,0},{2,3},{3,2},{4,5},{5,4},{6,7},{7,6},{8,9},{9,8},{10,11... | collective-permute-start | bytes 393224 | tf_op jit(solution)/shard_map/ppermute | solution.py:544
  5.9 1.6 %collective-permute-start.1 = (bf16[2,8,32,128]{3,2,1,0:T(8,128)(2,1)}, bf16[2,8,32,128]{3,2,1,0:T(8,128)(2,1)S(1)}, u32[]{:S(2)}, u32[]{:S(2)}) collective-permute-start(bf16[2,8,32,128]{3,2,1,0:T(8,128)(2,1)} %get-tuple-element.19), channel_id=1, source_target_pairs={{0,0},{1,2},{2,1},{3,3},{4,4},{5,6},{6,5},{7,7},{8,8},{9,10},{10,9... | collective-permute-start | bytes 393224 | tf_op jit(solution)/shard_map/ppermute | solution.py:545
  7.5 2.2 %collective-permute-done.got_first_ref = bf16[2,8,32,128]{3,2,1,0:T(8,128)(2,1)S(1)} collective-permute-done((bf16[2,8,32,128]{3,2,1,0:T(8,128)(2,1)}, bf16[2,8,32,128]{3,2,1,0:T(8,128)(2,1)S(1)}, u32[]{:S(2)}, u32[]{:S(2)}) %collective-permute-start) | collective-permute-done | bytes 131104 | tf_op jit(solution)/shard_map/ppermute | solution.py:544
  9.6 0.0 copy-start.4
  9.6 0.0 collective-permute-done.1.got_second_ref
  9.6 0.0 copy-start.5
  9.6 0.6 copy-done.4
  10.3 0.1 copy-done.5
  10.4 0.0 copy-start
  10.4 2.1 %deep.1 = (bf16[8,8,32,128]{3,2,1,0:T(8,128)(2,1)}, bf16[8,2,32,128]{3,2,1,0:T(8,128)(2,1)}, bf16[8,2,32,128]{3,2,1,0:T(8,128)(2,1)}) custom-call(bf16[4,8,32,128]{3,2,1,0:T(8,128)(2,1)} %get-tuple-element.17.cells_ref, bf16[2,8,32,128]{3,2,1,0:T(8,128)(2,1)} %copy-done.4, bf16[2,8,32,128]{3,2,1,0:T(8,128)(2,1)} %copy-done.5), custom_call_target="tpu_custom_call" | custom-call | tf_op jit(solution)/shard_map/deep/pallas_call | solution.py:547
  12.4 0.0 collective-permute-start.2
  12.4 1.6 %collective-permute-start.3 = (bf16[8,2,32,128]{3,2,1,0:T(8,128)(2,1)}, bf16[8,2,32,128]{3,2,1,0:T(8,128)(2,1)S(1)}, u32[]{:S(2)}, u32[]{:S(2)}) collective-permute-start(bf16[8,2,32,128]{3,2,1,0:T(8,128)(2,1)} %get-tuple-element.22), channel_id=1, source_target_pairs={{0,0},{4,8},{8,4},{12,12},{1,1},{5,9},{9,5},{13,13},{2,2},{6,10},{... | collective-permute-start | bytes 393224 | tf_op jit(solution)/shard_map/ppermute | solution.py:558
  14.0 0.0 copy-done
  14.0 0.2 copy.18
  14.2 0.2 reshape.31
  14.4 0.7 copy.19.weight_ref
  15.1 0.0 collective-permute-done.2.got_first_ref
  15.1 0.0 copy-start.2
  15.1 0.0 collective-permute-done.3.got_second_ref
  15.1 0.0 copy-start.3
  15.1 0.6 copy-done.2
  15.7 0.0 copy-done.3
  15.8 0.0 copy-start.1
  15.8 4.5 %first.1 = (f32[6,10,32,128]{3,2,1,0:T(8,128)}, f32[16,1,128]{2,1,0:T(1,128)}) custom-call(bf16[8,8,32,128]{3,2,1,0:T(8,128)(2,1)} %get-tuple-element.20.deep_ref, bf16[8,2,32,128]{3,2,1,0:T(8,128)(2,1)} %copy-done.2, bf16[8,2,32,128]{3,2,1,0:T(8,128)(2,1)} %copy-done.3, bf16[96,288]{1,0:T(8,128)(2,1)} %copy.19.weight_ref, f32[1,128]{1,0:T(1,128)} %get-tuple-element.23.peak_ref), custom_call_target="tpu_custom_call" | custom-call | tf_op jit(solution)/shard_map/first/pallas_call | solution.py:559
  20.3 12.0 %all-to-all-start = ((f32[16,1,128]{2,1,0:T(1,128)}), f32[16,1,128]{2,1,0:T(1,128)S(1)}, u32[]{:S(2)}, u32[]{:S(2)}) async-start(f32[16,1,128]{2,1,0:T(1,128)} %get-tuple-element.25), calls=%async_computation | async-start | bytes 16384 | tf_op jit(solution)/shard_map/all_to_all | solution.py:568
  32.3 0.0 copy-done.1
  32.3 0.2 copy.20
  32.5 0.2 reshape.33
  32.7 0.0 copy-start.6
  32.7 0.7 copy.21.weight_ref
  33.4 0.2 copy-done.6
  33.6 0.0 copy-start.7
  33.6 0.1 reshape.35
  33.8 0.7 copy-done.7
  34.6 0.8 %reshape.37.weight_ref = bf16[48,576]{1,0:T(8,128)(2,1)} reshape(bf16[3,16,9,64]{3,2,1,0:T(8,128)(2,1)S(1)} %bitcast.26) | data formatting | bytes 110592 | tf_op jit(solution)/shard_map/reshape | solution.py:499
  35.4 3.3 %all-to-all-done.rows_ref = f32[16,1,128]{2,1,0:T(1,128)S(1)} async-done(((f32[16,1,128]{2,1,0:T(1,128)}), f32[16,1,128]{2,1,0:T(1,128)S(1)}, u32[]{:S(2)}, u32[]{:S(2)}) %all-to-all-start) | async-done | bytes 8224 | tf_op jit(solution)/shard_map/all_to_all | solution.py:568
  38.7 0.0 copy-start.9
  38.7 0.6 copy-done.9
  39.3 3.8 %second.1 = (f32[4,8,32,128]{3,2,1,0:T(8,128)}, bf16[80,256]{1,0:T(8,128)(2,1)}) custom-call(f32[6,10,32,128]{3,2,1,0:T(8,128)} %get-tuple-element.24.raw_ref, f32[16,1,128]{2,1,0:T(1,128)} %copy-done.9, bf16[96,288]{1,0:T(8,128)(2,1)} %copy.21.weight_ref, f32[4,16]{1,0:T(4,128)} %hist_ref.5, f32[2,32]{1,0:T(2,128)} %gain_ref.3, f32[2,32]{1,0:T(2,128)} %shift_ref.3, ...), custom_call_target="tpu_custom_call" | custom-call | tf_op jit(solution)/shard_map/second/pallas_call | solution.py:569
  43.1 0.0 copy-start.8
  43.1 0.5 collective-permute-start.4
  43.7 0.8 %constant_dynamic-update-slice_fusion.3 = bf16[416,256]{1,0:T(8,128)(2,1)S(1)} fusion(bf16[80,256]{1,0:T(8,128)(2,1)} %get-tuple-element.27), kind=kLoop, calls=%fused_computation.7 | loop fusion | bytes 81920
  44.5 0.0 copy-done.8
  44.5 0.6 collective-permute-start.5
  45.1 3.2 %collective-permute-start.6 = (bf16[80,256]{1,0:T(8,128)(2,1)S(1)}, bf16[80,256]{1,0:T(8,128)(2,1)S(1)}, u32[]{:S(2)}, u32[]{:S(2)}) collective-permute-start(bf16[80,256]{1,0:T(8,128)(2,1)S(1)} %copy-done.8), channel_id=1, source_target_pairs={{0,3},{1,2},{2,1},{3,0},{4,7},{5,6},{6,5},{7,4},{8,11},{9,10},{10,... | collective-permute-start | bytes 122888 | tf_op jit(solution)/shard_map/ppermute | solution.py:592
  48.3 0.0 collective-permute-done.4
  48.3 1.4 %collective-permute-done.5 = bf16[80,256]{1,0:T(8,128)(2,1)S(1)} collective-permute-done((bf16[80,256]{1,0:T(8,128)(2,1)S(1)}, bf16[80,256]{1,0:T(8,128)(2,1)S(1)}, u32[]{:S(2)}, u32[]{:S(2)}) %collective-permute-start.5) | collective-permute-done | bytes 40992 | tf_op jit(solution)/shard_map/ppermute | solution.py:592
  49.8 1.1 %collective-permute-done.6 = bf16[80,256]{1,0:T(8,128)(2,1)S(1)} collective-permute-done((bf16[80,256]{1,0:T(8,128)(2,1)S(1)}, bf16[80,256]{1,0:T(8,128)(2,1)S(1)}, u32[]{:S(2)}, u32[]{:S(2)}) %collective-permute-start.6) | collective-permute-done | bytes 40992 | tf_op jit(solution)/shard_map/ppermute | solution.py:592
  50.9 9.2 %all-gather = bf16[1664,256]{1,0:T(8,128)(2,1)} all-gather(bf16[416,256]{1,0:T(8,128)(2,1)S(1)} %pad_dynamic-update-slice_fusion), channel_id=2, replica_groups=mesh['sample'=2,'sy'=4,'sz'=4] {'sy'}, dimensions={0}, use_global_device_ids=true | all-gather | bytes 1064960 | tf_op jit(solution)/shard_map/all_gather | solution.py:597
  60.1 12.1 %coarse.1 = (bf16[2,16,1024]{2,1,0:T(8,128)(2,1)}, f32[1,128]{1,0:T(1,128)}, f32[32,128]{1,0:T(8,128)}) custom-call(bf16[4,416,256]{2,1,0:T(8,128)(2,1)} %bitcast.22, f32[4,16]{1,0:T(4,128)} %hist_ref.5, f32[2,32]{1,0:T(2,128)} %gain_ref.3, f32[2,32]{1,0:T(2,128)} %shift_ref.3, f32[2,16]{1,0:T(2,128)} %gain_coarse_ref.3, f32[2,16]{1,0:T(2,128)} %shift_coarse_ref.3, ...), custom_call_target="tpu_custom_call" | custom-call | tf_op jit(solution)/shard_map/coarse/pallas_call | solution.py:598
  72.2 0.0 copy-start.10
  72.2 0.7 copy-done.10
  72.9 1.5 %collective-permute-start.7 = (f32[1,128]{1,0:T(1,128)S(1)}, f32[1,128]{1,0:T(1,128)S(1)}, u32[]{:S(2)}, u32[]{:S(2)}) collective-permute-start(f32[1,128]{1,0:T(1,128)S(1)} %copy-done.10), channel_id=1, source_target_pairs={{0,16},{16,0},{1,17},{17,1},{2,18},{18,2},{3,19},{19,3},{4,20},{20... | collective-permute-start | bytes 1544 | tf_op jit(solution)/shard_map/ppermute | solution.py:623
  74.4 1.5 %copy.24 = bf16[1,16,2,1024]{3,2,1,0:T(2,128)(2,1)} copy(bf16[1,16,2,1024]{3,1,2,0:T(8,128)(2,1)} %bitcast.31) | data formatting | bytes 131072
  75.9 2.4 %skip.1 = bf16[1,32,4,8,128]{4,3,2,1,0:T(8,128)(2,1)} custom-call(f32[4,8,32,128]{3,2,1,0:T(8,128)} %get-tuple-element.26.raw_ref, f32[32,128]{1,0:T(8,128)} %get-tuple-element.28.affine_ref), custom_call_target="tpu_custom_call" | custom-call | tf_op jit(solution)/shard_map/skip/pallas_call | solution.py:630
  78.3 0.0 collective-permute-done.7
  78.3 0.5 slice_bitcast_fusion
  (9 shorter events, 0.1 us)
Async XLA Ops:
  2.9 6.8 %collective-permute-start = (bf16[2,8,32,128]{3,2,1,0:T(8,128)(2,1)}, bf16[2,8,32,128]{3,2,1,0:T(8,128)(2,1)S(1)}, u32[]{:S(2)}, u32[]{:S(2)}) collective-permute-start(bf16[2,8,32,128]{3,2,1,0:T(8,128)(2,1)} %get-tuple-element.18), channel_id=1, source_target_pairs={{0,1},{1,0},{2,3},{3,2},{4,5},{5,4},{6,7},{7,6},{8,9},{9,8},{10,11... | collective-permute-start | bytes 393224 | tf_op jit(solution)/shard_map/ppermute | solution.py:544
  5.9 3.7 %collective-permute-start.1 = (bf16[2,8,32,128]{3,2,1,0:T(8,128)(2,1)}, bf16[2,8,32,128]{3,2,1,0:T(8,128)(2,1)S(1)}, u32[]{:S(2)}, u32[]{:S(2)}) collective-permute-start(bf16[2,8,32,128]{3,2,1,0:T(8,128)(2,1)} %get-tuple-element.19), channel_id=1, source_target_pairs={{0,0},{1,2},{2,1},{3,3},{4,4},{5,6},{6,5},{7,7},{8,8},{9,10},{10,9... | collective-permute-start | bytes 393224 | tf_op jit(solution)/shard_map/ppermute | solution.py:545
  9.6 0.6 copy-start.4
  9.6 0.7 copy-start.5
  10.4 3.6 %copy-start = (bf16[27,32,32]{2,1,0:T(8,128)(2,1)S(1)}, bf16[27,32,32]{2,1,0:T(8,128)(2,1)}, u32[]{:S(2)}) copy-start(bf16[27,32,32]{2,1,0:T(8,128)(2,1)} %param.12) | copy-start | bytes 165892
  12.4 2.7 %collective-permute-start.2 = (bf16[8,2,32,128]{3,2,1,0:T(8,128)(2,1)}, bf16[8,2,32,128]{3,2,1,0:T(8,128)(2,1)S(1)}, u32[]{:S(2)}, u32[]{:S(2)}) collective-permute-start(bf16[8,2,32,128]{3,2,1,0:T(8,128)(2,1)} %get-tuple-element.21), channel_id=1, source_target_pairs={{0,4},{4,0},{8,12},{12,8},{1,5},{5,1},{9,13},{13,9},{2,6},{6,2},{1... | collective-permute-start | bytes 393224 | tf_op jit(solution)/shard_map/ppermute | solution.py:557
  12.4 2.7 %collective-permute-start.3 = (bf16[8,2,32,128]{3,2,1,0:T(8,128)(2,1)}, bf16[8,2,32,128]{3,2,1,0:T(8,128)(2,1)S(1)}, u32[]{:S(2)}, u32[]{:S(2)}) collective-permute-start(bf16[8,2,32,128]{3,2,1,0:T(8,128)(2,1)} %get-tuple-element.22), channel_id=1, source_target_pairs={{0,0},{4,8},{8,4},{12,12},{1,1},{5,9},{9,5},{13,13},{2,2},{6,10},{... | collective-permute-start | bytes 393224 | tf_op jit(solution)/shard_map/ppermute | solution.py:558
  15.1 0.7 copy-start.2
  15.1 0.7 copy-start.3
  15.8 16.5 %copy-start.1 = (bf16[27,32,32]{2,1,0:T(8,128)(2,1)S(1)}, bf16[27,32,32]{2,1,0:T(8,128)(2,1)}, u32[]{:S(2)}) copy-start(bf16[27,32,32]{2,1,0:T(8,128)(2,1)} %param.13) | copy-start | bytes 165892
  20.3 18.4 %all-to-all-start = ((f32[16,1,128]{2,1,0:T(1,128)}), f32[16,1,128]{2,1,0:T(1,128)S(1)}, u32[]{:S(2)}, u32[]{:S(2)}) async-start(f32[16,1,128]{2,1,0:T(1,128)} %get-tuple-element.25), calls=%async_computation | async-start | bytes 16384 | tf_op jit(solution)/shard_map/all_to_all | solution.py:568
  32.7 0.9 %copy-start.6 = (bf16[27,16,32]{2,1,0:T(8,128)(2,1)S(1)}, bf16[27,16,32]{2,1,0:T(8,128)(2,1)}, u32[]{:S(2)}) copy-start(bf16[27,16,32]{2,1,0:T(8,128)(2,1)} %param.14) | copy-start | bytes 82948
  33.6 0.9 %copy-start.7 = (bf16[27,16,64]{2,1,0:T(8,128)(2,1)S(1)}, bf16[27,16,64]{2,1,0:T(8,128)(2,1)}, u32[]{:S(2)}) copy-start(bf16[27,16,64]{2,1,0:T(8,128)(2,1)} %param.15) | copy-start | bytes 165892
  38.7 0.6 copy-start.9
  43.1 1.4 %copy-start.8 = (bf16[80,256]{1,0:T(8,128)(2,1)S(1)}, bf16[80,256]{1,0:T(8,128)(2,1)}, u32[]{:S(2)}) copy-start(bf16[80,256]{1,0:T(8,128)(2,1)} %get-tuple-element.27) | copy-start | bytes 122884
  43.1 5.2 %collective-permute-start.4 = (bf16[80,256]{1,0:T(8,128)(2,1)}, bf16[80,256]{1,0:T(8,128)(2,1)S(1)}, u32[]{:S(2)}, u32[]{:S(2)}) collective-permute-start(bf16[80,256]{1,0:T(8,128)(2,1)} %get-tuple-element.27), channel_id=1, source_target_pairs={{0,1},{1,0},{2,3},{3,2},{4,5},{5,4},{6,7},{7,6},{8,9},{9,8},{10,11... | collective-permute-start | bytes 122888 | tf_op jit(solution)/shard_map/ppermute | solution.py:592
  44.5 5.3 %collective-permute-start.5 = (bf16[80,256]{1,0:T(8,128)(2,1)S(1)}, bf16[80,256]{1,0:T(8,128)(2,1)S(1)}, u32[]{:S(2)}, u32[]{:S(2)}) collective-permute-start(bf16[80,256]{1,0:T(8,128)(2,1)S(1)} %copy-done.8), channel_id=1, source_target_pairs={{0,2},{1,3},{2,0},{3,1},{4,6},{5,7},{6,4},{7,5},{8,10},{9,11},{10,... | collective-permute-start | bytes 122888 | tf_op jit(solution)/shard_map/ppermute | solution.py:592
  45.1 5.8 %collective-permute-start.6 = (bf16[80,256]{1,0:T(8,128)(2,1)S(1)}, bf16[80,256]{1,0:T(8,128)(2,1)S(1)}, u32[]{:S(2)}, u32[]{:S(2)}) collective-permute-start(bf16[80,256]{1,0:T(8,128)(2,1)S(1)} %copy-done.8), channel_id=1, source_target_pairs={{0,3},{1,2},{2,1},{3,0},{4,7},{5,6},{6,5},{7,4},{8,11},{9,10},{10,... | collective-permute-start | bytes 122888 | tf_op jit(solution)/shard_map/ppermute | solution.py:592
  72.2 0.7 copy-start.10
  72.9 5.4 %collective-permute-start.7 = (f32[1,128]{1,0:T(1,128)S(1)}, f32[1,128]{1,0:T(1,128)S(1)}, u32[]{:S(2)}, u32[]{:S(2)}) collective-permute-start(f32[1,128]{1,0:T(1,128)S(1)} %copy-done.10), channel_id=1, source_target_pairs={{0,16},{16,0},{1,17},{17,1},{2,18},{18,2},{3,19},{19,3},{4,20},{20... | collective-permute-start | bytes 1544 | tf_op jit(solution)/shard_map/ppermute | solution.py:623

commit v2 on v1

--- a/solution.py
+++ b/solution.py
@@ -12,8 +12,10 @@
 LANES = 128
 HALO = 2
 PEAK_AT = 64
+CODE_AT = 66
 GAIN_AT = 80
 SHIFT_AT = 96
+CODE_SPAN = 83.0
 
 
 def near(axis):
@@ -50,19 +52,43 @@
 
 def activated(values, scale, offset):
     normed = values * scale + offset
-    return jnp.where(normed >= 0, normed, leak_slope * normed).astype(bf16)
+    return jnp.maximum(normed, leak_slope * normed).astype(bf16)
 
 
 def peak_of(values):
+    values = values.astype(f32)
     return jnp.max(jnp.max(values, axis=1, keepdims=True), axis=0, keepdims=True)
 
 
 def bounded(values, bound):
-    return jnp.minimum(jnp.maximum(values.astype(f32), -bound), bound).astype(bf16)
+    return jnp.minimum(jnp.maximum(values, -bound), bound)
 
 
 def bound_of(hist_ref, level):
-    return jnp.max(hist_ref[level : level + 1, :], axis=1, keepdims=True)
+    return jnp.max(hist_ref[level : level + 1, :], axis=1, keepdims=True).astype(bf16)
+
+
+def matrix_of(weight, taps_ref):
+    taps, out_chan, in_chan = weight.shape
+    for dx in range(3):
+        taps_ref[dx * out_chan : (dx + 1) * out_chan, :] = jnp.concatenate(
+            [weight[3 * j + dx] for j in range(taps // 3)], axis=1
+        )
+
+
+def matrix_kernel(
+    peak_ref, first_ref, second_ref, third_ref, fourth_ref, m1_ref, m2_ref, m3_ref, m4_ref, wide_ref
+):
+    matrix_of(first_ref, m1_ref)
+    matrix_of(second_ref, m2_ref)
+    matrix_of(fourth_ref, m4_ref)
+    matrix_of(third_ref, wide_ref)
+    rows, span = m3_ref.shape[0] // 2, m3_ref.shape[1]
+    rest = wide_ref.shape[1] - span
+    m3_ref[:rows, :] = wide_ref[:, :span]
+    m3_ref[rows:, :] = jnp.concatenate(
+        [wide_ref[:, span:], jnp.zeros((rows, span - rest), bf16)], axis=1
+    )
 
 
 def tap_sum(left, middle, right, period):
@@ -81,7 +107,7 @@
     bound = bound_of(hist_ref, 0)
     for r in range(rows):
         cells_ref[r // height, r % height] = bounded(
-            wide_ref[pl.ds(r, channels, stride=rows), :], bound
+            wide_ref[pl.ds(r, channels, stride=rows), :].astype(bf16), bound
         )
     even = lax.axis_index("sz") % 2 == 0
     start_first = jnp.where(even, depth - HALO, 0)
@@ -100,17 +126,28 @@
     return below, above
 
 
-def deep_kernel(cells_ref, got_first_ref, got_second_ref, deep_ref, first_ref, second_ref):
+def deep_kernel(
+    cells_ref, got_first_ref, got_second_ref, matrix_ref, first_ref, second_ref, done
+):
     depth, height = cells_ref.shape[:2]
-    below, above = sides("sz", got_first_ref[...], got_second_ref[...])
-    deep_ref[0:HALO] = below
-    deep_ref[HALO : HALO + depth] = cells_ref[...]
-    deep_ref[HALO + depth :] = above
     even = lax.axis_index("sy") % 2 == 0
-    start_first = jnp.where(even, height - HALO, 0)
-    start_second = jnp.where(even, 0, height - HALO)
-    first_ref[...] = deep_ref[:, pl.ds(start_first, HALO)]
-    second_ref[...] = deep_ref[:, pl.ds(start_second, HALO)]
+    starts = (jnp.where(even, height - HALO, 0), jnp.where(even, 0, height - HALO))
+    odd_z = lax.axis_index("sz") % 2
+    places = (odd_z * 0 + (1 - odd_z) * (HALO + depth), odd_z * (HALO + depth))
+    copies = []
+    for side, (start, out_ref) in enumerate(zip(starts, (first_ref, second_ref))):
+        rows = pl.ds(start, HALO)
+        jobs = (
+            (got_first_ref.at[:, rows], out_ref.at[pl.ds(places[0], HALO)]),
+            (got_second_ref.at[:, rows], out_ref.at[pl.ds(places[1], HALO)]),
+            (cells_ref.at[:, rows], out_ref.at[HALO : HALO + depth]),
+        )
+        for which, (source, target) in enumerate(jobs):
+            copies.append(pltpu.make_async_copy(source, target, done.at[3 * side + which]))
+    for copy in copies:
+        copy.start()
+    for copy in copies:
+        copy.wait()
 
 
 def conv_rows(cells_ref, weight, z, y, out_chan):
@@ -137,15 +174,41 @@
 
 
 def first_kernel(
-    deep_ref, got_first_ref, got_second_ref, weight_ref, peak_ref, raw_ref, row_ref, cells_ref
+    own_ref,
+    z_first_ref,
+    z_second_ref,
+    y_first_ref,
+    y_second_ref,
+    weight_ref,
+    peak_ref,
+    raw_ref,
+    row_ref,
+    cells_ref,
 ):
     depth, height = raw_ref.shape[:2]
     channels = raw_ref.shape[2]
-    inner = deep_ref.shape[1]
-    below, above = sides("sy", got_first_ref[...], got_second_ref[...])
+    own_depth, own_height = own_ref.shape[:2]
+    below, above = sides("sz", z_first_ref[...], z_second_ref[...])
+    rows = slice(HALO, HALO + own_height)
+    cells_ref[0:HALO, rows] = below
+    cells_ref[HALO : HALO + own_depth, rows] = own_ref[...]
+    cells_ref[HALO + own_depth :, rows] = above
+    below, above = sides("sy", y_first_ref[...], y_second_ref[...])
     cells_ref[:, 0:HALO] = below
-    cells_ref[:, HALO : HALO + inner] = deep_ref[...]
-    cells_ref[:, HALO + inner :] = above
+    cells_ref[:, HALO + own_height :] = above
+
+    @pl.when(lax.axis_index("sz") == 0)
+    def _():
+        for edge in (slice(0, HALO), slice(HALO + own_height, 2 * HALO + own_height)):
+            cells_ref[0:HALO, edge] = jnp.zeros((HALO, HALO) + own_ref.shape[2:], bf16)
+
+    @pl.when(lax.axis_index("sz") == lax.axis_size("sz") - 1)
+    def _():
+        for edge in (slice(0, HALO), slice(HALO + own_height, 2 * HALO + own_height)):
+            cells_ref[HALO + own_depth :, edge] = jnp.zeros(
+                (HALO, HALO) + own_ref.shape[2:], bf16
+            )
+
     weight = weight_ref[...]
 
     def plane(z, sums):
@@ -204,28 +267,28 @@
 
         def plane(z, peak):
             inside_z = ((z > 0) | (at_z > 0)) & ((z < wide_depth - 1) | (at_z < last_z))
-            own = jnp.where((z >= 1) & (z < wide_depth - 1), 1.0, 0.0).astype(f32)
+            own = jnp.where((z >= 1) & (z < wide_depth - 1), 1.0, 0.0).astype(bf16)
             for y in range(wide_height):
                 inside = inside_z
                 if y == 0:
                     inside = inside & (at_y > 0)
                 if y == wide_height - 1:
                     inside = inside & (at_y < last_y)
-                hidden = activated(raw_ref[z, y], scale, offset).astype(f32)
+                hidden = activated(raw_ref[z, y], scale, offset)
                 if 1 <= y < wide_height - 1:
                     peak = jnp.maximum(peak, jnp.abs(hidden) * own)
-                clipped = jnp.minimum(jnp.maximum(hidden, -bound), bound)
-                hidden_ref[z, y] = jnp.where(inside, clipped, 0.0).astype(bf16)
+                inside = jnp.where(inside, 1.0, 0.0).astype(bf16)
+                hidden_ref[z, y] = bounded(hidden, bound) * inside
             return peak
 
         blank = jnp.zeros((channels, width), f32)
-        peak = lax.fori_loop(0, wide_depth, plane, blank)
+        peak = lax.fori_loop(0, wide_depth, plane, jnp.zeros((channels, width), bf16))
         weight = weight_ref[...]
         sign = jnp.where(column(gain_ref[1:2, :], channels, 0) >= 0, 1.0, -1.0).astype(f32)
         half_height = height // 2
 
         def pair(zp, sums):
-            total, square = sums
+            total, square, least, most = sums
             for yp in range(half_height):
                 best = None
                 for dz in range(2):
@@ -237,10 +300,18 @@
                         signed = outs[half] * sign
                         best = signed if best is None else jnp.maximum(best, signed)
                 best = jnp.maximum(best, pltpu.roll(best, LANES - 1, 1)) * sign
-                pool_ref[zp, yp] = best.astype(bf16)
-            return total, square
-
-        total, square = lax.fori_loop(0, depth // 2, pair, (blank, blank))
+                pool_ref[zp, yp] = best
+                least = jnp.minimum(least, best)
+                most = jnp.maximum(most, best)
+            return total, square, least, most
+
+        total, square, least, most = lax.fori_loop(
+            0, depth // 2, pair, (blank, blank, blank + 1e30, blank - 1e30)
+        )
+        most, least = peak_of(most), -peak_of(-least)
+        center = 0.5 * (most + least)
+        reach = jnp.maximum(0.5 * (most - least), 1e-30)
+        rate = CODE_SPAN / reach
         pick = jnp.where(
             lax.broadcasted_iota(jnp.int32, (2 * LANES, LANES), 0)
             == 2 * lax.broadcasted_iota(jnp.int32, (2 * LANES, LANES), 1),
@@ -250,6 +321,7 @@
         for zp in range(depth // 2):
             for yq in range(half_height // 2):
                 both = jnp.concatenate([pool_ref[zp, 2 * yq], pool_ref[zp, 2 * yq + 1]], axis=1)
+                both = jnp.exp((both - center) * rate).astype(bf16)
                 load_ref[
                     zp * channels : (zp + 1) * channels, yq * LANES : (yq + 1) * LANES
                 ] = jnp.dot(both, pick, preferred_element_type=f32).astype(bf16)
@@ -258,6 +330,8 @@
         row = row + as_row(jnp.sum(square, axis=1, keepdims=True), channels)
         row = row + at_lane(peak_vol, PEAK_AT)
         row = row + at_lane(peak_of(peak), PEAK_AT + 1)
+        row = row + at_lane(center, CODE_AT)
+        row = row + at_lane(reach / CODE_SPAN, CODE_AT + 1)
         row = row + as_row(column(gain_coarse_ref[0:1, :], mine, 0), GAIN_AT)
         row = row + as_row(column(shift_coarse_ref[0:1, :], mine, 0), SHIFT_AT)
         high = row.astype(bf16).astype(f32)
@@ -288,46 +362,38 @@
         store(2, j, jnp.where(lower, turned[j], after))
 
 
-def coarse_kernel(fine_cells, coarse_cells, load_rows, piece):
+def third_kernel(fine_cells, coarse_cells, load_rows, piece):
     def kernel(
         all_ref,
         hist_ref,
         gain_ref,
         shift_ref,
-        gain_coarse_ref,
-        shift_coarse_ref,
-        weight_ref,
         out_ref,
         peak_ref,
         affine_ref,
+        pool_ref,
         cells_ref,
         raw_ref,
-        hidden_ref,
-        last_ref,
     ):
         y_groups = all_ref.shape[0]
         z_groups = lax.axis_size("sz")
         span = all_ref.shape[2]
-        planes = raw_ref.shape[0]
+        planes, chan_all, flat = raw_ref.shape
         channels = gain_ref.shape[1]
-        chan_own = gain_coarse_ref.shape[1]
-        chan_all = raw_ref.shape[1]
-        flat = raw_ref.shape[2]
+        chan_own = piece // 3
         row_len = LANES // 2
         body = load_rows - 16
         z_own = body // channels
         at_z = lax.axis_index("sz")
         totals = jnp.zeros((16, LANES), f32)
         tops = jnp.zeros((1, LANES), f32)
-        gain_rows = []
+        rows = {}
         for s in range(y_groups):
             for k in range(z_groups):
                 parts = all_ref[s, k * load_rows + body : (k + 1) * load_rows, 0:LANES].astype(f32)
-                one = jnp.sum(parts, axis=0, keepdims=True)
                 totals = totals + parts
-                tops = jnp.maximum(tops, one)
-                if k == 0:
-                    gain_rows.append(one)
+                rows[s, k] = jnp.sum(parts, axis=0, keepdims=True)
+                tops = jnp.maximum(tops, rows[s, k])
         merged = jnp.sum(totals, axis=0, keepdims=True)
         scale, offset = affine(
             column(merged, channels, 0),
@@ -339,16 +405,21 @@
         lanes = lax.broadcasted_iota(jnp.int32, (channels, LANES), 1)
         affine_ref[...] = jnp.where(lanes == 0, scale, jnp.where(lanes == 1, offset, 0.0))
         bound = bound_of(hist_ref, 2)
-        peak_pool = jnp.zeros((channels, span), f32)
+        peak_pool = jnp.zeros((channels, span), bf16)
         for s in range(y_groups):
             for k in range(z_groups):
+                center = rows[s, k][:, CODE_AT : CODE_AT + 1]
+                reach = rows[s, k][:, CODE_AT + 1 : CODE_AT + 2]
+                rate = scale * reach
+                start = scale * center + offset
                 for zp in range(z_own):
                     at = k * load_rows + zp * channels
-                    value = activated(all_ref[s, at : at + channels, :].astype(f32), scale, offset)
-                    value = value.astype(f32)
+                    code = jnp.log(all_ref[s, at : at + channels, :].astype(f32))
+                    value = activated(code, rate, start)
                     peak_pool = jnp.maximum(peak_pool, jnp.abs(value))
-                    clipped = jnp.minimum(jnp.maximum(value, -bound), bound)
-                    raw_ref[(at_z ^ k) * z_own + zp, 0:channels, s * span : (s + 1) * span] = clipped
+                    pool_ref[(at_z ^ k) * z_own + zp, :, s * span : (s + 1) * span] = bounded(
+                        value, bound
+                    )
         cells_ref[0] = jnp.zeros(cells_ref.shape[1:], bf16)
         cells_ref[planes + 1] = jnp.zeros(cells_ref.shape[1:], bf16)
 
@@ -356,24 +427,18 @@
             def store(dy, j, value):
                 cells_ref[
                     z + 1, dy * channels : (dy + 1) * channels, j * LANES : (j + 1) * LANES
-                ] = value.astype(bf16)
-
-            spread_rows(raw_ref[z, 0:channels, :], store)
+                ] = value
+
+            spread_rows(pool_ref[z], store)
             return carry
 
         lax.fori_loop(0, planes, spread_pool, 0)
+        weights = z_groups * load_rows
         near_weight = jnp.concatenate(
-            [
-                all_ref[s, z_groups * load_rows : z_groups * load_rows + piece, :]
-                for s in range(y_groups)
-            ],
-            axis=0,
+            [all_ref[s, weights : weights + piece, :] for s in range(y_groups)], axis=0
         )
         far_weight = jnp.concatenate(
-            [
-                all_ref[s, z_groups * load_rows + piece :, 0 : 9 * channels - span]
-                for s in range(y_groups)
-            ],
+            [all_ref[s, weights + piece :, 0 : 9 * channels - span] for s in range(y_groups)],
             axis=0,
         )
 
@@ -411,34 +476,64 @@
                 jnp.sum(totals[s], axis=1, keepdims=True),
                 jnp.sum(squares[s], axis=1, keepdims=True),
                 coarse_cells,
-                column(gain_rows[s], chan_own, GAIN_AT),
-                column(gain_rows[s], chan_own, SHIFT_AT),
+                column(rows[s, 0], chan_own, GAIN_AT),
+                column(rows[s, 0], chan_own, SHIFT_AT),
             )
             for s in range(y_groups)
         ]
         scale = jnp.concatenate([one[0] for one in pairs], axis=0)
         offset = jnp.concatenate([one[1] for one in pairs], axis=0)
         bound = bound_of(hist_ref, 3)
+
+        def normed(z, peak):
+            for j in range(flat // LANES):
+                lanes = slice(j * LANES, (j + 1) * LANES)
+                value = activated(raw_ref[z, :, lanes], scale, offset)
+                peak = jnp.maximum(peak, jnp.abs(value))
+                out_ref[z, :, lanes] = bounded(value, bound)
+            return peak
+
+        peak_coarse = lax.fori_loop(0, planes, normed, jnp.zeros((chan_all, LANES), bf16))
+        row = at_lane(tops[:, PEAK_AT : PEAK_AT + 1], 0)
+        row = row + at_lane(tops[:, PEAK_AT + 1 : PEAK_AT + 2], 1)
+        row = row + at_lane(peak_of(peak_pool), 2)
+        row = row + at_lane(peak_of(peak_coarse), 3)
+        peak_ref[...] = row
+
+    return kernel
+
+
+def fourth_kernel(coarse_cells):
+    def kernel(
+        cells_ref,
+        weight_ref,
+        gain_ref,
+        shift_ref,
+        raw_ref,
+        affine_ref,
+        out_ref,
+        skip_ref,
+        hidden_ref,
+        last_ref,
+        wide_ref,
+    ):
+        planes, chan_all, flat = cells_ref.shape
+        chan_own, z_own = out_ref.shape[1:3]
+        span = 2 * LANES
+        row_len = LANES // 2
         hidden_ref[0] = jnp.zeros(hidden_ref.shape[1:], bf16)
         hidden_ref[planes + 1] = jnp.zeros(hidden_ref.shape[1:], bf16)
 
-        def spread_hidden(z, peak):
-            value = activated(raw_ref[z], scale, offset).astype(f32)
-            for j in range(flat // LANES):
-                peak = jnp.maximum(peak, jnp.abs(value[:, j * LANES : (j + 1) * LANES]))
-            clipped = jnp.minimum(jnp.maximum(value, -bound), bound)
-
+        def spread_hidden(z, carry):
             def store(dy, j, part):
                 hidden_ref[
                     z + 1, dy * chan_all : (dy + 1) * chan_all, j * LANES : (j + 1) * LANES
-                ] = part.astype(bf16)
-
-            spread_rows(clipped, store)
-            return peak
-
-        peak_coarse = lax.fori_loop(
-            0, planes, spread_hidden, jnp.zeros((chan_all, LANES), f32)
-        )
+                ] = part
+
+            spread_rows(cells_ref[z], store)
+            return carry
+
+        lax.fori_loop(0, planes, spread_hidden, 0)
         weight = weight_ref[...]
 
         def fourth(z, sums):
@@ -462,41 +557,32 @@
                     square = square + out * out
             return total, square
 
+        blank = jnp.zeros((chan_own, LANES), f32)
         total, square = lax.fori_loop(0, planes, fourth, (blank, blank))
         scale, offset = affine(
             jnp.sum(total, axis=1, keepdims=True),
             jnp.sum(square, axis=1, keepdims=True),
             coarse_cells,
-            column(gain_coarse_ref[1:2, :], chan_own, 0),
-            column(shift_coarse_ref[1:2, :], chan_own, 0),
-        )
-        for i in range(z_own):
-            out_ref[i] = activated(last_ref[at_z * z_own + i], scale, offset)
-        row = at_lane(jnp.max(tops[:, PEAK_AT : PEAK_AT + 1], axis=1, keepdims=True), 0)
-        row = row + at_lane(jnp.max(tops[:, PEAK_AT + 1 : PEAK_AT + 2], axis=1, keepdims=True), 1)
-        row = row + at_lane(peak_of(peak_pool), 2)
-        row = row + at_lane(peak_of(peak_coarse), 3)
-        peak_ref[...] = row
+            column(gain_ref[1:2, :], chan_own, 0),
+            column(shift_ref[1:2, :], chan_own, 0),
+        )
+        at_z = lax.axis_index("sz")
+        own = [
+            activated(last_ref[at_z * z_own + i], scale, offset).astype(f32) for i in range(z_own)
+        ]
+        for c in range(chan_own):
+            out_ref[0, c] = jnp.concatenate([one[c : c + 1] for one in own], axis=0).astype(bf16)
+        depth, height, channels, width = raw_ref.shape
+        rows = depth * height
+        scale = affine_ref[:, 0:1]
+        offset = affine_ref[:, 1:2]
+        for r in range(rows):
+            wide_ref[pl.ds(r, channels, stride=rows), :] = activated(
+                raw_ref[r // height, r % height], scale, offset
+            ).astype(f32)
+        skip_ref[0] = wide_ref[...].reshape(channels, depth, height, width).astype(bf16)
 
     return kernel
-
-
-def skip_kernel(raw_ref, affine_ref, out_ref, wide_ref):
-    depth, height, channels, width = raw_ref.shape
-    rows = depth * height
-    scale = affine_ref[:, 0:1]
-    offset = affine_ref[:, 1:2]
-    for r in range(rows):
-        wide_ref[pl.ds(r, channels, stride=rows), :] = activated(
-            raw_ref[r // height, r % height], scale, offset
-        ).astype(f32)
-    out_ref[0] = wide_ref[...].reshape(channels, depth, height, width).astype(bf16)
-
-
-def tap_matrix(weight):
-    taps, out_chan, in_chan = weight.shape
-    split = weight.reshape(taps // 3, 3, out_chan, in_chan)
-    return jnp.transpose(split, (1, 2, 0, 3)).reshape(3 * out_chan, (taps // 3) * in_chan)
 
 
 def shape(dims, dtype):
@@ -540,22 +626,37 @@
         scratch_shapes=[pltpu.VMEM((channels * depth * height, width), f32)],
         name="prep",
     )(volume, amax_history)
+    third_rows = 3 * chan_own
+    m1, m2, m3, m4 = pl.pallas_call(
+        matrix_kernel,
+        out_shape=(
+            shape((3 * channels, 9 * channels), bf16),
+            shape((3 * channels, 9 * channels), bf16),
+            shape((2 * third_rows, span), bf16),
+            shape((third_rows, 9 * chan_all), bf16),
+        ),
+        scratch_shapes=[pltpu.VMEM((third_rows, 9 * channels), bf16)],
+        name="matrices",
+    )(peak, conv_first, conv_second, conv_third, conv_fourth)
     pair_first, pair_second = near("sz")
-    first = lax.ppermute(first, "sz", pair_first)
-    second = lax.ppermute(second, "sz", pair_second)
+    z_first = lax.ppermute(first, "sz", pair_first)
+    z_second = lax.ppermute(second, "sz", pair_second)
     deep_depth = depth + 2 * HALO
-    deep, first, second = pl.pallas_call(
+    anywhere = pl.BlockSpec(memory_space=pl.ANY)
+    first, second = pl.pallas_call(
         deep_kernel,
+        in_specs=[anywhere] * 4,
+        out_specs=(anywhere, anywhere),
         out_shape=(
-            shape((deep_depth, height, channels, width), bf16),
             shape((deep_depth, HALO, channels, width), bf16),
             shape((deep_depth, HALO, channels, width), bf16),
         ),
+        scratch_shapes=[pltpu.SemaphoreType.DMA((6,))],
         name="deep",
-    )(cells, first, second)
+    )(cells, z_first, z_second, m1)
     pair_first, pair_second = near("sy")
-    first = lax.ppermute(first, "sy", pair_first)
-    second = lax.ppermute(second, "sy", pair_second)
+    y_first = lax.ppermute(first, "sy", pair_first)
+    y_second = lax.ppermute(second, "sy", pair_second)
     raw_first, row = pl.pallas_call(
         first_kernel,
         out_shape=(
@@ -564,7 +665,7 @@
         ),
         scratch_shapes=[pltpu.VMEM((deep_depth, height + 2 * HALO, channels, width), bf16)],
         name="first",
-    )(deep, first, second, tap_matrix(conv_first), peak)
+    )(cells, z_first, z_second, y_first, y_second, m1, peak)
     rows = lax.all_to_all(row, ("sy", "sz"), 0, 0, tiled=True)
     raw_second, load = pl.pallas_call(
         second_kernel(fine_cells),
@@ -574,67 +675,53 @@
         ),
         scratch_shapes=[
             pltpu.VMEM((depth + 2, height + 2, channels, width), bf16),
-            pltpu.VMEM((depth // 2, height // 2, channels, width), bf16),
+            pltpu.VMEM((depth // 2, height // 2, channels, width), f32),
         ],
         name="second",
-    )(
-        raw_first,
-        rows,
-        tap_matrix(conv_second),
-        amax_history,
-        gain_fine,
-        shift_fine,
-        gain_coarse,
-        shift_coarse,
-    )
+    )(raw_first, rows, m2, amax_history, gain_fine, shift_fine, gain_coarse, shift_coarse)
     loads = [load]
     for k in range(1, z_groups):
         loads.append(lax.ppermute(load, "sz", [(i, i ^ k) for i in range(z_groups)]))
-    third = tap_matrix(conv_third)
-    piece = third.shape[0]
-    loads.append(third[:, :span])
-    loads.append(jnp.pad(third[:, span:], ((0, 0), (0, 2 * span - third.shape[1]))))
+    loads.append(m3)
     gathered = lax.all_gather(jnp.concatenate(loads, axis=0), "sy", axis=0)
-    coarse, peaks, fine_affine = pl.pallas_call(
-        coarse_kernel(fine_cells, coarse_cells, load_rows, piece),
+    hidden, peaks, fine_affine = pl.pallas_call(
+        third_kernel(fine_cells, coarse_cells, load_rows, third_rows),
         out_shape=(
-            shape((depth // 2, chan_own, flat), bf16),
+            shape((planes, chan_all, flat), bf16),
             shape((1, LANES), f32),
             shape((channels, LANES), f32),
         ),
         scratch_shapes=[
+            pltpu.VMEM((planes, channels, flat), bf16),
             pltpu.VMEM((planes + 2, 3 * channels, flat), bf16),
             pltpu.VMEM((planes, chan_all, flat), f32),
-            pltpu.VMEM((planes + 2, 3 * chan_all, flat), bf16),
-            pltpu.VMEM((planes, chan_own, flat), f32),
         ],
-        name="coarse",
-    )(
-        gathered,
-        amax_history,
-        gain_fine,
-        shift_fine,
-        gain_coarse,
-        shift_coarse,
-        tap_matrix(conv_fourth),
-    )
+        name="third",
+    )(gathered, amax_history, gain_fine, shift_fine)
     if samples <= 4:
         others = [
             lax.ppermute(peaks, "sample", [(i, (i + k) % samples) for i in range(samples)])
             for k in range(1, samples)
         ]
-        for other in others:
-            peaks = jnp.maximum(peaks, other)
     else:
-        peaks = lax.pmax(peaks, "sample")
-    skip = pl.pallas_call(
-        skip_kernel,
-        out_shape=shape((1, channels, depth, height, width), bf16),
-        scratch_shapes=[pltpu.VMEM((channels * depth * height, width), f32)],
-        name="skip",
-    )(raw_second, fine_affine)
+        others = [lax.pmax(peaks, "sample")]
+    coarse, skip = pl.pallas_call(
+        fourth_kernel(coarse_cells),
+        out_shape=(
+            shape((1, chan_own, depth // 2, flat), bf16),
+            shape((1, channels, depth, height, width), bf16),
+        ),
+        scratch_shapes=[
+            pltpu.VMEM((planes + 2, 3 * chan_all, flat), bf16),
+            pltpu.VMEM((planes, chan_own, flat), f32),
+            pltpu.VMEM((channels * depth * height, width), f32),
+        ],
+        name="fourth",
+    )(hidden, m4, gain_coarse, shift_coarse, raw_second, fine_affine)
+    for other in others:
+        peaks = jnp.maximum(peaks, other)
     levels = amax_history.shape[0]
-    return skip, jnp.transpose(coarse, (1, 0, 2))[None], peaks[0, :levels]
+    return skip, coarse, peaks[0, :levels]
 
 
 def solution(mesh):

time: 79.3 us -> 84.2 us (1.062)
  blocking collectives: 9.2 us -> 27.3 us
  starting transfers between devices: 24 us -> 12.1 us
  Pallas kernels: 27.1 us -> 37 us
  waiting for transfers between devices: 8.03 us -> 1.73 us
  local copies, waits for them, and re-layouts: 9.66 us -> 4.79 us
    all_to_all x0 -> x1, blocking collectives: none -> 18.8 us  [per_device(): rows = lax.all_to_all(row, ('sy', 'sz'), 0, 0, tiled=True)]
    all_to_all x1 -> x0, starting transfers between devices: 12 us -> none  [per_device(): rows = lax.all_to_all(row, ('sy', 'sz'), 0, 0, tiled=True)]
    pallas_call x3 -> x4, Pallas kernels: 16.5 us -> 26.4 us  [the longest x1 9.09 us: per_device(): pl.pallas_call(deep_kernel, in_specs=[anywhere] * 4, out_specs=(anywhere,...]
    all_to_all x1 -> x0, waiting for transfers between devices: 3.32 us -> none  [per_device(): rows = lax.all_to_all(row, ('sy', 'sz'), 0, 0, tiled=True)]
    reshape x10 -> x0, local copies, waits for them, and re-layouts: 3.23 us -> none  [the longest x6 2.73 us: tap_matrix(): jnp.transpose(split, (1, 2, 0, 3))]
    ppermute x4, waiting for transfers between devices: 2.16 us -> 0.14 us  [the longest x1 0.13 us: per_device(): z_first = lax.ppermute(first, 'sz', pair_first)]
    unnamed x28 -> x16, local copies, waits for them, and re-layouts: 5.9 us -> 4.27 us
    ppermute x3, waiting for transfers between devices: 2.55 us -> 1.58 us  [per_device(): lax.ppermute(load, 'sz', [(i, i ^ k) for i in range(z_groups)])]
  transfers between devices with their start and end apart: 9 -> 8, of which waited for: 4 -> 2; matrix products, arithmetic and copies ran while one was open for 7% -> 1% of each run, Pallas kernels for 3% -> 11%
where the time goes in v2:
time: 84.2 us; the launch traced here: 83.7 us
  Pallas kernels  37 us (44%)
  blocking collectives  27.3 us (32%)
  starting transfers between devices  12.1 us (14%)
  local copies, waits for them, and re-layouts  4.79 us (6%)
  waiting for transfers between devices  1.73 us (2%)
    all_to_all x1, blocking collectives, per_device(): rows = lax.all_to_all(row, ('sy', 'sz'), 0, 0, tiled=True)  18.8 us
    pallas_call x1, Pallas kernels, per_device(): pl.pallas_call(deep_kernel, in_specs=[anywhere] * 4, out_specs=(anywhere,...  9.09 us
    all_gather x1, blocking collectives, per_device(): gathered = lax.all_gather(jnp.concatenate(loads, axis=0), 'sy', axis=0)  8.49 us
    pallas_call x1, Pallas kernels, per_device(): pl.pallas_call(third_kernel(fine_cells, coarse_cells, load_rows, third_ro...  8.22 us
    pallas_call x1, Pallas kernels, per_device(): pl.pallas_call(fourth_kernel(coarse_cells), out_shape=(shape((1, chan_own...  7.05 us
    pallas_call x1, Pallas kernels, per_device(): pl.pallas_call(first_kernel, out_shape=(shape((depth + 2, height + 2, cha...  4.57 us
    ppermute x3, starting transfers between devices, per_device(): lax.ppermute(load, 'sz', [(i, i ^ k) for i in range(z_groups)])  4.39 us
    unnamed x16, local copies, waits for them, and re-layouts  4.27 us
  transfers between devices with their start and end apart: 8, of which 2 were waited for; matrix products, arithmetic and copies ran while one was open for 1% of the time, Pallas kernels for 11%

profile of v2, /device:TPU:0, one launch (start us, length us, event | category | flops | bytes accessed | tf_op | source)
XLA Modules:
  0.0 83.7 jit_solution(11497103926897461435)
XLA Ops:
  0.6 2.2 %prep.1 = (bf16[4,8,32,128]{3,2,1,0:T(8,128)(2,1)}, bf16[2,8,32,128]{3,2,1,0:T(8,128)(2,1)}, bf16[2,8,32,128]{3,2,1,0:T(8,128)(2,1)}, f32[1,128]{1,0:T(1,128)}) custom-call(bf16[1,32,4,8,128]{4,3,2,1,0:T(8,128)(2,1)} %vol_ref.1, f32[4,16]{1,0:T(4,128)} %hist_ref.5), custom_call_target="tpu_custom_call" | custom-call | tf_op jit(solution)/shard_map/prep/pallas_call | solution.py:618
  2.9 3.1 %collective-permute-start = (bf16[2,8,32,128]{3,2,1,0:T(8,128)(2,1)}, bf16[2,8,32,128]{3,2,1,0:T(8,128)(2,1)S(1)}, u32[]{:S(2)}, u32[]{:S(2)}) collective-permute-start(bf16[2,8,32,128]{3,2,1,0:T(8,128)(2,1)} %get-tuple-element.23), channel_id=1, source_target_pairs={{0,1},{1,0},{2,3},{3,2},{4,5},{5,4},{6,7},{7,6},{8,9},{9,8},{10,11... | collective-permute-start | bytes 393224 | tf_op jit(solution)/shard_map/ppermute | solution.py:642
  5.9 1.6 %collective-permute-start.1 = (bf16[2,8,32,128]{3,2,1,0:T(8,128)(2,1)}, bf16[2,8,32,128]{3,2,1,0:T(8,128)(2,1)S(1)}, u32[]{:S(2)}, u32[]{:S(2)}) collective-permute-start(bf16[2,8,32,128]{3,2,1,0:T(8,128)(2,1)} %get-tuple-element.24), channel_id=1, source_target_pairs={{0,0},{1,2},{2,1},{3,3},{4,4},{5,6},{6,5},{7,7},{8,8},{9,10},{10,9... | collective-permute-start | bytes 393224 | tf_op jit(solution)/shard_map/ppermute | solution.py:643
  7.5 2.0 %matrices.1 = (bf16[96,288]{1,0:T(8,128)(2,1)}, bf16[96,288]{1,0:T(8,128)(2,1)}, bf16[96,256]{1,0:T(8,128)(2,1)}, bf16[48,576]{1,0:T(8,128)(2,1)}) custom-call(f32[1,128]{1,0:T(1,128)} %get-tuple-element.25.peak_ref, bf16[27,32,32]{2,1,0:T(8,128)(2,1)} %first_ref.1, bf16[27,32,32]{2,1,0:T(8,128)(2,1)} %second_ref.1, bf16[27,16,32]{2,1,0:T(8,128)(2,1)} %third_ref.1, ...), custom_call_target="tpu_custom_call" | custom-call | tf_op jit(solution)/shard_map/matrices/pallas_call | solution.py:630
  9.5 0.1 collective-permute-done.got_first_ref.z_first_ref
  9.6 0.0 copy-start
  9.6 0.0 collective-permute-done.1.got_second_ref.z_second_ref
  9.6 0.0 copy-start.1
  9.6 0.7 copy-done
  10.3 0.1 copy-done.1
  10.3 9.1 %deep.1 = (bf16[8,2,32,128]{3,2,1,0:T(8,128)(2,1)}, bf16[8,2,32,128]{3,2,1,0:T(8,128)(2,1)}) custom-call(bf16[4,8,32,128]{3,2,1,0:T(8,128)(2,1)} %get-tuple-element.22.cells_ref.own_ref, bf16[2,8,32,128]{3,2,1,0:T(8,128)(2,1)} %copy-done, bf16[2,8,32,128]{3,2,1,0:T(8,128)(2,1)} %copy-done.1, bf16[96,288]{1,0:T(8,128)(2,1)} %get-tuple-element.26.matrix_ref.weight_ref), custom_call_target="tpu_custom_call" | custom-call | tf_op jit(solution)/shard_map/deep/pallas_call | solution.py:646
  19.4 0.1 collective-permute-start.2
  19.5 1.6 %collective-permute-start.3 = (bf16[8,2,32,128]{3,2,1,0:T(8,128)(2,1)}, bf16[8,2,32,128]{3,2,1,0:T(8,128)(2,1)S(1)}, u32[]{:S(2)}, u32[]{:S(2)}) collective-permute-start(bf16[8,2,32,128]{3,2,1,0:T(8,128)(2,1)} %get-tuple-element.28), channel_id=1, source_target_pairs={{0,0},{4,8},{8,4},{12,12},{1,1},{5,9},{9,5},{13,13},{2,2},{6,10},{... | collective-permute-start | bytes 393224 | tf_op jit(solution)/shard_map/ppermute | solution.py:659
  21.1 0.0 collective-permute-done.2.y_first_ref
  21.1 0.0 copy-start.2
  21.1 0.0 collective-permute-done.3.y_second_ref
  21.1 0.6 copy-done.2
  21.7 0.0 copy-start.3
  21.7 0.7 copy-done.3
  22.4 4.6 %first.1 = (f32[6,10,32,128]{3,2,1,0:T(8,128)}, f32[16,1,128]{2,1,0:T(1,128)}) custom-call(bf16[4,8,32,128]{3,2,1,0:T(8,128)(2,1)} %get-tuple-element.22.cells_ref.own_ref, bf16[2,8,32,128]{3,2,1,0:T(8,128)(2,1)} %copy-done, bf16[2,8,32,128]{3,2,1,0:T(8,128)(2,1)} %copy-done.1, bf16[8,2,32,128]{3,2,1,0:T(8,128)(2,1)} %copy-done.2, ...), custom_call_target="tpu_custom_call" | custom-call | tf_op jit(solution)/shard_map/first/pallas_call | solution.py:660
  27.0 18.8 %all_to_all.5.rows_ref = f32[16,1,128]{2,1,0:T(1,128)} all-to-all(f32[16,1,128]{2,1,0:T(1,128)} %get-tuple-element.30), channel_id=1, replica_groups=mesh['sample'=2,'sy'=4,'sz'=4] {'sy','sz'}, dimensions={0} | all-to-all | bytes 16384 | tf_op jit(solution)/shard_map/all_to_all | solution.py:669
  45.8 3.8 %second.1 = (f32[4,8,32,128]{3,2,1,0:T(8,128)}, bf16[80,256]{1,0:T(8,128)(2,1)}) custom-call(f32[6,10,32,128]{3,2,1,0:T(8,128)} %get-tuple-element.29.raw_ref, f32[16,1,128]{2,1,0:T(1,128)} %all_to_all.5.rows_ref, bf16[96,288]{1,0:T(8,128)(2,1)} %get-tuple-element.31.weight_ref, f32[4,16]{1,0:T(4,128)} %hist_ref.5, f32[2,32]{1,0:T(2,128)} %gain_ref.4, ...), custom_call_target="tpu_custom_call" | custom-call | tf_op jit(solution)/shard_map/second/pallas_call | solution.py:670
  49.6 0.7 collective-permute-start.6
  50.3 1.1 %collective-permute-start.5 = (bf16[80,256]{1,0:T(8,128)(2,1)}, bf16[80,256]{1,0:T(8,128)(2,1)S(1)}, u32[]{:S(2)}, u32[]{:S(2)}) collective-permute-start(bf16[80,256]{1,0:T(8,128)(2,1)} %get-tuple-element.32), channel_id=1, source_target_pairs={{0,2},{1,3},{2,0},{3,1},{4,6},{5,7},{6,4},{7,5},{8,10},{9,11},{10,... | collective-permute-start | bytes 122888 | tf_op jit(solution)/shard_map/ppermute | solution.py:684
  51.5 2.5 %collective-permute-start.4 = (bf16[80,256]{1,0:T(8,128)(2,1)}, bf16[80,256]{1,0:T(8,128)(2,1)S(1)}, u32[]{:S(2)}, u32[]{:S(2)}) collective-permute-start(bf16[80,256]{1,0:T(8,128)(2,1)} %get-tuple-element.32), channel_id=1, source_target_pairs={{0,1},{1,0},{2,3},{3,2},{4,5},{5,4},{6,7},{7,6},{8,9},{9,8},{10,11... | collective-permute-start | bytes 122888 | tf_op jit(solution)/shard_map/ppermute | solution.py:684
  54.0 0.8 constant_dynamic-update-slice_fusion.4
  54.8 1.6 %collective-permute-done.4 = bf16[80,256]{1,0:T(8,128)(2,1)S(1)} collective-permute-done((bf16[80,256]{1,0:T(8,128)(2,1)}, bf16[80,256]{1,0:T(8,128)(2,1)S(1)}, u32[]{:S(2)}, u32[]{:S(2)}) %collective-permute-start.4) | collective-permute-done | bytes 40992 | tf_op jit(solution)/shard_map/ppermute | solution.py:684
  56.4 0.0 collective-permute-done.5
  56.4 0.0 copy-start.4
  56.4 0.0 collective-permute-done.6
  56.5 0.8 copy-done.4
  57.2 8.5 %all-gather = bf16[1664,256]{1,0:T(8,128)(2,1)} all-gather(bf16[416,256]{1,0:T(8,128)(2,1)S(1)} %constant_dynamic-update-slice_fusion), channel_id=2, replica_groups=mesh['sample'=2,'sy'=4,'sz'=4] {'sy'}, dimensions={0}, use_global_device_ids=true | all-gather | bytes 1064960 | tf_op jit(solution)/shard_map/all_gather | solution.py:686
  65.7 8.2 %third.1 = (bf16[8,64,1024]{2,1,0:T(8,128)(2,1)}, f32[1,128]{1,0:T(1,128)}, f32[32,128]{1,0:T(8,128)}) custom-call(bf16[4,416,256]{2,1,0:T(8,128)(2,1)} %bitcast.3, f32[4,16]{1,0:T(4,128)} %hist_ref.5, f32[2,32]{1,0:T(2,128)} %gain_ref.4, f32[2,32]{1,0:T(2,128)} %shift_ref.4), custom_call_target="tpu_custom_call" | custom-call | tf_op jit(solution)/shard_map/third/pallas_call | solution.py:687
  73.9 0.0 copy-start.5
  74.0 0.7 copy-done.5
  74.6 1.5 %collective-permute-start.7 = (f32[1,128]{1,0:T(1,128)S(1)}, f32[1,128]{1,0:T(1,128)S(1)}, u32[]{:S(2)}, u32[]{:S(2)}) collective-permute-start(f32[1,128]{1,0:T(1,128)S(1)} %copy-done.5), channel_id=1, source_target_pairs={{0,16},{16,0},{1,17},{17,1},{2,18},{18,2},{3,19},{19,3},{4,20},{20... | collective-permute-start | bytes 1544 | tf_op jit(solution)/shard_map/ppermute | solution.py:703
  76.1 7.0 %fourth.1 = (bf16[1,16,2,1024]{3,2,1,0:T(2,128)(2,1)}, bf16[1,32,4,8,128]{4,3,2,1,0:T(8,128)(2,1)}) custom-call(bf16[8,64,1024]{2,1,0:T(8,128)(2,1)} %get-tuple-element.34.cells_ref, bf16[48,576]{1,0:T(8,128)(2,1)} %get-tuple-element.35.weight_ref, f32[2,16]{1,0:T(2,128)} %gain_ref.5, f32[2,16]{1,0:T(2,128)} %shift_ref.5, ...), custom_call_target="tpu_custom_call" | custom-call | tf_op jit(solution)/shard_map/fourth/pallas_call | solution.py:708
  83.1 0.0 collective-permute-done.7
  83.2 0.5 slice_bitcast_fusion
  (5 shorter events, 0.0 us)
Async XLA Ops:
  2.9 6.8 %collective-permute-start = (bf16[2,8,32,128]{3,2,1,0:T(8,128)(2,1)}, bf16[2,8,32,128]{3,2,1,0:T(8,128)(2,1)S(1)}, u32[]{:S(2)}, u32[]{:S(2)}) collective-permute-start(bf16[2,8,32,128]{3,2,1,0:T(8,128)(2,1)} %get-tuple-element.23), channel_id=1, source_target_pairs={{0,1},{1,0},{2,3},{3,2},{4,5},{5,4},{6,7},{7,6},{8,9},{9,8},{10,11... | collective-permute-start | bytes 393224 | tf_op jit(solution)/shard_map/ppermute | solution.py:642
  5.9 3.7 %collective-permute-start.1 = (bf16[2,8,32,128]{3,2,1,0:T(8,128)(2,1)}, bf16[2,8,32,128]{3,2,1,0:T(8,128)(2,1)S(1)}, u32[]{:S(2)}, u32[]{:S(2)}) collective-permute-start(bf16[2,8,32,128]{3,2,1,0:T(8,128)(2,1)} %get-tuple-element.24), channel_id=1, source_target_pairs={{0,0},{1,2},{2,1},{3,3},{4,4},{5,6},{6,5},{7,7},{8,8},{9,10},{10,9... | collective-permute-start | bytes 393224 | tf_op jit(solution)/shard_map/ppermute | solution.py:643
  9.6 0.7 copy-start
  9.6 0.7 copy-start.1
  19.4 1.6 %collective-permute-start.2 = (bf16[8,2,32,128]{3,2,1,0:T(8,128)(2,1)}, bf16[8,2,32,128]{3,2,1,0:T(8,128)(2,1)S(1)}, u32[]{:S(2)}, u32[]{:S(2)}) collective-permute-start(bf16[8,2,32,128]{3,2,1,0:T(8,128)(2,1)} %get-tuple-element.27), channel_id=1, source_target_pairs={{0,4},{4,0},{8,12},{12,8},{1,5},{5,1},{9,13},{13,9},{2,6},{6,2},{1... | collective-permute-start | bytes 393224 | tf_op jit(solution)/shard_map/ppermute | solution.py:658
  19.5 1.6 %collective-permute-start.3 = (bf16[8,2,32,128]{3,2,1,0:T(8,128)(2,1)}, bf16[8,2,32,128]{3,2,1,0:T(8,128)(2,1)S(1)}, u32[]{:S(2)}, u32[]{:S(2)}) collective-permute-start(bf16[8,2,32,128]{3,2,1,0:T(8,128)(2,1)} %get-tuple-element.28), channel_id=1, source_target_pairs={{0,0},{4,8},{8,4},{12,12},{1,1},{5,9},{9,5},{13,13},{2,2},{6,10},{... | collective-permute-start | bytes 393224 | tf_op jit(solution)/shard_map/ppermute | solution.py:659
  21.1 0.6 copy-start.2
  21.7 0.7 copy-start.3
  49.6 6.8 %collective-permute-start.6 = (bf16[80,256]{1,0:T(8,128)(2,1)}, bf16[80,256]{1,0:T(8,128)(2,1)S(1)}, u32[]{:S(2)}, u32[]{:S(2)}) collective-permute-start(bf16[80,256]{1,0:T(8,128)(2,1)} %get-tuple-element.32), channel_id=1, source_target_pairs={{0,3},{1,2},{2,1},{3,0},{4,7},{5,6},{6,5},{7,4},{8,11},{9,10},{10,... | collective-permute-start | bytes 122888 | tf_op jit(solution)/shard_map/ppermute | solution.py:684
  50.3 6.1 %collective-permute-start.5 = (bf16[80,256]{1,0:T(8,128)(2,1)}, bf16[80,256]{1,0:T(8,128)(2,1)S(1)}, u32[]{:S(2)}, u32[]{:S(2)}) collective-permute-start(bf16[80,256]{1,0:T(8,128)(2,1)} %get-tuple-element.32), channel_id=1, source_target_pairs={{0,2},{1,3},{2,0},{3,1},{4,6},{5,7},{6,4},{7,5},{8,10},{9,11},{10,... | collective-permute-start | bytes 122888 | tf_op jit(solution)/shard_map/ppermute | solution.py:684
  51.5 4.9 %collective-permute-start.4 = (bf16[80,256]{1,0:T(8,128)(2,1)}, bf16[80,256]{1,0:T(8,128)(2,1)S(1)}, u32[]{:S(2)}, u32[]{:S(2)}) collective-permute-start(bf16[80,256]{1,0:T(8,128)(2,1)} %get-tuple-element.32), channel_id=1, source_target_pairs={{0,1},{1,0},{2,3},{3,2},{4,5},{5,4},{6,7},{7,6},{8,9},{9,8},{10,11... | collective-permute-start | bytes 122888 | tf_op jit(solution)/shard_map/ppermute | solution.py:684
  56.4 0.8 copy-start.4
  73.9 0.7 copy-start.5
  74.6 8.5 %collective-permute-start.7 = (f32[1,128]{1,0:T(1,128)S(1)}, f32[1,128]{1,0:T(1,128)S(1)}, u32[]{:S(2)}, u32[]{:S(2)}) collective-permute-start(f32[1,128]{1,0:T(1,128)S(1)} %copy-done.5), channel_id=1, source_target_pairs={{0,16},{16,0},{1,17},{17,1},{2,18},{18,2},{3,19},{19,3},{4,20},{20... | collective-permute-start | bytes 1544 | tf_op jit(solution)/shard_map/ppermute | solution.py:703

commit v3 on v2

--- a/solution.py
+++ b/solution.py
@@ -126,28 +126,17 @@
     return below, above
 
 
-def deep_kernel(
-    cells_ref, got_first_ref, got_second_ref, matrix_ref, first_ref, second_ref, done
-):
+def deep_kernel(cells_ref, got_first_ref, got_second_ref, matrix_ref, first_ref, second_ref):
     depth, height = cells_ref.shape[:2]
     even = lax.axis_index("sy") % 2 == 0
     starts = (jnp.where(even, height - HALO, 0), jnp.where(even, 0, height - HALO))
     odd_z = lax.axis_index("sz") % 2
-    places = (odd_z * 0 + (1 - odd_z) * (HALO + depth), odd_z * (HALO + depth))
-    copies = []
-    for side, (start, out_ref) in enumerate(zip(starts, (first_ref, second_ref))):
+    far = HALO + depth
+    for start, out_ref in zip(starts, (first_ref, second_ref)):
         rows = pl.ds(start, HALO)
-        jobs = (
-            (got_first_ref.at[:, rows], out_ref.at[pl.ds(places[0], HALO)]),
-            (got_second_ref.at[:, rows], out_ref.at[pl.ds(places[1], HALO)]),
-            (cells_ref.at[:, rows], out_ref.at[HALO : HALO + depth]),
-        )
-        for which, (source, target) in enumerate(jobs):
-            copies.append(pltpu.make_async_copy(source, target, done.at[3 * side + which]))
-    for copy in copies:
-        copy.start()
-    for copy in copies:
-        copy.wait()
+        out_ref[pl.ds((1 - odd_z) * far, HALO)] = got_first_ref[:, rows]
+        out_ref[pl.ds(odd_z * far, HALO)] = got_second_ref[:, rows]
+        out_ref[HALO:far] = cells_ref[:, rows]
 
 
 def conv_rows(cells_ref, weight, z, y, out_chan):
@@ -589,6 +578,14 @@
     return jax.ShapeDtypeStruct(dims, dtype)
 
 
+def near_shape(dims, dtype):
+    return pltpu.VMEM(dims, dtype)
+
+
+def held(value):
+    return pltpu.with_memory_space_constraint(value, pltpu.VMEM)
+
+
 def per_device(
     volume,
     amax_history,
@@ -618,10 +615,10 @@
     cells, first, second, peak = pl.pallas_call(
         prep_kernel,
         out_shape=(
-            shape((depth, height, channels, width), bf16),
-            shape((HALO, height, channels, width), bf16),
-            shape((HALO, height, channels, width), bf16),
-            shape((1, LANES), f32),
+            near_shape((depth, height, channels, width), bf16),
+            near_shape((HALO, height, channels, width), bf16),
+            near_shape((HALO, height, channels, width), bf16),
+            near_shape((1, LANES), f32),
         ),
         scratch_shapes=[pltpu.VMEM((channels * depth * height, width), f32)],
         name="prep",
@@ -630,55 +627,51 @@
     m1, m2, m3, m4 = pl.pallas_call(
         matrix_kernel,
         out_shape=(
-            shape((3 * channels, 9 * channels), bf16),
-            shape((3 * channels, 9 * channels), bf16),
-            shape((2 * third_rows, span), bf16),
-            shape((third_rows, 9 * chan_all), bf16),
+            near_shape((3 * channels, 9 * channels), bf16),
+            near_shape((3 * channels, 9 * channels), bf16),
+            near_shape((2 * third_rows, span), bf16),
+            near_shape((third_rows, 9 * chan_all), bf16),
         ),
         scratch_shapes=[pltpu.VMEM((third_rows, 9 * channels), bf16)],
         name="matrices",
-    )(peak, conv_first, conv_second, conv_third, conv_fourth)
+    )(held(peak), conv_first, conv_second, conv_third, conv_fourth)
     pair_first, pair_second = near("sz")
     z_first = lax.ppermute(first, "sz", pair_first)
     z_second = lax.ppermute(second, "sz", pair_second)
     deep_depth = depth + 2 * HALO
-    anywhere = pl.BlockSpec(memory_space=pl.ANY)
     first, second = pl.pallas_call(
         deep_kernel,
-        in_specs=[anywhere] * 4,
-        out_specs=(anywhere, anywhere),
         out_shape=(
-            shape((deep_depth, HALO, channels, width), bf16),
-            shape((deep_depth, HALO, channels, width), bf16),
+            near_shape((deep_depth, HALO, channels, width), bf16),
+            near_shape((deep_depth, HALO, channels, width), bf16),
         ),
-        scratch_shapes=[pltpu.SemaphoreType.DMA((6,))],
         name="deep",
-    )(cells, z_first, z_second, m1)
+    )(held(cells), held(z_first), held(z_second), held(m1))
     pair_first, pair_second = near("sy")
     y_first = lax.ppermute(first, "sy", pair_first)
     y_second = lax.ppermute(second, "sy", pair_second)
     raw_first, row = pl.pallas_call(
         first_kernel,
         out_shape=(
-            shape((depth + 2, height + 2, channels, width), f32),
-            shape((group, 1, LANES), f32),
+            near_shape((depth + 2, height + 2, channels, width), f32),
+            near_shape((group, 1, LANES), f32),
         ),
         scratch_shapes=[pltpu.VMEM((deep_depth, height + 2 * HALO, channels, width), bf16)],
         name="first",
-    )(cells, z_first, z_second, y_first, y_second, m1, peak)
+    )(*(held(x) for x in (cells, z_first, z_second, y_first, y_second, m1, peak)))
     rows = lax.all_to_all(row, ("sy", "sz"), 0, 0, tiled=True)
     raw_second, load = pl.pallas_call(
         second_kernel(fine_cells),
         out_shape=(
-            shape((depth, height, channels, width), f32),
-            shape((load_rows, span), bf16),
+            near_shape((depth, height, channels, width), f32),
+            near_shape((load_rows, span), bf16),
         ),
         scratch_shapes=[
             pltpu.VMEM((depth + 2, height + 2, channels, width), bf16),
             pltpu.VMEM((depth // 2, height // 2, channels, width), f32),
         ],
         name="second",
-    )(raw_first, rows, m2, amax_history, gain_fine, shift_fine, gain_coarse, shift_coarse)
+    )(held(raw_first), held(rows), held(m2), amax_history, gain_fine, shift_fine, gain_coarse, shift_coarse)
     loads = [load]
     for k in range(1, z_groups):
         loads.append(lax.ppermute(load, "sz", [(i, i ^ k) for i in range(z_groups)]))
@@ -687,9 +680,9 @@
     hidden, peaks, fine_affine = pl.pallas_call(
         third_kernel(fine_cells, coarse_cells, load_rows, third_rows),
         out_shape=(
-            shape((planes, chan_all, flat), bf16),
-            shape((1, LANES), f32),
-            shape((channels, LANES), f32),
+            near_shape((planes, chan_all, flat), bf16),
+            near_shape((1, LANES), f32),
+            near_shape((channels, LANES), f32),
         ),
         scratch_shapes=[
             pltpu.VMEM((planes, channels, flat), bf16),
@@ -697,7 +690,7 @@
             pltpu.VMEM((planes, chan_all, flat), f32),
         ],
         name="third",
-    )(gathered, amax_history, gain_fine, shift_fine)
+    )(held(gathered), amax_history, gain_fine, shift_fine)
     if samples <= 4:
         others = [
             lax.ppermute(peaks, "sample", [(i, (i + k) % samples) for i in range(samples)])
@@ -717,7 +710,7 @@
             pltpu.VMEM((channels * depth * height, width), f32),
         ],
         name="fourth",
-    )(hidden, m4, gain_coarse, shift_coarse, raw_second, fine_affine)
+    )(held(hidden), held(m4), gain_coarse, shift_coarse, held(raw_second), held(fine_affine))
     for other in others:
         peaks = jnp.maximum(peaks, other)
     levels = amax_history.shape[0]

time: 84.2 us -> 65.1 us (0.77)
  Pallas kernels: 37 us -> 21.2 us
  local copies, waits for them, and re-layouts: 4.79 us -> 0.54 us
  waiting for transfers between devices: 1.73 us -> 4.34 us
  starting transfers between devices: 12.1 us -> 10.5 us
    pallas_call x5, Pallas kernels: 21.7 us -> 8.03 us  [the longest x1 2.68 us: per_device(): pl.pallas_call(second_kernel(fine_cells), out_shape=(near_shape((depth, h...]
    unnamed x16 -> x4, local copies, waits for them, and re-layouts: 4.27 us -> 0.01 us
    pallas_call x1, Pallas kernels: 8.22 us -> 6.87 us  [per_device(): pl.pallas_call(third_kernel(fine_cells, coarse_cells, load_rows, third_ro...]
    ppermute x1, waiting for transfers between devices: 0.13 us -> 1.46 us  [per_device(): z_first = lax.ppermute(first, 'sz', pair_first)]
    ppermute x1, starting transfers between devices: 1.55 us -> 0.66 us  [per_device(): z_second = lax.ppermute(second, 'sz', pair_second)]
    ppermute x1, starting transfers between devices: 1.56 us -> 0.67 us  [per_device(): y_second = lax.ppermute(second, 'sy', pair_second)]
  transfers between devices with their start and end apart: 8 -> 8, of which waited for: 2 -> 4; matrix products, arithmetic and copies ran while one was open for 1% -> 0% of each run, Pallas kernels for 11% -> 12%
where the time goes in v3:
time: 65.1 us; the launch traced here: 64.8 us
  blocking collectives  27.5 us (42%)
  Pallas kernels  21.2 us (33%)
  starting transfers between devices  10.5 us (16%)
  waiting for transfers between devices  4.34 us (7%)
  between operations  0.71 us (1%)
    all_to_all x1, blocking collectives, per_device(): rows = lax.all_to_all(row, ('sy', 'sz'), 0, 0, tiled=True)  19.4 us
    all_gather x1, blocking collectives, per_device(): gathered = lax.all_gather(jnp.concatenate(loads, axis=0), 'sy', axis=0)  8.04 us
    pallas_call x1, Pallas kernels, per_device(): pl.pallas_call(third_kernel(fine_cells, coarse_cells, load_rows, third_ro...  6.87 us
    pallas_call x1, Pallas kernels, per_device(): pl.pallas_call(fourth_kernel(coarse_cells), out_shape=(shape((1, chan_own...  6.3 us
    ppermute x3, starting transfers between devices, per_device(): lax.ppermute(load, 'sz', [(i, i ^ k) for i in range(z_groups)])  4.45 us
    ppermute x1, starting transfers between devices, per_device(): z_first = lax.ppermute(first, 'sz', pair_first)  3.12 us
    pallas_call x1, Pallas kernels, per_device(): pl.pallas_call(second_kernel(fine_cells), out_shape=(near_shape((depth, h...  2.68 us
    pallas_call x1, Pallas kernels, per_device(): pl.pallas_call(first_kernel, out_shape=(near_shape((depth + 2, height + 2...  2.49 us
  transfers between devices with their start and end apart: 8, of which 4 were waited for; matrix products, arithmetic and copies ran while one was open for 0% of the time, Pallas kernels for 12%

profile of v3, /device:TPU:0, one launch (start us, length us, event | category | flops | bytes accessed | tf_op | source)
XLA Modules:
  0.0 64.8 jit_solution(5817200310110049615)
XLA Ops:
  0.6 1.5 %prep.1 = (bf16[4,8,32,128]{3,2,1,0:T(8,128)(2,1)S(1)}, bf16[2,8,32,128]{3,2,1,0:T(8,128)(2,1)S(1)}, bf16[2,8,32,128]{3,2,1,0:T(8,128)(2,1)S(1)}, f32[1,128]{1,0:T(1,128)S(1)}) custom-call(bf16[1,32,4,8,128]{4,3,2,1,0:T(8,128)(2,1)} %vol_ref.1, f32[4,16]{1,0:T(4,128)} %hist_ref.5), custom_call_target="tpu_custom_call" | custom-call | tf_op jit(solution)/shard_map/prep/pallas_call | solution.py:615
  2.1 3.1 %collective-permute-start = (bf16[2,8,32,128]{3,2,1,0:T(8,128)(2,1)S(1)}, bf16[2,8,32,128]{3,2,1,0:T(8,128)(2,1)S(1)}, u32[]{:S(2)}, u32[]{:S(2)}) collective-permute-start(bf16[2,8,32,128]{3,2,1,0:T(8,128)(2,1)S(1)} %get-tuple-element.23), channel_id=1, source_target_pairs={{0,1},{1,0},{2,3},{3,2},{4,5},{5,4},{6,7},{7,6},{8,9},{9,8},{10,11... | collective-permute-start | bytes 393224 | tf_op jit(solution)/shard_map/ppermute | solution.py:639
  5.2 0.7 %collective-permute-start.1 = (bf16[2,8,32,128]{3,2,1,0:T(8,128)(2,1)S(1)}, bf16[2,8,32,128]{3,2,1,0:T(8,128)(2,1)S(1)}, u32[]{:S(2)}, u32[]{:S(2)}) collective-permute-start(bf16[2,8,32,128]{3,2,1,0:T(8,128)(2,1)S(1)} %get-tuple-element.24), channel_id=1, source_target_pairs={{0,0},{1,2},{2,1},{3,3},{4,4},{5,6},{6,5},{7,7},{8,8},{9,10},{10,9... | collective-permute-start | bytes 393224 | tf_op jit(solution)/shard_map/ppermute | solution.py:640
  5.9 1.4 %matrices.1 = (bf16[96,288]{1,0:T(8,128)(2,1)S(1)}, bf16[96,288]{1,0:T(8,128)(2,1)S(1)}, bf16[96,256]{1,0:T(8,128)(2,1)S(1)}, bf16[48,576]{1,0:T(8,128)(2,1)S(1)}) custom-call(f32[1,128]{1,0:T(1,128)S(1)} %get-tuple-element.25.peak_ref, bf16[27,32,32]{2,1,0:T(8,128)(2,1)} %first_ref.1, bf16[27,32,32]{2,1,0:T(8,128)(2,1)} %second_ref.1, ...), custom_call_target="tpu_custom_call" | custom-call | tf_op jit(solution)/shard_map/matrices/pallas_call | solution.py:627
  7.3 1.5 %collective-permute-done.got_first_ref.z_first_ref = bf16[2,8,32,128]{3,2,1,0:T(8,128)(2,1)S(1)} collective-permute-done((bf16[2,8,32,128]{3,2,1,0:T(8,128)(2,1)S(1)}, bf16[2,8,32,128]{3,2,1,0:T(8,128)(2,1)S(1)}, u32[]{:S(2)}, u32[]{:S(2)}) %collective-permute-start) | collective-permute-done | bytes 131104 | tf_op jit(solution)/shard_map/ppermute | solution.py:639
  8.7 0.0 collective-permute-done.1.got_second_ref.z_second_ref
  8.8 0.1 collective-permute-start.2
  8.8 0.7 %collective-permute-start.3 = (bf16[8,2,32,128]{3,2,1,0:T(8,128)(2,1)S(1)}, bf16[8,2,32,128]{3,2,1,0:T(8,128)(2,1)S(1)}, u32[]{:S(2)}, u32[]{:S(2)}) collective-permute-start(bf16[8,2,32,128]{3,2,1,0:T(8,128)(2,1)S(1)} %get-tuple-element.28), channel_id=1, source_target_pairs={{0,0},{4,8},{8,4},{12,12},{1,1},{5,9},{9,5},{13,13},{2,2},{6,10},{... | collective-permute-start | bytes 393224 | tf_op jit(solution)/shard_map/ppermute | solution.py:652
  9.5 0.7 %collective-permute-done.2.y_first_ref = bf16[8,2,32,128]{3,2,1,0:T(8,128)(2,1)S(1)} collective-permute-done((bf16[8,2,32,128]{3,2,1,0:T(8,128)(2,1)S(1)}, bf16[8,2,32,128]{3,2,1,0:T(8,128)(2,1)S(1)}, u32[]{:S(2)}, u32[]{:S(2)}) %collective-permute-start.2) | collective-permute-done | bytes 131104 | tf_op jit(solution)/shard_map/ppermute | solution.py:651
  10.2 0.0 collective-permute-done.3.y_second_ref
  10.2 2.5 %first.1 = (f32[6,10,32,128]{3,2,1,0:T(8,128)S(1)}, f32[16,1,128]{2,1,0:T(1,128)S(1)}) custom-call(bf16[4,8,32,128]{3,2,1,0:T(8,128)(2,1)S(1)} %get-tuple-element.22.cells_ref.own_ref, bf16[2,8,32,128]{3,2,1,0:T(8,128)(2,1)S(1)} %collective-permute-done.got_first_ref.z_first_ref, ...), custom_call_target="tpu_custom_call" | custom-call | tf_op jit(solution)/shard_map/first/pallas_call | solution.py:653
  12.7 19.4 %all_to_all.5.rows_ref = f32[16,1,128]{2,1,0:T(1,128)S(1)} all-to-all(f32[16,1,128]{2,1,0:T(1,128)S(1)} %get-tuple-element.30), channel_id=1, replica_groups=mesh['sample'=2,'sy'=4,'sz'=4] {'sy','sz'}, dimensions={0} | all-to-all | bytes 16384 | tf_op jit(solution)/shard_map/all_to_all | solution.py:662
  32.1 2.7 %second.1 = (f32[4,8,32,128]{3,2,1,0:T(8,128)S(1)}, bf16[80,256]{1,0:T(8,128)(2,1)S(1)}) custom-call(f32[6,10,32,128]{3,2,1,0:T(8,128)S(1)} %get-tuple-element.29.raw_ref, f32[16,1,128]{2,1,0:T(1,128)S(1)} %all_to_all.5.rows_ref, bf16[96,288]{1,0:T(8,128)(2,1)S(1)} %get-tuple-element.31.weight_ref, f32[4,16]{1,0:T(4,128)} %hist_ref.5, f32[2,32]{1,0:T(2,128)} %gain_ref.4, ...), custom_call_target="tpu_custom_call" | custom-call | tf_op jit(solution)/shard_map/second/pallas_call | solution.py:663
  34.8 0.6 collective-permute-start.6
  35.4 1.4 %collective-permute-start.5 = (bf16[80,256]{1,0:T(8,128)(2,1)S(1)}, bf16[80,256]{1,0:T(8,128)(2,1)S(1)}, u32[]{:S(2)}, u32[]{:S(2)}) collective-permute-start(bf16[80,256]{1,0:T(8,128)(2,1)S(1)} %get-tuple-element.32), channel_id=1, source_target_pairs={{0,2},{1,3},{2,0},{3,1},{4,6},{5,7},{6,4},{7,5},{8,10},{9,11},{10,... | collective-permute-start | bytes 122888 | tf_op jit(solution)/shard_map/ppermute | solution.py:677
  36.8 2.4 %collective-permute-start.4 = (bf16[80,256]{1,0:T(8,128)(2,1)S(1)}, bf16[80,256]{1,0:T(8,128)(2,1)S(1)}, u32[]{:S(2)}, u32[]{:S(2)}) collective-permute-start(bf16[80,256]{1,0:T(8,128)(2,1)S(1)} %get-tuple-element.32), channel_id=1, source_target_pairs={{0,1},{1,0},{2,3},{3,2},{4,5},{5,4},{6,7},{7,6},{8,9},{9,8},{10,11... | collective-permute-start | bytes 122888 | tf_op jit(solution)/shard_map/ppermute | solution.py:677
  39.2 2.0 %collective-permute-done.4 = bf16[80,256]{1,0:T(8,128)(2,1)S(1)} collective-permute-done((bf16[80,256]{1,0:T(8,128)(2,1)S(1)}, bf16[80,256]{1,0:T(8,128)(2,1)S(1)}, u32[]{:S(2)}, u32[]{:S(2)}) %collective-permute-start.4) | collective-permute-done | bytes 40992 | tf_op jit(solution)/shard_map/ppermute | solution.py:677
  41.3 0.2 collective-permute-done.5
  41.4 0.0 collective-permute-done.6
  41.5 8.0 %all-gather = bf16[1664,256]{1,0:T(8,128)(2,1)S(1)} all-gather(bf16[416,256]{1,0:T(8,128)(2,1)S(1)} %constant_dynamic-update-slice_fusion), channel_id=2, replica_groups=mesh['sample'=2,'sy'=4,'sz'=4] {'sy'}, dimensions={0}, use_global_device_ids=true | all-gather | bytes 1064960 | tf_op jit(solution)/shard_map/all_gather | solution.py:679
  49.5 6.9 %third.1 = (bf16[8,64,1024]{2,1,0:T(8,128)(2,1)S(1)}, f32[1,128]{1,0:T(1,128)S(1)}, f32[32,128]{1,0:T(8,128)S(1)}) custom-call(bf16[4,416,256]{2,1,0:T(8,128)(2,1)S(1)} %bitcast.3, f32[4,16]{1,0:T(4,128)} %hist_ref.5, f32[2,32]{1,0:T(2,128)} %gain_ref.4, f32[2,32]{1,0:T(2,128)} %shift_ref.4), custom_call_target="tpu_custom_call" | custom-call | tf_op jit(solution)/shard_map/third/pallas_call | solution.py:680
  56.4 1.6 %collective-permute-start.7 = (f32[1,128]{1,0:T(1,128)S(1)}, f32[1,128]{1,0:T(1,128)S(1)}, u32[]{:S(2)}, u32[]{:S(2)}) collective-permute-start(f32[1,128]{1,0:T(1,128)S(1)} %get-tuple-element.40), channel_id=1, source_target_pairs={{0,16},{16,0},{1,17},{17,1},{2,18},{18,2},{3,19},{19,3},{4,20},{20... | collective-permute-start | bytes 1544 | tf_op jit(solution)/shard_map/ppermute | solution.py:696
  57.9 6.3 %fourth.1 = (bf16[1,16,2,1024]{3,2,1,0:T(2,128)(2,1)}, bf16[1,32,4,8,128]{4,3,2,1,0:T(8,128)(2,1)}) custom-call(bf16[8,64,1024]{2,1,0:T(8,128)(2,1)S(1)} %get-tuple-element.34.cells_ref, bf16[48,576]{1,0:T(8,128)(2,1)S(1)} %get-tuple-element.35.weight_ref, f32[2,16]{1,0:T(2,128)} %gain_ref.5, f32[2,16]{1,0:T(2,128)} %shift_ref.5, ...), custom_call_target="tpu_custom_call" | custom-call | tf_op jit(solution)/shard_map/fourth/pallas_call | solution.py:701
  64.2 0.0 collective-permute-done.7
  64.3 0.5 slice_bitcast_fusion
  (7 shorter events, 0.0 us)
Async XLA Ops:
  2.1 6.6 %collective-permute-start = (bf16[2,8,32,128]{3,2,1,0:T(8,128)(2,1)S(1)}, bf16[2,8,32,128]{3,2,1,0:T(8,128)(2,1)S(1)}, u32[]{:S(2)}, u32[]{:S(2)}) collective-permute-start(bf16[2,8,32,128]{3,2,1,0:T(8,128)(2,1)S(1)} %get-tuple-element.23), channel_id=1, source_target_pairs={{0,1},{1,0},{2,3},{3,2},{4,5},{5,4},{6,7},{7,6},{8,9},{9,8},{10,11... | collective-permute-start | bytes 393224 | tf_op jit(solution)/shard_map/ppermute | solution.py:639
  5.2 3.5 %collective-permute-start.1 = (bf16[2,8,32,128]{3,2,1,0:T(8,128)(2,1)S(1)}, bf16[2,8,32,128]{3,2,1,0:T(8,128)(2,1)S(1)}, u32[]{:S(2)}, u32[]{:S(2)}) collective-permute-start(bf16[2,8,32,128]{3,2,1,0:T(8,128)(2,1)S(1)} %get-tuple-element.24), channel_id=1, source_target_pairs={{0,0},{1,2},{2,1},{3,3},{4,4},{5,6},{6,5},{7,7},{8,8},{9,10},{10,9... | collective-permute-start | bytes 393224 | tf_op jit(solution)/shard_map/ppermute | solution.py:640
  8.8 1.4 %collective-permute-start.2 = (bf16[8,2,32,128]{3,2,1,0:T(8,128)(2,1)S(1)}, bf16[8,2,32,128]{3,2,1,0:T(8,128)(2,1)S(1)}, u32[]{:S(2)}, u32[]{:S(2)}) collective-permute-start(bf16[8,2,32,128]{3,2,1,0:T(8,128)(2,1)S(1)} %get-tuple-element.27), channel_id=1, source_target_pairs={{0,4},{4,0},{8,12},{12,8},{1,5},{5,1},{9,13},{13,9},{2,6},{6,2},{1... | collective-permute-start | bytes 393224 | tf_op jit(solution)/shard_map/ppermute | solution.py:651
  8.8 1.3 %collective-permute-start.3 = (bf16[8,2,32,128]{3,2,1,0:T(8,128)(2,1)S(1)}, bf16[8,2,32,128]{3,2,1,0:T(8,128)(2,1)S(1)}, u32[]{:S(2)}, u32[]{:S(2)}) collective-permute-start(bf16[8,2,32,128]{3,2,1,0:T(8,128)(2,1)S(1)} %get-tuple-element.28), channel_id=1, source_target_pairs={{0,0},{4,8},{8,4},{12,12},{1,1},{5,9},{9,5},{13,13},{2,2},{6,10},{... | collective-permute-start | bytes 393224 | tf_op jit(solution)/shard_map/ppermute | solution.py:652
  34.8 6.7 %collective-permute-start.6 = (bf16[80,256]{1,0:T(8,128)(2,1)S(1)}, bf16[80,256]{1,0:T(8,128)(2,1)S(1)}, u32[]{:S(2)}, u32[]{:S(2)}) collective-permute-start(bf16[80,256]{1,0:T(8,128)(2,1)S(1)} %get-tuple-element.32), channel_id=1, source_target_pairs={{0,3},{1,2},{2,1},{3,0},{4,7},{5,6},{6,5},{7,4},{8,11},{9,10},{10,... | collective-permute-start | bytes 122888 | tf_op jit(solution)/shard_map/ppermute | solution.py:677
  35.4 6.0 %collective-permute-start.5 = (bf16[80,256]{1,0:T(8,128)(2,1)S(1)}, bf16[80,256]{1,0:T(8,128)(2,1)S(1)}, u32[]{:S(2)}, u32[]{:S(2)}) collective-permute-start(bf16[80,256]{1,0:T(8,128)(2,1)S(1)} %get-tuple-element.32), channel_id=1, source_target_pairs={{0,2},{1,3},{2,0},{3,1},{4,6},{5,7},{6,4},{7,5},{8,10},{9,11},{10,... | collective-permute-start | bytes 122888 | tf_op jit(solution)/shard_map/ppermute | solution.py:677
  36.8 4.4 %collective-permute-start.4 = (bf16[80,256]{1,0:T(8,128)(2,1)S(1)}, bf16[80,256]{1,0:T(8,128)(2,1)S(1)}, u32[]{:S(2)}, u32[]{:S(2)}) collective-permute-start(bf16[80,256]{1,0:T(8,128)(2,1)S(1)} %get-tuple-element.32), channel_id=1, source_target_pairs={{0,1},{1,0},{2,3},{3,2},{4,5},{5,4},{6,7},{7,6},{8,9},{9,8},{10,11... | collective-permute-start | bytes 122888 | tf_op jit(solution)/shard_map/ppermute | solution.py:677
  56.4 7.9 %collective-permute-start.7 = (f32[1,128]{1,0:T(1,128)S(1)}, f32[1,128]{1,0:T(1,128)S(1)}, u32[]{:S(2)}, u32[]{:S(2)}) collective-permute-start(f32[1,128]{1,0:T(1,128)S(1)} %get-tuple-element.40), channel_id=1, source_target_pairs={{0,16},{16,0},{1,17},{17,1},{2,18},{18,2},{3,19},{19,3},{4,20},{20... | collective-permute-start | bytes 1544 | tf_op jit(solution)/shard_map/ppermute | solution.py:696

commit v4 on v3

--- a/solution.py
+++ b/solution.py
@@ -7,6 +7,13 @@
 
 norm_eps = 1e-05
 leak_slope = 0.01
+UNROLL_FIRST = 1
+UNROLL_HIDDEN = 1
+UNROLL_SECOND = 1
+UNROLL_SPREAD = 1
+UNROLL_THIRD = 1
+UNROLL_NORMED = 1
+UNROLL_FOURTH = 1
 f32 = jnp.float32
 bf16 = jnp.bfloat16
 LANES = 128
@@ -64,30 +71,79 @@
     return jnp.minimum(jnp.maximum(values, -bound), bound)
 
 
+BOUND_AT = 4
+LAST_AT = 8
+
+
 def bound_of(hist_ref, level):
-    return jnp.max(hist_ref[level : level + 1, :], axis=1, keepdims=True).astype(bf16)
-
-
-def matrix_of(weight, taps_ref):
-    taps, out_chan, in_chan = weight.shape
+    return jnp.max(hist_ref[level : level + 1, :], axis=1, keepdims=True)
+
+
+def lane_of(param_ref, lane, channels):
+    return param_ref[0:channels, lane : lane + 1]
+
+
+def clip_bound(param_ref, level):
+    return param_ref[0:1, BOUND_AT + level : BOUND_AT + level + 1].astype(bf16)
+
+
+def matrix_of(weight, taps_ref, groups):
+    out_chan = weight.shape[1]
     for dx in range(3):
         taps_ref[dx * out_chan : (dx + 1) * out_chan, :] = jnp.concatenate(
-            [weight[3 * j + dx] for j in range(taps // 3)], axis=1
+            [weight[3 * j + dx] for j in groups], axis=1
         )
 
 
 def matrix_kernel(
-    peak_ref, first_ref, second_ref, third_ref, fourth_ref, m1_ref, m2_ref, m3_ref, m4_ref, wide_ref
+    peak_ref,
+    first_ref,
+    second_ref,
+    third_ref,
+    fourth_ref,
+    hist_ref,
+    gain_ref,
+    shift_ref,
+    gain_coarse_ref,
+    shift_coarse_ref,
+    m1_ref,
+    m2_ref,
+    m3_ref,
+    m4_ref,
+    param_ref,
+    gain_row_ref,
 ):
-    matrix_of(first_ref, m1_ref)
-    matrix_of(second_ref, m2_ref)
-    matrix_of(fourth_ref, m4_ref)
-    matrix_of(third_ref, wide_ref)
-    rows, span = m3_ref.shape[0] // 2, m3_ref.shape[1]
-    rest = wide_ref.shape[1] - span
-    m3_ref[:rows, :] = wide_ref[:, :span]
-    m3_ref[rows:, :] = jnp.concatenate(
-        [wide_ref[:, span:], jnp.zeros((rows, span - rest), bf16)], axis=1
+    taps = first_ref.shape[0]
+    matrix_of(first_ref, m1_ref, range(taps // 3))
+    matrix_of(second_ref, m2_ref, range(taps // 3))
+    own = third_ref.shape[1]
+    matrix_of(third_ref, m3_ref.at[0 : 3 * own], range(taps // 3 - 1))
+    last = [third_ref[taps - 3 + dx] for dx in range(3)]
+    rest = m3_ref.shape[1] - 3 * third_ref.shape[2]
+    m3_ref[3 * own :, :] = jnp.concatenate(last + [jnp.zeros((own, rest), bf16)], axis=1)
+    for dy in range(3):
+        for dx in range(3):
+            at = (3 * dy + dx) * own
+            m4_ref[at : at + own, :] = jnp.concatenate(
+                [fourth_ref[9 * dz + 3 * dy + dx] for dz in range(3)], axis=1
+            )
+    channels = param_ref.shape[0]
+    lanes = lax.broadcasted_iota(jnp.int32, (channels, LANES), 1)
+    params = jnp.zeros((channels, LANES), f32)
+    columns = []
+    for layer in range(2):
+        columns.append((2 * layer, column(gain_ref[layer : layer + 1, :], channels, 0)))
+        columns.append((2 * layer + 1, column(shift_ref[layer : layer + 1, :], channels, 0)))
+    for level in range(hist_ref.shape[0]):
+        columns.append((BOUND_AT + level, bound_of(hist_ref, level)))
+    pad = jnp.zeros((channels - own, 1), f32)
+    for place, ref in ((LAST_AT, gain_coarse_ref), (LAST_AT + 1, shift_coarse_ref)):
+        columns.append((place, jnp.concatenate([column(ref[1:2, :], own, 0), pad], axis=0)))
+    for lane, value in columns:
+        params = jnp.where(lanes == lane, value, params)
+    param_ref[...] = params
+    gain_row_ref[...] = as_row(column(gain_coarse_ref[0:1, :], own, 0), GAIN_AT) + as_row(
+        column(shift_coarse_ref[0:1, :], own, 0), SHIFT_AT
     )
 
 
@@ -104,7 +160,7 @@
     wide = vol_ref[0].astype(f32).reshape(channels * rows, width)
     wide_ref[...] = wide
     peak_ref[...] = jnp.broadcast_to(peak_of(jnp.abs(wide)), (1, LANES))
-    bound = bound_of(hist_ref, 0)
+    bound = bound_of(hist_ref, 0).astype(bf16)
     for r in range(rows):
         cells_ref[r // height, r % height] = bounded(
             wide_ref[pl.ds(r, channels, stride=rows), :].astype(bf16), bound
@@ -214,7 +270,7 @@
         return total, square
 
     blank = jnp.zeros((channels, LANES), f32)
-    total, square = lax.fori_loop(0, depth, plane, (blank, blank))
+    total, square = lax.fori_loop(0, depth, plane, (blank, blank), unroll=UNROLL_FIRST)
     row = as_row(jnp.sum(total, axis=1, keepdims=True), 0)
     row = row + as_row(jnp.sum(square, axis=1, keepdims=True), channels)
     row = row + at_lane(peak_ref[...], PEAK_AT)
@@ -226,11 +282,8 @@
         raw_ref,
         rows_ref,
         weight_ref,
-        hist_ref,
-        gain_ref,
-        shift_ref,
-        gain_coarse_ref,
-        shift_coarse_ref,
+        param_ref,
+        gain_row_ref,
         out_ref,
         load_ref,
         hidden_ref,
@@ -245,10 +298,10 @@
             column(merged, channels, 0),
             column(merged, channels, channels),
             cell_count,
-            column(gain_ref[0:1, :], channels, 0),
-            column(shift_ref[0:1, :], channels, 0),
-        )
-        bound = bound_of(hist_ref, 1)
+            lane_of(param_ref, 0, channels),
+            lane_of(param_ref, 1, channels),
+        )
+        bound = clip_bound(param_ref, 1)
         at_z = lax.axis_index("sz")
         at_y = lax.axis_index("sy")
         last_z = lax.axis_size("sz") - 1
@@ -271,9 +324,11 @@
             return peak
 
         blank = jnp.zeros((channels, width), f32)
-        peak = lax.fori_loop(0, wide_depth, plane, jnp.zeros((channels, width), bf16))
+        peak = lax.fori_loop(
+            0, wide_depth, plane, jnp.zeros((channels, width), bf16), unroll=UNROLL_HIDDEN
+        )
         weight = weight_ref[...]
-        sign = jnp.where(column(gain_ref[1:2, :], channels, 0) >= 0, 1.0, -1.0).astype(f32)
+        sign = jnp.where(lane_of(param_ref, 2, channels) >= 0, 1.0, -1.0).astype(f32)
         half_height = height // 2
 
         def pair(zp, sums):
@@ -295,7 +350,11 @@
             return total, square, least, most
 
         total, square, least, most = lax.fori_loop(
-            0, depth // 2, pair, (blank, blank, blank + 1e30, blank - 1e30)
+            0,
+            depth // 2,
+            pair,
+            (blank, blank, blank + 1e30, blank - 1e30),
+            unroll=UNROLL_SECOND,
         )
         most, least = peak_of(most), -peak_of(-least)
         center = 0.5 * (most + least)
@@ -314,15 +373,13 @@
                 load_ref[
                     zp * channels : (zp + 1) * channels, yq * LANES : (yq + 1) * LANES
                 ] = jnp.dot(both, pick, preferred_element_type=f32).astype(bf16)
-        mine = gain_coarse_ref.shape[1]
         row = as_row(jnp.sum(total, axis=1, keepdims=True), 0)
         row = row + as_row(jnp.sum(square, axis=1, keepdims=True), channels)
         row = row + at_lane(peak_vol, PEAK_AT)
         row = row + at_lane(peak_of(peak), PEAK_AT + 1)
         row = row + at_lane(center, CODE_AT)
         row = row + at_lane(reach / CODE_SPAN, CODE_AT + 1)
-        row = row + as_row(column(gain_coarse_ref[0:1, :], mine, 0), GAIN_AT)
-        row = row + as_row(column(shift_coarse_ref[0:1, :], mine, 0), SHIFT_AT)
+        row = row + gain_row_ref[...]
         high = row.astype(bf16).astype(f32)
         middle = (row - high).astype(bf16).astype(f32)
         low = row - high - middle
@@ -354,22 +411,24 @@
 def third_kernel(fine_cells, coarse_cells, load_rows, piece):
     def kernel(
         all_ref,
-        hist_ref,
-        gain_ref,
-        shift_ref,
+        param_ref,
+        fine_ref,
         out_ref,
         peak_ref,
-        affine_ref,
+        skip_ref,
         pool_ref,
         cells_ref,
         raw_ref,
+        wide_ref,
+        narrow_ref,
+        done,
     ):
         y_groups = all_ref.shape[0]
         z_groups = lax.axis_size("sz")
         span = all_ref.shape[2]
         planes, chan_all, flat = raw_ref.shape
-        channels = gain_ref.shape[1]
-        chan_own = piece // 3
+        channels = fine_ref.shape[2]
+        chan_own = piece // 4
         row_len = LANES // 2
         body = load_rows - 16
         z_own = body // channels
@@ -388,12 +447,19 @@
             column(merged, channels, 0),
             column(merged, channels, channels),
             fine_cells,
-            column(gain_ref[1:2, :], channels, 0),
-            column(shift_ref[1:2, :], channels, 0),
-        )
-        lanes = lax.broadcasted_iota(jnp.int32, (channels, LANES), 1)
-        affine_ref[...] = jnp.where(lanes == 0, scale, jnp.where(lanes == 1, offset, 0.0))
-        bound = bound_of(hist_ref, 2)
+            lane_of(param_ref, 2, channels),
+            lane_of(param_ref, 3, channels),
+        )
+        depth, height = fine_ref.shape[:2]
+        fine_rows = depth * height
+        for r in range(fine_rows):
+            wide_ref[pl.ds(r, channels, stride=fine_rows), :] = activated(
+                fine_ref[r // height, r % height], scale, offset
+            ).astype(f32)
+        narrow_ref[...] = wide_ref[...].reshape(narrow_ref.shape).astype(bf16)
+        skip_copy = pltpu.make_async_copy(narrow_ref, skip_ref.at[0], done)
+        skip_copy.start()
+        bound = clip_bound(param_ref, 2)
         peak_pool = jnp.zeros((channels, span), bf16)
         for s in range(y_groups):
             for k in range(z_groups):
@@ -411,41 +477,58 @@
                     )
         cells_ref[0] = jnp.zeros(cells_ref.shape[1:], bf16)
         cells_ref[planes + 1] = jnp.zeros(cells_ref.shape[1:], bf16)
+        places = (0, channels, 3 * channels)
+        edge = lax.broadcasted_iota(jnp.int32, (channels, LANES), 1) % row_len
 
         def spread_pool(z, carry):
             def store(dy, j, value):
-                cells_ref[
-                    z + 1, dy * channels : (dy + 1) * channels, j * LANES : (j + 1) * LANES
-                ] = value
+                lanes = slice(j * LANES, (j + 1) * LANES)
+                cells_ref[z + 1, places[dy] : places[dy] + channels, lanes] = value
+                if dy == 2:
+                    blank = jnp.zeros_like(value)
+                    up = jnp.where(edge == 0, blank, pltpu.roll(value, 1, 1))
+                    down = jnp.where(edge == row_len - 1, blank, pltpu.roll(value, LANES - 1, 1))
+                    cells_ref[z + 1, 2 * channels : 3 * channels, lanes] = up
+                    cells_ref[z + 1, 4 * channels :, lanes] = down
 
             spread_rows(pool_ref[z], store)
             return carry
 
-        lax.fori_loop(0, planes, spread_pool, 0)
+        lax.fori_loop(0, planes, spread_pool, 0, unroll=UNROLL_SPREAD)
         weights = z_groups * load_rows
+        main = 3 * chan_own
         near_weight = jnp.concatenate(
-            [all_ref[s, weights : weights + piece, :] for s in range(y_groups)], axis=0
+            [all_ref[s, weights : weights + main, :] for s in range(y_groups)], axis=0
         )
         far_weight = jnp.concatenate(
-            [all_ref[s, weights + piece :, 0 : 9 * channels - span] for s in range(y_groups)],
-            axis=0,
+            [all_ref[s, weights + main :, 0 : 3 * channels] for s in range(y_groups)], axis=0
         )
 
         def third(z, sums):
             totals, squares = list(sums[0]), list(sums[1])
             for t in range(flat // span):
-                window = jnp.concatenate(
-                    [cells_ref[z + dz, :, t * span : (t + 1) * span] for dz in range(3)], axis=0
+                lanes = slice(t * span, (t + 1) * span)
+                window = []
+                for dz in range(3):
+                    window.append(cells_ref[z + dz, 0 : 2 * channels, lanes])
+                    if dz < 2:
+                        window.append(cells_ref[z + dz, 3 * channels : 4 * channels, lanes])
+                window = jnp.concatenate(window, axis=0)
+                taps = jnp.dot(near_weight, window, preferred_element_type=f32)
+                rest = jnp.dot(
+                    far_weight,
+                    cells_ref[z + 2, 2 * channels :, lanes],
+                    preferred_element_type=f32,
                 )
-                taps = jnp.dot(near_weight, window[:span], preferred_element_type=f32)
-                taps = taps + jnp.dot(far_weight, window[span:], preferred_element_type=f32)
                 for s in range(y_groups):
                     for half in range(span // LANES):
-                        at = s * piece
-                        part = taps[at : at + piece, half * LANES : (half + 1) * LANES]
+                        at = s * main
+                        lanes = slice(half * LANES, (half + 1) * LANES)
+                        part = taps[at : at + main, lanes]
                         out = tap_sum(
                             part[:chan_own],
-                            part[chan_own : 2 * chan_own],
+                            part[chan_own : 2 * chan_own]
+                            + rest[s * chan_own : (s + 1) * chan_own, lanes],
                             part[2 * chan_own :],
                             row_len,
                         )
@@ -459,7 +542,7 @@
 
         blank = jnp.zeros((chan_own, LANES), f32)
         zero = tuple(blank for _ in range(y_groups))
-        totals, squares = lax.fori_loop(0, planes, third, (zero, zero))
+        totals, squares = lax.fori_loop(0, planes, third, (zero, zero), unroll=UNROLL_THIRD)
         pairs = [
             affine(
                 jnp.sum(totals[s], axis=1, keepdims=True),
@@ -472,7 +555,7 @@
         ]
         scale = jnp.concatenate([one[0] for one in pairs], axis=0)
         offset = jnp.concatenate([one[1] for one in pairs], axis=0)
-        bound = bound_of(hist_ref, 3)
+        bound = clip_bound(param_ref, 3)
 
         def normed(z, peak):
             for j in range(flat // LANES):
@@ -482,78 +565,77 @@
                 out_ref[z, :, lanes] = bounded(value, bound)
             return peak
 
-        peak_coarse = lax.fori_loop(0, planes, normed, jnp.zeros((chan_all, LANES), bf16))
+        peak_coarse = lax.fori_loop(
+            0, planes, normed, jnp.zeros((chan_all, LANES), bf16), unroll=UNROLL_NORMED
+        )
         row = at_lane(tops[:, PEAK_AT : PEAK_AT + 1], 0)
         row = row + at_lane(tops[:, PEAK_AT + 1 : PEAK_AT + 2], 1)
         row = row + at_lane(peak_of(peak_pool), 2)
         row = row + at_lane(peak_of(peak_coarse), 3)
         peak_ref[...] = row
+        skip_copy.wait()
 
     return kernel
 
 
 def fourth_kernel(coarse_cells):
-    def kernel(
-        cells_ref,
-        weight_ref,
-        gain_ref,
-        shift_ref,
-        raw_ref,
-        affine_ref,
-        out_ref,
-        skip_ref,
-        hidden_ref,
-        last_ref,
-        wide_ref,
-    ):
+    def kernel(cells_ref, weight_ref, param_ref, out_ref, last_ref):
         planes, chan_all, flat = cells_ref.shape
         chan_own, z_own = out_ref.shape[1:3]
         span = 2 * LANES
         row_len = LANES // 2
-        hidden_ref[0] = jnp.zeros(hidden_ref.shape[1:], bf16)
-        hidden_ref[planes + 1] = jnp.zeros(hidden_ref.shape[1:], bf16)
-
-        def spread_hidden(z, carry):
-            def store(dy, j, part):
-                hidden_ref[
-                    z + 1, dy * chan_all : (dy + 1) * chan_all, j * LANES : (j + 1) * LANES
-                ] = part
-
-            spread_rows(cells_ref[z], store)
-            return carry
-
-        lax.fori_loop(0, planes, spread_hidden, 0)
+        count = flat // LANES
         weight = weight_ref[...]
-
-        def fourth(z, sums):
+        lower = lax.broadcasted_iota(jnp.int32, (chan_own, LANES), 1) < row_len
+        blank = jnp.zeros((chan_own, LANES), f32)
+
+        def plane(z, taps_of, sums):
             total, square = sums
+            by_row = [[], [], []]
             for t in range(flat // span):
-                window = jnp.concatenate(
-                    [hidden_ref[z + dz, :, t * span : (t + 1) * span] for dz in range(3)], axis=0
-                )
-                taps = jnp.dot(weight, window, preferred_element_type=f32)
+                taps = taps_of(z, slice(t * span, (t + 1) * span))
                 for half in range(span // LANES):
                     part = taps[:, half * LANES : (half + 1) * LANES]
-                    out = tap_sum(
-                        part[:chan_own],
-                        part[chan_own : 2 * chan_own],
-                        part[2 * chan_own :],
-                        row_len,
-                    )
-                    start = t * span + half * LANES
-                    last_ref[z, :, start : start + LANES] = out
-                    total = total + out
-                    square = square + out * out
+                    for dy in range(3):
+                        three = [
+                            part[(3 * dy + dx) * chan_own : (3 * dy + dx + 1) * chan_own]
+                            for dx in range(3)
+                        ]
+                        by_row[dy].append(tap_sum(*three, row_len))
+            turned = [[pltpu.roll(one, row_len, 1) for one in by_row[dy]] for dy in (0, 2)]
+            for j in range(count):
+                before = turned[0][j - 1] if j > 0 else blank
+                after = turned[1][j + 1] if j + 1 < count else blank
+                out = by_row[1][j] + jnp.where(lower, before, turned[0][j])
+                out = out + jnp.where(lower, turned[1][j], after)
+                last_ref[z, :, j * LANES : (j + 1) * LANES] = out
+                total = total + out
+                square = square + out * out
             return total, square
 
-        blank = jnp.zeros((chan_own, LANES), f32)
-        total, square = lax.fori_loop(0, planes, fourth, (blank, blank))
+        def inner(z, lanes):
+            window = jnp.concatenate([cells_ref[z + dz, :, lanes] for dz in (-1, 0, 1)], axis=0)
+            return jnp.dot(weight, window, preferred_element_type=f32)
+
+        def lowest(z, lanes):
+            window = jnp.concatenate([cells_ref[z + dz, :, lanes] for dz in (0, 1)], axis=0)
+            return jnp.dot(weight[:, chan_all:], window, preferred_element_type=f32)
+
+        def highest(z, lanes):
+            window = jnp.concatenate([cells_ref[z + dz, :, lanes] for dz in (-1, 0)], axis=0)
+            return jnp.dot(weight[:, : 2 * chan_all], window, preferred_element_type=f32)
+
+        sums = plane(0, lowest, (blank, blank))
+        sums = lax.fori_loop(
+            1, planes - 1, lambda z, sums: plane(z, inner, sums), sums, unroll=UNROLL_FOURTH
+        )
+        total, square = plane(planes - 1, highest, sums)
         scale, offset = affine(
             jnp.sum(total, axis=1, keepdims=True),
             jnp.sum(square, axis=1, keepdims=True),
             coarse_cells,
-            column(gain_ref[1:2, :], chan_own, 0),
-            column(shift_ref[1:2, :], chan_own, 0),
+            lane_of(param_ref, LAST_AT, chan_own),
+            lane_of(param_ref, LAST_AT + 1, chan_own),
         )
         at_z = lax.axis_index("sz")
         own = [
@@ -561,15 +643,6 @@
         ]
         for c in range(chan_own):
             out_ref[0, c] = jnp.concatenate([one[c : c + 1] for one in own], axis=0).astype(bf16)
-        depth, height, channels, width = raw_ref.shape
-        rows = depth * height
-        scale = affine_ref[:, 0:1]
-        offset = affine_ref[:, 1:2]
-        for r in range(rows):
-            wide_ref[pl.ds(r, channels, stride=rows), :] = activated(
-                raw_ref[r // height, r % height], scale, offset
-            ).astype(f32)
-        skip_ref[0] = wide_ref[...].reshape(channels, depth, height, width).astype(bf16)
 
     return kernel
 
@@ -623,18 +696,30 @@
         scratch_shapes=[pltpu.VMEM((channels * depth * height, width), f32)],
         name="prep",
     )(volume, amax_history)
-    third_rows = 3 * chan_own
-    m1, m2, m3, m4 = pl.pallas_call(
+    third_rows = 4 * chan_own
+    m1, m2, m3, m4, params, gain_row = pl.pallas_call(
         matrix_kernel,
         out_shape=(
             near_shape((3 * channels, 9 * channels), bf16),
             near_shape((3 * channels, 9 * channels), bf16),
-            near_shape((2 * third_rows, span), bf16),
-            near_shape((third_rows, 9 * chan_all), bf16),
+            near_shape((third_rows, 8 * channels), bf16),
+            near_shape((9 * chan_own, 3 * chan_all), bf16),
+            near_shape((channels, LANES), f32),
+            near_shape((1, LANES), f32),
         ),
-        scratch_shapes=[pltpu.VMEM((third_rows, 9 * channels), bf16)],
         name="matrices",
-    )(held(peak), conv_first, conv_second, conv_third, conv_fourth)
+    )(
+        held(peak),
+        conv_first,
+        conv_second,
+        conv_third,
+        conv_fourth,
+        amax_history,
+        gain_fine,
+        shift_fine,
+        gain_coarse,
+        shift_coarse,
+    )
     pair_first, pair_second = near("sz")
     z_first = lax.ppermute(first, "sz", pair_first)
     z_second = lax.ppermute(second, "sz", pair_second)
@@ -671,26 +756,34 @@
             pltpu.VMEM((depth // 2, height // 2, channels, width), f32),
         ],
         name="second",
-    )(held(raw_first), held(rows), held(m2), amax_history, gain_fine, shift_fine, gain_coarse, shift_coarse)
+    )(*(held(x) for x in (raw_first, rows, m2, params, gain_row)))
     loads = [load]
     for k in range(1, z_groups):
         loads.append(lax.ppermute(load, "sz", [(i, i ^ k) for i in range(z_groups)]))
     loads.append(m3)
     gathered = lax.all_gather(jnp.concatenate(loads, axis=0), "sy", axis=0)
-    hidden, peaks, fine_affine = pl.pallas_call(
+    hidden, peaks, skip = pl.pallas_call(
         third_kernel(fine_cells, coarse_cells, load_rows, third_rows),
         out_shape=(
             near_shape((planes, chan_all, flat), bf16),
             near_shape((1, LANES), f32),
-            near_shape((channels, LANES), f32),
+            shape((1, channels, depth, height, width), bf16),
+        ),
+        out_specs=(
+            pl.BlockSpec(memory_space=pltpu.VMEM),
+            pl.BlockSpec(memory_space=pltpu.VMEM),
+            pl.BlockSpec(memory_space=pl.ANY),
         ),
         scratch_shapes=[
             pltpu.VMEM((planes, channels, flat), bf16),
-            pltpu.VMEM((planes + 2, 3 * channels, flat), bf16),
+            pltpu.VMEM((planes + 2, 5 * channels, flat), bf16),
             pltpu.VMEM((planes, chan_all, flat), f32),
+            pltpu.VMEM((channels * depth * height, width), f32),
+            pltpu.VMEM((channels, depth, height, width), bf16),
+            pltpu.SemaphoreType.DMA,
         ],
         name="third",
-    )(held(gathered), amax_history, gain_fine, shift_fine)
+    )(*(held(x) for x in (gathered, params, raw_second)))
     if samples <= 4:
         others = [
             lax.ppermute(peaks, "sample", [(i, (i + k) % samples) for i in range(samples)])
@@ -698,19 +791,12 @@
         ]
     else:
         others = [lax.pmax(peaks, "sample")]
-    coarse, skip = pl.pallas_call(
+    coarse = pl.pallas_call(
         fourth_kernel(coarse_cells),
-        out_shape=(
-            shape((1, chan_own, depth // 2, flat), bf16),
-            shape((1, channels, depth, height, width), bf16),
-        ),
-        scratch_shapes=[
-            pltpu.VMEM((planes + 2, 3 * chan_all, flat), bf16),
-            pltpu.VMEM((planes, chan_own, flat), f32),
-            pltpu.VMEM((channels * depth * height, width), f32),
-        ],
+        out_shape=shape((1, chan_own, depth // 2, flat), bf16),
+        scratch_shapes=[pltpu.VMEM((planes, chan_own, flat), f32)],
         name="fourth",
-    )(held(hidden), held(m4), gain_coarse, shift_coarse, held(raw_second), held(fine_affine))
+    )(*(held(x) for x in (hidden, m4, params)))
     for other in others:
         peaks = jnp.maximum(peaks, other)
     levels = amax_history.shape[0]

time: 65.1 us -> 63.5 us (0.975)
  Pallas kernels: 21.2 us -> 19.3 us
  local copies, waits for them, and re-layouts: 0.54 us -> 1.34 us
    pallas_call x1, Pallas kernels: 6.3 us -> 4.19 us  [per_device(): pl.pallas_call(fourth_kernel(coarse_cells), out_shape=shape((1, chan_own,...]
    unnamed x4 -> x8, local copies, waits for them, and re-layouts: 0.01 us -> 0.82 us
  transfers between devices with their start and end apart: 8 -> 8, of which waited for: 4 -> 4; matrix products, arithmetic and copies ran while one was open for 0% -> 0% of each run, Pallas kernels for 12% -> 9%
where the time goes in v4:
time: 63.5 us; the launch traced here: 63.3 us
  blocking collectives  27.2 us (43%)
  Pallas kernels  19.3 us (30%)
  starting transfers between devices  10.5 us (17%)
  waiting for transfers between devices  4.23 us (7%)
  local copies, waits for them, and re-layouts  1.34 us (2%)
  between operations  0.73 us (1%)
    all_to_all x1, blocking collectives, per_device(): rows = lax.all_to_all(row, ('sy', 'sz'), 0, 0, tiled=True)  19.4 us
    all_gather x1, blocking collectives, per_device(): gathered = lax.all_gather(jnp.concatenate(loads, axis=0), 'sy', axis=0)  7.81 us
    pallas_call x1, Pallas kernels, per_device(): pl.pallas_call(third_kernel(fine_cells, coarse_cells, load_rows, third_ro...  7.27 us
    ppermute x3, starting transfers between devices, per_device(): lax.ppermute(load, 'sz', [(i, i ^ k) for i in range(z_groups)])  4.39 us
    pallas_call x1, Pallas kernels, per_device(): pl.pallas_call(fourth_kernel(coarse_cells), out_shape=shape((1, chan_own,...  4.19 us
    ppermute x1, starting transfers between devices, per_device(): z_first = lax.ppermute(first, 'sz', pair_first)  3.12 us
    pallas_call x1, Pallas kernels, per_device(): pl.pallas_call(first_kernel, out_shape=(near_shape((depth + 2, height + 2...  2.49 us
    pallas_call x1, Pallas kernels, per_device(): pl.pallas_call(second_kernel(fine_cells), out_shape=(near_shape((depth, h...  2.35 us
  transfers between devices with their start and end apart: 8, of which 4 were waited for; matrix products, arithmetic and copies ran while one was open for 0% of the time, Pallas kernels for 9%

profile of v4, /device:TPU:0, one launch (start us, length us, event | category | flops | bytes accessed | tf_op | source)
XLA Modules:
  0.0 63.3 jit_solution(66681262329332786)
XLA Ops:
  0.6 1.5 %prep.1 = (bf16[4,8,32,128]{3,2,1,0:T(8,128)(2,1)S(1)}, bf16[2,8,32,128]{3,2,1,0:T(8,128)(2,1)S(1)}, bf16[2,8,32,128]{3,2,1,0:T(8,128)(2,1)S(1)}, f32[1,128]{1,0:T(1,128)S(1)}) custom-call(bf16[1,32,4,8,128]{4,3,2,1,0:T(8,128)(2,1)} %vol_ref.1, f32[4,16]{1,0:T(4,128)} %hist_ref.3), custom_call_target="tpu_custom_call" | custom-call | tf_op jit(solution)/shard_map/prep/pallas_call | solution.py:688
  2.1 3.1 %collective-permute-start = (bf16[2,8,32,128]{3,2,1,0:T(8,128)(2,1)S(1)}, bf16[2,8,32,128]{3,2,1,0:T(8,128)(2,1)S(1)}, u32[]{:S(2)}, u32[]{:S(2)}) collective-permute-start(bf16[2,8,32,128]{3,2,1,0:T(8,128)(2,1)S(1)} %get-tuple-element.23), channel_id=1, source_target_pairs={{0,1},{1,0},{2,3},{3,2},{4,5},{5,4},{6,7},{7,6},{8,9},{9,8},{10,11... | collective-permute-start | bytes 393224 | tf_op jit(solution)/shard_map/ppermute | solution.py:724
  5.2 0.7 %collective-permute-start.1 = (bf16[2,8,32,128]{3,2,1,0:T(8,128)(2,1)S(1)}, bf16[2,8,32,128]{3,2,1,0:T(8,128)(2,1)S(1)}, u32[]{:S(2)}, u32[]{:S(2)}) collective-permute-start(bf16[2,8,32,128]{3,2,1,0:T(8,128)(2,1)S(1)} %get-tuple-element.24), channel_id=1, source_target_pairs={{0,0},{1,2},{2,1},{3,3},{4,4},{5,6},{6,5},{7,7},{8,8},{9,10},{10,9... | collective-permute-start | bytes 393224 | tf_op jit(solution)/shard_map/ppermute | solution.py:725
  5.9 1.5 %matrices.1 = (bf16[96,288]{1,0:T(8,128)(2,1)S(1)}, bf16[96,288]{1,0:T(8,128)(2,1)S(1)}, bf16[64,256]{1,0:T(8,128)(2,1)S(1)}, bf16[144,192]{1,0:T(8,128)(2,1)S(1...) custom-call(f32[1,128]{1,0:T(1,128)S(1)} %get-tuple-element.25.peak_ref, bf16[27,32,32]{2,1,0:T(8,128)(2,1)} %first_ref.1, ...), custom_call_target="tpu_custom_call" | custom-call | tf_op jit(solution)/shard_map/matrices/pallas_call | solution.py:700
  7.4 1.3 %collective-permute-done.got_first_ref.z_first_ref = bf16[2,8,32,128]{3,2,1,0:T(8,128)(2,1)S(1)} collective-permute-done((bf16[2,8,32,128]{3,2,1,0:T(8,128)(2,1)S(1)}, bf16[2,8,32,128]{3,2,1,0:T(8,128)(2,1)S(1)}, u32[]{:S(2)}, u32[]{:S(2)}) %collective-permute-start) | collective-permute-done | bytes 131104 | tf_op jit(solution)/shard_map/ppermute | solution.py:724
  8.7 0.0 collective-permute-done.1.got_second_ref.z_second_ref
  8.8 0.1 collective-permute-start.2
  8.8 0.7 %collective-permute-start.3 = (bf16[8,2,32,128]{3,2,1,0:T(8,128)(2,1)S(1)}, bf16[8,2,32,128]{3,2,1,0:T(8,128)(2,1)S(1)}, u32[]{:S(2)}, u32[]{:S(2)}) collective-permute-start(bf16[8,2,32,128]{3,2,1,0:T(8,128)(2,1)S(1)} %get-tuple-element.28), channel_id=1, source_target_pairs={{0,0},{4,8},{8,4},{12,12},{1,1},{5,9},{9,5},{13,13},{2,2},{6,10},{... | collective-permute-start | bytes 393224 | tf_op jit(solution)/shard_map/ppermute | solution.py:737
  9.5 0.7 %collective-permute-done.2.y_first_ref = bf16[8,2,32,128]{3,2,1,0:T(8,128)(2,1)S(1)} collective-permute-done((bf16[8,2,32,128]{3,2,1,0:T(8,128)(2,1)S(1)}, bf16[8,2,32,128]{3,2,1,0:T(8,128)(2,1)S(1)}, u32[]{:S(2)}, u32[]{:S(2)}) %collective-permute-start.2) | collective-permute-done | bytes 131104 | tf_op jit(solution)/shard_map/ppermute | solution.py:736
  10.2 0.0 collective-permute-done.3.y_second_ref
  10.2 2.5 %first.1 = (f32[6,10,32,128]{3,2,1,0:T(8,128)S(1)}, f32[16,1,128]{2,1,0:T(1,128)S(1)}) custom-call(bf16[4,8,32,128]{3,2,1,0:T(8,128)(2,1)S(1)} %get-tuple-element.22.cells_ref.own_ref, bf16[2,8,32,128]{3,2,1,0:T(8,128)(2,1)S(1)} %collective-permute-done.got_first_ref.z_first_ref, ...), custom_call_target="tpu_custom_call" | custom-call | tf_op jit(solution)/shard_map/first/pallas_call | solution.py:738
  12.7 19.4 %all_to_all.5.rows_ref = f32[16,1,128]{2,1,0:T(1,128)S(1)} all-to-all(f32[16,1,128]{2,1,0:T(1,128)S(1)} %get-tuple-element.30), channel_id=1, replica_groups=mesh['sample'=2,'sy'=4,'sz'=4] {'sy','sz'}, dimensions={0} | all-to-all | bytes 16384 | tf_op jit(solution)/shard_map/all_to_all | solution.py:747
  32.1 2.3 %second.1 = (f32[4,8,32,128]{3,2,1,0:T(8,128)S(1)}, bf16[80,256]{1,0:T(8,128)(2,1)S(1)}) custom-call(f32[6,10,32,128]{3,2,1,0:T(8,128)S(1)} %get-tuple-element.29.raw_ref, f32[16,1,128]{2,1,0:T(1,128)S(1)} %all_to_all.5.rows_ref, bf16[96,288]{1,0:T(8,128)(2,1)S(1)} %get-tuple-element.31.weight_ref, f32[32,128]{1,0:T(8,128)S(1)} %get-tuple-element.32.param_ref, ...), custom_call_target="tpu_custom_call" | custom-call | tf_op jit(solution)/shard_map/second/pallas_call | solution.py:748
  34.4 0.0 copy-start
  34.5 0.8 %copy-done = f32[4,8,32,128]{3,2,1,0:T(8,128)} copy-done((f32[4,8,32,128]{3,2,1,0:T(8,128)}, f32[4,8,32,128]{3,2,1,0:T(8,128)S(1)}, u32[]{:S(2)}) %copy-start) | copy-done | bytes 524312
  35.2 0.6 collective-permute-start.6
  35.8 1.4 %collective-permute-start.5 = (bf16[80,256]{1,0:T(8,128)(2,1)S(1)}, bf16[80,256]{1,0:T(8,128)(2,1)S(1)}, u32[]{:S(2)}, u32[]{:S(2)}) collective-permute-start(bf16[80,256]{1,0:T(8,128)(2,1)S(1)} %get-tuple-element.34), channel_id=1, source_target_pairs={{0,2},{1,3},{2,0},{3,1},{4,6},{5,7},{6,4},{7,5},{8,10},{9,11},{10,... | collective-permute-start | bytes 122888 | tf_op jit(solution)/shard_map/ppermute | solution.py:762
  37.3 2.4 %collective-permute-start.4 = (bf16[80,256]{1,0:T(8,128)(2,1)S(1)}, bf16[80,256]{1,0:T(8,128)(2,1)S(1)}, u32[]{:S(2)}, u32[]{:S(2)}) collective-permute-start(bf16[80,256]{1,0:T(8,128)(2,1)S(1)} %get-tuple-element.34), channel_id=1, source_target_pairs={{0,1},{1,0},{2,3},{3,2},{4,5},{5,4},{6,7},{7,6},{8,9},{9,8},{10,11... | collective-permute-start | bytes 122888 | tf_op jit(solution)/shard_map/ppermute | solution.py:762
  39.6 2.0 %collective-permute-done.4 = bf16[80,256]{1,0:T(8,128)(2,1)S(1)} collective-permute-done((bf16[80,256]{1,0:T(8,128)(2,1)S(1)}, bf16[80,256]{1,0:T(8,128)(2,1)S(1)}, u32[]{:S(2)}, u32[]{:S(2)}) %collective-permute-start.4) | collective-permute-done | bytes 40992 | tf_op jit(solution)/shard_map/ppermute | solution.py:762
  41.7 0.2 collective-permute-done.5
  41.9 0.0 collective-permute-done.6
  41.9 0.0 copy-start.1
  41.9 7.8 %all-gather = bf16[1536,256]{1,0:T(8,128)(2,1)S(1)} all-gather(bf16[384,256]{1,0:T(8,128)(2,1)S(1)} %constant_dynamic-update-slice_fusion), channel_id=2, replica_groups=mesh['sample'=2,'sy'=4,'sz'=4] {'sy'}, dimensions={0}, use_global_device_ids=true | all-gather | bytes 983040 | tf_op jit(solution)/shard_map/all_gather | solution.py:764
  49.7 0.0 copy-done.1
  49.7 7.3 %third.1 = (bf16[8,64,1024]{2,1,0:T(8,128)(2,1)S(1)}, f32[1,128]{1,0:T(1,128)S(1)}, bf16[1,32,4,8,128]{4,3,2,1,0:T(8,128)(2,1)}) custom-call(bf16[4,384,256]{2,1,0:T(8,128)(2,1)S(1)} %bitcast.3, f32[32,128]{1,0:T(8,128)S(1)} %get-tuple-element.32.param_ref, f32[4,8,32,128]{3,2,1,0:T(8,128)S(1)} %copy-done.1), custom_call_target="tpu_custom_call" | custom-call | tf_op jit(solution)/shard_map/third/pallas_call | solution.py:765
  57.0 1.6 %collective-permute-start.7 = (f32[1,128]{1,0:T(1,128)S(1)}, f32[1,128]{1,0:T(1,128)S(1)}, u32[]{:S(2)}, u32[]{:S(2)}) collective-permute-start(f32[1,128]{1,0:T(1,128)S(1)} %get-tuple-element.40), channel_id=1, source_target_pairs={{0,16},{16,0},{1,17},{17,1},{2,18},{18,2},{3,19},{19,3},{4,20},{20... | collective-permute-start | bytes 1544 | tf_op jit(solution)/shard_map/ppermute | solution.py:789
  58.6 4.2 %fourth.1 = bf16[1,16,2,1024]{3,2,1,0:T(2,128)(2,1)} custom-call(bf16[8,64,1024]{2,1,0:T(8,128)(2,1)S(1)} %get-tuple-element.38.cells_ref, bf16[144,192]{1,0:T(8,128)(2,1)S(1)} %get-tuple-element.39.weight_ref, f32[32,128]{1,0:T(8,128)S(1)} %get-tuple-element.32.param_ref), custom_call_target="tpu_custom_call" | custom-call | tf_op jit(solution)/shard_map/fourth/pallas_call | solution.py:794
  62.7 0.0 collective-permute-done.7
  62.7 0.5 slice_bitcast_fusion
  (7 shorter events, 0.0 us)
Async XLA Ops:
  2.1 6.6 %collective-permute-start = (bf16[2,8,32,128]{3,2,1,0:T(8,128)(2,1)S(1)}, bf16[2,8,32,128]{3,2,1,0:T(8,128)(2,1)S(1)}, u32[]{:S(2)}, u32[]{:S(2)}) collective-permute-start(bf16[2,8,32,128]{3,2,1,0:T(8,128)(2,1)S(1)} %get-tuple-element.23), channel_id=1, source_target_pairs={{0,1},{1,0},{2,3},{3,2},{4,5},{5,4},{6,7},{7,6},{8,9},{9,8},{10,11... | collective-permute-start | bytes 393224 | tf_op jit(solution)/shard_map/ppermute | solution.py:724
  5.2 3.5 %collective-permute-start.1 = (bf16[2,8,32,128]{3,2,1,0:T(8,128)(2,1)S(1)}, bf16[2,8,32,128]{3,2,1,0:T(8,128)(2,1)S(1)}, u32[]{:S(2)}, u32[]{:S(2)}) collective-permute-start(bf16[2,8,32,128]{3,2,1,0:T(8,128)(2,1)S(1)} %get-tuple-element.24), channel_id=1, source_target_pairs={{0,0},{1,2},{2,1},{3,3},{4,4},{5,6},{6,5},{7,7},{8,8},{9,10},{10,9... | collective-permute-start | bytes 393224 | tf_op jit(solution)/shard_map/ppermute | solution.py:725
  8.8 1.4 %collective-permute-start.2 = (bf16[8,2,32,128]{3,2,1,0:T(8,128)(2,1)S(1)}, bf16[8,2,32,128]{3,2,1,0:T(8,128)(2,1)S(1)}, u32[]{:S(2)}, u32[]{:S(2)}) collective-permute-start(bf16[8,2,32,128]{3,2,1,0:T(8,128)(2,1)S(1)} %get-tuple-element.27), channel_id=1, source_target_pairs={{0,4},{4,0},{8,12},{12,8},{1,5},{5,1},{9,13},{13,9},{2,6},{6,2},{1... | collective-permute-start | bytes 393224 | tf_op jit(solution)/shard_map/ppermute | solution.py:736
  8.8 1.3 %collective-permute-start.3 = (bf16[8,2,32,128]{3,2,1,0:T(8,128)(2,1)S(1)}, bf16[8,2,32,128]{3,2,1,0:T(8,128)(2,1)S(1)}, u32[]{:S(2)}, u32[]{:S(2)}) collective-permute-start(bf16[8,2,32,128]{3,2,1,0:T(8,128)(2,1)S(1)} %get-tuple-element.28), channel_id=1, source_target_pairs={{0,0},{4,8},{8,4},{12,12},{1,1},{5,9},{9,5},{13,13},{2,2},{6,10},{... | collective-permute-start | bytes 393224 | tf_op jit(solution)/shard_map/ppermute | solution.py:737
  34.4 0.8 %copy-start = (f32[4,8,32,128]{3,2,1,0:T(8,128)}, f32[4,8,32,128]{3,2,1,0:T(8,128)S(1)}, u32[]{:S(2)}) copy-start(f32[4,8,32,128]{3,2,1,0:T(8,128)S(1)} %get-tuple-element.36.fine_ref) | copy-start | bytes 1572868
  35.2 6.6 %collective-permute-start.6 = (bf16[80,256]{1,0:T(8,128)(2,1)S(1)}, bf16[80,256]{1,0:T(8,128)(2,1)S(1)}, u32[]{:S(2)}, u32[]{:S(2)}) collective-permute-start(bf16[80,256]{1,0:T(8,128)(2,1)S(1)} %get-tuple-element.34), channel_id=1, source_target_pairs={{0,3},{1,2},{2,1},{3,0},{4,7},{5,6},{6,5},{7,4},{8,11},{9,10},{10,... | collective-permute-start | bytes 122888 | tf_op jit(solution)/shard_map/ppermute | solution.py:762
  35.8 6.0 %collective-permute-start.5 = (bf16[80,256]{1,0:T(8,128)(2,1)S(1)}, bf16[80,256]{1,0:T(8,128)(2,1)S(1)}, u32[]{:S(2)}, u32[]{:S(2)}) collective-permute-start(bf16[80,256]{1,0:T(8,128)(2,1)S(1)} %get-tuple-element.34), channel_id=1, source_target_pairs={{0,2},{1,3},{2,0},{3,1},{4,6},{5,7},{6,4},{7,5},{8,10},{9,11},{10,... | collective-permute-start | bytes 122888 | tf_op jit(solution)/shard_map/ppermute | solution.py:762
  37.3 4.4 %collective-permute-start.4 = (bf16[80,256]{1,0:T(8,128)(2,1)S(1)}, bf16[80,256]{1,0:T(8,128)(2,1)S(1)}, u32[]{:S(2)}, u32[]{:S(2)}) collective-permute-start(bf16[80,256]{1,0:T(8,128)(2,1)S(1)} %get-tuple-element.34), channel_id=1, source_target_pairs={{0,1},{1,0},{2,3},{3,2},{4,5},{5,4},{6,7},{7,6},{8,9},{9,8},{10,11... | collective-permute-start | bytes 122888 | tf_op jit(solution)/shard_map/ppermute | solution.py:762
  41.9 7.8 %copy-start.1 = (f32[4,8,32,128]{3,2,1,0:T(8,128)S(1)}, f32[4,8,32,128]{3,2,1,0:T(8,128)}, u32[]{:S(2)}) copy-start(f32[4,8,32,128]{3,2,1,0:T(8,128)} %copy-done) | copy-start | bytes 1572868
  57.0 5.7 %collective-permute-start.7 = (f32[1,128]{1,0:T(1,128)S(1)}, f32[1,128]{1,0:T(1,128)S(1)}, u32[]{:S(2)}, u32[]{:S(2)}) collective-permute-start(f32[1,128]{1,0:T(1,128)S(1)} %get-tuple-element.40), channel_id=1, source_target_pairs={{0,16},{16,0},{1,17},{17,1},{2,18},{18,2},{3,19},{19,3},{4,20},{20... | collective-permute-start | bytes 1544 | tf_op jit(solution)/shard_map/ppermute | solution.py:789

commit v5 on v4

--- a/solution.py
+++ b/solution.py
@@ -7,13 +7,6 @@
 
 norm_eps = 1e-05
 leak_slope = 0.01
-UNROLL_FIRST = 1
-UNROLL_HIDDEN = 1
-UNROLL_SECOND = 1
-UNROLL_SPREAD = 1
-UNROLL_THIRD = 1
-UNROLL_NORMED = 1
-UNROLL_FOURTH = 1
 f32 = jnp.float32
 bf16 = jnp.bfloat16
 LANES = 128
@@ -25,7 +18,7 @@
 CODE_SPAN = 83.0
 
 
-def near(axis):
+def pairings(axis):
     count = lax.axis_size(axis)
     first = [(i, i ^ 1) for i in range(count)]
     second = [(i, min(max(((i + 1) ^ 1) - 1, 0), count - 1)) for i in range(count)]
@@ -64,7 +57,7 @@
 
 def peak_of(values):
     values = values.astype(f32)
-    return jnp.max(jnp.max(values, axis=1, keepdims=True), axis=0, keepdims=True)
+    return jnp.max(jnp.max(values, axis=0, keepdims=True), axis=1, keepdims=True)
 
 
 def bounded(values, bound):
@@ -154,17 +147,16 @@
     return middle + jnp.where(lane == 0, 0.0, up) + jnp.where(lane == period - 1, 0.0, down)
 
 
-def prep_kernel(vol_ref, hist_ref, cells_ref, first_ref, second_ref, peak_ref, wide_ref):
-    channels, depth, height, width = vol_ref.shape[1:]
-    rows = depth * height
-    wide = vol_ref[0].astype(f32).reshape(channels * rows, width)
-    wide_ref[...] = wide
-    peak_ref[...] = jnp.broadcast_to(peak_of(jnp.abs(wide)), (1, LANES))
+def prep_kernel(vol_ref, hist_ref, cells_ref, first_ref, second_ref, peak_ref):
+    depth = vol_ref.shape[2]
     bound = bound_of(hist_ref, 0).astype(bf16)
-    for r in range(rows):
-        cells_ref[r // height, r % height] = bounded(
-            wide_ref[pl.ds(r, channels, stride=rows), :].astype(bf16), bound
-        )
+    top = jnp.zeros(cells_ref.shape[2:], bf16)
+    for z in range(depth):
+        rows = jnp.transpose(vol_ref[0, :, z], (1, 0, 2))
+        for y in range(rows.shape[0]):
+            top = jnp.maximum(top, jnp.abs(rows[y]))
+            cells_ref[z, y] = bounded(rows[y], bound)
+    peak_ref[...] = jnp.broadcast_to(peak_of(top), (1, LANES))
     even = lax.axis_index("sz") % 2 == 0
     start_first = jnp.where(even, depth - HALO, 0)
     start_second = jnp.where(even, 0, depth - HALO)
@@ -195,12 +187,10 @@
         out_ref[HALO:far] = cells_ref[:, rows]
 
 
-def conv_rows(cells_ref, weight, z, y, out_chan):
+def conv_rows(cell, weight, z, rows, out_chan):
     window = jnp.concatenate(
         [
-            jnp.concatenate(
-                [cells_ref[z + dz, y + dy], cells_ref[z + dz, y + 1 + dy]], axis=1
-            )
+            jnp.concatenate([cell(z + dz, y + dy) for y in rows], axis=1)
             for dz in range(3)
             for dy in range(3)
         ],
@@ -218,59 +208,65 @@
     return outs
 
 
-def first_kernel(
-    own_ref,
-    z_first_ref,
-    z_second_ref,
-    y_first_ref,
-    y_second_ref,
-    weight_ref,
-    peak_ref,
-    raw_ref,
-    row_ref,
-    cells_ref,
-):
-    depth, height = raw_ref.shape[:2]
-    channels = raw_ref.shape[2]
-    own_depth, own_height = own_ref.shape[:2]
-    below, above = sides("sz", z_first_ref[...], z_second_ref[...])
-    rows = slice(HALO, HALO + own_height)
-    cells_ref[0:HALO, rows] = below
-    cells_ref[HALO : HALO + own_depth, rows] = own_ref[...]
-    cells_ref[HALO + own_depth :, rows] = above
-    below, above = sides("sy", y_first_ref[...], y_second_ref[...])
-    cells_ref[:, 0:HALO] = below
-    cells_ref[:, HALO + own_height :] = above
-
-    @pl.when(lax.axis_index("sz") == 0)
-    def _():
-        for edge in (slice(0, HALO), slice(HALO + own_height, 2 * HALO + own_height)):
-            cells_ref[0:HALO, edge] = jnp.zeros((HALO, HALO) + own_ref.shape[2:], bf16)
-
-    @pl.when(lax.axis_index("sz") == lax.axis_size("sz") - 1)
-    def _():
-        for edge in (slice(0, HALO), slice(HALO + own_height, 2 * HALO + own_height)):
-            cells_ref[HALO + own_depth :, edge] = jnp.zeros(
-                (HALO, HALO) + own_ref.shape[2:], bf16
-            )
-
+def first_inner_kernel(own_ref, got_first_ref, got_second_ref, weight_ref, deep_ref, raw_ref, sum_ref):
+    depth, count, channels = raw_ref.shape[:3]
+    own_depth = own_ref.shape[0]
+    below, above = sides("sz", got_first_ref[...], got_second_ref[...])
+    deep_ref[0:HALO] = below
+    deep_ref[HALO : HALO + own_depth] = own_ref[...]
+    deep_ref[HALO + own_depth :] = above
     weight = weight_ref[...]
-
-    def plane(z, sums):
-        total, square = sums
-        own = jnp.where((z >= 1) & (z < depth - 1), 1.0, 0.0).astype(f32)
-        for y in range(0, height, 2):
-            outs = conv_rows(cells_ref, weight, z, y, channels)
+    total = jnp.zeros((channels, LANES), f32)
+    square = total
+    for z in range(depth):
+        for y in range(0, count, 2):
+            outs = conv_rows(lambda z, y: deep_ref[z, y], weight, z, (y, y + 1), channels)
             for half in range(2):
                 raw_ref[z, y + half] = outs[half]
-                if 1 <= y + half < height - 1:
-                    mine = outs[half] * own
-                    total = total + mine
-                    square = square + mine * mine
-        return total, square
-
-    blank = jnp.zeros((channels, LANES), f32)
-    total, square = lax.fori_loop(0, depth, plane, (blank, blank), unroll=UNROLL_FIRST)
+                if 1 <= z < depth - 1:
+                    total = total + outs[half]
+                    square = square + outs[half] * outs[half]
+    sum_ref[0] = total
+    sum_ref[1] = square
+
+
+def first_outer_kernel(
+    deep_ref, got_first_ref, got_second_ref, weight_ref, peak_ref, sum_ref, raw_ref, row_ref, edge_ref
+):
+    depth, count, channels = raw_ref.shape[:3]
+    planes, own_height = deep_ref.shape[:2]
+    below, above = sides("sy", got_first_ref[...], got_second_ref[...])
+    edge_ref[0] = below
+    edge_ref[1] = above
+
+    for at_end, end in (
+        (lax.axis_index("sz") == 0, slice(0, HALO)),
+        (lax.axis_index("sz") == lax.axis_size("sz") - 1, slice(planes - HALO, planes)),
+    ):
+
+        @pl.when(at_end)
+        def _():
+            edge_ref[:, end] = jnp.zeros((2, HALO) + edge_ref.shape[2:], bf16)
+
+    def cell(z, y):
+        if y < HALO:
+            return edge_ref[0, z, y]
+        if y < HALO + own_height:
+            return deep_ref[z, y - HALO]
+        return edge_ref[1, z, y - HALO - own_height]
+
+    weight = weight_ref[...]
+    total = sum_ref[0]
+    square = sum_ref[1]
+    last = own_height + 2 - 1
+    for z in range(depth):
+        for place, rows in ((0, (0, 1)), (2, (last - 1, last))):
+            outs = conv_rows(cell, weight, z, rows, channels)
+            for half in range(2):
+                raw_ref[z, place + half] = outs[half]
+                if 1 <= z < depth - 1 and 1 <= rows[half] < last:
+                    total = total + outs[half]
+                    square = square + outs[half] * outs[half]
     row = as_row(jnp.sum(total, axis=1, keepdims=True), 0)
     row = row + as_row(jnp.sum(square, axis=1, keepdims=True), channels)
     row = row + at_lane(peak_ref[...], PEAK_AT)
@@ -279,7 +275,8 @@
 
 def second_kernel(cell_count):
     def kernel(
-        raw_ref,
+        inner_ref,
+        outer_ref,
         rows_ref,
         weight_ref,
         param_ref,
@@ -288,9 +285,11 @@
         load_ref,
         hidden_ref,
         pool_ref,
+        raw_ref,
+        done,
     ):
-        wide_depth, wide_height, channels, width = raw_ref.shape
-        depth, height = out_ref.shape[:2]
+        depth, height, channels, width = raw_ref.shape
+        wide_depth, wide_height = hidden_ref.shape[:2]
         rows = rows_ref[...]
         merged = jnp.sum(rows, axis=0)
         peak_vol = jnp.max(rows, axis=0)
@@ -306,39 +305,48 @@
         at_y = lax.axis_index("sy")
         last_z = lax.axis_size("sz") - 1
         last_y = lax.axis_size("sy") - 1
-
-        def plane(z, peak):
-            inside_z = ((z > 0) | (at_z > 0)) & ((z < wide_depth - 1) | (at_z < last_z))
-            own = jnp.where((z >= 1) & (z < wide_depth - 1), 1.0, 0.0).astype(bf16)
+        peak = jnp.zeros((channels, width), bf16)
+        for z in range(wide_depth):
             for y in range(wide_height):
-                inside = inside_z
-                if y == 0:
-                    inside = inside & (at_y > 0)
-                if y == wide_height - 1:
-                    inside = inside & (at_y < last_y)
-                hidden = activated(raw_ref[z, y], scale, offset)
-                if 1 <= y < wide_height - 1:
-                    peak = jnp.maximum(peak, jnp.abs(hidden) * own)
-                inside = jnp.where(inside, 1.0, 0.0).astype(bf16)
-                hidden_ref[z, y] = bounded(hidden, bound) * inside
-            return peak
+                if y < HALO:
+                    raw = outer_ref[z, y]
+                elif y < height:
+                    raw = inner_ref[z, y - HALO]
+                else:
+                    raw = outer_ref[z, y - height + HALO]
+                hidden = activated(raw, scale, offset)
+                if 1 <= y < wide_height - 1 and 1 <= z < wide_depth - 1:
+                    peak = jnp.maximum(peak, jnp.abs(hidden))
+                hidden_ref[z, y] = bounded(hidden, bound)
+        outside = (
+            (at_z == 0, (slice(0, 1), slice(0, wide_height))),
+            (at_z == last_z, (slice(wide_depth - 1, wide_depth), slice(0, wide_height))),
+            (at_y == 0, (slice(0, wide_depth), slice(0, 1))),
+            (at_y == last_y, (slice(0, wide_depth), slice(wide_height - 1, wide_height))),
+        )
+        for at_end, (zs, ys) in outside:
+
+            @pl.when(at_end)
+            def _():
+                count = (zs.stop - zs.start, ys.stop - ys.start)
+                hidden_ref[zs, ys] = jnp.zeros(count + (channels, width), bf16)
 
         blank = jnp.zeros((channels, width), f32)
-        peak = lax.fori_loop(
-            0, wide_depth, plane, jnp.zeros((channels, width), bf16), unroll=UNROLL_HIDDEN
-        )
         weight = weight_ref[...]
         sign = jnp.where(lane_of(param_ref, 2, channels) >= 0, 1.0, -1.0).astype(f32)
         half_height = height // 2
-
-        def pair(zp, sums):
-            total, square, least, most = sums
+        total, square, least, most = blank, blank, blank + 1e30, blank - 1e30
+        copies = []
+        for zp in range(depth // 2):
             for yp in range(half_height):
                 best = None
                 for dz in range(2):
-                    outs = conv_rows(hidden_ref, weight, 2 * zp + dz, 2 * yp, channels)
+                    z = 2 * zp + dz
+                    outs = conv_rows(
+                        lambda z, y: hidden_ref[z, y], weight, z, (2 * yp, 2 * yp + 1), channels
+                    )
                     for half in range(2):
-                        out_ref[2 * zp + dz, 2 * yp + half] = outs[half]
+                        raw_ref[z, 2 * yp + half] = outs[half]
                         total = total + outs[half]
                         square = square + outs[half] * outs[half]
                         signed = outs[half] * sign
@@ -347,15 +355,9 @@
                 pool_ref[zp, yp] = best
                 least = jnp.minimum(least, best)
                 most = jnp.maximum(most, best)
-            return total, square, least, most
-
-        total, square, least, most = lax.fori_loop(
-            0,
-            depth // 2,
-            pair,
-            (blank, blank, blank + 1e30, blank - 1e30),
-            unroll=UNROLL_SECOND,
-        )
+            pair = slice(2 * zp, 2 * zp + 2)
+            copies.append(pltpu.make_async_copy(raw_ref.at[pair], out_ref.at[pair], done.at[zp]))
+            copies[-1].start()
         most, least = peak_of(most), -peak_of(-least)
         center = 0.5 * (most + least)
         reach = jnp.maximum(0.5 * (most - least), 1e-30)
@@ -390,6 +392,8 @@
         body = (depth // 2) * channels
         load_ref[body:, 0:LANES] = parts.astype(bf16)
         load_ref[body:, LANES:] = jnp.zeros((16, load_ref.shape[1] - LANES), bf16)
+        for copy in copies:
+            copy.wait()
 
     return kernel
 
@@ -412,22 +416,18 @@
     def kernel(
         all_ref,
         param_ref,
-        fine_ref,
         out_ref,
         peak_ref,
-        skip_ref,
+        affine_ref,
         pool_ref,
         cells_ref,
         raw_ref,
-        wide_ref,
-        narrow_ref,
-        done,
     ):
         y_groups = all_ref.shape[0]
         z_groups = lax.axis_size("sz")
         span = all_ref.shape[2]
         planes, chan_all, flat = raw_ref.shape
-        channels = fine_ref.shape[2]
+        channels = pool_ref.shape[1]
         chan_own = piece // 4
         row_len = LANES // 2
         body = load_rows - 16
@@ -450,15 +450,8 @@
             lane_of(param_ref, 2, channels),
             lane_of(param_ref, 3, channels),
         )
-        depth, height = fine_ref.shape[:2]
-        fine_rows = depth * height
-        for r in range(fine_rows):
-            wide_ref[pl.ds(r, channels, stride=fine_rows), :] = activated(
-                fine_ref[r // height, r % height], scale, offset
-            ).astype(f32)
-        narrow_ref[...] = wide_ref[...].reshape(narrow_ref.shape).astype(bf16)
-        skip_copy = pltpu.make_async_copy(narrow_ref, skip_ref.at[0], done)
-        skip_copy.start()
+        lanes = lax.broadcasted_iota(jnp.int32, (channels, LANES), 1)
+        affine_ref[...] = jnp.where(lanes == 0, scale, jnp.where(lanes == 1, offset, 0.0))
         bound = clip_bound(param_ref, 2)
         peak_pool = jnp.zeros((channels, span), bf16)
         for s in range(y_groups):
@@ -480,7 +473,8 @@
         places = (0, channels, 3 * channels)
         edge = lax.broadcasted_iota(jnp.int32, (channels, LANES), 1) % row_len
 
-        def spread_pool(z, carry):
+        for z in range(planes):
+
             def store(dy, j, value):
                 lanes = slice(j * LANES, (j + 1) * LANES)
                 cells_ref[z + 1, places[dy] : places[dy] + channels, lanes] = value
@@ -492,9 +486,7 @@
                     cells_ref[z + 1, 4 * channels :, lanes] = down
 
             spread_rows(pool_ref[z], store)
-            return carry
-
-        lax.fori_loop(0, planes, spread_pool, 0, unroll=UNROLL_SPREAD)
+
         weights = z_groups * load_rows
         main = 3 * chan_own
         near_weight = jnp.concatenate(
@@ -504,8 +496,10 @@
             [all_ref[s, weights + main :, 0 : 3 * channels] for s in range(y_groups)], axis=0
         )
 
-        def third(z, sums):
-            totals, squares = list(sums[0]), list(sums[1])
+        blank = jnp.zeros((chan_own, LANES), f32)
+        totals = [blank for _ in range(y_groups)]
+        squares = [blank for _ in range(y_groups)]
+        for z in range(planes):
             for t in range(flat // span):
                 lanes = slice(t * span, (t + 1) * span)
                 window = []
@@ -538,11 +532,6 @@
                         ] = out
                         totals[s] = totals[s] + out
                         squares[s] = squares[s] + out * out
-            return tuple(totals), tuple(squares)
-
-        blank = jnp.zeros((chan_own, LANES), f32)
-        zero = tuple(blank for _ in range(y_groups))
-        totals, squares = lax.fori_loop(0, planes, third, (zero, zero), unroll=UNROLL_THIRD)
         pairs = [
             affine(
                 jnp.sum(totals[s], axis=1, keepdims=True),
@@ -557,29 +546,38 @@
         offset = jnp.concatenate([one[1] for one in pairs], axis=0)
         bound = clip_bound(param_ref, 3)
 
-        def normed(z, peak):
+        peak = jnp.zeros((chan_all, LANES), bf16)
+        for z in range(planes):
             for j in range(flat // LANES):
                 lanes = slice(j * LANES, (j + 1) * LANES)
                 value = activated(raw_ref[z, :, lanes], scale, offset)
                 peak = jnp.maximum(peak, jnp.abs(value))
                 out_ref[z, :, lanes] = bounded(value, bound)
-            return peak
-
-        peak_coarse = lax.fori_loop(
-            0, planes, normed, jnp.zeros((chan_all, LANES), bf16), unroll=UNROLL_NORMED
-        )
         row = at_lane(tops[:, PEAK_AT : PEAK_AT + 1], 0)
         row = row + at_lane(tops[:, PEAK_AT + 1 : PEAK_AT + 2], 1)
         row = row + at_lane(peak_of(peak_pool), 2)
-        row = row + at_lane(peak_of(peak_coarse), 3)
-        peak_ref[...] = row
-        skip_copy.wait()
+        row = row + at_lane(peak_of(peak), 3)
+        peak_ref[...] = row[:, : peak_ref.shape[1]]
 
     return kernel
 
 
 def fourth_kernel(coarse_cells):
-    def kernel(cells_ref, weight_ref, param_ref, out_ref, last_ref):
+    def kernel(
+        cells_ref,
+        weight_ref,
+        param_ref,
+        affine_ref,
+        raw_ref,
+        out_ref,
+        skip_ref,
+        last_ref,
+        fine_ref,
+        narrow_ref,
+        done,
+    ):
+        fetch = pltpu.make_async_copy(raw_ref, fine_ref, done.at[0])
+        fetch.start()
         planes, chan_all, flat = cells_ref.shape
         chan_own, z_own = out_ref.shape[1:3]
         span = 2 * LANES
@@ -626,9 +624,20 @@
             return jnp.dot(weight[:, : 2 * chan_all], window, preferred_element_type=f32)
 
         sums = plane(0, lowest, (blank, blank))
-        sums = lax.fori_loop(
-            1, planes - 1, lambda z, sums: plane(z, inner, sums), sums, unroll=UNROLL_FOURTH
-        )
+        for z in range(1, planes // 2):
+            sums = plane(z, inner, sums)
+        fetch.wait()
+        scale = affine_ref[:, 0:1]
+        offset = affine_ref[:, 1:2]
+        for z in range(fine_ref.shape[0]):
+            act = jnp.stack(
+                [activated(fine_ref[z, y], scale, offset) for y in range(fine_ref.shape[1])]
+            )
+            narrow_ref[:, z] = jnp.transpose(act, (1, 0, 2))
+        send = pltpu.make_async_copy(narrow_ref, skip_ref.at[0], done.at[1])
+        send.start()
+        for z in range(planes // 2, planes - 1):
+            sums = plane(z, inner, sums)
         total, square = plane(planes - 1, highest, sums)
         scale, offset = affine(
             jnp.sum(total, axis=1, keepdims=True),
@@ -643,6 +652,7 @@
         ]
         for c in range(chan_own):
             out_ref[0, c] = jnp.concatenate([one[c : c + 1] for one in own], axis=0).astype(bf16)
+        send.wait()
 
     return kernel
 
@@ -693,7 +703,6 @@
             near_shape((HALO, height, channels, width), bf16),
             near_shape((1, LANES), f32),
         ),
-        scratch_shapes=[pltpu.VMEM((channels * depth * height, width), f32)],
         name="prep",
     )(volume, amax_history)
     third_rows = 4 * chan_own
@@ -720,10 +729,12 @@
         gain_coarse,
         shift_coarse,
     )
-    pair_first, pair_second = near("sz")
+    pair_first, pair_second = pairings("sz")
     z_first = lax.ppermute(first, "sz", pair_first)
     z_second = lax.ppermute(second, "sz", pair_second)
     deep_depth = depth + 2 * HALO
+    anywhere = pl.BlockSpec(memory_space=pl.ANY)
+    levels = amax_history.shape[0]
     first, second = pl.pallas_call(
         deep_kernel,
         out_shape=(
@@ -732,58 +743,62 @@
         ),
         name="deep",
     )(held(cells), held(z_first), held(z_second), held(m1))
-    pair_first, pair_second = near("sy")
+    pair_first, pair_second = pairings("sy")
     y_first = lax.ppermute(first, "sy", pair_first)
     y_second = lax.ppermute(second, "sy", pair_second)
-    raw_first, row = pl.pallas_call(
-        first_kernel,
+    deep, raw_inner, sums = pl.pallas_call(
+        first_inner_kernel,
         out_shape=(
-            near_shape((depth + 2, height + 2, channels, width), f32),
+            near_shape((deep_depth, height, channels, width), bf16),
+            near_shape((depth + 2, height - 2, channels, width), f32),
+            near_shape((2, channels, LANES), f32),
+        ),
+        name="first_inner",
+    )(*(held(x) for x in (cells, z_first, z_second, m1)))
+    raw_outer, row = pl.pallas_call(
+        first_outer_kernel,
+        out_shape=(
+            near_shape((depth + 2, 2 * HALO, channels, width), f32),
             near_shape((group, 1, LANES), f32),
         ),
-        scratch_shapes=[pltpu.VMEM((deep_depth, height + 2 * HALO, channels, width), bf16)],
-        name="first",
-    )(*(held(x) for x in (cells, z_first, z_second, y_first, y_second, m1, peak)))
+        scratch_shapes=[pltpu.VMEM((2, deep_depth, HALO, channels, width), bf16)],
+        name="first_outer",
+    )(*(held(x) for x in (deep, y_first, y_second, m1, peak, sums)))
     rows = lax.all_to_all(row, ("sy", "sz"), 0, 0, tiled=True)
     raw_second, load = pl.pallas_call(
         second_kernel(fine_cells),
         out_shape=(
-            near_shape((depth, height, channels, width), f32),
+            shape((depth, height, channels, width), f32),
             near_shape((load_rows, span), bf16),
         ),
+        out_specs=(anywhere, pl.BlockSpec(memory_space=pltpu.VMEM)),
         scratch_shapes=[
             pltpu.VMEM((depth + 2, height + 2, channels, width), bf16),
             pltpu.VMEM((depth // 2, height // 2, channels, width), f32),
+            pltpu.VMEM((depth, height, channels, width), f32),
+            pltpu.SemaphoreType.DMA((depth // 2,)),
         ],
         name="second",
-    )(*(held(x) for x in (raw_first, rows, m2, params, gain_row)))
+    )(*(held(x) for x in (raw_inner, raw_outer, rows, m2, params, gain_row)))
     loads = [load]
     for k in range(1, z_groups):
         loads.append(lax.ppermute(load, "sz", [(i, i ^ k) for i in range(z_groups)]))
     loads.append(m3)
     gathered = lax.all_gather(jnp.concatenate(loads, axis=0), "sy", axis=0)
-    hidden, peaks, skip = pl.pallas_call(
+    hidden, peaks, fine_affine = pl.pallas_call(
         third_kernel(fine_cells, coarse_cells, load_rows, third_rows),
         out_shape=(
             near_shape((planes, chan_all, flat), bf16),
-            near_shape((1, LANES), f32),
-            shape((1, channels, depth, height, width), bf16),
-        ),
-        out_specs=(
-            pl.BlockSpec(memory_space=pltpu.VMEM),
-            pl.BlockSpec(memory_space=pltpu.VMEM),
-            pl.BlockSpec(memory_space=pl.ANY),
+            near_shape((1, levels), f32),
+            near_shape((channels, LANES), f32),
         ),
         scratch_shapes=[
             pltpu.VMEM((planes, channels, flat), bf16),
             pltpu.VMEM((planes + 2, 5 * channels, flat), bf16),
             pltpu.VMEM((planes, chan_all, flat), f32),
-            pltpu.VMEM((channels * depth * height, width), f32),
-            pltpu.VMEM((channels, depth, height, width), bf16),
-            pltpu.SemaphoreType.DMA,
         ],
         name="third",
-    )(*(held(x) for x in (gathered, params, raw_second)))
+    )(held(gathered), held(params))
     if samples <= 4:
         others = [
             lax.ppermute(peaks, "sample", [(i, (i + k) % samples) for i in range(samples)])
@@ -791,16 +806,26 @@
         ]
     else:
         others = [lax.pmax(peaks, "sample")]
-    coarse = pl.pallas_call(
+    near = pl.BlockSpec(memory_space=pltpu.VMEM)
+    coarse, skip = pl.pallas_call(
         fourth_kernel(coarse_cells),
-        out_shape=shape((1, chan_own, depth // 2, flat), bf16),
-        scratch_shapes=[pltpu.VMEM((planes, chan_own, flat), f32)],
+        out_shape=(
+            shape((1, chan_own, depth // 2, flat), bf16),
+            shape((1, channels, depth, height, width), bf16),
+        ),
+        in_specs=[near, near, near, near, anywhere],
+        out_specs=(near, anywhere),
+        scratch_shapes=[
+            pltpu.VMEM((planes, chan_own, flat), f32),
+            pltpu.VMEM((depth, height, channels, width), f32),
+            pltpu.VMEM((channels, depth, height, width), bf16),
+            pltpu.SemaphoreType.DMA((2,)),
+        ],
         name="fourth",
-    )(*(held(x) for x in (hidden, m4, params)))
+    )(*(held(x) for x in (hidden, m4, params, fine_affine)), raw_second)
     for other in others:
         peaks = jnp.maximum(peaks, other)
-    levels = amax_history.shape[0]
-    return skip, coarse, peaks[0, :levels]
+    return skip, coarse, peaks.reshape(levels)
 
 
 def solution(mesh):

time: 63.5 us -> 55.9 us (0.88)
  Pallas kernels: 19.3 us -> 13.5 us
  local copies, waits for them, and re-layouts: 1.34 us -> 0.02 us
  waiting for transfers between devices: 4.23 us -> 3.55 us
    pallas_call x1, Pallas kernels: 7.27 us -> 3.67 us  [per_device(): pl.pallas_call(third_kernel(fine_cells, coarse_cells, load_rows, third_ro...]
    pallas_call x3 -> x4, Pallas kernels: 9.03 us -> 7.2 us  [the longest x1 3.46 us: per_device(): pl.pallas_call(fourth_kernel(coarse_cells), out_shape=(shape((1, chan_own...]
    unnamed x8 -> x4, local copies, waits for them, and re-layouts: 0.82 us -> 0.01 us
    ppermute x1, waiting for transfers between devices: 0.66 us -> 0.01 us  [per_device(): y_first = lax.ppermute(first, 'sy', pair_first)]
  transfers between devices with their start and end apart: 8 -> 8, of which waited for: 4 -> 3; matrix products, arithmetic and copies ran while one was open for 0% -> 0% of each run, Pallas kernels for 9% -> 10%
where the time goes in v5:
time: 55.9 us; the launch traced here: 55.7 us
  blocking collectives  26.8 us (48%)
  Pallas kernels  13.5 us (24%)
  starting transfers between devices  10.5 us (19%)
  waiting for transfers between devices  3.55 us (6%)
  between operations  0.74 us (1%)
    all_to_all x1, blocking collectives, per_device(): rows = lax.all_to_all(row, ('sy', 'sz'), 0, 0, tiled=True)  19.1 us
    all_gather x1, blocking collectives, per_device(): gathered = lax.all_gather(jnp.concatenate(loads, axis=0), 'sy', axis=0)  7.68 us
    ppermute x3, starting transfers between devices, per_device(): lax.ppermute(load, 'sz', [(i, i ^ k) for i in range(z_groups)])  4.45 us
    pallas_call x1, Pallas kernels, per_device(): pl.pallas_call(third_kernel(fine_cells, coarse_cells, load_rows, third_ro...  3.67 us
    pallas_call x1, Pallas kernels, per_device(): pl.pallas_call(fourth_kernel(coarse_cells), out_shape=(shape((1, chan_own...  3.46 us
    ppermute x1, starting transfers between devices, per_device(): z_first = lax.ppermute(first, 'sz', pair_first)  3.12 us
    ppermute x3, waiting for transfers between devices, per_device(): lax.ppermute(load, 'sz', [(i, i ^ k) for i in range(z_groups)])  2.2 us
    pallas_call x1, Pallas kernels, per_device(): pl.pallas_call(second_kernel(fine_cells), out_shape=(shape((depth, height...  2.05 us
  transfers between devices with their start and end apart: 8, of which 3 were waited for; matrix products, arithmetic and copies ran while one was open for 0% of the time, Pallas kernels for 10%

profile of v5, /device:TPU:0, one launch (start us, length us, event | category | flops | bytes accessed | tf_op | source)
XLA Modules:
  0.0 55.7 jit_solution(11568511336451981049)
XLA Ops:
  0.6 1.2 %prep.1 = (bf16[4,8,32,128]{3,2,1,0:T(8,128)(2,1)S(1)}, bf16[2,8,32,128]{3,2,1,0:T(8,128)(2,1)S(1)}, bf16[2,8,32,128]{3,2,1,0:T(8,128)(2,1)S(1)}, f32[1,128]{1,0:T(1,128)S(1)}) custom-call(bf16[1,32,4,8,128]{4,3,2,1,0:T(8,128)(2,1)} %vol_ref.1, f32[4,16]{1,0:T(4,128)} %hist_ref.3), custom_call_target="tpu_custom_call" | custom-call | tf_op jit(solution)/shard_map/prep/pallas_call | solution.py:698
  1.8 3.1 %collective-permute-start = (bf16[2,8,32,128]{3,2,1,0:T(8,128)(2,1)S(1)}, bf16[2,8,32,128]{3,2,1,0:T(8,128)(2,1)S(1)}, u32[]{:S(2)}, u32[]{:S(2)}) collective-permute-start(bf16[2,8,32,128]{3,2,1,0:T(8,128)(2,1)S(1)} %get-tuple-element.28), channel_id=1, source_target_pairs={{0,1},{1,0},{2,3},{3,2},{4,5},{5,4},{6,7},{7,6},{8,9},{9,8},{10,11... | collective-permute-start | bytes 393224 | tf_op jit(solution)/shard_map/ppermute | solution.py:733
  4.9 0.7 %collective-permute-start.1 = (bf16[2,8,32,128]{3,2,1,0:T(8,128)(2,1)S(1)}, bf16[2,8,32,128]{3,2,1,0:T(8,128)(2,1)S(1)}, u32[]{:S(2)}, u32[]{:S(2)}) collective-permute-start(bf16[2,8,32,128]{3,2,1,0:T(8,128)(2,1)S(1)} %get-tuple-element.29), channel_id=1, source_target_pairs={{0,0},{1,2},{2,1},{3,3},{4,4},{5,6},{6,5},{7,7},{8,8},{9,10},{10,9... | collective-permute-start | bytes 393224 | tf_op jit(solution)/shard_map/ppermute | solution.py:734
  5.6 1.5 %matrices.1 = (bf16[96,288]{1,0:T(8,128)(2,1)S(1)}, bf16[96,288]{1,0:T(8,128)(2,1)S(1)}, bf16[64,256]{1,0:T(8,128)(2,1)S(1)}, bf16[144,192]{1,0:T(8,128)(2,1)S(1...) custom-call(f32[1,128]{1,0:T(1,128)S(1)} %get-tuple-element.30.peak_ref, bf16[27,32,32]{2,1,0:T(8,128)(2,1)} %first_ref.1, ...), custom_call_target="tpu_custom_call" | custom-call | tf_op jit(solution)/shard_map/matrices/pallas_call | solution.py:709
  7.1 1.3 %collective-permute-done.got_first_ref = bf16[2,8,32,128]{3,2,1,0:T(8,128)(2,1)S(1)} collective-permute-done((bf16[2,8,32,128]{3,2,1,0:T(8,128)(2,1)S(1)}, bf16[2,8,32,128]{3,2,1,0:T(8,128)(2,1)S(1)}, u32[]{:S(2)}, u32[]{:S(2)}) %collective-permute-start) | collective-permute-done | bytes 131104 | tf_op jit(solution)/shard_map/ppermute | solution.py:733
  8.4 0.0 collective-permute-done.1.got_second_ref
  8.5 0.1 collective-permute-start.2
  8.5 0.7 %collective-permute-start.3 = (bf16[8,2,32,128]{3,2,1,0:T(8,128)(2,1)S(1)}, bf16[8,2,32,128]{3,2,1,0:T(8,128)(2,1)S(1)}, u32[]{:S(2)}, u32[]{:S(2)}) collective-permute-start(bf16[8,2,32,128]{3,2,1,0:T(8,128)(2,1)S(1)} %get-tuple-element.35), channel_id=1, source_target_pairs={{0,0},{4,8},{8,4},{12,12},{1,1},{5,9},{9,5},{13,13},{2,2},{6,10},{... | collective-permute-start | bytes 393224 | tf_op jit(solution)/shard_map/ppermute | solution.py:748
  9.2 0.9 %first_inner.1 = (bf16[8,8,32,128]{3,2,1,0:T(8,128)(2,1)S(1)}, f32[6,6,32,128]{3,2,1,0:T(8,128)S(1)}, f32[2,32,128]{2,1,0:T(8,128)S(1)}) custom-call(bf16[4,8,32,128]{3,2,1,0:T(8,128)(2,1)S(1)} %get-tuple-element.27.own_ref.cells_ref, bf16[2,8,32,128]{3,2,1,0:T(8,128)(2,1)S(1)} %collective-permute-done.got_first_ref, ...), custom_call_target="tpu_custom_call" | custom-call | tf_op jit(solution)/shard_map/first_inner/pallas_call | solution.py:749
  10.1 0.0 collective-permute-done.2.got_first_ref
  10.1 0.0 collective-permute-done.3.got_second_ref
  10.1 0.8 %first_outer.1 = (f32[6,4,32,128]{3,2,1,0:T(8,128)S(1)}, f32[16,1,128]{2,1,0:T(1,128)S(1)}) custom-call(bf16[8,8,32,128]{3,2,1,0:T(8,128)(2,1)S(1)} %get-tuple-element.33.deep_ref, bf16[8,2,32,128]{3,2,1,0:T(8,128)(2,1)S(1)} %collective-permute-done.2.got_first_ref, bf16[8,2,32,128]{3,2,1,0:T(8,128)(2,1)S(1)} %collective-permute-done.3.got_second_ref, ...), custom_call_target="tpu_custom_call" | custom-call | tf_op jit(solution)/shard_map/first_outer/pallas_call | solution.py:758
  10.9 19.1 %all_to_all.5.rows_ref = f32[16,1,128]{2,1,0:T(1,128)S(1)} all-to-all(f32[16,1,128]{2,1,0:T(1,128)S(1)} %get-tuple-element.38), channel_id=1, replica_groups=mesh['sample'=2,'sy'=4,'sz'=4] {'sy','sz'}, dimensions={0} | all-to-all | bytes 16384 | tf_op jit(solution)/shard_map/all_to_all | solution.py:767
  30.1 2.0 %second.1 = (f32[4,8,32,128]{3,2,1,0:T(8,128)}, bf16[80,256]{1,0:T(8,128)(2,1)S(1)}) custom-call(f32[6,6,32,128]{3,2,1,0:T(8,128)S(1)} %get-tuple-element.32.inner_ref, f32[6,4,32,128]{3,2,1,0:T(8,128)S(1)} %get-tuple-element.37.outer_ref, f32[16,1,128]{2,1,0:T(1,128)S(1)} %all_to_all.5.rows_ref, bf16[96,288]{1,0:T(8,128)(2,1)S(1)} %get-tuple-element.39.weight_ref, ...), custom_call_target="tpu_custom_call" | custom-call | tf_op jit(solution)/shard_map/second/pallas_call | solution.py:768
  32.1 0.6 %collective-permute-start.6 = (bf16[80,256]{1,0:T(8,128)(2,1)S(1)}, bf16[80,256]{1,0:T(8,128)(2,1)S(1)}, u32[]{:S(2)}, u32[]{:S(2)}) collective-permute-start(bf16[80,256]{1,0:T(8,128)(2,1)S(1)} %get-tuple-element.42), channel_id=1, source_target_pairs={{0,3},{1,2},{2,1},{3,0},{4,7},{5,6},{6,5},{7,4},{8,11},{9,10},{10,... | collective-permute-start | bytes 122888 | tf_op jit(solution)/shard_map/ppermute | solution.py:785
  32.8 1.4 %collective-permute-start.5 = (bf16[80,256]{1,0:T(8,128)(2,1)S(1)}, bf16[80,256]{1,0:T(8,128)(2,1)S(1)}, u32[]{:S(2)}, u32[]{:S(2)}) collective-permute-start(bf16[80,256]{1,0:T(8,128)(2,1)S(1)} %get-tuple-element.42), channel_id=1, source_target_pairs={{0,2},{1,3},{2,0},{3,1},{4,6},{5,7},{6,4},{7,5},{8,10},{9,11},{10,... | collective-permute-start | bytes 122888 | tf_op jit(solution)/shard_map/ppermute | solution.py:785
  34.2 2.4 %collective-permute-start.4 = (bf16[80,256]{1,0:T(8,128)(2,1)S(1)}, bf16[80,256]{1,0:T(8,128)(2,1)S(1)}, u32[]{:S(2)}, u32[]{:S(2)}) collective-permute-start(bf16[80,256]{1,0:T(8,128)(2,1)S(1)} %get-tuple-element.42), channel_id=1, source_target_pairs={{0,1},{1,0},{2,3},{3,2},{4,5},{5,4},{6,7},{7,6},{8,9},{9,8},{10,11... | collective-permute-start | bytes 122888 | tf_op jit(solution)/shard_map/ppermute | solution.py:785
  36.6 2.0 %collective-permute-done.4 = bf16[80,256]{1,0:T(8,128)(2,1)S(1)} collective-permute-done((bf16[80,256]{1,0:T(8,128)(2,1)S(1)}, bf16[80,256]{1,0:T(8,128)(2,1)S(1)}, u32[]{:S(2)}, u32[]{:S(2)}) %collective-permute-start.4) | collective-permute-done | bytes 40992 | tf_op jit(solution)/shard_map/ppermute | solution.py:785
  38.6 0.2 collective-permute-done.5
  38.8 0.0 collective-permute-done.6
  38.8 7.7 %all-gather = bf16[1536,256]{1,0:T(8,128)(2,1)S(1)} all-gather(bf16[384,256]{1,0:T(8,128)(2,1)S(1)} %constant_dynamic-update-slice_fusion), channel_id=2, replica_groups=mesh['sample'=2,'sy'=4,'sz'=4] {'sy'}, dimensions={0}, use_global_device_ids=true | all-gather | bytes 983040 | tf_op jit(solution)/shard_map/all_gather | solution.py:787
  46.5 3.7 %third.1 = (bf16[8,64,1024]{2,1,0:T(8,128)(2,1)S(1)}, f32[1,4]{1,0:T(1,128)S(1)}, f32[32,128]{1,0:T(8,128)S(1)}) custom-call(bf16[4,384,256]{2,1,0:T(8,128)(2,1)S(1)} %bitcast.3, f32[32,128]{1,0:T(8,128)S(1)} %get-tuple-element.40.param_ref), custom_call_target="tpu_custom_call" | custom-call | tf_op jit(solution)/shard_map/third/pallas_call | solution.py:788
  50.2 1.5 %collective-permute-start.7 = (f32[1,4]{1,0:T(1,128)S(1)}, f32[1,4]{1,0:T(1,128)S(1)}, u32[]{:S(2)}, u32[]{:S(2)}) collective-permute-start(f32[1,4]{1,0:T(1,128)S(1)} %get-tuple-element.50), channel_id=1, source_target_pairs={{0,16},{16,0},{1,17},{17,1},{2,18},{18,2},{3,19},{19,3},{4,20},{20... | collective-permute-start | bytes 56 | tf_op jit(solution)/shard_map/ppermute | solution.py:804
  51.7 3.5 %fourth.1 = (bf16[1,16,2,1024]{3,2,1,0:T(2,128)(2,1)}, bf16[1,32,4,8,128]{4,3,2,1,0:T(8,128)(2,1)}) custom-call(bf16[8,64,1024]{2,1,0:T(8,128)(2,1)S(1)} %get-tuple-element.44.cells_ref, bf16[144,192]{1,0:T(8,128)(2,1)S(1)} %get-tuple-element.45.weight_ref, f32[32,128]{1,0:T(8,128)S(1)} %get-tuple-element.40.param_ref, ...), custom_call_target="tpu_custom_call" | custom-call | tf_op jit(solution)/shard_map/fourth/pallas_call | solution.py:810
  55.1 0.0 collective-permute-done.7
  55.1 0.5 maximum_bitcast_fusion
  (6 shorter events, 0.0 us)
Async XLA Ops:
  1.8 6.6 %collective-permute-start = (bf16[2,8,32,128]{3,2,1,0:T(8,128)(2,1)S(1)}, bf16[2,8,32,128]{3,2,1,0:T(8,128)(2,1)S(1)}, u32[]{:S(2)}, u32[]{:S(2)}) collective-permute-start(bf16[2,8,32,128]{3,2,1,0:T(8,128)(2,1)S(1)} %get-tuple-element.28), channel_id=1, source_target_pairs={{0,1},{1,0},{2,3},{3,2},{4,5},{5,4},{6,7},{7,6},{8,9},{9,8},{10,11... | collective-permute-start | bytes 393224 | tf_op jit(solution)/shard_map/ppermute | solution.py:733
  4.9 3.5 %collective-permute-start.1 = (bf16[2,8,32,128]{3,2,1,0:T(8,128)(2,1)S(1)}, bf16[2,8,32,128]{3,2,1,0:T(8,128)(2,1)S(1)}, u32[]{:S(2)}, u32[]{:S(2)}) collective-permute-start(bf16[2,8,32,128]{3,2,1,0:T(8,128)(2,1)S(1)} %get-tuple-element.29), channel_id=1, source_target_pairs={{0,0},{1,2},{2,1},{3,3},{4,4},{5,6},{6,5},{7,7},{8,8},{9,10},{10,9... | collective-permute-start | bytes 393224 | tf_op jit(solution)/shard_map/ppermute | solution.py:734
  8.5 1.7 %collective-permute-start.2 = (bf16[8,2,32,128]{3,2,1,0:T(8,128)(2,1)S(1)}, bf16[8,2,32,128]{3,2,1,0:T(8,128)(2,1)S(1)}, u32[]{:S(2)}, u32[]{:S(2)}) collective-permute-start(bf16[8,2,32,128]{3,2,1,0:T(8,128)(2,1)S(1)} %get-tuple-element.34), channel_id=1, source_target_pairs={{0,4},{4,0},{8,12},{12,8},{1,5},{5,1},{9,13},{13,9},{2,6},{6,2},{1... | collective-permute-start | bytes 393224 | tf_op jit(solution)/shard_map/ppermute | solution.py:747
  8.5 1.6 %collective-permute-start.3 = (bf16[8,2,32,128]{3,2,1,0:T(8,128)(2,1)S(1)}, bf16[8,2,32,128]{3,2,1,0:T(8,128)(2,1)S(1)}, u32[]{:S(2)}, u32[]{:S(2)}) collective-permute-start(bf16[8,2,32,128]{3,2,1,0:T(8,128)(2,1)S(1)} %get-tuple-element.35), channel_id=1, source_target_pairs={{0,0},{4,8},{8,4},{12,12},{1,1},{5,9},{9,5},{13,13},{2,2},{6,10},{... | collective-permute-start | bytes 393224 | tf_op jit(solution)/shard_map/ppermute | solution.py:748
  32.1 6.7 %collective-permute-start.6 = (bf16[80,256]{1,0:T(8,128)(2,1)S(1)}, bf16[80,256]{1,0:T(8,128)(2,1)S(1)}, u32[]{:S(2)}, u32[]{:S(2)}) collective-permute-start(bf16[80,256]{1,0:T(8,128)(2,1)S(1)} %get-tuple-element.42), channel_id=1, source_target_pairs={{0,3},{1,2},{2,1},{3,0},{4,7},{5,6},{6,5},{7,4},{8,11},{9,10},{10,... | collective-permute-start | bytes 122888 | tf_op jit(solution)/shard_map/ppermute | solution.py:785
  32.8 6.0 %collective-permute-start.5 = (bf16[80,256]{1,0:T(8,128)(2,1)S(1)}, bf16[80,256]{1,0:T(8,128)(2,1)S(1)}, u32[]{:S(2)}, u32[]{:S(2)}) collective-permute-start(bf16[80,256]{1,0:T(8,128)(2,1)S(1)} %get-tuple-element.42), channel_id=1, source_target_pairs={{0,2},{1,3},{2,0},{3,1},{4,6},{5,7},{6,4},{7,5},{8,10},{9,11},{10,... | collective-permute-start | bytes 122888 | tf_op jit(solution)/shard_map/ppermute | solution.py:785
  34.2 4.4 %collective-permute-start.4 = (bf16[80,256]{1,0:T(8,128)(2,1)S(1)}, bf16[80,256]{1,0:T(8,128)(2,1)S(1)}, u32[]{:S(2)}, u32[]{:S(2)}) collective-permute-start(bf16[80,256]{1,0:T(8,128)(2,1)S(1)} %get-tuple-element.42), channel_id=1, source_target_pairs={{0,1},{1,0},{2,3},{3,2},{4,5},{5,4},{6,7},{7,6},{8,9},{9,8},{10,11... | collective-permute-start | bytes 122888 | tf_op jit(solution)/shard_map/ppermute | solution.py:785
  50.2 5.0 %collective-permute-start.7 = (f32[1,4]{1,0:T(1,128)S(1)}, f32[1,4]{1,0:T(1,128)S(1)}, u32[]{:S(2)}, u32[]{:S(2)}) collective-permute-start(f32[1,4]{1,0:T(1,128)S(1)} %get-tuple-element.50), channel_id=1, source_target_pairs={{0,16},{16,0},{1,17},{17,1},{2,18},{18,2},{3,19},{19,3},{4,20},{20... | collective-permute-start | bytes 56 | tf_op jit(solution)/shard_map/ppermute | solution.py:804

commit v6 on v5

--- a/solution.py
+++ b/solution.py
@@ -16,6 +16,7 @@
 GAIN_AT = 80
 SHIFT_AT = 96
 CODE_SPAN = 83.0
+ROWS = 8
 
 
 def pairings(axis):
@@ -355,9 +356,13 @@
                 pool_ref[zp, yp] = best
                 least = jnp.minimum(least, best)
                 most = jnp.maximum(most, best)
-            pair = slice(2 * zp, 2 * zp + 2)
-            copies.append(pltpu.make_async_copy(raw_ref.at[pair], out_ref.at[pair], done.at[zp]))
-            copies[-1].start()
+                part = (slice(2 * zp, 2 * zp + 2), slice(2 * yp, 2 * yp + 2))
+                copies.append(
+                    pltpu.make_async_copy(
+                        raw_ref.at[part], out_ref.at[part], done.at[zp * half_height + yp]
+                    )
+                )
+                copies[-1].start()
         most, least = peak_of(most), -peak_of(-least)
         center = 0.5 * (most + least)
         reach = jnp.maximum(0.5 * (most - least), 1e-30)
@@ -385,55 +390,37 @@
         high = row.astype(bf16).astype(f32)
         middle = (row - high).astype(bf16).astype(f32)
         low = row - high - middle
-        level = lax.broadcasted_iota(jnp.int32, (16, LANES), 0)
+        level = lax.broadcasted_iota(jnp.int32, (ROWS, LANES), 0)
         parts = jnp.where(
             level == 0, high, jnp.where(level == 1, middle, jnp.where(level == 2, low, 0.0))
         )
         body = (depth // 2) * channels
         load_ref[body:, 0:LANES] = parts.astype(bf16)
-        load_ref[body:, LANES:] = jnp.zeros((16, load_ref.shape[1] - LANES), bf16)
+        load_ref[body:, LANES:] = jnp.zeros((ROWS, load_ref.shape[1] - LANES), bf16)
         for copy in copies:
             copy.wait()
 
     return kernel
 
 
-def spread_rows(cells, store):
-    count = cells.shape[1] // LANES
-    parts = [cells[:, j * LANES : (j + 1) * LANES] for j in range(count)]
-    turned = [pltpu.roll(part, LANES // 2, 1) for part in parts]
-    lower = lax.broadcasted_iota(jnp.int32, parts[0].shape, 1) < LANES // 2
-    blank = jnp.zeros_like(parts[0])
-    for j in range(count):
-        before = turned[j - 1] if j > 0 else blank
-        after = turned[j + 1] if j + 1 < count else blank
-        store(0, j, jnp.where(lower, before, turned[j]))
-        store(1, j, parts[j])
-        store(2, j, jnp.where(lower, turned[j], after))
+def turned(cells):
+    return pltpu.roll(cells, LANES // 2, 1)
 
 
 def third_kernel(fine_cells, coarse_cells, load_rows, piece):
-    def kernel(
-        all_ref,
-        param_ref,
-        out_ref,
-        peak_ref,
-        affine_ref,
-        pool_ref,
-        cells_ref,
-        raw_ref,
-    ):
+    def kernel(all_ref, param_ref, out_ref, peak_ref, affine_ref, cells_ref, raw_ref):
         y_groups = all_ref.shape[0]
         z_groups = lax.axis_size("sz")
         span = all_ref.shape[2]
         planes, chan_all, flat = raw_ref.shape
-        channels = pool_ref.shape[1]
+        channels = cells_ref.shape[1] // 3
         chan_own = piece // 4
         row_len = LANES // 2
-        body = load_rows - 16
+        blocks = flat // LANES
+        body = load_rows - ROWS
         z_own = body // channels
         at_z = lax.axis_index("sz")
-        totals = jnp.zeros((16, LANES), f32)
+        totals = jnp.zeros((ROWS, LANES), f32)
         tops = jnp.zeros((1, LANES), f32)
         rows = {}
         for s in range(y_groups):
@@ -453,40 +440,55 @@
         lanes = lax.broadcasted_iota(jnp.int32, (channels, LANES), 1)
         affine_ref[...] = jnp.where(lanes == 0, scale, jnp.where(lanes == 1, offset, 0.0))
         bound = clip_bound(param_ref, 2)
-        peak_pool = jnp.zeros((channels, span), bf16)
-        for s in range(y_groups):
-            for k in range(z_groups):
-                center = rows[s, k][:, CODE_AT : CODE_AT + 1]
-                reach = rows[s, k][:, CODE_AT + 1 : CODE_AT + 2]
-                rate = scale * reach
-                start = scale * center + offset
-                for zp in range(z_own):
-                    at = k * load_rows + zp * channels
-                    code = jnp.log(all_ref[s, at : at + channels, :].astype(f32))
-                    value = activated(code, rate, start)
-                    peak_pool = jnp.maximum(peak_pool, jnp.abs(value))
-                    pool_ref[(at_z ^ k) * z_own + zp, :, s * span : (s + 1) * span] = bounded(
-                        value, bound
-                    )
+        lower = lanes < row_len
+        edge = lanes % row_len
+        blank = jnp.zeros((channels, LANES), bf16)
+        middle = slice(channels, 2 * channels)
+
+        def at_block(block):
+            return slice(block * LANES, (block + 1) * LANES)
+
+        def keep(place, block, value):
+            cells_ref[place, middle, at_block(block)] = value
+            if block >= 2:
+                cells_ref[place, :channels, at_block(block)] = jnp.where(
+                    edge == 0, blank, pltpu.roll(value, 1, 1)
+                )
+                cells_ref[place, 2 * channels :, at_block(block)] = jnp.where(
+                    edge == row_len - 1, blank, pltpu.roll(value, LANES - 1, 1)
+                )
+
         cells_ref[0] = jnp.zeros(cells_ref.shape[1:], bf16)
         cells_ref[planes + 1] = jnp.zeros(cells_ref.shape[1:], bf16)
-        places = (0, channels, 3 * channels)
-        edge = lax.broadcasted_iota(jnp.int32, (channels, LANES), 1) % row_len
-
-        for z in range(planes):
-
-            def store(dy, j, value):
-                lanes = slice(j * LANES, (j + 1) * LANES)
-                cells_ref[z + 1, places[dy] : places[dy] + channels, lanes] = value
-                if dy == 2:
-                    blank = jnp.zeros_like(value)
-                    up = jnp.where(edge == 0, blank, pltpu.roll(value, 1, 1))
-                    down = jnp.where(edge == row_len - 1, blank, pltpu.roll(value, LANES - 1, 1))
-                    cells_ref[z + 1, 2 * channels : 3 * channels, lanes] = up
-                    cells_ref[z + 1, 4 * channels :, lanes] = down
-
-            spread_rows(pool_ref[z], store)
-
+        peak_pool = jnp.zeros((channels, span), bf16)
+        half_groups = y_groups // 2
+        for k in range(z_groups):
+            for zp in range(z_own):
+                place = (at_z ^ k) * z_own + zp + 1
+                at = k * load_rows + zp * channels
+                ends = []
+                for s in range(half_groups):
+                    both = []
+                    for own in (s, s + half_groups):
+                        center = rows[own, k][:, CODE_AT : CODE_AT + 1]
+                        reach = rows[own, k][:, CODE_AT + 1 : CODE_AT + 2]
+                        code = jnp.log(all_ref[own, at : at + channels, :].astype(f32))
+                        value = activated(code, scale * reach, scale * center + offset)
+                        peak_pool = jnp.maximum(peak_pool, jnp.abs(value))
+                        both.append(bounded(value, bound))
+                    for q in range(span // LANES):
+                        low, high = (one[:, at_block(q)] for one in both)
+                        block = s * (span // row_len) + 2 * q
+                        one = jnp.where(lower, low, turned(high))
+                        two = jnp.where(lower, turned(low), high)
+                        keep(place, block + 1, one)
+                        keep(place, block + 2, two)
+                        if block == 0:
+                            ends.append((blocks + 1, jnp.where(lower, turned(one), blank)))
+                        if block + 2 == blocks:
+                            ends.append((0, jnp.where(lower, blank, turned(two))))
+                for block, value in ends:
+                    keep(place, block, value)
         weights = z_groups * load_rows
         main = 3 * chan_own
         near_weight = jnp.concatenate(
@@ -495,40 +497,39 @@
         far_weight = jnp.concatenate(
             [all_ref[s, weights + main :, 0 : 3 * channels] for s in range(y_groups)], axis=0
         )
-
         blank = jnp.zeros((chan_own, LANES), f32)
         totals = [blank for _ in range(y_groups)]
         squares = [blank for _ in range(y_groups)]
+        width = 2 * LANES
         for z in range(planes):
-            for t in range(flat // span):
-                lanes = slice(t * span, (t + 1) * span)
-                window = []
-                for dz in range(3):
-                    window.append(cells_ref[z + dz, 0 : 2 * channels, lanes])
-                    if dz < 2:
-                        window.append(cells_ref[z + dz, 3 * channels : 4 * channels, lanes])
-                window = jnp.concatenate(window, axis=0)
-                taps = jnp.dot(near_weight, window, preferred_element_type=f32)
+            for t in range(blocks // 2):
+                window = [
+                    cells_ref[z + dz, middle, (2 * t + dy) * LANES : (2 * t + dy) * LANES + width]
+                    for dz in range(3)
+                    for dy in range(3)
+                    if dz + dy < 4
+                ]
+                taps = jnp.dot(
+                    near_weight, jnp.concatenate(window, axis=0), preferred_element_type=f32
+                )
                 rest = jnp.dot(
                     far_weight,
-                    cells_ref[z + 2, 2 * channels :, lanes],
+                    cells_ref[z + 2, :, (2 * t + 2) * LANES : (2 * t + 2) * LANES + width],
                     preferred_element_type=f32,
                 )
                 for s in range(y_groups):
-                    for half in range(span // LANES):
+                    for half in range(2):
                         at = s * main
-                        lanes = slice(half * LANES, (half + 1) * LANES)
-                        part = taps[at : at + main, lanes]
+                        part = taps[at : at + main, at_block(half)]
                         out = tap_sum(
                             part[:chan_own],
                             part[chan_own : 2 * chan_own]
-                            + rest[s * chan_own : (s + 1) * chan_own, lanes],
+                            + rest[s * chan_own : (s + 1) * chan_own, at_block(half)],
                             part[2 * chan_own :],
                             row_len,
                         )
-                        start = t * span + half * LANES
                         raw_ref[
-                            z, s * chan_own : (s + 1) * chan_own, start : start + LANES
+                            z, s * chan_own : (s + 1) * chan_own, at_block(2 * t + half)
                         ] = out
                         totals[s] = totals[s] + out
                         squares[s] = squares[s] + out * out
@@ -545,14 +546,12 @@
         scale = jnp.concatenate([one[0] for one in pairs], axis=0)
         offset = jnp.concatenate([one[1] for one in pairs], axis=0)
         bound = clip_bound(param_ref, 3)
-
         peak = jnp.zeros((chan_all, LANES), bf16)
         for z in range(planes):
-            for j in range(flat // LANES):
-                lanes = slice(j * LANES, (j + 1) * LANES)
-                value = activated(raw_ref[z, :, lanes], scale, offset)
+            for j in range(blocks):
+                value = activated(raw_ref[z, :, at_block(j)], scale, offset)
                 peak = jnp.maximum(peak, jnp.abs(value))
-                out_ref[z, :, lanes] = bounded(value, bound)
+                out_ref[z, :, at_block(j)] = bounded(value, bound)
         row = at_lane(tops[:, PEAK_AT : PEAK_AT + 1], 0)
         row = row + at_lane(tops[:, PEAK_AT + 1 : PEAK_AT + 2], 1)
         row = row + at_lane(peak_of(peak_pool), 2)
@@ -580,52 +579,56 @@
         fetch.start()
         planes, chan_all, flat = cells_ref.shape
         chan_own, z_own = out_ref.shape[1:3]
-        span = 2 * LANES
         row_len = LANES // 2
-        count = flat // LANES
+        blocks = flat // LANES
         weight = weight_ref[...]
         lower = lax.broadcasted_iota(jnp.int32, (chan_own, LANES), 1) < row_len
         blank = jnp.zeros((chan_own, LANES), f32)
 
-        def plane(z, taps_of, sums):
+        def at_block(block):
+            return slice(block * LANES, (block + 1) * LANES)
+
+        def plane(z, sums):
             total, square = sums
-            by_row = [[], [], []]
-            for t in range(flat // span):
-                taps = taps_of(z, slice(t * span, (t + 1) * span))
-                for half in range(span // LANES):
-                    part = taps[:, half * LANES : (half + 1) * LANES]
-                    for dy in range(3):
-                        three = [
-                            part[(3 * dy + dx) * chan_own : (3 * dy + dx + 1) * chan_own]
-                            for dx in range(3)
-                        ]
-                        by_row[dy].append(tap_sum(*three, row_len))
-            turned = [[pltpu.roll(one, row_len, 1) for one in by_row[dy]] for dy in (0, 2)]
-            for j in range(count):
-                before = turned[0][j - 1] if j > 0 else blank
-                after = turned[1][j + 1] if j + 1 < count else blank
-                out = by_row[1][j] + jnp.where(lower, before, turned[0][j])
-                out = out + jnp.where(lower, turned[1][j], after)
-                last_ref[z, :, j * LANES : (j + 1) * LANES] = out
+            depths = [dz for dz in range(3) if 0 <= z + dz - 1 < planes]
+            columns = slice(depths[0] * chan_all, (depths[-1] + 1) * chan_all)
+            parts = []
+            for t in range(blocks // 2):
+                window = jnp.concatenate(
+                    [
+                        cells_ref[z + dz - 1, :, 2 * t * LANES : 2 * (t + 1) * LANES]
+                        for dz in depths
+                    ],
+                    axis=0,
+                )
+                taps = jnp.dot(weight[:, columns], window, preferred_element_type=f32)
+                parts.extend(taps[:, at_block(half)] for half in range(2))
+
+            def tap(dy, dx, j):
+                at = (3 * dy + dx) * chan_own
+                return parts[j][at : at + chan_own]
+
+            for j in range(blocks):
+                three = []
+                for dx in range(3):
+                    if j > 0:
+                        before = tap(0, dx, j - 1)
+                    else:
+                        before = jnp.where(lower, blank, turned(tap(0, dx, blocks - 1)))
+                    if j + 1 < blocks:
+                        after = tap(2, dx, j + 1)
+                    else:
+                        after = jnp.where(lower, turned(tap(2, dx, 0)), blank)
+                    three.append(tap(1, dx, j) + before + after)
+                out = tap_sum(*three, row_len)
+                last_ref[z, :, at_block(j)] = out
                 total = total + out
                 square = square + out * out
             return total, square
 
-        def inner(z, lanes):
-            window = jnp.concatenate([cells_ref[z + dz, :, lanes] for dz in (-1, 0, 1)], axis=0)
-            return jnp.dot(weight, window, preferred_element_type=f32)
-
-        def lowest(z, lanes):
-            window = jnp.concatenate([cells_ref[z + dz, :, lanes] for dz in (0, 1)], axis=0)
-            return jnp.dot(weight[:, chan_all:], window, preferred_element_type=f32)
-
-        def highest(z, lanes):
-            window = jnp.concatenate([cells_ref[z + dz, :, lanes] for dz in (-1, 0)], axis=0)
-            return jnp.dot(weight[:, : 2 * chan_all], window, preferred_element_type=f32)
-
-        sums = plane(0, lowest, (blank, blank))
-        for z in range(1, planes // 2):
-            sums = plane(z, inner, sums)
+        sums = (blank, blank)
+        for z in range(planes // 2):
+            sums = plane(z, sums)
         fetch.wait()
         scale = affine_ref[:, 0:1]
         offset = affine_ref[:, 1:2]
@@ -636,9 +639,9 @@
             narrow_ref[:, z] = jnp.transpose(act, (1, 0, 2))
         send = pltpu.make_async_copy(narrow_ref, skip_ref.at[0], done.at[1])
         send.start()
-        for z in range(planes // 2, planes - 1):
-            sums = plane(z, inner, sums)
-        total, square = plane(planes - 1, highest, sums)
+        for z in range(planes // 2, planes):
+            sums = plane(z, sums)
+        total, square = sums
         scale, offset = affine(
             jnp.sum(total, axis=1, keepdims=True),
             jnp.sum(square, axis=1, keepdims=True),
@@ -647,9 +650,18 @@
             lane_of(param_ref, LAST_AT + 1, chan_own),
         )
         at_z = lax.axis_index("sz")
-        own = [
-            activated(last_ref[at_z * z_own + i], scale, offset).astype(f32) for i in range(z_own)
-        ]
+        own = []
+        for i in range(z_own):
+            cells = activated(last_ref[at_z * z_own + i], scale, offset).astype(f32)
+            natural = []
+            for p in range(blocks):
+                row = (2 * p) % blocks
+                first, second = cells[:, at_block(row)], cells[:, at_block(row + 1)]
+                if 2 * p < blocks:
+                    natural.append(jnp.where(lower, first, turned(second)))
+                else:
+                    natural.append(jnp.where(lower, turned(first), second))
+            own.append(jnp.concatenate(natural, axis=1))
         for c in range(chan_own):
             out_ref[0, c] = jnp.concatenate([one[c : c + 1] for one in own], axis=0).astype(bf16)
         send.wait()
@@ -693,7 +705,7 @@
     planes = (depth // 2) * z_groups
     flat = span * y_groups
     group = z_groups * y_groups
-    load_rows = (depth // 2) * channels + 16
+    load_rows = (depth // 2) * channels + ROWS
 
     cells, first, second, peak = pl.pallas_call(
         prep_kernel,
@@ -776,7 +788,7 @@
             pltpu.VMEM((depth + 2, height + 2, channels, width), bf16),
             pltpu.VMEM((depth // 2, height // 2, channels, width), f32),
             pltpu.VMEM((depth, height, channels, width), f32),
-            pltpu.SemaphoreType.DMA((depth // 2,)),
+            pltpu.SemaphoreType.DMA(((depth // 2) * (height // 2),)),
         ],
         name="second",
     )(*(held(x) for x in (raw_inner, raw_outer, rows, m2, params, gain_row)))
@@ -793,8 +805,7 @@
             near_shape((channels, LANES), f32),
         ),
         scratch_shapes=[
-            pltpu.VMEM((planes, channels, flat), bf16),
-            pltpu.VMEM((planes + 2, 5 * channels, flat), bf16),
+            pltpu.VMEM((planes + 2, 3 * channels, flat + 2 * LANES), bf16),
             pltpu.VMEM((planes, chan_all, flat), f32),
         ],
         name="third",

time: 55.9 us -> 55.9 us (level)
  transfers between devices with their start and end apart: 8 -> 8, of which waited for: 3 -> 2; matrix products, arithmetic and copies ran while one was open for 0% -> 0% of each run, Pallas kernels for 10% -> 11%
where the time goes in v6:
time: 55.9 us; the launch traced here: 55.6 us
  blocking collectives  26.5 us (47%)
  Pallas kernels  14 us (25%)
  starting transfers between devices  10.5 us (19%)
  waiting for transfers between devices  3.38 us (6%)
  between operations  0.76 us (1%)
    all_to_all x1, blocking collectives, per_device(): rows = lax.all_to_all(row, ('sy', 'sz'), 0, 0, tiled=True)  19.1 us
    all_gather x1, blocking collectives, per_device(): gathered = lax.all_gather(jnp.concatenate(loads, axis=0), 'sy', axis=0)  7.34 us
    ppermute x3, starting transfers between devices, per_device(): lax.ppermute(load, 'sz', [(i, i ^ k) for i in range(z_groups)])  4.45 us
    pallas_call x1, Pallas kernels, per_device(): pl.pallas_call(third_kernel(fine_cells, coarse_cells, load_rows, third_ro...  3.82 us
    pallas_call x1, Pallas kernels, per_device(): pl.pallas_call(fourth_kernel(coarse_cells), out_shape=(shape((1, chan_own...  3.79 us
    ppermute x1, starting transfers between devices, per_device(): z_first = lax.ppermute(first, 'sz', pair_first)  3.12 us
    ppermute x3, waiting for transfers between devices, per_device(): lax.ppermute(load, 'sz', [(i, i ^ k) for i in range(z_groups)])  2.03 us
    pallas_call x1, Pallas kernels, per_device(): pl.pallas_call(second_kernel(fine_cells), out_shape=(shape((depth, height...  2.01 us
  transfers between devices with their start and end apart: 8, of which 2 were waited for; matrix products, arithmetic and copies ran while one was open for 0% of the time, Pallas kernels for 11%

profile of v6, /device:TPU:0, one launch (start us, length us, event | category | flops | bytes accessed | tf_op | source)
XLA Modules:
  0.0 55.6 jit_solution(3975837415112663566)
XLA Ops:
  0.6 1.2 %prep.1 = (bf16[4,8,32,128]{3,2,1,0:T(8,128)(2,1)S(1)}, bf16[2,8,32,128]{3,2,1,0:T(8,128)(2,1)S(1)}, bf16[2,8,32,128]{3,2,1,0:T(8,128)(2,1)S(1)}, f32[1,128]{1,0:T(1,128)S(1)}) custom-call(bf16[1,32,4,8,128]{4,3,2,1,0:T(8,128)(2,1)} %vol_ref.1, f32[4,16]{1,0:T(4,128)} %hist_ref.3), custom_call_target="tpu_custom_call" | custom-call | tf_op jit(solution)/shard_map/prep/pallas_call | solution.py:710
  1.8 3.1 %collective-permute-start = (bf16[2,8,32,128]{3,2,1,0:T(8,128)(2,1)S(1)}, bf16[2,8,32,128]{3,2,1,0:T(8,128)(2,1)S(1)}, u32[]{:S(2)}, u32[]{:S(2)}) collective-permute-start(bf16[2,8,32,128]{3,2,1,0:T(8,128)(2,1)S(1)} %get-tuple-element.28), channel_id=1, source_target_pairs={{0,1},{1,0},{2,3},{3,2},{4,5},{5,4},{6,7},{7,6},{8,9},{9,8},{10,11... | collective-permute-start | bytes 393224 | tf_op jit(solution)/shard_map/ppermute | solution.py:745
  4.9 0.7 %collective-permute-start.1 = (bf16[2,8,32,128]{3,2,1,0:T(8,128)(2,1)S(1)}, bf16[2,8,32,128]{3,2,1,0:T(8,128)(2,1)S(1)}, u32[]{:S(2)}, u32[]{:S(2)}) collective-permute-start(bf16[2,8,32,128]{3,2,1,0:T(8,128)(2,1)S(1)} %get-tuple-element.29), channel_id=1, source_target_pairs={{0,0},{1,2},{2,1},{3,3},{4,4},{5,6},{6,5},{7,7},{8,8},{9,10},{10,9... | collective-permute-start | bytes 393224 | tf_op jit(solution)/shard_map/ppermute | solution.py:746
  5.6 1.5 %matrices.1 = (bf16[96,288]{1,0:T(8,128)(2,1)S(1)}, bf16[96,288]{1,0:T(8,128)(2,1)S(1)}, bf16[64,256]{1,0:T(8,128)(2,1)S(1)}, bf16[144,192]{1,0:T(8,128)(2,1)S(1...) custom-call(f32[1,128]{1,0:T(1,128)S(1)} %get-tuple-element.30.peak_ref, bf16[27,32,32]{2,1,0:T(8,128)(2,1)} %first_ref.1, ...), custom_call_target="tpu_custom_call" | custom-call | tf_op jit(solution)/shard_map/matrices/pallas_call | solution.py:721
  7.1 1.3 %collective-permute-done.got_first_ref = bf16[2,8,32,128]{3,2,1,0:T(8,128)(2,1)S(1)} collective-permute-done((bf16[2,8,32,128]{3,2,1,0:T(8,128)(2,1)S(1)}, bf16[2,8,32,128]{3,2,1,0:T(8,128)(2,1)S(1)}, u32[]{:S(2)}, u32[]{:S(2)}) %collective-permute-start) | collective-permute-done | bytes 131104 | tf_op jit(solution)/shard_map/ppermute | solution.py:745
  8.4 0.0 collective-permute-done.1.got_second_ref
  8.5 0.1 collective-permute-start.2
  8.5 0.7 %collective-permute-start.3 = (bf16[8,2,32,128]{3,2,1,0:T(8,128)(2,1)S(1)}, bf16[8,2,32,128]{3,2,1,0:T(8,128)(2,1)S(1)}, u32[]{:S(2)}, u32[]{:S(2)}) collective-permute-start(bf16[8,2,32,128]{3,2,1,0:T(8,128)(2,1)S(1)} %get-tuple-element.35), channel_id=1, source_target_pairs={{0,0},{4,8},{8,4},{12,12},{1,1},{5,9},{9,5},{13,13},{2,2},{6,10},{... | collective-permute-start | bytes 393224 | tf_op jit(solution)/shard_map/ppermute | solution.py:760
  9.2 0.9 %first_inner.1 = (bf16[8,8,32,128]{3,2,1,0:T(8,128)(2,1)S(1)}, f32[6,6,32,128]{3,2,1,0:T(8,128)S(1)}, f32[2,32,128]{2,1,0:T(8,128)S(1)}) custom-call(bf16[4,8,32,128]{3,2,1,0:T(8,128)(2,1)S(1)} %get-tuple-element.27.own_ref.cells_ref, bf16[2,8,32,128]{3,2,1,0:T(8,128)(2,1)S(1)} %collective-permute-done.got_first_ref, ...), custom_call_target="tpu_custom_call" | custom-call | tf_op jit(solution)/shard_map/first_inner/pallas_call | solution.py:761
  10.1 0.0 collective-permute-done.2.got_first_ref
  10.1 0.0 collective-permute-done.3.got_second_ref
  10.1 0.8 %first_outer.1 = (f32[6,4,32,128]{3,2,1,0:T(8,128)S(1)}, f32[16,1,128]{2,1,0:T(1,128)S(1)}) custom-call(bf16[8,8,32,128]{3,2,1,0:T(8,128)(2,1)S(1)} %get-tuple-element.33.deep_ref, bf16[8,2,32,128]{3,2,1,0:T(8,128)(2,1)S(1)} %collective-permute-done.2.got_first_ref, bf16[8,2,32,128]{3,2,1,0:T(8,128)(2,1)S(1)} %collective-permute-done.3.got_second_ref, ...), custom_call_target="tpu_custom_call" | custom-call | tf_op jit(solution)/shard_map/first_outer/pallas_call | solution.py:770
  10.9 19.1 %all_to_all.5.rows_ref = f32[16,1,128]{2,1,0:T(1,128)S(1)} all-to-all(f32[16,1,128]{2,1,0:T(1,128)S(1)} %get-tuple-element.38), channel_id=1, replica_groups=mesh['sample'=2,'sy'=4,'sz'=4] {'sy','sz'}, dimensions={0} | all-to-all | bytes 16384 | tf_op jit(solution)/shard_map/all_to_all | solution.py:779
  30.1 2.0 %second.1 = (f32[4,8,32,128]{3,2,1,0:T(8,128)}, bf16[72,256]{1,0:T(8,128)(2,1)S(1)}) custom-call(f32[6,6,32,128]{3,2,1,0:T(8,128)S(1)} %get-tuple-element.32.inner_ref, f32[6,4,32,128]{3,2,1,0:T(8,128)S(1)} %get-tuple-element.37.outer_ref, f32[16,1,128]{2,1,0:T(1,128)S(1)} %all_to_all.5.rows_ref, bf16[96,288]{1,0:T(8,128)(2,1)S(1)} %get-tuple-element.39.weight_ref, ...), custom_call_target="tpu_custom_call" | custom-call | tf_op jit(solution)/shard_map/second/pallas_call | solution.py:780
  32.1 0.6 %collective-permute-start.6 = (bf16[72,256]{1,0:T(8,128)(2,1)S(1)}, bf16[72,256]{1,0:T(8,128)(2,1)S(1)}, u32[]{:S(2)}, u32[]{:S(2)}) collective-permute-start(bf16[72,256]{1,0:T(8,128)(2,1)S(1)} %get-tuple-element.42), channel_id=1, source_target_pairs={{0,3},{1,2},{2,1},{3,0},{4,7},{5,6},{6,5},{7,4},{8,11},{9,10},{10,... | collective-permute-start | bytes 110600 | tf_op jit(solution)/shard_map/ppermute | solution.py:797
  32.7 1.4 %collective-permute-start.5 = (bf16[72,256]{1,0:T(8,128)(2,1)S(1)}, bf16[72,256]{1,0:T(8,128)(2,1)S(1)}, u32[]{:S(2)}, u32[]{:S(2)}) collective-permute-start(bf16[72,256]{1,0:T(8,128)(2,1)S(1)} %get-tuple-element.42), channel_id=1, source_target_pairs={{0,2},{1,3},{2,0},{3,1},{4,6},{5,7},{6,4},{7,5},{8,10},{9,11},{10,... | collective-permute-start | bytes 110600 | tf_op jit(solution)/shard_map/ppermute | solution.py:797
  34.1 2.4 %collective-permute-start.4 = (bf16[72,256]{1,0:T(8,128)(2,1)S(1)}, bf16[72,256]{1,0:T(8,128)(2,1)S(1)}, u32[]{:S(2)}, u32[]{:S(2)}) collective-permute-start(bf16[72,256]{1,0:T(8,128)(2,1)S(1)} %get-tuple-element.42), channel_id=1, source_target_pairs={{0,1},{1,0},{2,3},{3,2},{4,5},{5,4},{6,7},{7,6},{8,9},{9,8},{10,11... | collective-permute-start | bytes 110600 | tf_op jit(solution)/shard_map/ppermute | solution.py:797
  36.6 2.0 %collective-permute-done.4 = bf16[72,256]{1,0:T(8,128)(2,1)S(1)} collective-permute-done((bf16[72,256]{1,0:T(8,128)(2,1)S(1)}, bf16[72,256]{1,0:T(8,128)(2,1)S(1)}, u32[]{:S(2)}, u32[]{:S(2)}) %collective-permute-start.4) | collective-permute-done | bytes 36896 | tf_op jit(solution)/shard_map/ppermute | solution.py:797
  38.6 0.0 collective-permute-done.5
  38.6 0.0 collective-permute-done.6
  38.6 7.3 %all-gather = bf16[1408,256]{1,0:T(8,128)(2,1)S(1)} all-gather(bf16[352,256]{1,0:T(8,128)(2,1)S(1)} %constant_dynamic-update-slice_fusion), channel_id=2, replica_groups=mesh['sample'=2,'sy'=4,'sz'=4] {'sy'}, dimensions={0}, use_global_device_ids=true | all-gather | bytes 901120 | tf_op jit(solution)/shard_map/all_gather | solution.py:799
  46.0 3.8 %third.1 = (bf16[8,64,1024]{2,1,0:T(8,128)(2,1)S(1)}, f32[1,4]{1,0:T(1,128)S(1)}, f32[32,128]{1,0:T(8,128)S(1)}) custom-call(bf16[4,352,256]{2,1,0:T(8,128)(2,1)S(1)} %bitcast.3, f32[32,128]{1,0:T(8,128)S(1)} %get-tuple-element.40.param_ref), custom_call_target="tpu_custom_call" | custom-call | tf_op jit(solution)/shard_map/third/pallas_call | solution.py:800
  49.8 1.5 %collective-permute-start.7 = (f32[1,4]{1,0:T(1,128)S(1)}, f32[1,4]{1,0:T(1,128)S(1)}, u32[]{:S(2)}, u32[]{:S(2)}) collective-permute-start(f32[1,4]{1,0:T(1,128)S(1)} %get-tuple-element.50), channel_id=1, source_target_pairs={{0,16},{16,0},{1,17},{17,1},{2,18},{18,2},{3,19},{19,3},{4,20},{20... | collective-permute-start | bytes 56 | tf_op jit(solution)/shard_map/ppermute | solution.py:815
  51.3 3.8 %fourth.1 = (bf16[1,16,2,1024]{3,2,1,0:T(2,128)(2,1)}, bf16[1,32,4,8,128]{4,3,2,1,0:T(8,128)(2,1)}) custom-call(bf16[8,64,1024]{2,1,0:T(8,128)(2,1)S(1)} %get-tuple-element.44.cells_ref, bf16[144,192]{1,0:T(8,128)(2,1)S(1)} %get-tuple-element.45.weight_ref, f32[32,128]{1,0:T(8,128)S(1)} %get-tuple-element.40.param_ref, ...), custom_call_target="tpu_custom_call" | custom-call | tf_op jit(solution)/shard_map/fourth/pallas_call | solution.py:821
  55.1 0.0 collective-permute-done.7
  55.1 0.5 maximum_bitcast_fusion
  (6 shorter events, 0.0 us)
Async XLA Ops:
  1.8 6.6 %collective-permute-start = (bf16[2,8,32,128]{3,2,1,0:T(8,128)(2,1)S(1)}, bf16[2,8,32,128]{3,2,1,0:T(8,128)(2,1)S(1)}, u32[]{:S(2)}, u32[]{:S(2)}) collective-permute-start(bf16[2,8,32,128]{3,2,1,0:T(8,128)(2,1)S(1)} %get-tuple-element.28), channel_id=1, source_target_pairs={{0,1},{1,0},{2,3},{3,2},{4,5},{5,4},{6,7},{7,6},{8,9},{9,8},{10,11... | collective-permute-start | bytes 393224 | tf_op jit(solution)/shard_map/ppermute | solution.py:745
  4.9 3.5 %collective-permute-start.1 = (bf16[2,8,32,128]{3,2,1,0:T(8,128)(2,1)S(1)}, bf16[2,8,32,128]{3,2,1,0:T(8,128)(2,1)S(1)}, u32[]{:S(2)}, u32[]{:S(2)}) collective-permute-start(bf16[2,8,32,128]{3,2,1,0:T(8,128)(2,1)S(1)} %get-tuple-element.29), channel_id=1, source_target_pairs={{0,0},{1,2},{2,1},{3,3},{4,4},{5,6},{6,5},{7,7},{8,8},{9,10},{10,9... | collective-permute-start | bytes 393224 | tf_op jit(solution)/shard_map/ppermute | solution.py:746
  8.5 1.7 %collective-permute-start.2 = (bf16[8,2,32,128]{3,2,1,0:T(8,128)(2,1)S(1)}, bf16[8,2,32,128]{3,2,1,0:T(8,128)(2,1)S(1)}, u32[]{:S(2)}, u32[]{:S(2)}) collective-permute-start(bf16[8,2,32,128]{3,2,1,0:T(8,128)(2,1)S(1)} %get-tuple-element.34), channel_id=1, source_target_pairs={{0,4},{4,0},{8,12},{12,8},{1,5},{5,1},{9,13},{13,9},{2,6},{6,2},{1... | collective-permute-start | bytes 393224 | tf_op jit(solution)/shard_map/ppermute | solution.py:759
  8.5 1.6 %collective-permute-start.3 = (bf16[8,2,32,128]{3,2,1,0:T(8,128)(2,1)S(1)}, bf16[8,2,32,128]{3,2,1,0:T(8,128)(2,1)S(1)}, u32[]{:S(2)}, u32[]{:S(2)}) collective-permute-start(bf16[8,2,32,128]{3,2,1,0:T(8,128)(2,1)S(1)} %get-tuple-element.35), channel_id=1, source_target_pairs={{0,0},{4,8},{8,4},{12,12},{1,1},{5,9},{9,5},{13,13},{2,2},{6,10},{... | collective-permute-start | bytes 393224 | tf_op jit(solution)/shard_map/ppermute | solution.py:760
  32.1 6.5 %collective-permute-start.6 = (bf16[72,256]{1,0:T(8,128)(2,1)S(1)}, bf16[72,256]{1,0:T(8,128)(2,1)S(1)}, u32[]{:S(2)}, u32[]{:S(2)}) collective-permute-start(bf16[72,256]{1,0:T(8,128)(2,1)S(1)} %get-tuple-element.42), channel_id=1, source_target_pairs={{0,3},{1,2},{2,1},{3,0},{4,7},{5,6},{6,5},{7,4},{8,11},{9,10},{10,... | collective-permute-start | bytes 110600 | tf_op jit(solution)/shard_map/ppermute | solution.py:797
  32.7 5.8 %collective-permute-start.5 = (bf16[72,256]{1,0:T(8,128)(2,1)S(1)}, bf16[72,256]{1,0:T(8,128)(2,1)S(1)}, u32[]{:S(2)}, u32[]{:S(2)}) collective-permute-start(bf16[72,256]{1,0:T(8,128)(2,1)S(1)} %get-tuple-element.42), channel_id=1, source_target_pairs={{0,2},{1,3},{2,0},{3,1},{4,6},{5,7},{6,4},{7,5},{8,10},{9,11},{10,... | collective-permute-start | bytes 110600 | tf_op jit(solution)/shard_map/ppermute | solution.py:797
  34.1 4.4 %collective-permute-start.4 = (bf16[72,256]{1,0:T(8,128)(2,1)S(1)}, bf16[72,256]{1,0:T(8,128)(2,1)S(1)}, u32[]{:S(2)}, u32[]{:S(2)}) collective-permute-start(bf16[72,256]{1,0:T(8,128)(2,1)S(1)} %get-tuple-element.42), channel_id=1, source_target_pairs={{0,1},{1,0},{2,3},{3,2},{4,5},{5,4},{6,7},{7,6},{8,9},{9,8},{10,11... | collective-permute-start | bytes 110600 | tf_op jit(solution)/shard_map/ppermute | solution.py:797
  49.8 5.3 %collective-permute-start.7 = (f32[1,4]{1,0:T(1,128)S(1)}, f32[1,4]{1,0:T(1,128)S(1)}, u32[]{:S(2)}, u32[]{:S(2)}) collective-permute-start(f32[1,4]{1,0:T(1,128)S(1)} %get-tuple-element.50), channel_id=1, source_target_pairs={{0,16},{16,0},{1,17},{17,1},{2,18},{18,2},{3,19},{19,3},{4,20},{20... | collective-permute-start | bytes 56 | tf_op jit(solution)/shard_map/ppermute | solution.py:815

commit v7 on v6

--- a/solution.py
+++ b/solution.py
@@ -11,6 +11,7 @@
 bf16 = jnp.bfloat16
 LANES = 128
 HALO = 2
+KERNEL_BYTES = 24 * 1024 * 1024
 PEAK_AT = 64
 CODE_AT = 66
 GAIN_AT = 80
@@ -282,12 +283,10 @@
         weight_ref,
         param_ref,
         gain_row_ref,
-        out_ref,
+        raw_ref,
         load_ref,
         hidden_ref,
         pool_ref,
-        raw_ref,
-        done,
     ):
         depth, height, channels, width = raw_ref.shape
         wide_depth, wide_height = hidden_ref.shape[:2]
@@ -337,7 +336,6 @@
         sign = jnp.where(lane_of(param_ref, 2, channels) >= 0, 1.0, -1.0).astype(f32)
         half_height = height // 2
         total, square, least, most = blank, blank, blank + 1e30, blank - 1e30
-        copies = []
         for zp in range(depth // 2):
             for yp in range(half_height):
                 best = None
@@ -356,13 +354,6 @@
                 pool_ref[zp, yp] = best
                 least = jnp.minimum(least, best)
                 most = jnp.maximum(most, best)
-                part = (slice(2 * zp, 2 * zp + 2), slice(2 * yp, 2 * yp + 2))
-                copies.append(
-                    pltpu.make_async_copy(
-                        raw_ref.at[part], out_ref.at[part], done.at[zp * half_height + yp]
-                    )
-                )
-                copies[-1].start()
         most, least = peak_of(most), -peak_of(-least)
         center = 0.5 * (most + least)
         reach = jnp.maximum(0.5 * (most - least), 1e-30)
@@ -397,8 +388,6 @@
         body = (depth // 2) * channels
         load_ref[body:, 0:LANES] = parts.astype(bf16)
         load_ref[body:, LANES:] = jnp.zeros((ROWS, load_ref.shape[1] - LANES), bf16)
-        for copy in copies:
-            copy.wait()
 
     return kernel
 
@@ -408,7 +397,7 @@
 
 
 def third_kernel(fine_cells, coarse_cells, load_rows, piece):
-    def kernel(all_ref, param_ref, out_ref, peak_ref, affine_ref, cells_ref, raw_ref):
+    def kernel(all_ref, param_ref, raw_ref, peak_ref, affine_ref, next_ref, cells_ref):
         y_groups = all_ref.shape[0]
         z_groups = lax.axis_size("sz")
         span = all_ref.shape[2]
@@ -500,6 +489,8 @@
         blank = jnp.zeros((chan_own, LANES), f32)
         totals = [blank for _ in range(y_groups)]
         squares = [blank for _ in range(y_groups)]
+        leasts = [blank + 1e30 for _ in range(y_groups)]
+        mosts = [blank - 1e30 for _ in range(y_groups)]
         width = 2 * LANES
         for z in range(planes):
             for t in range(blocks // 2):
@@ -533,6 +524,8 @@
                         ] = out
                         totals[s] = totals[s] + out
                         squares[s] = squares[s] + out * out
+                        leasts[s] = jnp.minimum(leasts[s], out)
+                        mosts[s] = jnp.maximum(mosts[s], out)
         pairs = [
             affine(
                 jnp.sum(totals[s], axis=1, keepdims=True),
@@ -545,13 +538,12 @@
         ]
         scale = jnp.concatenate([one[0] for one in pairs], axis=0)
         offset = jnp.concatenate([one[1] for one in pairs], axis=0)
-        bound = clip_bound(param_ref, 3)
+        lanes = lax.broadcasted_iota(jnp.int32, (chan_all, LANES), 1)
+        next_ref[...] = jnp.where(lanes == 0, scale, jnp.where(lanes == 1, offset, 0.0))
         peak = jnp.zeros((chan_all, LANES), bf16)
-        for z in range(planes):
-            for j in range(blocks):
-                value = activated(raw_ref[z, :, at_block(j)], scale, offset)
-                peak = jnp.maximum(peak, jnp.abs(value))
-                out_ref[z, :, at_block(j)] = bounded(value, bound)
+        for extreme in (leasts, mosts):
+            value = activated(jnp.concatenate(extreme, axis=0), scale, offset)
+            peak = jnp.maximum(peak, jnp.abs(value))
         row = at_lane(tops[:, PEAK_AT : PEAK_AT + 1], 0)
         row = row + at_lane(tops[:, PEAK_AT + 1 : PEAK_AT + 2], 1)
         row = row + at_lane(peak_of(peak_pool), 2)
@@ -563,20 +555,31 @@
 
 def fourth_kernel(coarse_cells):
     def kernel(
-        cells_ref,
+        raw_ref,
         weight_ref,
         param_ref,
         affine_ref,
-        raw_ref,
+        next_ref,
+        fine_ref,
         out_ref,
         skip_ref,
+        cells_ref,
         last_ref,
-        fine_ref,
         narrow_ref,
         done,
     ):
-        fetch = pltpu.make_async_copy(raw_ref, fine_ref, done.at[0])
-        fetch.start()
+        scale = affine_ref[:, 0:1]
+        offset = affine_ref[:, 1:2]
+        sends = []
+        for z in range(fine_ref.shape[0]):
+            act = jnp.stack(
+                [activated(fine_ref[z, y], scale, offset) for y in range(fine_ref.shape[1])]
+            )
+            narrow_ref[:, z] = jnp.transpose(act, (1, 0, 2))
+            sends.append(
+                pltpu.make_async_copy(narrow_ref.at[:, z], skip_ref.at[0, :, z], done.at[z])
+            )
+            sends[-1].start()
         planes, chan_all, flat = cells_ref.shape
         chan_own, z_own = out_ref.shape[1:3]
         row_len = LANES // 2
@@ -584,9 +587,17 @@
         weight = weight_ref[...]
         lower = lax.broadcasted_iota(jnp.int32, (chan_own, LANES), 1) < row_len
         blank = jnp.zeros((chan_own, LANES), f32)
+        bound = clip_bound(param_ref, 3)
+        scale = next_ref[:, 0:1]
+        offset = next_ref[:, 1:2]
 
         def at_block(block):
             return slice(block * LANES, (block + 1) * LANES)
+
+        def normed(z):
+            for j in range(blocks):
+                value = activated(raw_ref[z, :, at_block(j)], scale, offset)
+                cells_ref[z, :, at_block(j)] = bounded(value, bound)
 
         def plane(z, sums):
             total, square = sums
@@ -627,19 +638,10 @@
             return total, square
 
         sums = (blank, blank)
-        for z in range(planes // 2):
-            sums = plane(z, sums)
-        fetch.wait()
-        scale = affine_ref[:, 0:1]
-        offset = affine_ref[:, 1:2]
-        for z in range(fine_ref.shape[0]):
-            act = jnp.stack(
-                [activated(fine_ref[z, y], scale, offset) for y in range(fine_ref.shape[1])]
-            )
-            narrow_ref[:, z] = jnp.transpose(act, (1, 0, 2))
-        send = pltpu.make_async_copy(narrow_ref, skip_ref.at[0], done.at[1])
-        send.start()
-        for z in range(planes // 2, planes):
+        normed(0)
+        for z in range(planes):
+            if z + 1 < planes:
+                normed(z + 1)
             sums = plane(z, sums)
         total, square = sums
         scale, offset = affine(
@@ -664,7 +666,8 @@
             own.append(jnp.concatenate(natural, axis=1))
         for c in range(chan_own):
             out_ref[0, c] = jnp.concatenate([one[c : c + 1] for one in own], axis=0).astype(bf16)
-        send.wait()
+        for send in sends:
+            send.wait()
 
     return kernel
 
@@ -780,16 +783,14 @@
     raw_second, load = pl.pallas_call(
         second_kernel(fine_cells),
         out_shape=(
-            shape((depth, height, channels, width), f32),
+            near_shape((depth, height, channels, width), f32),
             near_shape((load_rows, span), bf16),
         ),
-        out_specs=(anywhere, pl.BlockSpec(memory_space=pltpu.VMEM)),
         scratch_shapes=[
             pltpu.VMEM((depth + 2, height + 2, channels, width), bf16),
             pltpu.VMEM((depth // 2, height // 2, channels, width), f32),
-            pltpu.VMEM((depth, height, channels, width), f32),
-            pltpu.SemaphoreType.DMA(((depth // 2) * (height // 2),)),
         ],
+        compiler_params=pltpu.CompilerParams(vmem_limit_bytes=KERNEL_BYTES),
         name="second",
     )(*(held(x) for x in (raw_inner, raw_outer, rows, m2, params, gain_row)))
     loads = [load]
@@ -797,17 +798,16 @@
         loads.append(lax.ppermute(load, "sz", [(i, i ^ k) for i in range(z_groups)]))
     loads.append(m3)
     gathered = lax.all_gather(jnp.concatenate(loads, axis=0), "sy", axis=0)
-    hidden, peaks, fine_affine = pl.pallas_call(
+    raw_third, peaks, fine_affine, next_affine = pl.pallas_call(
         third_kernel(fine_cells, coarse_cells, load_rows, third_rows),
         out_shape=(
-            near_shape((planes, chan_all, flat), bf16),
+            near_shape((planes, chan_all, flat), f32),
             near_shape((1, levels), f32),
             near_shape((channels, LANES), f32),
+            near_shape((chan_all, LANES), f32),
         ),
-        scratch_shapes=[
-            pltpu.VMEM((planes + 2, 3 * channels, flat + 2 * LANES), bf16),
-            pltpu.VMEM((planes, chan_all, flat), f32),
-        ],
+        scratch_shapes=[pltpu.VMEM((planes + 2, 3 * channels, flat + 2 * LANES), bf16)],
+        compiler_params=pltpu.CompilerParams(vmem_limit_bytes=KERNEL_BYTES),
         name="third",
     )(held(gathered), held(params))
     if samples <= 4:
@@ -824,16 +824,16 @@
             shape((1, chan_own, depth // 2, flat), bf16),
             shape((1, channels, depth, height, width), bf16),
         ),
-        in_specs=[near, near, near, near, anywhere],
         out_specs=(near, anywhere),
         scratch_shapes=[
+            pltpu.VMEM((planes, chan_all, flat), bf16),
             pltpu.VMEM((planes, chan_own, flat), f32),
-            pltpu.VMEM((depth, height, channels, width), f32),
             pltpu.VMEM((channels, depth, height, width), bf16),
-            pltpu.SemaphoreType.DMA((2,)),
+            pltpu.SemaphoreType.DMA((depth,)),
         ],
+        compiler_params=pltpu.CompilerParams(vmem_limit_bytes=KERNEL_BYTES),
         name="fourth",
-    )(*(held(x) for x in (hidden, m4, params, fine_affine)), raw_second)
+    )(*(held(x) for x in (raw_third, m4, params, fine_affine, next_affine, raw_second)))
     for other in others:
         peaks = jnp.maximum(peaks, other)
     return skip, coarse, peaks.reshape(levels)

time: 55.9 us -> 53.9 us (0.964)
  Pallas kernels: 14 us -> 12.1 us
    pallas_call x1, Pallas kernels: 3.79 us -> 2.76 us  [per_device(): pl.pallas_call(fourth_kernel(coarse_cells), out_shape=(shape((1, chan_own...]
  transfers between devices with their start and end apart: 8 -> 8, of which waited for: 2 -> 2; matrix products, arithmetic and copies ran while one was open for 0% -> 0% of each run, Pallas kernels for 11% -> 10%
where the time goes in v7:
time: 53.9 us; the launch traced here: 53.7 us
  blocking collectives  26.5 us (49%)
  Pallas kernels  12.1 us (22%)
  starting transfers between devices  10.5 us (19%)
  waiting for transfers between devices  3.38 us (6%)
  between operations  0.76 us (1%)
    all_to_all x1, blocking collectives, per_device(): rows = lax.all_to_all(row, ('sy', 'sz'), 0, 0, tiled=True)  19.1 us
    all_gather x1, blocking collectives, per_device(): gathered = lax.all_gather(jnp.concatenate(loads, axis=0), 'sy', axis=0)  7.35 us
    ppermute x3, starting transfers between devices, per_device(): lax.ppermute(load, 'sz', [(i, i ^ k) for i in range(z_groups)])  4.45 us
    pallas_call x1, Pallas kernels, per_device(): pl.pallas_call(third_kernel(fine_cells, coarse_cells, load_rows, third_ro...  3.3 us
    ppermute x1, starting transfers between devices, per_device(): z_first = lax.ppermute(first, 'sz', pair_first)  3.12 us
    pallas_call x1, Pallas kernels, per_device(): pl.pallas_call(fourth_kernel(coarse_cells), out_shape=(shape((1, chan_own...  2.76 us
    ppermute x3, waiting for transfers between devices, per_device(): lax.ppermute(load, 'sz', [(i, i ^ k) for i in range(z_groups)])  2.03 us
    pallas_call x1, Pallas kernels, per_device(): pl.pallas_call(second_kernel(fine_cells), out_shape=(near_shape((depth, h...  1.64 us
  transfers between devices with their start and end apart: 8, of which 2 were waited for; matrix products, arithmetic and copies ran while one was open for 0% of the time, Pallas kernels for 10%

profile of v7, /device:TPU:0, one launch (start us, length us, event | category | flops | bytes accessed | tf_op | source)
XLA Modules:
  0.0 53.7 jit_solution(7816128634867787009)
XLA Ops:
  0.6 1.2 %prep.1 = (bf16[4,8,32,128]{3,2,1,0:T(8,128)(2,1)S(1)}, bf16[2,8,32,128]{3,2,1,0:T(8,128)(2,1)S(1)}, bf16[2,8,32,128]{3,2,1,0:T(8,128)(2,1)S(1)}, f32[1,128]{1,0:T(1,128)S(1)}) custom-call(bf16[1,32,4,8,128]{4,3,2,1,0:T(8,128)(2,1)} %vol_ref.1, f32[4,16]{1,0:T(4,128)} %hist_ref.3), custom_call_target="tpu_custom_call" | custom-call | tf_op jit(solution)/shard_map/prep/pallas_call | solution.py:713
  1.8 3.1 %collective-permute-start = (bf16[2,8,32,128]{3,2,1,0:T(8,128)(2,1)S(1)}, bf16[2,8,32,128]{3,2,1,0:T(8,128)(2,1)S(1)}, u32[]{:S(2)}, u32[]{:S(2)}) collective-permute-start(bf16[2,8,32,128]{3,2,1,0:T(8,128)(2,1)S(1)} %get-tuple-element.29), channel_id=1, source_target_pairs={{0,1},{1,0},{2,3},{3,2},{4,5},{5,4},{6,7},{7,6},{8,9},{9,8},{10,11... | collective-permute-start | bytes 393224 | tf_op jit(solution)/shard_map/ppermute | solution.py:748
  4.9 0.7 %collective-permute-start.1 = (bf16[2,8,32,128]{3,2,1,0:T(8,128)(2,1)S(1)}, bf16[2,8,32,128]{3,2,1,0:T(8,128)(2,1)S(1)}, u32[]{:S(2)}, u32[]{:S(2)}) collective-permute-start(bf16[2,8,32,128]{3,2,1,0:T(8,128)(2,1)S(1)} %get-tuple-element.30), channel_id=1, source_target_pairs={{0,0},{1,2},{2,1},{3,3},{4,4},{5,6},{6,5},{7,7},{8,8},{9,10},{10,9... | collective-permute-start | bytes 393224 | tf_op jit(solution)/shard_map/ppermute | solution.py:749
  5.6 1.5 %matrices.1 = (bf16[96,288]{1,0:T(8,128)(2,1)S(1)}, bf16[96,288]{1,0:T(8,128)(2,1)S(1)}, bf16[64,256]{1,0:T(8,128)(2,1)S(1)}, bf16[144,192]{1,0:T(8,128)(2,1)S(1...) custom-call(f32[1,128]{1,0:T(1,128)S(1)} %get-tuple-element.31.peak_ref, bf16[27,32,32]{2,1,0:T(8,128)(2,1)} %first_ref.1, ...), custom_call_target="tpu_custom_call" | custom-call | tf_op jit(solution)/shard_map/matrices/pallas_call | solution.py:724
  7.1 1.3 %collective-permute-done.got_first_ref = bf16[2,8,32,128]{3,2,1,0:T(8,128)(2,1)S(1)} collective-permute-done((bf16[2,8,32,128]{3,2,1,0:T(8,128)(2,1)S(1)}, bf16[2,8,32,128]{3,2,1,0:T(8,128)(2,1)S(1)}, u32[]{:S(2)}, u32[]{:S(2)}) %collective-permute-start) | collective-permute-done | bytes 131104 | tf_op jit(solution)/shard_map/ppermute | solution.py:748
  8.4 0.0 collective-permute-done.1.got_second_ref
  8.5 0.1 collective-permute-start.2
  8.5 0.7 %collective-permute-start.3 = (bf16[8,2,32,128]{3,2,1,0:T(8,128)(2,1)S(1)}, bf16[8,2,32,128]{3,2,1,0:T(8,128)(2,1)S(1)}, u32[]{:S(2)}, u32[]{:S(2)}) collective-permute-start(bf16[8,2,32,128]{3,2,1,0:T(8,128)(2,1)S(1)} %get-tuple-element.36), channel_id=1, source_target_pairs={{0,0},{4,8},{8,4},{12,12},{1,1},{5,9},{9,5},{13,13},{2,2},{6,10},{... | collective-permute-start | bytes 393224 | tf_op jit(solution)/shard_map/ppermute | solution.py:763
  9.2 0.9 %first_inner.1 = (bf16[8,8,32,128]{3,2,1,0:T(8,128)(2,1)S(1)}, f32[6,6,32,128]{3,2,1,0:T(8,128)S(1)}, f32[2,32,128]{2,1,0:T(8,128)S(1)}) custom-call(bf16[4,8,32,128]{3,2,1,0:T(8,128)(2,1)S(1)} %get-tuple-element.28.own_ref.cells_ref, bf16[2,8,32,128]{3,2,1,0:T(8,128)(2,1)S(1)} %collective-permute-done.got_first_ref, ...), custom_call_target="tpu_custom_call" | custom-call | tf_op jit(solution)/shard_map/first_inner/pallas_call | solution.py:764
  10.1 0.0 collective-permute-done.2.got_first_ref
  10.1 0.0 collective-permute-done.3.got_second_ref
  10.1 0.8 %first_outer.1 = (f32[6,4,32,128]{3,2,1,0:T(8,128)S(1)}, f32[16,1,128]{2,1,0:T(1,128)S(1)}) custom-call(bf16[8,8,32,128]{3,2,1,0:T(8,128)(2,1)S(1)} %get-tuple-element.34.deep_ref, bf16[8,2,32,128]{3,2,1,0:T(8,128)(2,1)S(1)} %collective-permute-done.2.got_first_ref, bf16[8,2,32,128]{3,2,1,0:T(8,128)(2,1)S(1)} %collective-permute-done.3.got_second_ref, ...), custom_call_target="tpu_custom_call" | custom-call | tf_op jit(solution)/shard_map/first_outer/pallas_call | solution.py:773
  10.9 19.1 %all_to_all.5.rows_ref = f32[16,1,128]{2,1,0:T(1,128)S(1)} all-to-all(f32[16,1,128]{2,1,0:T(1,128)S(1)} %get-tuple-element.39), channel_id=1, replica_groups=mesh['sample'=2,'sy'=4,'sz'=4] {'sy','sz'}, dimensions={0} | all-to-all | bytes 16384 | tf_op jit(solution)/shard_map/all_to_all | solution.py:782
  30.1 1.6 %second.1 = (f32[4,8,32,128]{3,2,1,0:T(8,128)S(1)}, bf16[72,256]{1,0:T(8,128)(2,1)S(1)}) custom-call(f32[6,6,32,128]{3,2,1,0:T(8,128)S(1)} %get-tuple-element.33.inner_ref, f32[6,4,32,128]{3,2,1,0:T(8,128)S(1)} %get-tuple-element.38.outer_ref, f32[16,1,128]{2,1,0:T(1,128)S(1)} %all_to_all.5.rows_ref, bf16[96,288]{1,0:T(8,128)(2,1)S(1)} %get-tuple-element.40.weight_ref, ...), custom_call_target="tpu_custom_call" | custom-call | tf_op jit(solution)/shard_map/second/pallas_call | solution.py:783
  31.7 0.7 %collective-permute-start.6 = (bf16[72,256]{1,0:T(8,128)(2,1)S(1)}, bf16[72,256]{1,0:T(8,128)(2,1)S(1)}, u32[]{:S(2)}, u32[]{:S(2)}) collective-permute-start(bf16[72,256]{1,0:T(8,128)(2,1)S(1)} %get-tuple-element.43), channel_id=1, source_target_pairs={{0,3},{1,2},{2,1},{3,0},{4,7},{5,6},{6,5},{7,4},{8,11},{9,10},{10,... | collective-permute-start | bytes 110600 | tf_op jit(solution)/shard_map/ppermute | solution.py:798
  32.4 1.4 %collective-permute-start.5 = (bf16[72,256]{1,0:T(8,128)(2,1)S(1)}, bf16[72,256]{1,0:T(8,128)(2,1)S(1)}, u32[]{:S(2)}, u32[]{:S(2)}) collective-permute-start(bf16[72,256]{1,0:T(8,128)(2,1)S(1)} %get-tuple-element.43), channel_id=1, source_target_pairs={{0,2},{1,3},{2,0},{3,1},{4,6},{5,7},{6,4},{7,5},{8,10},{9,11},{10,... | collective-permute-start | bytes 110600 | tf_op jit(solution)/shard_map/ppermute | solution.py:798
  33.8 2.4 %collective-permute-start.4 = (bf16[72,256]{1,0:T(8,128)(2,1)S(1)}, bf16[72,256]{1,0:T(8,128)(2,1)S(1)}, u32[]{:S(2)}, u32[]{:S(2)}) collective-permute-start(bf16[72,256]{1,0:T(8,128)(2,1)S(1)} %get-tuple-element.43), channel_id=1, source_target_pairs={{0,1},{1,0},{2,3},{3,2},{4,5},{5,4},{6,7},{7,6},{8,9},{9,8},{10,11... | collective-permute-start | bytes 110600 | tf_op jit(solution)/shard_map/ppermute | solution.py:798
  36.2 2.0 %collective-permute-done.4 = bf16[72,256]{1,0:T(8,128)(2,1)S(1)} collective-permute-done((bf16[72,256]{1,0:T(8,128)(2,1)S(1)}, bf16[72,256]{1,0:T(8,128)(2,1)S(1)}, u32[]{:S(2)}, u32[]{:S(2)}) %collective-permute-start.4) | collective-permute-done | bytes 36896 | tf_op jit(solution)/shard_map/ppermute | solution.py:798
  38.2 0.0 collective-permute-done.5
  38.2 0.0 collective-permute-done.6
  38.3 7.3 %all-gather = bf16[1408,256]{1,0:T(8,128)(2,1)S(1)} all-gather(bf16[352,256]{1,0:T(8,128)(2,1)S(1)} %constant_dynamic-update-slice_fusion), channel_id=2, replica_groups=mesh['sample'=2,'sy'=4,'sz'=4] {'sy'}, dimensions={0}, use_global_device_ids=true | all-gather | bytes 901120 | tf_op jit(solution)/shard_map/all_gather | solution.py:800
  45.6 3.3 %third.1 = (f32[8,64,1024]{2,1,0:T(8,128)S(1)}, f32[1,4]{1,0:T(1,128)S(1)}, f32[32,128]{1,0:T(8,128)S(1)}, f32[64,128]{1,0:T(8,128)S(1)}) custom-call(bf16[4,352,256]{2,1,0:T(8,128)(2,1)S(1)} %bitcast.3, f32[32,128]{1,0:T(8,128)S(1)} %get-tuple-element.41.param_ref), custom_call_target="tpu_custom_call" | custom-call | tf_op jit(solution)/shard_map/third/pallas_call | solution.py:801
  48.9 1.5 %collective-permute-start.7 = (f32[1,4]{1,0:T(1,128)S(1)}, f32[1,4]{1,0:T(1,128)S(1)}, u32[]{:S(2)}, u32[]{:S(2)}) collective-permute-start(f32[1,4]{1,0:T(1,128)S(1)} %get-tuple-element.52), channel_id=1, source_target_pairs={{0,16},{16,0},{1,17},{17,1},{2,18},{18,2},{3,19},{19,3},{4,20},{20... | collective-permute-start | bytes 56 | tf_op jit(solution)/shard_map/ppermute | solution.py:815
  50.4 2.8 %fourth.1 = (bf16[1,16,2,1024]{3,2,1,0:T(2,128)(2,1)}, bf16[1,32,4,8,128]{4,3,2,1,0:T(8,128)(2,1)}) custom-call(f32[8,64,1024]{2,1,0:T(8,128)S(1)} %get-tuple-element.45.raw_ref, bf16[144,192]{1,0:T(8,128)(2,1)S(1)} %get-tuple-element.46.weight_ref, f32[32,128]{1,0:T(8,128)S(1)} %get-tuple-element.41.param_ref, f32[32,128]{1,0:T(8,128)S(1)} %get-tuple-element.47.affine_ref, ...), custom_call_target="tpu_custom_call" | custom-call | tf_op jit(solution)/shard_map/fourth/pallas_call | solution.py:821
  53.2 0.0 collective-permute-done.7
  53.2 0.5 maximum_bitcast_fusion
  (6 shorter events, 0.0 us)
Async XLA Ops:
  1.8 6.6 %collective-permute-start = (bf16[2,8,32,128]{3,2,1,0:T(8,128)(2,1)S(1)}, bf16[2,8,32,128]{3,2,1,0:T(8,128)(2,1)S(1)}, u32[]{:S(2)}, u32[]{:S(2)}) collective-permute-start(bf16[2,8,32,128]{3,2,1,0:T(8,128)(2,1)S(1)} %get-tuple-element.29), channel_id=1, source_target_pairs={{0,1},{1,0},{2,3},{3,2},{4,5},{5,4},{6,7},{7,6},{8,9},{9,8},{10,11... | collective-permute-start | bytes 393224 | tf_op jit(solution)/shard_map/ppermute | solution.py:748
  4.9 3.5 %collective-permute-start.1 = (bf16[2,8,32,128]{3,2,1,0:T(8,128)(2,1)S(1)}, bf16[2,8,32,128]{3,2,1,0:T(8,128)(2,1)S(1)}, u32[]{:S(2)}, u32[]{:S(2)}) collective-permute-start(bf16[2,8,32,128]{3,2,1,0:T(8,128)(2,1)S(1)} %get-tuple-element.30), channel_id=1, source_target_pairs={{0,0},{1,2},{2,1},{3,3},{4,4},{5,6},{6,5},{7,7},{8,8},{9,10},{10,9... | collective-permute-start | bytes 393224 | tf_op jit(solution)/shard_map/ppermute | solution.py:749
  8.5 1.7 %collective-permute-start.2 = (bf16[8,2,32,128]{3,2,1,0:T(8,128)(2,1)S(1)}, bf16[8,2,32,128]{3,2,1,0:T(8,128)(2,1)S(1)}, u32[]{:S(2)}, u32[]{:S(2)}) collective-permute-start(bf16[8,2,32,128]{3,2,1,0:T(8,128)(2,1)S(1)} %get-tuple-element.35), channel_id=1, source_target_pairs={{0,4},{4,0},{8,12},{12,8},{1,5},{5,1},{9,13},{13,9},{2,6},{6,2},{1... | collective-permute-start | bytes 393224 | tf_op jit(solution)/shard_map/ppermute | solution.py:762
  8.5 1.6 %collective-permute-start.3 = (bf16[8,2,32,128]{3,2,1,0:T(8,128)(2,1)S(1)}, bf16[8,2,32,128]{3,2,1,0:T(8,128)(2,1)S(1)}, u32[]{:S(2)}, u32[]{:S(2)}) collective-permute-start(bf16[8,2,32,128]{3,2,1,0:T(8,128)(2,1)S(1)} %get-tuple-element.36), channel_id=1, source_target_pairs={{0,0},{4,8},{8,4},{12,12},{1,1},{5,9},{9,5},{13,13},{2,2},{6,10},{... | collective-permute-start | bytes 393224 | tf_op jit(solution)/shard_map/ppermute | solution.py:763
  31.7 6.5 %collective-permute-start.6 = (bf16[72,256]{1,0:T(8,128)(2,1)S(1)}, bf16[72,256]{1,0:T(8,128)(2,1)S(1)}, u32[]{:S(2)}, u32[]{:S(2)}) collective-permute-start(bf16[72,256]{1,0:T(8,128)(2,1)S(1)} %get-tuple-element.43), channel_id=1, source_target_pairs={{0,3},{1,2},{2,1},{3,0},{4,7},{5,6},{6,5},{7,4},{8,11},{9,10},{10,... | collective-permute-start | bytes 110600 | tf_op jit(solution)/shard_map/ppermute | solution.py:798
  32.4 5.8 %collective-permute-start.5 = (bf16[72,256]{1,0:T(8,128)(2,1)S(1)}, bf16[72,256]{1,0:T(8,128)(2,1)S(1)}, u32[]{:S(2)}, u32[]{:S(2)}) collective-permute-start(bf16[72,256]{1,0:T(8,128)(2,1)S(1)} %get-tuple-element.43), channel_id=1, source_target_pairs={{0,2},{1,3},{2,0},{3,1},{4,6},{5,7},{6,4},{7,5},{8,10},{9,11},{10,... | collective-permute-start | bytes 110600 | tf_op jit(solution)/shard_map/ppermute | solution.py:798
  33.8 4.4 %collective-permute-start.4 = (bf16[72,256]{1,0:T(8,128)(2,1)S(1)}, bf16[72,256]{1,0:T(8,128)(2,1)S(1)}, u32[]{:S(2)}, u32[]{:S(2)}) collective-permute-start(bf16[72,256]{1,0:T(8,128)(2,1)S(1)} %get-tuple-element.43), channel_id=1, source_target_pairs={{0,1},{1,0},{2,3},{3,2},{4,5},{5,4},{6,7},{7,6},{8,9},{9,8},{10,11... | collective-permute-start | bytes 110600 | tf_op jit(solution)/shard_map/ppermute | solution.py:798
  48.9 4.3 %collective-permute-start.7 = (f32[1,4]{1,0:T(1,128)S(1)}, f32[1,4]{1,0:T(1,128)S(1)}, u32[]{:S(2)}, u32[]{:S(2)}) collective-permute-start(f32[1,4]{1,0:T(1,128)S(1)} %get-tuple-element.52), channel_id=1, source_target_pairs={{0,16},{16,0},{1,17},{17,1},{2,18},{18,2},{3,19},{19,3},{4,20},{20... | collective-permute-start | bytes 56 | tf_op jit(solution)/shard_map/ppermute | solution.py:815

commit v8 on v7

--- a/solution.py
+++ b/solution.py
@@ -397,7 +397,10 @@
 
 
 def third_kernel(fine_cells, coarse_cells, load_rows, piece):
-    def kernel(all_ref, param_ref, raw_ref, peak_ref, affine_ref, next_ref, cells_ref):
+    def kernel(*refs):
+        all_ref, param_ref = refs[:2]
+        piece_refs = refs[2:-7]
+        raw_ref, peak_ref, affine_ref, next_ref, cells_ref, near_ref, far_ref = refs[-7:]
         y_groups = all_ref.shape[0]
         z_groups = lax.axis_size("sz")
         span = all_ref.shape[2]
@@ -478,14 +481,13 @@
                             ends.append((0, jnp.where(lower, blank, turned(two))))
                 for block, value in ends:
                     keep(place, block, value)
-        weights = z_groups * load_rows
         main = 3 * chan_own
-        near_weight = jnp.concatenate(
-            [all_ref[s, weights : weights + main, :] for s in range(y_groups)], axis=0
-        )
-        far_weight = jnp.concatenate(
-            [all_ref[s, weights + main :, 0 : 3 * channels] for s in range(y_groups)], axis=0
-        )
+        at_y = lax.axis_index("sy")
+        for k, piece_ref in enumerate(piece_refs):
+            near_ref[pl.ds((at_y ^ k) * main, main), :] = piece_ref[:main, :]
+            far_ref[pl.ds((at_y ^ k) * chan_own, chan_own), :] = piece_ref[main:, : 3 * channels]
+        near_weight = near_ref[...]
+        far_weight = far_ref[...]
         blank = jnp.zeros((chan_own, LANES), f32)
         totals = [blank for _ in range(y_groups)]
         squares = [blank for _ in range(y_groups)]
@@ -581,7 +583,7 @@
             )
             sends[-1].start()
         planes, chan_all, flat = cells_ref.shape
-        chan_own, z_own = out_ref.shape[1:3]
+        chan_own, z_own = out_ref.shape[:2]
         row_len = LANES // 2
         blocks = flat // LANES
         weight = weight_ref[...]
@@ -665,11 +667,21 @@
                     natural.append(jnp.where(lower, turned(first), second))
             own.append(jnp.concatenate(natural, axis=1))
         for c in range(chan_own):
-            out_ref[0, c] = jnp.concatenate([one[c : c + 1] for one in own], axis=0).astype(bf16)
+            out_ref[c] = jnp.concatenate([one[c : c + 1] for one in own], axis=0).astype(bf16)
         for send in sends:
             send.wait()
 
     return kernel
+
+
+def final_kernel(*refs):
+    cells_ref, peak_ref = refs[:2]
+    out_ref, top_ref = refs[-2:]
+    out_ref[0] = cells_ref[...]
+    top = peak_ref[...]
+    for ref in refs[2:-2]:
+        top = jnp.maximum(top, ref[...])
+    top_ref[...] = top
 
 
 def shape(dims, dtype):
@@ -744,6 +756,9 @@
         gain_coarse,
         shift_coarse,
     )
+    pieces = [m3]
+    for k in range(1, y_groups):
+        pieces.append(lax.ppermute(m3, "sy", [(i, i ^ k) for i in range(y_groups)]))
     pair_first, pair_second = pairings("sz")
     z_first = lax.ppermute(first, "sz", pair_first)
     z_second = lax.ppermute(second, "sz", pair_second)
@@ -796,7 +811,6 @@
     loads = [load]
     for k in range(1, z_groups):
         loads.append(lax.ppermute(load, "sz", [(i, i ^ k) for i in range(z_groups)]))
-    loads.append(m3)
     gathered = lax.all_gather(jnp.concatenate(loads, axis=0), "sy", axis=0)
     raw_third, peaks, fine_affine, next_affine = pl.pallas_call(
         third_kernel(fine_cells, coarse_cells, load_rows, third_rows),
@@ -806,10 +820,14 @@
             near_shape((channels, LANES), f32),
             near_shape((chan_all, LANES), f32),
         ),
-        scratch_shapes=[pltpu.VMEM((planes + 2, 3 * channels, flat + 2 * LANES), bf16)],
+        scratch_shapes=[
+            pltpu.VMEM((planes + 2, 3 * channels, flat + 2 * LANES), bf16),
+            pltpu.VMEM((3 * chan_all, 8 * channels), bf16),
+            pltpu.VMEM((chan_all, 3 * channels), bf16),
+        ],
         compiler_params=pltpu.CompilerParams(vmem_limit_bytes=KERNEL_BYTES),
         name="third",
-    )(held(gathered), held(params))
+    )(*(held(x) for x in (gathered, params, *pieces)))
     if samples <= 4:
         others = [
             lax.ppermute(peaks, "sample", [(i, (i + k) % samples) for i in range(samples)])
@@ -821,7 +839,7 @@
     coarse, skip = pl.pallas_call(
         fourth_kernel(coarse_cells),
         out_shape=(
-            shape((1, chan_own, depth // 2, flat), bf16),
+            near_shape((chan_own, depth // 2, flat), bf16),
             shape((1, channels, depth, height, width), bf16),
         ),
         out_specs=(near, anywhere),
@@ -834,8 +852,14 @@
         compiler_params=pltpu.CompilerParams(vmem_limit_bytes=KERNEL_BYTES),
         name="fourth",
     )(*(held(x) for x in (raw_third, m4, params, fine_affine, next_affine, raw_second)))
-    for other in others:
-        peaks = jnp.maximum(peaks, other)
+    coarse, peaks = pl.pallas_call(
+        final_kernel,
+        out_shape=(
+            shape((1, chan_own, depth // 2, flat), bf16),
+            shape((1, levels), f32),
+        ),
+        name="final",
+    )(*(held(x) for x in (coarse, peaks, *others)))
     return skip, coarse, peaks.reshape(levels)
 
 

time: 53.9 us -> 53.2 us (0.987)
  waiting for transfers between devices: 3.38 us -> 2.31 us
  starting transfers between devices: 10.5 us -> 11.5 us
    ppermute x3, waiting for transfers between devices: 2.03 us -> 0.95 us  [per_device(): lax.ppermute(load, 'sz', [(i, i ^ k) for i in range(z_groups)])]
    ppermute x0 -> x3, starting transfers between devices: none -> 1.07 us  [per_device(): pieces.append(lax.ppermute(m3, 'sy', [(i, i ^ k) for i in range(y_groups)]))]
    pallas_call x1 -> x2, Pallas kernels: 2.76 us -> 2.74 us  [the longest x1 2.1 us: per_device(): pl.pallas_call(fourth_kernel(coarse_cells), out_shape=(near_shape((chan_o...]
  transfers between devices with their start and end apart: 8 -> 11, of which waited for: 2 -> 3; matrix products, arithmetic and copies ran while one was open for 0% -> 0% of each run, Pallas kernels for 10% -> 8%
where the time goes in v8:
time: 53.2 us; the launch traced here: 53 us
  blocking collectives  26.3 us (49%)
  Pallas kernels  12.1 us (23%)
  starting transfers between devices  11.5 us (22%)
  waiting for transfers between devices  2.31 us (4%)
  between operations  0.74 us (1%)
    all_to_all x1, blocking collectives, per_device(): rows = lax.all_to_all(row, ('sy', 'sz'), 0, 0, tiled=True)  19.1 us
    all_gather x1, blocking collectives, per_device(): gathered = lax.all_gather(jnp.concatenate(loads, axis=0), 'sy', axis=0)  7.19 us
    ppermute x3, starting transfers between devices, per_device(): lax.ppermute(load, 'sz', [(i, i ^ k) for i in range(z_groups)])  4.45 us
    pallas_call x1, Pallas kernels, per_device(): pl.pallas_call(third_kernel(fine_cells, coarse_cells, load_rows, third_ro...  3.32 us
    ppermute x1, starting transfers between devices, per_device(): z_first = lax.ppermute(first, 'sz', pair_first)  3.12 us
    pallas_call x1, Pallas kernels, per_device(): pl.pallas_call(fourth_kernel(coarse_cells), out_shape=(near_shape((chan_o...  2.1 us
    pallas_call x1, Pallas kernels, per_device(): pl.pallas_call(second_kernel(fine_cells), out_shape=(near_shape((depth, h...  1.64 us
    ppermute x1, starting transfers between devices, per_device(): lax.ppermute(peaks, 'sample', [(i, (i + k) % samples) for i in range(samp...  1.5 us
  transfers between devices with their start and end apart: 11, of which 3 were waited for; matrix products, arithmetic and copies ran while one was open for 0% of the time, Pallas kernels for 8%

profile of v8, /device:TPU:0, one launch (start us, length us, event | category | flops | bytes accessed | tf_op | source)
XLA Modules:
  0.0 53.0 jit_solution(16916439460017359689)
XLA Ops:
  0.6 1.2 %prep.1 = (bf16[4,8,32,128]{3,2,1,0:T(8,128)(2,1)S(1)}, bf16[2,8,32,128]{3,2,1,0:T(8,128)(2,1)S(1)}, bf16[2,8,32,128]{3,2,1,0:T(8,128)(2,1)S(1)}, f32[1,128]{1,0:T(1,128)S(1)}) custom-call(bf16[1,32,4,8,128]{4,3,2,1,0:T(8,128)(2,1)} %vol_ref.1, f32[4,16]{1,0:T(4,128)} %hist_ref.3), custom_call_target="tpu_custom_call" | custom-call | tf_op jit(solution)/shard_map/prep/pallas_call | solution.py:725
  1.8 3.1 %collective-permute-start = (bf16[2,8,32,128]{3,2,1,0:T(8,128)(2,1)S(1)}, bf16[2,8,32,128]{3,2,1,0:T(8,128)(2,1)S(1)}, u32[]{:S(2)}, u32[]{:S(2)}) collective-permute-start(bf16[2,8,32,128]{3,2,1,0:T(8,128)(2,1)S(1)} %get-tuple-element.31), channel_id=1, source_target_pairs={{0,1},{1,0},{2,3},{3,2},{4,5},{5,4},{6,7},{7,6},{8,9},{9,8},{10,11... | collective-permute-start | bytes 393224 | tf_op jit(solution)/shard_map/ppermute | solution.py:763
  4.9 0.7 %collective-permute-start.1 = (bf16[2,8,32,128]{3,2,1,0:T(8,128)(2,1)S(1)}, bf16[2,8,32,128]{3,2,1,0:T(8,128)(2,1)S(1)}, u32[]{:S(2)}, u32[]{:S(2)}) collective-permute-start(bf16[2,8,32,128]{3,2,1,0:T(8,128)(2,1)S(1)} %get-tuple-element.32), channel_id=1, source_target_pairs={{0,0},{1,2},{2,1},{3,3},{4,4},{5,6},{6,5},{7,7},{8,8},{9,10},{10,9... | collective-permute-start | bytes 393224 | tf_op jit(solution)/shard_map/ppermute | solution.py:764
  5.6 1.5 %matrices.1 = (bf16[96,288]{1,0:T(8,128)(2,1)S(1)}, bf16[96,288]{1,0:T(8,128)(2,1)S(1)}, bf16[64,256]{1,0:T(8,128)(2,1)S(1)}, bf16[144,192]{1,0:T(8,128)(2,1)S(1...) custom-call(f32[1,128]{1,0:T(1,128)S(1)} %get-tuple-element.33.peak_ref, bf16[27,32,32]{2,1,0:T(8,128)(2,1)} %first_ref.1, ...), custom_call_target="tpu_custom_call" | custom-call | tf_op jit(solution)/shard_map/matrices/pallas_call | solution.py:736
  7.1 1.3 %collective-permute-done.got_first_ref = bf16[2,8,32,128]{3,2,1,0:T(8,128)(2,1)S(1)} collective-permute-done((bf16[2,8,32,128]{3,2,1,0:T(8,128)(2,1)S(1)}, bf16[2,8,32,128]{3,2,1,0:T(8,128)(2,1)S(1)}, u32[]{:S(2)}, u32[]{:S(2)}) %collective-permute-start) | collective-permute-done | bytes 131104 | tf_op jit(solution)/shard_map/ppermute | solution.py:763
  8.4 0.0 collective-permute-done.1.got_second_ref
  8.5 0.1 collective-permute-start.2
  8.5 0.7 %collective-permute-start.3 = (bf16[8,2,32,128]{3,2,1,0:T(8,128)(2,1)S(1)}, bf16[8,2,32,128]{3,2,1,0:T(8,128)(2,1)S(1)}, u32[]{:S(2)}, u32[]{:S(2)}) collective-permute-start(bf16[8,2,32,128]{3,2,1,0:T(8,128)(2,1)S(1)} %get-tuple-element.38), channel_id=1, source_target_pairs={{0,0},{4,8},{8,4},{12,12},{1,1},{5,9},{9,5},{13,13},{2,2},{6,10},{... | collective-permute-start | bytes 393224 | tf_op jit(solution)/shard_map/ppermute | solution.py:778
  9.2 0.9 %first_inner.1 = (bf16[8,8,32,128]{3,2,1,0:T(8,128)(2,1)S(1)}, f32[6,6,32,128]{3,2,1,0:T(8,128)S(1)}, f32[2,32,128]{2,1,0:T(8,128)S(1)}) custom-call(bf16[4,8,32,128]{3,2,1,0:T(8,128)(2,1)S(1)} %get-tuple-element.30.own_ref.cells_ref, bf16[2,8,32,128]{3,2,1,0:T(8,128)(2,1)S(1)} %collective-permute-done.got_first_ref, ...), custom_call_target="tpu_custom_call" | custom-call | tf_op jit(solution)/shard_map/first_inner/pallas_call | solution.py:779
  10.1 0.0 collective-permute-done.2.got_first_ref
  10.1 0.0 collective-permute-done.3.got_second_ref
  10.1 0.8 %first_outer.1 = (f32[6,4,32,128]{3,2,1,0:T(8,128)S(1)}, f32[16,1,128]{2,1,0:T(1,128)S(1)}) custom-call(bf16[8,8,32,128]{3,2,1,0:T(8,128)(2,1)S(1)} %get-tuple-element.36.deep_ref, bf16[8,2,32,128]{3,2,1,0:T(8,128)(2,1)S(1)} %collective-permute-done.2.got_first_ref, bf16[8,2,32,128]{3,2,1,0:T(8,128)(2,1)S(1)} %collective-permute-done.3.got_second_ref, ...), custom_call_target="tpu_custom_call" | custom-call | tf_op jit(solution)/shard_map/first_outer/pallas_call | solution.py:788
  10.9 19.1 %all_to_all.5.rows_ref = f32[16,1,128]{2,1,0:T(1,128)S(1)} all-to-all(f32[16,1,128]{2,1,0:T(1,128)S(1)} %get-tuple-element.41), channel_id=1, replica_groups=mesh['sample'=2,'sy'=4,'sz'=4] {'sy','sz'}, dimensions={0} | all-to-all | bytes 16384 | tf_op jit(solution)/shard_map/all_to_all | solution.py:797
  30.1 1.6 %second.1 = (f32[4,8,32,128]{3,2,1,0:T(8,128)S(1)}, bf16[72,256]{1,0:T(8,128)(2,1)S(1)}) custom-call(f32[6,6,32,128]{3,2,1,0:T(8,128)S(1)} %get-tuple-element.35.inner_ref, f32[6,4,32,128]{3,2,1,0:T(8,128)S(1)} %get-tuple-element.40.outer_ref, f32[16,1,128]{2,1,0:T(1,128)S(1)} %all_to_all.5.rows_ref, bf16[96,288]{1,0:T(8,128)(2,1)S(1)} %get-tuple-element.42.weight_ref, ...), custom_call_target="tpu_custom_call" | custom-call | tf_op jit(solution)/shard_map/second/pallas_call | solution.py:798
  31.7 0.7 %collective-permute-start.6 = (bf16[72,256]{1,0:T(8,128)(2,1)S(1)}, bf16[72,256]{1,0:T(8,128)(2,1)S(1)}, u32[]{:S(2)}, u32[]{:S(2)}) collective-permute-start(bf16[72,256]{1,0:T(8,128)(2,1)S(1)} %get-tuple-element.45), channel_id=1, source_target_pairs={{0,3},{1,2},{2,1},{3,0},{4,7},{5,6},{6,5},{7,4},{8,11},{9,10},{10,... | collective-permute-start | bytes 110600 | tf_op jit(solution)/shard_map/ppermute | solution.py:813
  32.4 1.4 %collective-permute-start.5 = (bf16[72,256]{1,0:T(8,128)(2,1)S(1)}, bf16[72,256]{1,0:T(8,128)(2,1)S(1)}, u32[]{:S(2)}, u32[]{:S(2)}) collective-permute-start(bf16[72,256]{1,0:T(8,128)(2,1)S(1)} %get-tuple-element.45), channel_id=1, source_target_pairs={{0,2},{1,3},{2,0},{3,1},{4,6},{5,7},{6,4},{7,5},{8,10},{9,11},{10,... | collective-permute-start | bytes 110600 | tf_op jit(solution)/shard_map/ppermute | solution.py:813
  33.8 2.4 %collective-permute-start.4 = (bf16[72,256]{1,0:T(8,128)(2,1)S(1)}, bf16[72,256]{1,0:T(8,128)(2,1)S(1)}, u32[]{:S(2)}, u32[]{:S(2)}) collective-permute-start(bf16[72,256]{1,0:T(8,128)(2,1)S(1)} %get-tuple-element.45), channel_id=1, source_target_pairs={{0,1},{1,0},{2,3},{3,2},{4,5},{5,4},{6,7},{7,6},{8,9},{9,8},{10,11... | collective-permute-start | bytes 110600 | tf_op jit(solution)/shard_map/ppermute | solution.py:813
  36.2 0.0 collective-permute-start.9
  36.2 0.6 %collective-permute-start.8 = (bf16[64,256]{1,0:T(8,128)(2,1)S(1)}, bf16[64,256]{1,0:T(8,128)(2,1)S(1)}, u32[]{:S(2)}, u32[]{:S(2)}) collective-permute-start(bf16[64,256]{1,0:T(8,128)(2,1)S(1)} %get-tuple-element.46.refs_2_), channel_id=1, source_target_pairs={{0,8},{4,12},{8,0},{12,4},{1,9},{5,13},{9,1},{13,5},{2,10},{6,14},... | collective-permute-start | bytes 98312 | tf_op jit(solution)/shard_map/ppermute | solution.py:761
  36.8 0.8 %collective-permute-done.6 = bf16[72,256]{1,0:T(8,128)(2,1)S(1)} collective-permute-done((bf16[72,256]{1,0:T(8,128)(2,1)S(1)}, bf16[72,256]{1,0:T(8,128)(2,1)S(1)}, u32[]{:S(2)}, u32[]{:S(2)}) %collective-permute-start.6) | collective-permute-done | bytes 36896 | tf_op jit(solution)/shard_map/ppermute | solution.py:813
  37.6 0.5 collective-permute-start.7
  38.0 0.0 collective-permute-done.5
  38.1 0.1 collective-permute-done.4
  38.2 7.2 %all-gather = bf16[1152,256]{1,0:T(8,128)(2,1)S(1)} all-gather(bf16[288,256]{1,0:T(8,128)(2,1)S(1)} %pad_maximum_fusion), channel_id=2, replica_groups=mesh['sample'=2,'sy'=4,'sz'=4] {'sy'}, dimensions={0}, use_global_device_ids=true | all-gather | bytes 737280 | tf_op jit(solution)/shard_map/all_gather | solution.py:814
  45.4 0.0 collective-permute-done.9.refs_5_
  45.4 0.0 collective-permute-done.8.refs_4_
  45.4 0.0 collective-permute-done.7.refs_3_
  45.4 3.3 %third.1 = (f32[8,64,1024]{2,1,0:T(8,128)S(1)}, f32[1,4]{1,0:T(1,128)S(1)}, f32[32,128]{1,0:T(8,128)S(1)}, f32[64,128]{1,0:T(8,128)S(1)}) custom-call(bf16[4,288,256]{2,1,0:T(8,128)(2,1)S(1)} %bitcast.2, f32[32,128]{1,0:T(8,128)S(1)} %get-tuple-element.43.param_ref.refs_1_, bf16[64,256]{1,0:T(8,128)(2,1)S(1)} %get-tuple-element.46.refs_2_, ...), custom_call_target="tpu_custom_call" | custom-call | tf_op jit(solution)/shard_map/third/pallas_call | solution.py:815
  48.7 1.5 %collective-permute-start.10 = (f32[1,4]{1,0:T(1,128)S(1)}, f32[1,4]{1,0:T(1,128)S(1)}, u32[]{:S(2)}, u32[]{:S(2)}) collective-permute-start(f32[1,4]{1,0:T(1,128)S(1)} %get-tuple-element.54.refs_1_), channel_id=1, source_target_pairs={{0,16},{16,0},{1,17},{17,1},{2,18},{18,2},{3,19},{19,3},{4,20},{20... | collective-permute-start | bytes 56 | tf_op jit(solution)/shard_map/ppermute | solution.py:833
  50.2 2.1 %fourth.1 = (bf16[16,2,1024]{2,1,0:T(2,128)(2,1)S(1)}, bf16[1,32,4,8,128]{4,3,2,1,0:T(8,128)(2,1)}) custom-call(f32[8,64,1024]{2,1,0:T(8,128)S(1)} %get-tuple-element.47.raw_ref, bf16[144,192]{1,0:T(8,128)(2,1)S(1)} %get-tuple-element.48.weight_ref, f32[32,128]{1,0:T(8,128)S(1)} %get-tuple-element.43.param_ref.refs_1_, ...), custom_call_target="tpu_custom_call" | custom-call | tf_op jit(solution)/shard_map/fourth/pallas_call | solution.py:839
  52.4 0.0 collective-permute-done.10.refs_2_
  52.4 0.6 %final.1 = (bf16[1,16,2,1024]{3,2,1,0:T(2,128)(2,1)}, f32[1,4]{1,0:T(1,128)}) custom-call(bf16[16,2,1024]{2,1,0:T(2,128)(2,1)S(1)} %get-tuple-element.53.refs_0_, f32[1,4]{1,0:T(1,128)S(1)} %get-tuple-element.54.refs_1_, f32[1,4]{1,0:T(1,128)S(1)} %collective-permute-done.10.refs_2_), custom_call_target="tpu_custom_call" | custom-call | tf_op jit(solution)/shard_map/final/pallas_call | solution.py:855
  (2 shorter events, 0.0 us)
Async XLA Ops:
  1.8 6.6 %collective-permute-start = (bf16[2,8,32,128]{3,2,1,0:T(8,128)(2,1)S(1)}, bf16[2,8,32,128]{3,2,1,0:T(8,128)(2,1)S(1)}, u32[]{:S(2)}, u32[]{:S(2)}) collective-permute-start(bf16[2,8,32,128]{3,2,1,0:T(8,128)(2,1)S(1)} %get-tuple-element.31), channel_id=1, source_target_pairs={{0,1},{1,0},{2,3},{3,2},{4,5},{5,4},{6,7},{7,6},{8,9},{9,8},{10,11... | collective-permute-start | bytes 393224 | tf_op jit(solution)/shard_map/ppermute | solution.py:763
  4.9 3.5 %collective-permute-start.1 = (bf16[2,8,32,128]{3,2,1,0:T(8,128)(2,1)S(1)}, bf16[2,8,32,128]{3,2,1,0:T(8,128)(2,1)S(1)}, u32[]{:S(2)}, u32[]{:S(2)}) collective-permute-start(bf16[2,8,32,128]{3,2,1,0:T(8,128)(2,1)S(1)} %get-tuple-element.32), channel_id=1, source_target_pairs={{0,0},{1,2},{2,1},{3,3},{4,4},{5,6},{6,5},{7,7},{8,8},{9,10},{10,9... | collective-permute-start | bytes 393224 | tf_op jit(solution)/shard_map/ppermute | solution.py:764
  8.5 1.7 %collective-permute-start.2 = (bf16[8,2,32,128]{3,2,1,0:T(8,128)(2,1)S(1)}, bf16[8,2,32,128]{3,2,1,0:T(8,128)(2,1)S(1)}, u32[]{:S(2)}, u32[]{:S(2)}) collective-permute-start(bf16[8,2,32,128]{3,2,1,0:T(8,128)(2,1)S(1)} %get-tuple-element.37), channel_id=1, source_target_pairs={{0,4},{4,0},{8,12},{12,8},{1,5},{5,1},{9,13},{13,9},{2,6},{6,2},{1... | collective-permute-start | bytes 393224 | tf_op jit(solution)/shard_map/ppermute | solution.py:777
  8.5 1.6 %collective-permute-start.3 = (bf16[8,2,32,128]{3,2,1,0:T(8,128)(2,1)S(1)}, bf16[8,2,32,128]{3,2,1,0:T(8,128)(2,1)S(1)}, u32[]{:S(2)}, u32[]{:S(2)}) collective-permute-start(bf16[8,2,32,128]{3,2,1,0:T(8,128)(2,1)S(1)} %get-tuple-element.38), channel_id=1, source_target_pairs={{0,0},{4,8},{8,4},{12,12},{1,1},{5,9},{9,5},{13,13},{2,2},{6,10},{... | collective-permute-start | bytes 393224 | tf_op jit(solution)/shard_map/ppermute | solution.py:778
  31.7 5.9 %collective-permute-start.6 = (bf16[72,256]{1,0:T(8,128)(2,1)S(1)}, bf16[72,256]{1,0:T(8,128)(2,1)S(1)}, u32[]{:S(2)}, u32[]{:S(2)}) collective-permute-start(bf16[72,256]{1,0:T(8,128)(2,1)S(1)} %get-tuple-element.45), channel_id=1, source_target_pairs={{0,3},{1,2},{2,1},{3,0},{4,7},{5,6},{6,5},{7,4},{8,11},{9,10},{10,... | collective-permute-start | bytes 110600 | tf_op jit(solution)/shard_map/ppermute | solution.py:813
  32.4 5.7 %collective-permute-start.5 = (bf16[72,256]{1,0:T(8,128)(2,1)S(1)}, bf16[72,256]{1,0:T(8,128)(2,1)S(1)}, u32[]{:S(2)}, u32[]{:S(2)}) collective-permute-start(bf16[72,256]{1,0:T(8,128)(2,1)S(1)} %get-tuple-element.45), channel_id=1, source_target_pairs={{0,2},{1,3},{2,0},{3,1},{4,6},{5,7},{6,4},{7,5},{8,10},{9,11},{10,... | collective-permute-start | bytes 110600 | tf_op jit(solution)/shard_map/ppermute | solution.py:813
  33.8 4.4 %collective-permute-start.4 = (bf16[72,256]{1,0:T(8,128)(2,1)S(1)}, bf16[72,256]{1,0:T(8,128)(2,1)S(1)}, u32[]{:S(2)}, u32[]{:S(2)}) collective-permute-start(bf16[72,256]{1,0:T(8,128)(2,1)S(1)} %get-tuple-element.45), channel_id=1, source_target_pairs={{0,1},{1,0},{2,3},{3,2},{4,5},{5,4},{6,7},{7,6},{8,9},{9,8},{10,11... | collective-permute-start | bytes 110600 | tf_op jit(solution)/shard_map/ppermute | solution.py:813
  36.2 9.2 %collective-permute-start.9 = (bf16[64,256]{1,0:T(8,128)(2,1)S(1)}, bf16[64,256]{1,0:T(8,128)(2,1)S(1)}, u32[]{:S(2)}, u32[]{:S(2)}) collective-permute-start(bf16[64,256]{1,0:T(8,128)(2,1)S(1)} %get-tuple-element.46.refs_2_), channel_id=1, source_target_pairs={{0,12},{4,8},{8,4},{12,0},{1,13},{5,9},{9,5},{13,1},{2,14},{6,10},... | collective-permute-start | bytes 98312 | tf_op jit(solution)/shard_map/ppermute | solution.py:761
  36.2 9.2 %collective-permute-start.8 = (bf16[64,256]{1,0:T(8,128)(2,1)S(1)}, bf16[64,256]{1,0:T(8,128)(2,1)S(1)}, u32[]{:S(2)}, u32[]{:S(2)}) collective-permute-start(bf16[64,256]{1,0:T(8,128)(2,1)S(1)} %get-tuple-element.46.refs_2_), channel_id=1, source_target_pairs={{0,8},{4,12},{8,0},{12,4},{1,9},{5,13},{9,1},{13,5},{2,10},{6,14},... | collective-permute-start | bytes 98312 | tf_op jit(solution)/shard_map/ppermute | solution.py:761
  37.6 7.8 %collective-permute-start.7 = (bf16[64,256]{1,0:T(8,128)(2,1)S(1)}, bf16[64,256]{1,0:T(8,128)(2,1)S(1)}, u32[]{:S(2)}, u32[]{:S(2)}) collective-permute-start(bf16[64,256]{1,0:T(8,128)(2,1)S(1)} %get-tuple-element.46.refs_2_), channel_id=1, source_target_pairs={{0,4},{4,0},{8,12},{12,8},{1,5},{5,1},{9,13},{13,9},{2,6},{6,2},{1... | collective-permute-start | bytes 98312 | tf_op jit(solution)/shard_map/ppermute | solution.py:761
  48.7 3.6 %collective-permute-start.10 = (f32[1,4]{1,0:T(1,128)S(1)}, f32[1,4]{1,0:T(1,128)S(1)}, u32[]{:S(2)}, u32[]{:S(2)}) collective-permute-start(f32[1,4]{1,0:T(1,128)S(1)} %get-tuple-element.54.refs_1_), channel_id=1, source_target_pairs={{0,16},{16,0},{1,17},{17,1},{2,18},{18,2},{3,19},{19,3},{4,20},{20... | collective-permute-start | bytes 56 | tf_op jit(solution)/shard_map/ppermute | solution.py:833

commit v9 on v8

--- a/solution.py
+++ b/solution.py
@@ -149,21 +149,28 @@
     return middle + jnp.where(lane == 0, 0.0, up) + jnp.where(lane == period - 1, 0.0, down)
 
 
-def prep_kernel(vol_ref, hist_ref, cells_ref, first_ref, second_ref, peak_ref):
+def slab_kernel(vol_ref, first_ref, second_ref, done):
     depth = vol_ref.shape[2]
+    even = lax.axis_index("sz") % 2
+    starts = ((1 - even) * (depth - HALO), even * (depth - HALO))
+    copies = []
+    for which, (start, target) in enumerate(zip(starts, (first_ref, second_ref))):
+        source = vol_ref.at[0, :, pl.ds(start, HALO)]
+        copies.append(pltpu.make_async_copy(source, target, done.at[which]))
+        copies[-1].start()
+    for copy in copies:
+        copy.wait()
+
+
+def prep_kernel(vol_ref, hist_ref, cells_ref, peak_ref):
     bound = bound_of(hist_ref, 0).astype(bf16)
     top = jnp.zeros(cells_ref.shape[2:], bf16)
-    for z in range(depth):
+    for z in range(vol_ref.shape[2]):
         rows = jnp.transpose(vol_ref[0, :, z], (1, 0, 2))
         for y in range(rows.shape[0]):
             top = jnp.maximum(top, jnp.abs(rows[y]))
             cells_ref[z, y] = bounded(rows[y], bound)
     peak_ref[...] = jnp.broadcast_to(peak_of(top), (1, LANES))
-    even = lax.axis_index("sz") % 2 == 0
-    start_first = jnp.where(even, depth - HALO, 0)
-    start_second = jnp.where(even, 0, depth - HALO)
-    first_ref[...] = cells_ref[pl.ds(start_first, HALO)]
-    second_ref[...] = cells_ref[pl.ds(start_second, HALO)]
 
 
 def sides(axis, first, second):
@@ -176,16 +183,31 @@
     return below, above
 
 
-def deep_kernel(cells_ref, got_first_ref, got_second_ref, matrix_ref, first_ref, second_ref):
+def deep_kernel(
+    cells_ref,
+    got_first_ref,
+    got_second_ref,
+    param_ref,
+    z_first_ref,
+    z_second_ref,
+    first_ref,
+    second_ref,
+):
     depth, height = cells_ref.shape[:2]
+    bound = clip_bound(param_ref, 0)
+    for source, target in ((got_first_ref, z_first_ref), (got_second_ref, z_second_ref)):
+        for z in range(HALO):
+            rows = jnp.transpose(source[:, z], (1, 0, 2))
+            for y in range(height):
+                target[z, y] = bounded(rows[y], bound)
     even = lax.axis_index("sy") % 2 == 0
     starts = (jnp.where(even, height - HALO, 0), jnp.where(even, 0, height - HALO))
     odd_z = lax.axis_index("sz") % 2
     far = HALO + depth
     for start, out_ref in zip(starts, (first_ref, second_ref)):
         rows = pl.ds(start, HALO)
-        out_ref[pl.ds((1 - odd_z) * far, HALO)] = got_first_ref[:, rows]
-        out_ref[pl.ds(odd_z * far, HALO)] = got_second_ref[:, rows]
+        out_ref[pl.ds((1 - odd_z) * far, HALO)] = z_first_ref[:, rows]
+        out_ref[pl.ds(odd_z * far, HALO)] = z_second_ref[:, rows]
         out_ref[HALO:far] = cells_ref[:, rows]
 
 
@@ -405,7 +427,7 @@
         z_groups = lax.axis_size("sz")
         span = all_ref.shape[2]
         planes, chan_all, flat = raw_ref.shape
-        channels = cells_ref.shape[1] // 3
+        channels = cells_ref.shape[2] // 3
         chan_own = piece // 4
         row_len = LANES // 2
         blocks = flat // LANES
@@ -441,22 +463,20 @@
             return slice(block * LANES, (block + 1) * LANES)
 
         def keep(place, block, value):
-            cells_ref[place, middle, at_block(block)] = value
+            cells_ref[place, block, middle] = value
             if block >= 2:
-                cells_ref[place, :channels, at_block(block)] = jnp.where(
+                cells_ref[place, block, :channels] = jnp.where(
                     edge == 0, blank, pltpu.roll(value, 1, 1)
                 )
-                cells_ref[place, 2 * channels :, at_block(block)] = jnp.where(
+                cells_ref[place, block, 2 * channels :] = jnp.where(
                     edge == row_len - 1, blank, pltpu.roll(value, LANES - 1, 1)
                 )
 
-        cells_ref[0] = jnp.zeros(cells_ref.shape[1:], bf16)
-        cells_ref[planes + 1] = jnp.zeros(cells_ref.shape[1:], bf16)
         peak_pool = jnp.zeros((channels, span), bf16)
         half_groups = y_groups // 2
         for k in range(z_groups):
             for zp in range(z_own):
-                place = (at_z ^ k) * z_own + zp + 1
+                place = (at_z ^ k) * z_own + zp
                 at = k * load_rows + zp * channels
                 ends = []
                 for s in range(half_groups):
@@ -493,34 +513,39 @@
         squares = [blank for _ in range(y_groups)]
         leasts = [blank + 1e30 for _ in range(y_groups)]
         mosts = [blank - 1e30 for _ in range(y_groups)]
-        width = 2 * LANES
         for z in range(planes):
             for t in range(blocks // 2):
+                depths = [dz for dz in range(3) if 0 <= z + dz - 1 < planes]
+
+                def cells(dz, dy, which):
+                    return jnp.concatenate(
+                        [cells_ref[z + dz - 1, 2 * t + dy + half, which] for half in range(2)],
+                        axis=1,
+                    )
+
                 window = [
-                    cells_ref[z + dz, middle, (2 * t + dy) * LANES : (2 * t + dy) * LANES + width]
-                    for dz in range(3)
-                    for dy in range(3)
-                    if dz + dy < 4
+                    cells(dz, dy, middle) for dz in depths for dy in range(3) if dz + dy < 4
                 ]
+                first = 3 * depths[0] * channels
                 taps = jnp.dot(
-                    near_weight, jnp.concatenate(window, axis=0), preferred_element_type=f32
-                )
-                rest = jnp.dot(
-                    far_weight,
-                    cells_ref[z + 2, :, (2 * t + 2) * LANES : (2 * t + 2) * LANES + width],
+                    near_weight[:, first : first + len(window) * channels],
+                    jnp.concatenate(window, axis=0),
                     preferred_element_type=f32,
                 )
+                rest = None
+                if depths[-1] == 2:
+                    rest = jnp.dot(
+                        far_weight, cells(2, 2, slice(None)), preferred_element_type=f32
+                    )
                 for s in range(y_groups):
                     for half in range(2):
                         at = s * main
                         part = taps[at : at + main, at_block(half)]
-                        out = tap_sum(
-                            part[:chan_own],
-                            part[chan_own : 2 * chan_own]
-                            + rest[s * chan_own : (s + 1) * chan_own, at_block(half)],
-                            part[2 * chan_own :],
-                            row_len,
-                        )
+                        center = part[chan_own : 2 * chan_own]
+                        if rest is not None:
+                            own = slice(s * chan_own, (s + 1) * chan_own)
+                            center = center + rest[own, at_block(half)]
+                        out = tap_sum(part[:chan_own], center, part[2 * chan_own :], row_len)
                         raw_ref[
                             z, s * chan_own : (s + 1) * chan_own, at_block(2 * t + half)
                         ] = out
@@ -722,12 +747,23 @@
     group = z_groups * y_groups
     load_rows = (depth // 2) * channels + ROWS
 
-    cells, first, second, peak = pl.pallas_call(
+    anywhere = pl.BlockSpec(memory_space=pl.ANY)
+    near = pl.BlockSpec(memory_space=pltpu.VMEM)
+    z_first, z_second = pl.pallas_call(
+        slab_kernel,
+        in_specs=[anywhere],
+        out_specs=(near, near),
+        out_shape=(
+            near_shape((channels, HALO, height, width), bf16),
+            near_shape((channels, HALO, height, width), bf16),
+        ),
+        scratch_shapes=[pltpu.SemaphoreType.DMA((2,))],
+        name="slabs",
+    )(volume)
+    cells, peak = pl.pallas_call(
         prep_kernel,
         out_shape=(
             near_shape((depth, height, channels, width), bf16),
-            near_shape((HALO, height, channels, width), bf16),
-            near_shape((HALO, height, channels, width), bf16),
             near_shape((1, LANES), f32),
         ),
         name="prep",
@@ -760,19 +796,20 @@
     for k in range(1, y_groups):
         pieces.append(lax.ppermute(m3, "sy", [(i, i ^ k) for i in range(y_groups)]))
     pair_first, pair_second = pairings("sz")
-    z_first = lax.ppermute(first, "sz", pair_first)
-    z_second = lax.ppermute(second, "sz", pair_second)
+    z_first = lax.ppermute(z_first, "sz", pair_first)
+    z_second = lax.ppermute(z_second, "sz", pair_second)
     deep_depth = depth + 2 * HALO
-    anywhere = pl.BlockSpec(memory_space=pl.ANY)
     levels = amax_history.shape[0]
-    first, second = pl.pallas_call(
+    z_first, z_second, first, second = pl.pallas_call(
         deep_kernel,
         out_shape=(
+            near_shape((HALO, height, channels, width), bf16),
+            near_shape((HALO, height, channels, width), bf16),
             near_shape((deep_depth, HALO, channels, width), bf16),
             near_shape((deep_depth, HALO, channels, width), bf16),
         ),
         name="deep",
-    )(held(cells), held(z_first), held(z_second), held(m1))
+    )(*(held(x) for x in (cells, z_first, z_second, params)))
     pair_first, pair_second = pairings("sy")
     y_first = lax.ppermute(first, "sy", pair_first)
     y_second = lax.ppermute(second, "sy", pair_second)
@@ -821,7 +858,7 @@
             near_shape((chan_all, LANES), f32),
         ),
         scratch_shapes=[
-            pltpu.VMEM((planes + 2, 3 * channels, flat + 2 * LANES), bf16),
+            pltpu.VMEM((planes, flat // LANES + 2, 3 * channels, LANES), bf16),
             pltpu.VMEM((3 * chan_all, 8 * channels), bf16),
             pltpu.VMEM((chan_all, 3 * channels), bf16),
         ],
@@ -835,7 +872,6 @@
         ]
     else:
         others = [lax.pmax(peaks, "sample")]
-    near = pl.BlockSpec(memory_space=pltpu.VMEM)
     coarse, skip = pl.pallas_call(
         fourth_kernel(coarse_cells),
         out_shape=(

time: 53.2 us -> 53.1 us (level)
  waiting for transfers between devices: 2.31 us -> 1.17 us
  Pallas kernels: 12.1 us -> 13.1 us
    pallas_call x1 -> x2, Pallas kernels: 0.02 us -> 1.19 us  [the longest x1 1 us: per_device(): pl.pallas_call(slab_kernel, in_specs=[anywhere], out_specs=(near, near),...]
    ppermute x2, waiting for transfers between devices: 1.35 us -> 0.2 us  [the longest x1 0.19 us: per_device(): z_first = lax.ppermute(z_first, 'sz', pair_first)]
  transfers between devices with their start and end apart: 11 -> 11, of which waited for: 3 -> 3; matrix products, arithmetic and copies ran while one was open for 0% -> 0% of each run, Pallas kernels for 8% -> 11%
where the time goes in v9:
time: 53.1 us; the launch traced here: 52.9 us
  blocking collectives  26.3 us (50%)
  Pallas kernels  13.1 us (25%)
  starting transfers between devices  11.5 us (22%)
  waiting for transfers between devices  1.17 us (2%)
  between operations  0.74 us (1%)
    all_to_all x1, blocking collectives, per_device(): rows = lax.all_to_all(row, ('sy', 'sz'), 0, 0, tiled=True)  19.1 us
    all_gather x1, blocking collectives, per_device(): gathered = lax.all_gather(jnp.concatenate(loads, axis=0), 'sy', axis=0)  7.18 us
    ppermute x3, starting transfers between devices, per_device(): lax.ppermute(load, 'sz', [(i, i ^ k) for i in range(z_groups)])  4.45 us
    pallas_call x1, Pallas kernels, per_device(): pl.pallas_call(third_kernel(fine_cells, coarse_cells, load_rows, third_ro...  3.21 us
    ppermute x1, starting transfers between devices, per_device(): z_first = lax.ppermute(z_first, 'sz', pair_first)  3.12 us
    pallas_call x1, Pallas kernels, per_device(): pl.pallas_call(fourth_kernel(coarse_cells), out_shape=(near_shape((chan_o...  2.1 us
    pallas_call x1, Pallas kernels, per_device(): pl.pallas_call(second_kernel(fine_cells), out_shape=(near_shape((depth, h...  1.66 us
    ppermute x1, starting transfers between devices, per_device(): lax.ppermute(peaks, 'sample', [(i, (i + k) % samples) for i in range(samp...  1.49 us
  transfers between devices with their start and end apart: 11, of which 3 were waited for; matrix products, arithmetic and copies ran while one was open for 0% of the time, Pallas kernels for 11%

profile of v9, /device:TPU:0, one launch (start us, length us, event | category | flops | bytes accessed | tf_op | source)
XLA Modules:
  0.0 52.9 jit_solution(12557873368558756644)
XLA Ops:
  0.6 1.0 %slabs.1 = (bf16[32,2,8,128]{3,2,1,0:T(8,128)(2,1)S(1)}, bf16[32,2,8,128]{3,2,1,0:T(8,128)(2,1)S(1)}) custom-call(bf16[1,32,4,8,128]{4,3,2,1,0:T(8,128)(2,1)} %vol_ref.3), custom_call_target="tpu_custom_call" | custom-call | tf_op jit(solution)/shard_map/slabs/pallas_call | solution.py:752
  1.6 3.1 %collective-permute-start = (bf16[32,2,8,128]{3,2,1,0:T(8,128)(2,1)S(1)}, bf16[32,2,8,128]{3,2,1,0:T(8,128)(2,1)S(1)}, u32[]{:S(2)}, u32[]{:S(2)}) collective-permute-start(bf16[32,2,8,128]{3,2,1,0:T(8,128)(2,1)S(1)} %get-tuple-element.33), channel_id=1, source_target_pairs={{0,1},{1,0},{2,3},{3,2},{4,5},{5,4},{6,7},{7,6},{8,9},{9,8},{10,11... | collective-permute-start | bytes 393224 | tf_op jit(solution)/shard_map/ppermute | solution.py:799
  4.8 0.7 %collective-permute-start.1 = (bf16[32,2,8,128]{3,2,1,0:T(8,128)(2,1)S(1)}, bf16[32,2,8,128]{3,2,1,0:T(8,128)(2,1)S(1)}, u32[]{:S(2)}, u32[]{:S(2)}) collective-permute-start(bf16[32,2,8,128]{3,2,1,0:T(8,128)(2,1)S(1)} %get-tuple-element.34), channel_id=1, source_target_pairs={{0,0},{1,2},{2,1},{3,3},{4,4},{5,6},{6,5},{7,7},{8,8},{9,10},{10,9... | collective-permute-start | bytes 393224 | tf_op jit(solution)/shard_map/ppermute | solution.py:800
  5.4 1.2 %prep.1 = (bf16[4,8,32,128]{3,2,1,0:T(8,128)(2,1)S(1)}, f32[1,128]{1,0:T(1,128)S(1)}) custom-call(bf16[1,32,4,8,128]{4,3,2,1,0:T(8,128)(2,1)} %vol_ref.3, f32[4,16]{1,0:T(4,128)} %hist_ref.3), custom_call_target="tpu_custom_call" | custom-call | tf_op jit(solution)/shard_map/prep/pallas_call | solution.py:763
  6.6 1.5 %matrices.1 = (bf16[96,288]{1,0:T(8,128)(2,1)S(1)}, bf16[96,288]{1,0:T(8,128)(2,1)S(1)}, bf16[64,256]{1,0:T(8,128)(2,1)S(1)}, bf16[144,192]{1,0:T(8,128)(2,1)S(1...) custom-call(f32[1,128]{1,0:T(1,128)S(1)} %get-tuple-element.35.peak_ref, bf16[27,32,32]{2,1,0:T(8,128)(2,1)} %first_ref.1, ...), custom_call_target="tpu_custom_call" | custom-call | tf_op jit(solution)/shard_map/matrices/pallas_call | solution.py:772
  8.1 0.2 collective-permute-done.got_first_ref
  8.2 0.0 collective-permute-done.1.got_second_ref
  8.3 0.2 deep.1
  8.4 0.1 collective-permute-start.2
  8.5 0.7 %collective-permute-start.3 = (bf16[8,2,32,128]{3,2,1,0:T(8,128)(2,1)S(1)}, bf16[8,2,32,128]{3,2,1,0:T(8,128)(2,1)S(1)}, u32[]{:S(2)}, u32[]{:S(2)}) collective-permute-start(bf16[8,2,32,128]{3,2,1,0:T(8,128)(2,1)S(1)} %get-tuple-element.43), channel_id=1, source_target_pairs={{0,0},{4,8},{8,4},{12,12},{1,1},{5,9},{9,5},{13,13},{2,2},{6,10},{... | collective-permute-start | bytes 393224 | tf_op jit(solution)/shard_map/ppermute | solution.py:815
  9.2 0.9 %first_inner.1 = (bf16[8,8,32,128]{3,2,1,0:T(8,128)(2,1)S(1)}, f32[6,6,32,128]{3,2,1,0:T(8,128)S(1)}, f32[2,32,128]{2,1,0:T(8,128)S(1)}) custom-call(bf16[4,8,32,128]{3,2,1,0:T(8,128)(2,1)S(1)} %get-tuple-element.32.cells_ref.own_ref, bf16[2,8,32,128]{3,2,1,0:T(8,128)(2,1)S(1)} %get-tuple-element.37.got_first_ref, ...), custom_call_target="tpu_custom_call" | custom-call | tf_op jit(solution)/shard_map/first_inner/pallas_call | solution.py:816
  10.1 0.0 collective-permute-done.2.got_first_ref
  10.1 0.0 collective-permute-done.3.got_second_ref
  10.1 0.8 %first_outer.1 = (f32[6,4,32,128]{3,2,1,0:T(8,128)S(1)}, f32[16,1,128]{2,1,0:T(1,128)S(1)}) custom-call(bf16[8,8,32,128]{3,2,1,0:T(8,128)(2,1)S(1)} %get-tuple-element.41.deep_ref, bf16[8,2,32,128]{3,2,1,0:T(8,128)(2,1)S(1)} %collective-permute-done.2.got_first_ref, bf16[8,2,32,128]{3,2,1,0:T(8,128)(2,1)S(1)} %collective-permute-done.3.got_second_ref, ...), custom_call_target="tpu_custom_call" | custom-call | tf_op jit(solution)/shard_map/first_outer/pallas_call | solution.py:825
  10.9 19.1 %all_to_all.5.rows_ref = f32[16,1,128]{2,1,0:T(1,128)S(1)} all-to-all(f32[16,1,128]{2,1,0:T(1,128)S(1)} %get-tuple-element.46), channel_id=1, replica_groups=mesh['sample'=2,'sy'=4,'sz'=4] {'sy','sz'}, dimensions={0} | all-to-all | bytes 16384 | tf_op jit(solution)/shard_map/all_to_all | solution.py:834
  30.1 1.7 %second.1 = (f32[4,8,32,128]{3,2,1,0:T(8,128)S(1)}, bf16[72,256]{1,0:T(8,128)(2,1)S(1)}) custom-call(f32[6,6,32,128]{3,2,1,0:T(8,128)S(1)} %get-tuple-element.40.inner_ref, f32[6,4,32,128]{3,2,1,0:T(8,128)S(1)} %get-tuple-element.45.outer_ref, f32[16,1,128]{2,1,0:T(1,128)S(1)} %all_to_all.5.rows_ref, bf16[96,288]{1,0:T(8,128)(2,1)S(1)} %get-tuple-element.47.weight_ref, ...), custom_call_target="tpu_custom_call" | custom-call | tf_op jit(solution)/shard_map/second/pallas_call | solution.py:835
  31.7 0.6 %collective-permute-start.6 = (bf16[72,256]{1,0:T(8,128)(2,1)S(1)}, bf16[72,256]{1,0:T(8,128)(2,1)S(1)}, u32[]{:S(2)}, u32[]{:S(2)}) collective-permute-start(bf16[72,256]{1,0:T(8,128)(2,1)S(1)} %get-tuple-element.49), channel_id=1, source_target_pairs={{0,3},{1,2},{2,1},{3,0},{4,7},{5,6},{6,5},{7,4},{8,11},{9,10},{10,... | collective-permute-start | bytes 110600 | tf_op jit(solution)/shard_map/ppermute | solution.py:850
  32.4 1.4 %collective-permute-start.5 = (bf16[72,256]{1,0:T(8,128)(2,1)S(1)}, bf16[72,256]{1,0:T(8,128)(2,1)S(1)}, u32[]{:S(2)}, u32[]{:S(2)}) collective-permute-start(bf16[72,256]{1,0:T(8,128)(2,1)S(1)} %get-tuple-element.49), channel_id=1, source_target_pairs={{0,2},{1,3},{2,0},{3,1},{4,6},{5,7},{6,4},{7,5},{8,10},{9,11},{10,... | collective-permute-start | bytes 110600 | tf_op jit(solution)/shard_map/ppermute | solution.py:850
  33.8 2.4 %collective-permute-start.4 = (bf16[72,256]{1,0:T(8,128)(2,1)S(1)}, bf16[72,256]{1,0:T(8,128)(2,1)S(1)}, u32[]{:S(2)}, u32[]{:S(2)}) collective-permute-start(bf16[72,256]{1,0:T(8,128)(2,1)S(1)} %get-tuple-element.49), channel_id=1, source_target_pairs={{0,1},{1,0},{2,3},{3,2},{4,5},{5,4},{6,7},{7,6},{8,9},{9,8},{10,11... | collective-permute-start | bytes 110600 | tf_op jit(solution)/shard_map/ppermute | solution.py:850
  36.2 0.0 collective-permute-start.9
  36.2 0.6 %collective-permute-start.8 = (bf16[64,256]{1,0:T(8,128)(2,1)S(1)}, bf16[64,256]{1,0:T(8,128)(2,1)S(1)}, u32[]{:S(2)}, u32[]{:S(2)}) collective-permute-start(bf16[64,256]{1,0:T(8,128)(2,1)S(1)} %get-tuple-element.50.refs_2_), channel_id=1, source_target_pairs={{0,8},{4,12},{8,0},{12,4},{1,9},{5,13},{9,1},{13,5},{2,10},{6,14},... | collective-permute-start | bytes 98312 | tf_op jit(solution)/shard_map/ppermute | solution.py:797
  36.8 0.8 %collective-permute-done.6 = bf16[72,256]{1,0:T(8,128)(2,1)S(1)} collective-permute-done((bf16[72,256]{1,0:T(8,128)(2,1)S(1)}, bf16[72,256]{1,0:T(8,128)(2,1)S(1)}, u32[]{:S(2)}, u32[]{:S(2)}) %collective-permute-start.6) | collective-permute-done | bytes 36896 | tf_op jit(solution)/shard_map/ppermute | solution.py:850
  37.6 0.5 collective-permute-start.7
  38.1 0.0 collective-permute-done.5
  38.1 0.1 collective-permute-done.4
  38.2 7.2 %all-gather = bf16[1152,256]{1,0:T(8,128)(2,1)S(1)} all-gather(bf16[288,256]{1,0:T(8,128)(2,1)S(1)} %pad_maximum_fusion), channel_id=2, replica_groups=mesh['sample'=2,'sy'=4,'sz'=4] {'sy'}, dimensions={0}, use_global_device_ids=true | all-gather | bytes 737280 | tf_op jit(solution)/shard_map/all_gather | solution.py:851
  45.4 0.0 collective-permute-done.9.refs_5_
  45.4 0.0 collective-permute-done.8.refs_4_
  45.4 0.0 collective-permute-done.7.refs_3_
  45.4 3.2 %third.1 = (f32[8,64,1024]{2,1,0:T(8,128)S(1)}, f32[1,4]{1,0:T(1,128)S(1)}, f32[32,128]{1,0:T(8,128)S(1)}, f32[64,128]{1,0:T(8,128)S(1)}) custom-call(bf16[4,288,256]{2,1,0:T(8,128)(2,1)S(1)} %bitcast.2, f32[32,128]{1,0:T(8,128)S(1)} %get-tuple-element.36.param_ref.refs_1_, bf16[64,256]{1,0:T(8,128)(2,1)S(1)} %get-tuple-element.50.refs_2_, ...), custom_call_target="tpu_custom_call" | custom-call | tf_op jit(solution)/shard_map/third/pallas_call | solution.py:852
  48.6 1.5 %collective-permute-start.10 = (f32[1,4]{1,0:T(1,128)S(1)}, f32[1,4]{1,0:T(1,128)S(1)}, u32[]{:S(2)}, u32[]{:S(2)}) collective-permute-start(f32[1,4]{1,0:T(1,128)S(1)} %get-tuple-element.58.refs_1_), channel_id=1, source_target_pairs={{0,16},{16,0},{1,17},{17,1},{2,18},{18,2},{3,19},{19,3},{4,20},{20... | collective-permute-start | bytes 56 | tf_op jit(solution)/shard_map/ppermute | solution.py:870
  50.1 2.1 %fourth.1 = (bf16[16,2,1024]{2,1,0:T(2,128)(2,1)S(1)}, bf16[1,32,4,8,128]{4,3,2,1,0:T(8,128)(2,1)}) custom-call(f32[8,64,1024]{2,1,0:T(8,128)S(1)} %get-tuple-element.51.raw_ref, bf16[144,192]{1,0:T(8,128)(2,1)S(1)} %get-tuple-element.52.weight_ref, f32[32,128]{1,0:T(8,128)S(1)} %get-tuple-element.36.param_ref.refs_1_, ...), custom_call_target="tpu_custom_call" | custom-call | tf_op jit(solution)/shard_map/fourth/pallas_call | solution.py:875
  52.2 0.0 collective-permute-done.10.refs_2_
  52.3 0.6 %final.1 = (bf16[1,16,2,1024]{3,2,1,0:T(2,128)(2,1)}, f32[1,4]{1,0:T(1,128)}) custom-call(bf16[16,2,1024]{2,1,0:T(2,128)(2,1)S(1)} %get-tuple-element.57.refs_0_, f32[1,4]{1,0:T(1,128)S(1)} %get-tuple-element.58.refs_1_, f32[1,4]{1,0:T(1,128)S(1)} %collective-permute-done.10.refs_2_), custom_call_target="tpu_custom_call" | custom-call | tf_op jit(solution)/shard_map/final/pallas_call | solution.py:891
  (1 shorter events, 0.0 us)
Async XLA Ops:
  1.6 6.6 %collective-permute-start = (bf16[32,2,8,128]{3,2,1,0:T(8,128)(2,1)S(1)}, bf16[32,2,8,128]{3,2,1,0:T(8,128)(2,1)S(1)}, u32[]{:S(2)}, u32[]{:S(2)}) collective-permute-start(bf16[32,2,8,128]{3,2,1,0:T(8,128)(2,1)S(1)} %get-tuple-element.33), channel_id=1, source_target_pairs={{0,1},{1,0},{2,3},{3,2},{4,5},{5,4},{6,7},{7,6},{8,9},{9,8},{10,11... | collective-permute-start | bytes 393224 | tf_op jit(solution)/shard_map/ppermute | solution.py:799
  4.8 3.5 %collective-permute-start.1 = (bf16[32,2,8,128]{3,2,1,0:T(8,128)(2,1)S(1)}, bf16[32,2,8,128]{3,2,1,0:T(8,128)(2,1)S(1)}, u32[]{:S(2)}, u32[]{:S(2)}) collective-permute-start(bf16[32,2,8,128]{3,2,1,0:T(8,128)(2,1)S(1)} %get-tuple-element.34), channel_id=1, source_target_pairs={{0,0},{1,2},{2,1},{3,3},{4,4},{5,6},{6,5},{7,7},{8,8},{9,10},{10,9... | collective-permute-start | bytes 393224 | tf_op jit(solution)/shard_map/ppermute | solution.py:800
  8.4 1.7 %collective-permute-start.2 = (bf16[8,2,32,128]{3,2,1,0:T(8,128)(2,1)S(1)}, bf16[8,2,32,128]{3,2,1,0:T(8,128)(2,1)S(1)}, u32[]{:S(2)}, u32[]{:S(2)}) collective-permute-start(bf16[8,2,32,128]{3,2,1,0:T(8,128)(2,1)S(1)} %get-tuple-element.42), channel_id=1, source_target_pairs={{0,4},{4,0},{8,12},{12,8},{1,5},{5,1},{9,13},{13,9},{2,6},{6,2},{1... | collective-permute-start | bytes 393224 | tf_op jit(solution)/shard_map/ppermute | solution.py:814
  8.5 1.6 %collective-permute-start.3 = (bf16[8,2,32,128]{3,2,1,0:T(8,128)(2,1)S(1)}, bf16[8,2,32,128]{3,2,1,0:T(8,128)(2,1)S(1)}, u32[]{:S(2)}, u32[]{:S(2)}) collective-permute-start(bf16[8,2,32,128]{3,2,1,0:T(8,128)(2,1)S(1)} %get-tuple-element.43), channel_id=1, source_target_pairs={{0,0},{4,8},{8,4},{12,12},{1,1},{5,9},{9,5},{13,13},{2,2},{6,10},{... | collective-permute-start | bytes 393224 | tf_op jit(solution)/shard_map/ppermute | solution.py:815
  31.7 5.9 %collective-permute-start.6 = (bf16[72,256]{1,0:T(8,128)(2,1)S(1)}, bf16[72,256]{1,0:T(8,128)(2,1)S(1)}, u32[]{:S(2)}, u32[]{:S(2)}) collective-permute-start(bf16[72,256]{1,0:T(8,128)(2,1)S(1)} %get-tuple-element.49), channel_id=1, source_target_pairs={{0,3},{1,2},{2,1},{3,0},{4,7},{5,6},{6,5},{7,4},{8,11},{9,10},{10,... | collective-permute-start | bytes 110600 | tf_op jit(solution)/shard_map/ppermute | solution.py:850
  32.4 5.7 %collective-permute-start.5 = (bf16[72,256]{1,0:T(8,128)(2,1)S(1)}, bf16[72,256]{1,0:T(8,128)(2,1)S(1)}, u32[]{:S(2)}, u32[]{:S(2)}) collective-permute-start(bf16[72,256]{1,0:T(8,128)(2,1)S(1)} %get-tuple-element.49), channel_id=1, source_target_pairs={{0,2},{1,3},{2,0},{3,1},{4,6},{5,7},{6,4},{7,5},{8,10},{9,11},{10,... | collective-permute-start | bytes 110600 | tf_op jit(solution)/shard_map/ppermute | solution.py:850
  33.8 4.4 %collective-permute-start.4 = (bf16[72,256]{1,0:T(8,128)(2,1)S(1)}, bf16[72,256]{1,0:T(8,128)(2,1)S(1)}, u32[]{:S(2)}, u32[]{:S(2)}) collective-permute-start(bf16[72,256]{1,0:T(8,128)(2,1)S(1)} %get-tuple-element.49), channel_id=1, source_target_pairs={{0,1},{1,0},{2,3},{3,2},{4,5},{5,4},{6,7},{7,6},{8,9},{9,8},{10,11... | collective-permute-start | bytes 110600 | tf_op jit(solution)/shard_map/ppermute | solution.py:850
  36.2 9.2 %collective-permute-start.9 = (bf16[64,256]{1,0:T(8,128)(2,1)S(1)}, bf16[64,256]{1,0:T(8,128)(2,1)S(1)}, u32[]{:S(2)}, u32[]{:S(2)}) collective-permute-start(bf16[64,256]{1,0:T(8,128)(2,1)S(1)} %get-tuple-element.50.refs_2_), channel_id=1, source_target_pairs={{0,12},{4,8},{8,4},{12,0},{1,13},{5,9},{9,5},{13,1},{2,14},{6,10},... | collective-permute-start | bytes 98312 | tf_op jit(solution)/shard_map/ppermute | solution.py:797
  36.2 9.2 %collective-permute-start.8 = (bf16[64,256]{1,0:T(8,128)(2,1)S(1)}, bf16[64,256]{1,0:T(8,128)(2,1)S(1)}, u32[]{:S(2)}, u32[]{:S(2)}) collective-permute-start(bf16[64,256]{1,0:T(8,128)(2,1)S(1)} %get-tuple-element.50.refs_2_), channel_id=1, source_target_pairs={{0,8},{4,12},{8,0},{12,4},{1,9},{5,13},{9,1},{13,5},{2,10},{6,14},... | collective-permute-start | bytes 98312 | tf_op jit(solution)/shard_map/ppermute | solution.py:797
  37.6 7.8 %collective-permute-start.7 = (bf16[64,256]{1,0:T(8,128)(2,1)S(1)}, bf16[64,256]{1,0:T(8,128)(2,1)S(1)}, u32[]{:S(2)}, u32[]{:S(2)}) collective-permute-start(bf16[64,256]{1,0:T(8,128)(2,1)S(1)} %get-tuple-element.50.refs_2_), channel_id=1, source_target_pairs={{0,4},{4,0},{8,12},{12,8},{1,5},{5,1},{9,13},{13,9},{2,6},{6,2},{1... | collective-permute-start | bytes 98312 | tf_op jit(solution)/shard_map/ppermute | solution.py:797
  48.6 3.6 %collective-permute-start.10 = (f32[1,4]{1,0:T(1,128)S(1)}, f32[1,4]{1,0:T(1,128)S(1)}, u32[]{:S(2)}, u32[]{:S(2)}) collective-permute-start(f32[1,4]{1,0:T(1,128)S(1)} %get-tuple-element.58.refs_1_), channel_id=1, source_target_pairs={{0,16},{16,0},{1,17},{17,1},{2,18},{18,2},{3,19},{19,3},{4,20},{20... | collective-permute-start | bytes 56 | tf_op jit(solution)/shard_map/ppermute | solution.py:870

commit v10 on v9

--- a/solution.py
+++ b/solution.py
@@ -11,6 +11,7 @@
 bf16 = jnp.bfloat16
 LANES = 128
 HALO = 2
+SLAB_PARTS = 4
 KERNEL_BYTES = 24 * 1024 * 1024
 PEAK_AT = 64
 CODE_AT = 66
@@ -154,10 +155,13 @@
     even = lax.axis_index("sz") % 2
     starts = ((1 - even) * (depth - HALO), even * (depth - HALO))
     copies = []
-    for which, (start, target) in enumerate(zip(starts, (first_ref, second_ref))):
-        source = vol_ref.at[0, :, pl.ds(start, HALO)]
-        copies.append(pltpu.make_async_copy(source, target, done.at[which]))
-        copies[-1].start()
+    group = first_ref.shape[0] // SLAB_PARTS
+    for start, target in zip(starts, (first_ref, second_ref)):
+        for part in range(SLAB_PARTS):
+            own = slice(part * group, (part + 1) * group)
+            source = vol_ref.at[0, own, pl.ds(start, HALO)]
+            copies.append(pltpu.make_async_copy(source, target.at[own], done.at[len(copies)]))
+            copies[-1].start()
     for copy in copies:
         copy.wait()
 
@@ -260,17 +264,13 @@
     depth, count, channels = raw_ref.shape[:3]
     planes, own_height = deep_ref.shape[:2]
     below, above = sides("sy", got_first_ref[...], got_second_ref[...])
-    edge_ref[0] = below
-    edge_ref[1] = above
-
-    for at_end, end in (
-        (lax.axis_index("sz") == 0, slice(0, HALO)),
-        (lax.axis_index("sz") == lax.axis_size("sz") - 1, slice(planes - HALO, planes)),
-    ):
-
-        @pl.when(at_end)
-        def _():
-            edge_ref[:, end] = jnp.zeros((2, HALO) + edge_ref.shape[2:], bf16)
+    at_z = lax.axis_index("sz")
+    lowest = jnp.where(at_z > 0, 1.0, 0.0).astype(bf16)
+    highest = jnp.where(at_z < lax.axis_size("sz") - 1, 1.0, 0.0).astype(bf16)
+    for side, cells in enumerate((below, above)):
+        edge_ref[side, :HALO] = cells[:HALO] * lowest
+        edge_ref[side, HALO : planes - HALO] = cells[HALO : planes - HALO]
+        edge_ref[side, planes - HALO :] = cells[planes - HALO :] * highest
 
     def cell(z, y):
         if y < HALO:
@@ -327,6 +327,12 @@
         at_y = lax.axis_index("sy")
         last_z = lax.axis_size("sz") - 1
         last_y = lax.axis_size("sy") - 1
+
+        def one_if(inside):
+            return jnp.where(inside, 1.0, 0.0).astype(bf16)
+
+        edges_z = (one_if(at_z > 0), one_if(at_z < last_z))
+        edges_y = (one_if(at_y > 0), one_if(at_y < last_y))
         peak = jnp.zeros((channels, width), bf16)
         for z in range(wide_depth):
             for y in range(wide_height):
@@ -339,20 +345,11 @@
                 hidden = activated(raw, scale, offset)
                 if 1 <= y < wide_height - 1 and 1 <= z < wide_depth - 1:
                     peak = jnp.maximum(peak, jnp.abs(hidden))
-                hidden_ref[z, y] = bounded(hidden, bound)
-        outside = (
-            (at_z == 0, (slice(0, 1), slice(0, wide_height))),
-            (at_z == last_z, (slice(wide_depth - 1, wide_depth), slice(0, wide_height))),
-            (at_y == 0, (slice(0, wide_depth), slice(0, 1))),
-            (at_y == last_y, (slice(0, wide_depth), slice(wide_height - 1, wide_height))),
-        )
-        for at_end, (zs, ys) in outside:
-
-            @pl.when(at_end)
-            def _():
-                count = (zs.stop - zs.start, ys.stop - ys.start)
-                hidden_ref[zs, ys] = jnp.zeros(count + (channels, width), bf16)
-
+                hidden = bounded(hidden, bound)
+                for place, last, edges in ((z, wide_depth - 1, edges_z), (y, wide_height - 1, edges_y)):
+                    if place in (0, last):
+                        hidden = hidden * edges[place == last]
+                hidden_ref[z, y] = hidden
         blank = jnp.zeros((channels, width), f32)
         weight = weight_ref[...]
         sign = jnp.where(lane_of(param_ref, 2, channels) >= 0, 1.0, -1.0).astype(f32)
@@ -757,7 +754,7 @@
             near_shape((channels, HALO, height, width), bf16),
             near_shape((channels, HALO, height, width), bf16),
         ),
-        scratch_shapes=[pltpu.SemaphoreType.DMA((2,))],
+        scratch_shapes=[pltpu.SemaphoreType.DMA((2 * SLAB_PARTS,))],
         name="slabs",
     )(volume)
     cells, peak = pl.pallas_call(

time: 53.1 us -> 52.9 us (level)
  no operation moved by 1% of the time
where the time goes in v10:
time: 52.9 us; the launch traced here: 52.6 us
  blocking collectives  26.3 us (50%)
  Pallas kernels  12.8 us (24%)
  starting transfers between devices  11.5 us (22%)
  waiting for transfers between devices  1.17 us (2%)
  between operations  0.74 us (1%)
    all_to_all x1, blocking collectives, per_device(): rows = lax.all_to_all(row, ('sy', 'sz'), 0, 0, tiled=True)  19.1 us
    all_gather x1, blocking collectives, per_device(): gathered = lax.all_gather(jnp.concatenate(loads, axis=0), 'sy', axis=0)  7.19 us
    ppermute x3, starting transfers between devices, per_device(): lax.ppermute(load, 'sz', [(i, i ^ k) for i in range(z_groups)])  4.45 us
    pallas_call x1, Pallas kernels, per_device(): pl.pallas_call(third_kernel(fine_cells, coarse_cells, load_rows, third_ro...  3.22 us
    ppermute x1, starting transfers between devices, per_device(): z_first = lax.ppermute(z_first, 'sz', pair_first)  3.12 us
    pallas_call x1, Pallas kernels, per_device(): pl.pallas_call(fourth_kernel(coarse_cells), out_shape=(near_shape((chan_o...  2.1 us
    ppermute x1, starting transfers between devices, per_device(): lax.ppermute(peaks, 'sample', [(i, (i + k) % samples) for i in range(samp...  1.49 us
    pallas_call x1, Pallas kernels, per_device(): pl.pallas_call(matrix_kernel, out_shape=(near_shape((3 * channels, 9 * ch...  1.47 us
  transfers between devices with their start and end apart: 11, of which 3 were waited for; matrix products, arithmetic and copies ran while one was open for 0% of the time, Pallas kernels for 11%

profile of v10, /device:TPU:0, one launch (start us, length us, event | category | flops | bytes accessed | tf_op | source)
XLA Modules:
  0.0 52.6 jit_solution(10676898131898804757)
XLA Ops:
  0.6 1.0 %slabs.1 = (bf16[32,2,8,128]{3,2,1,0:T(8,128)(2,1)S(1)}, bf16[32,2,8,128]{3,2,1,0:T(8,128)(2,1)S(1)}) custom-call(bf16[1,32,4,8,128]{4,3,2,1,0:T(8,128)(2,1)} %vol_ref.3), custom_call_target="tpu_custom_call" | custom-call | tf_op jit(solution)/shard_map/slabs/pallas_call | solution.py:749
  1.6 3.1 %collective-permute-start = (bf16[32,2,8,128]{3,2,1,0:T(8,128)(2,1)S(1)}, bf16[32,2,8,128]{3,2,1,0:T(8,128)(2,1)S(1)}, u32[]{:S(2)}, u32[]{:S(2)}) collective-permute-start(bf16[32,2,8,128]{3,2,1,0:T(8,128)(2,1)S(1)} %get-tuple-element.33), channel_id=1, source_target_pairs={{0,1},{1,0},{2,3},{3,2},{4,5},{5,4},{6,7},{7,6},{8,9},{9,8},{10,11... | collective-permute-start | bytes 393224 | tf_op jit(solution)/shard_map/ppermute | solution.py:796
  4.7 0.7 %collective-permute-start.1 = (bf16[32,2,8,128]{3,2,1,0:T(8,128)(2,1)S(1)}, bf16[32,2,8,128]{3,2,1,0:T(8,128)(2,1)S(1)}, u32[]{:S(2)}, u32[]{:S(2)}) collective-permute-start(bf16[32,2,8,128]{3,2,1,0:T(8,128)(2,1)S(1)} %get-tuple-element.34), channel_id=1, source_target_pairs={{0,0},{1,2},{2,1},{3,3},{4,4},{5,6},{6,5},{7,7},{8,8},{9,10},{10,9... | collective-permute-start | bytes 393224 | tf_op jit(solution)/shard_map/ppermute | solution.py:797
  5.4 1.2 %prep.1 = (bf16[4,8,32,128]{3,2,1,0:T(8,128)(2,1)S(1)}, f32[1,128]{1,0:T(1,128)S(1)}) custom-call(bf16[1,32,4,8,128]{4,3,2,1,0:T(8,128)(2,1)} %vol_ref.3, f32[4,16]{1,0:T(4,128)} %hist_ref.3), custom_call_target="tpu_custom_call" | custom-call | tf_op jit(solution)/shard_map/prep/pallas_call | solution.py:760
  6.5 1.5 %matrices.1 = (bf16[96,288]{1,0:T(8,128)(2,1)S(1)}, bf16[96,288]{1,0:T(8,128)(2,1)S(1)}, bf16[64,256]{1,0:T(8,128)(2,1)S(1)}, bf16[144,192]{1,0:T(8,128)(2,1)S(1...) custom-call(f32[1,128]{1,0:T(1,128)S(1)} %get-tuple-element.35.peak_ref, bf16[27,32,32]{2,1,0:T(8,128)(2,1)} %first_ref.1, ...), custom_call_target="tpu_custom_call" | custom-call | tf_op jit(solution)/shard_map/matrices/pallas_call | solution.py:769
  8.0 0.2 collective-permute-done.got_first_ref
  8.2 0.0 collective-permute-done.1.got_second_ref
  8.2 0.2 deep.1
  8.4 0.1 collective-permute-start.2
  8.5 0.7 %collective-permute-start.3 = (bf16[8,2,32,128]{3,2,1,0:T(8,128)(2,1)S(1)}, bf16[8,2,32,128]{3,2,1,0:T(8,128)(2,1)S(1)}, u32[]{:S(2)}, u32[]{:S(2)}) collective-permute-start(bf16[8,2,32,128]{3,2,1,0:T(8,128)(2,1)S(1)} %get-tuple-element.43), channel_id=1, source_target_pairs={{0,0},{4,8},{8,4},{12,12},{1,1},{5,9},{9,5},{13,13},{2,2},{6,10},{... | collective-permute-start | bytes 393224 | tf_op jit(solution)/shard_map/ppermute | solution.py:812
  9.2 0.9 %first_inner.1 = (bf16[8,8,32,128]{3,2,1,0:T(8,128)(2,1)S(1)}, f32[6,6,32,128]{3,2,1,0:T(8,128)S(1)}, f32[2,32,128]{2,1,0:T(8,128)S(1)}) custom-call(bf16[4,8,32,128]{3,2,1,0:T(8,128)(2,1)S(1)} %get-tuple-element.32.cells_ref.own_ref, bf16[2,8,32,128]{3,2,1,0:T(8,128)(2,1)S(1)} %get-tuple-element.37.got_first_ref, ...), custom_call_target="tpu_custom_call" | custom-call | tf_op jit(solution)/shard_map/first_inner/pallas_call | solution.py:813
  10.1 0.0 collective-permute-done.2.got_first_ref
  10.1 0.0 collective-permute-done.3.got_second_ref
  10.1 0.7 %first_outer.1 = (f32[6,4,32,128]{3,2,1,0:T(8,128)S(1)}, f32[16,1,128]{2,1,0:T(1,128)S(1)}) custom-call(bf16[8,8,32,128]{3,2,1,0:T(8,128)(2,1)S(1)} %get-tuple-element.41.deep_ref, bf16[8,2,32,128]{3,2,1,0:T(8,128)(2,1)S(1)} %collective-permute-done.2.got_first_ref, bf16[8,2,32,128]{3,2,1,0:T(8,128)(2,1)S(1)} %collective-permute-done.3.got_second_ref, ...), custom_call_target="tpu_custom_call" | custom-call | tf_op jit(solution)/shard_map/first_outer/pallas_call | solution.py:822
  10.8 19.1 %all_to_all.5.rows_ref = f32[16,1,128]{2,1,0:T(1,128)S(1)} all-to-all(f32[16,1,128]{2,1,0:T(1,128)S(1)} %get-tuple-element.46), channel_id=1, replica_groups=mesh['sample'=2,'sy'=4,'sz'=4] {'sy','sz'}, dimensions={0} | all-to-all | bytes 16384 | tf_op jit(solution)/shard_map/all_to_all | solution.py:831
  30.0 1.4 %second.1 = (f32[4,8,32,128]{3,2,1,0:T(8,128)S(1)}, bf16[72,256]{1,0:T(8,128)(2,1)S(1)}) custom-call(f32[6,6,32,128]{3,2,1,0:T(8,128)S(1)} %get-tuple-element.40.inner_ref, f32[6,4,32,128]{3,2,1,0:T(8,128)S(1)} %get-tuple-element.45.outer_ref, f32[16,1,128]{2,1,0:T(1,128)S(1)} %all_to_all.5.rows_ref, bf16[96,288]{1,0:T(8,128)(2,1)S(1)} %get-tuple-element.47.weight_ref, ...), custom_call_target="tpu_custom_call" | custom-call | tf_op jit(solution)/shard_map/second/pallas_call | solution.py:832
  31.4 0.7 %collective-permute-start.6 = (bf16[72,256]{1,0:T(8,128)(2,1)S(1)}, bf16[72,256]{1,0:T(8,128)(2,1)S(1)}, u32[]{:S(2)}, u32[]{:S(2)}) collective-permute-start(bf16[72,256]{1,0:T(8,128)(2,1)S(1)} %get-tuple-element.49), channel_id=1, source_target_pairs={{0,3},{1,2},{2,1},{3,0},{4,7},{5,6},{6,5},{7,4},{8,11},{9,10},{10,... | collective-permute-start | bytes 110600 | tf_op jit(solution)/shard_map/ppermute | solution.py:847
  32.1 1.4 %collective-permute-start.5 = (bf16[72,256]{1,0:T(8,128)(2,1)S(1)}, bf16[72,256]{1,0:T(8,128)(2,1)S(1)}, u32[]{:S(2)}, u32[]{:S(2)}) collective-permute-start(bf16[72,256]{1,0:T(8,128)(2,1)S(1)} %get-tuple-element.49), channel_id=1, source_target_pairs={{0,2},{1,3},{2,0},{3,1},{4,6},{5,7},{6,4},{7,5},{8,10},{9,11},{10,... | collective-permute-start | bytes 110600 | tf_op jit(solution)/shard_map/ppermute | solution.py:847
  33.5 2.4 %collective-permute-start.4 = (bf16[72,256]{1,0:T(8,128)(2,1)S(1)}, bf16[72,256]{1,0:T(8,128)(2,1)S(1)}, u32[]{:S(2)}, u32[]{:S(2)}) collective-permute-start(bf16[72,256]{1,0:T(8,128)(2,1)S(1)} %get-tuple-element.49), channel_id=1, source_target_pairs={{0,1},{1,0},{2,3},{3,2},{4,5},{5,4},{6,7},{7,6},{8,9},{9,8},{10,11... | collective-permute-start | bytes 110600 | tf_op jit(solution)/shard_map/ppermute | solution.py:847
  35.9 0.0 collective-permute-start.9
  35.9 0.6 %collective-permute-start.8 = (bf16[64,256]{1,0:T(8,128)(2,1)S(1)}, bf16[64,256]{1,0:T(8,128)(2,1)S(1)}, u32[]{:S(2)}, u32[]{:S(2)}) collective-permute-start(bf16[64,256]{1,0:T(8,128)(2,1)S(1)} %get-tuple-element.50.refs_2_), channel_id=1, source_target_pairs={{0,8},{4,12},{8,0},{12,4},{1,9},{5,13},{9,1},{13,5},{2,10},{6,14},... | collective-permute-start | bytes 98312 | tf_op jit(solution)/shard_map/ppermute | solution.py:794
  36.5 0.8 %collective-permute-done.6 = bf16[72,256]{1,0:T(8,128)(2,1)S(1)} collective-permute-done((bf16[72,256]{1,0:T(8,128)(2,1)S(1)}, bf16[72,256]{1,0:T(8,128)(2,1)S(1)}, u32[]{:S(2)}, u32[]{:S(2)}) %collective-permute-start.6) | collective-permute-done | bytes 36896 | tf_op jit(solution)/shard_map/ppermute | solution.py:847
  37.3 0.5 collective-permute-start.7
  37.7 0.0 collective-permute-done.5
  37.8 0.1 collective-permute-done.4
  37.9 7.2 %all-gather = bf16[1152,256]{1,0:T(8,128)(2,1)S(1)} all-gather(bf16[288,256]{1,0:T(8,128)(2,1)S(1)} %pad_maximum_fusion), channel_id=2, replica_groups=mesh['sample'=2,'sy'=4,'sz'=4] {'sy'}, dimensions={0}, use_global_device_ids=true | all-gather | bytes 737280 | tf_op jit(solution)/shard_map/all_gather | solution.py:848
  45.1 0.0 collective-permute-done.9.refs_5_
  45.1 0.0 collective-permute-done.8.refs_4_
  45.1 0.0 collective-permute-done.7.refs_3_
  45.1 3.2 %third.1 = (f32[8,64,1024]{2,1,0:T(8,128)S(1)}, f32[1,4]{1,0:T(1,128)S(1)}, f32[32,128]{1,0:T(8,128)S(1)}, f32[64,128]{1,0:T(8,128)S(1)}) custom-call(bf16[4,288,256]{2,1,0:T(8,128)(2,1)S(1)} %bitcast.2, f32[32,128]{1,0:T(8,128)S(1)} %get-tuple-element.36.param_ref.refs_1_, bf16[64,256]{1,0:T(8,128)(2,1)S(1)} %get-tuple-element.50.refs_2_, ...), custom_call_target="tpu_custom_call" | custom-call | tf_op jit(solution)/shard_map/third/pallas_call | solution.py:849
  48.4 1.5 %collective-permute-start.10 = (f32[1,4]{1,0:T(1,128)S(1)}, f32[1,4]{1,0:T(1,128)S(1)}, u32[]{:S(2)}, u32[]{:S(2)}) collective-permute-start(f32[1,4]{1,0:T(1,128)S(1)} %get-tuple-element.58.refs_1_), channel_id=1, source_target_pairs={{0,16},{16,0},{1,17},{17,1},{2,18},{18,2},{3,19},{19,3},{4,20},{20... | collective-permute-start | bytes 56 | tf_op jit(solution)/shard_map/ppermute | solution.py:867
  49.8 2.1 %fourth.1 = (bf16[16,2,1024]{2,1,0:T(2,128)(2,1)S(1)}, bf16[1,32,4,8,128]{4,3,2,1,0:T(8,128)(2,1)}) custom-call(f32[8,64,1024]{2,1,0:T(8,128)S(1)} %get-tuple-element.51.raw_ref, bf16[144,192]{1,0:T(8,128)(2,1)S(1)} %get-tuple-element.52.weight_ref, f32[32,128]{1,0:T(8,128)S(1)} %get-tuple-element.36.param_ref.refs_1_, ...), custom_call_target="tpu_custom_call" | custom-call | tf_op jit(solution)/shard_map/fourth/pallas_call | solution.py:872
  52.0 0.0 collective-permute-done.10.refs_2_
  52.0 0.6 %final.1 = (bf16[1,16,2,1024]{3,2,1,0:T(2,128)(2,1)}, f32[1,4]{1,0:T(1,128)}) custom-call(bf16[16,2,1024]{2,1,0:T(2,128)(2,1)S(1)} %get-tuple-element.57.refs_0_, f32[1,4]{1,0:T(1,128)S(1)} %get-tuple-element.58.refs_1_, f32[1,4]{1,0:T(1,128)S(1)} %collective-permute-done.10.refs_2_), custom_call_target="tpu_custom_call" | custom-call | tf_op jit(solution)/shard_map/final/pallas_call | solution.py:888
  (1 shorter events, 0.0 us)
Async XLA Ops:
  1.6 6.6 %collective-permute-start = (bf16[32,2,8,128]{3,2,1,0:T(8,128)(2,1)S(1)}, bf16[32,2,8,128]{3,2,1,0:T(8,128)(2,1)S(1)}, u32[]{:S(2)}, u32[]{:S(2)}) collective-permute-start(bf16[32,2,8,128]{3,2,1,0:T(8,128)(2,1)S(1)} %get-tuple-element.33), channel_id=1, source_target_pairs={{0,1},{1,0},{2,3},{3,2},{4,5},{5,4},{6,7},{7,6},{8,9},{9,8},{10,11... | collective-permute-start | bytes 393224 | tf_op jit(solution)/shard_map/ppermute | solution.py:796
  4.7 3.5 %collective-permute-start.1 = (bf16[32,2,8,128]{3,2,1,0:T(8,128)(2,1)S(1)}, bf16[32,2,8,128]{3,2,1,0:T(8,128)(2,1)S(1)}, u32[]{:S(2)}, u32[]{:S(2)}) collective-permute-start(bf16[32,2,8,128]{3,2,1,0:T(8,128)(2,1)S(1)} %get-tuple-element.34), channel_id=1, source_target_pairs={{0,0},{1,2},{2,1},{3,3},{4,4},{5,6},{6,5},{7,7},{8,8},{9,10},{10,9... | collective-permute-start | bytes 393224 | tf_op jit(solution)/shard_map/ppermute | solution.py:797
  8.4 1.7 %collective-permute-start.2 = (bf16[8,2,32,128]{3,2,1,0:T(8,128)(2,1)S(1)}, bf16[8,2,32,128]{3,2,1,0:T(8,128)(2,1)S(1)}, u32[]{:S(2)}, u32[]{:S(2)}) collective-permute-start(bf16[8,2,32,128]{3,2,1,0:T(8,128)(2,1)S(1)} %get-tuple-element.42), channel_id=1, source_target_pairs={{0,4},{4,0},{8,12},{12,8},{1,5},{5,1},{9,13},{13,9},{2,6},{6,2},{1... | collective-permute-start | bytes 393224 | tf_op jit(solution)/shard_map/ppermute | solution.py:811
  8.5 1.6 %collective-permute-start.3 = (bf16[8,2,32,128]{3,2,1,0:T(8,128)(2,1)S(1)}, bf16[8,2,32,128]{3,2,1,0:T(8,128)(2,1)S(1)}, u32[]{:S(2)}, u32[]{:S(2)}) collective-permute-start(bf16[8,2,32,128]{3,2,1,0:T(8,128)(2,1)S(1)} %get-tuple-element.43), channel_id=1, source_target_pairs={{0,0},{4,8},{8,4},{12,12},{1,1},{5,9},{9,5},{13,13},{2,2},{6,10},{... | collective-permute-start | bytes 393224 | tf_op jit(solution)/shard_map/ppermute | solution.py:812
  31.4 5.9 %collective-permute-start.6 = (bf16[72,256]{1,0:T(8,128)(2,1)S(1)}, bf16[72,256]{1,0:T(8,128)(2,1)S(1)}, u32[]{:S(2)}, u32[]{:S(2)}) collective-permute-start(bf16[72,256]{1,0:T(8,128)(2,1)S(1)} %get-tuple-element.49), channel_id=1, source_target_pairs={{0,3},{1,2},{2,1},{3,0},{4,7},{5,6},{6,5},{7,4},{8,11},{9,10},{10,... | collective-permute-start | bytes 110600 | tf_op jit(solution)/shard_map/ppermute | solution.py:847
  32.1 5.7 %collective-permute-start.5 = (bf16[72,256]{1,0:T(8,128)(2,1)S(1)}, bf16[72,256]{1,0:T(8,128)(2,1)S(1)}, u32[]{:S(2)}, u32[]{:S(2)}) collective-permute-start(bf16[72,256]{1,0:T(8,128)(2,1)S(1)} %get-tuple-element.49), channel_id=1, source_target_pairs={{0,2},{1,3},{2,0},{3,1},{4,6},{5,7},{6,4},{7,5},{8,10},{9,11},{10,... | collective-permute-start | bytes 110600 | tf_op jit(solution)/shard_map/ppermute | solution.py:847
  33.5 4.4 %collective-permute-start.4 = (bf16[72,256]{1,0:T(8,128)(2,1)S(1)}, bf16[72,256]{1,0:T(8,128)(2,1)S(1)}, u32[]{:S(2)}, u32[]{:S(2)}) collective-permute-start(bf16[72,256]{1,0:T(8,128)(2,1)S(1)} %get-tuple-element.49), channel_id=1, source_target_pairs={{0,1},{1,0},{2,3},{3,2},{4,5},{5,4},{6,7},{7,6},{8,9},{9,8},{10,11... | collective-permute-start | bytes 110600 | tf_op jit(solution)/shard_map/ppermute | solution.py:847
  35.9 9.2 %collective-permute-start.9 = (bf16[64,256]{1,0:T(8,128)(2,1)S(1)}, bf16[64,256]{1,0:T(8,128)(2,1)S(1)}, u32[]{:S(2)}, u32[]{:S(2)}) collective-permute-start(bf16[64,256]{1,0:T(8,128)(2,1)S(1)} %get-tuple-element.50.refs_2_), channel_id=1, source_target_pairs={{0,12},{4,8},{8,4},{12,0},{1,13},{5,9},{9,5},{13,1},{2,14},{6,10},... | collective-permute-start | bytes 98312 | tf_op jit(solution)/shard_map/ppermute | solution.py:794
  35.9 9.2 %collective-permute-start.8 = (bf16[64,256]{1,0:T(8,128)(2,1)S(1)}, bf16[64,256]{1,0:T(8,128)(2,1)S(1)}, u32[]{:S(2)}, u32[]{:S(2)}) collective-permute-start(bf16[64,256]{1,0:T(8,128)(2,1)S(1)} %get-tuple-element.50.refs_2_), channel_id=1, source_target_pairs={{0,8},{4,12},{8,0},{12,4},{1,9},{5,13},{9,1},{13,5},{2,10},{6,14},... | collective-permute-start | bytes 98312 | tf_op jit(solution)/shard_map/ppermute | solution.py:794
  37.3 7.8 %collective-permute-start.7 = (bf16[64,256]{1,0:T(8,128)(2,1)S(1)}, bf16[64,256]{1,0:T(8,128)(2,1)S(1)}, u32[]{:S(2)}, u32[]{:S(2)}) collective-permute-start(bf16[64,256]{1,0:T(8,128)(2,1)S(1)} %get-tuple-element.50.refs_2_), channel_id=1, source_target_pairs={{0,4},{4,0},{8,12},{12,8},{1,5},{5,1},{9,13},{13,9},{2,6},{6,2},{1... | collective-permute-start | bytes 98312 | tf_op jit(solution)/shard_map/ppermute | solution.py:794
  48.4 3.6 %collective-permute-start.10 = (f32[1,4]{1,0:T(1,128)S(1)}, f32[1,4]{1,0:T(1,128)S(1)}, u32[]{:S(2)}, u32[]{:S(2)}) collective-permute-start(f32[1,4]{1,0:T(1,128)S(1)} %get-tuple-element.58.refs_1_), channel_id=1, source_target_pairs={{0,16},{16,0},{1,17},{17,1},{2,18},{18,2},{3,19},{19,3},{4,20},{20... | collective-permute-start | bytes 56 | tf_op jit(solution)/shard_map/ppermute | solution.py:867

commit v11 on v10

--- a/solution.py
+++ b/solution.py
@@ -471,31 +471,30 @@
 
         peak_pool = jnp.zeros((channels, span), bf16)
         half_groups = y_groups // 2
-        for k in range(z_groups):
-            for zp in range(z_own):
+        for s in range(half_groups):
+            for k, zp in [(k, zp) for k in range(z_groups) for zp in range(z_own)]:
                 place = (at_z ^ k) * z_own + zp
                 at = k * load_rows + zp * channels
                 ends = []
-                for s in range(half_groups):
-                    both = []
-                    for own in (s, s + half_groups):
-                        center = rows[own, k][:, CODE_AT : CODE_AT + 1]
-                        reach = rows[own, k][:, CODE_AT + 1 : CODE_AT + 2]
-                        code = jnp.log(all_ref[own, at : at + channels, :].astype(f32))
-                        value = activated(code, scale * reach, scale * center + offset)
-                        peak_pool = jnp.maximum(peak_pool, jnp.abs(value))
-                        both.append(bounded(value, bound))
-                    for q in range(span // LANES):
-                        low, high = (one[:, at_block(q)] for one in both)
-                        block = s * (span // row_len) + 2 * q
-                        one = jnp.where(lower, low, turned(high))
-                        two = jnp.where(lower, turned(low), high)
-                        keep(place, block + 1, one)
-                        keep(place, block + 2, two)
-                        if block == 0:
-                            ends.append((blocks + 1, jnp.where(lower, turned(one), blank)))
-                        if block + 2 == blocks:
-                            ends.append((0, jnp.where(lower, blank, turned(two))))
+                both = []
+                for own in (s, s + half_groups):
+                    center = rows[own, k][:, CODE_AT : CODE_AT + 1]
+                    reach = rows[own, k][:, CODE_AT + 1 : CODE_AT + 2]
+                    code = jnp.log(all_ref[own, at : at + channels, :].astype(f32))
+                    value = activated(code, scale * reach, scale * center + offset)
+                    peak_pool = jnp.maximum(peak_pool, jnp.abs(value))
+                    both.append(bounded(value, bound))
+                for q in range(span // LANES):
+                    low, high = (one[:, at_block(q)] for one in both)
+                    block = s * (span // row_len) + 2 * q
+                    one = jnp.where(lower, low, turned(high))
+                    two = jnp.where(lower, turned(low), high)
+                    keep(place, block + 1, one)
+                    keep(place, block + 2, two)
+                    if block == 0:
+                        ends.append((blocks + 1, jnp.where(lower, turned(one), blank)))
+                    if block + 2 == blocks:
+                        ends.append((0, jnp.where(lower, blank, turned(two))))
                 for block, value in ends:
                     keep(place, block, value)
         main = 3 * chan_own
@@ -510,8 +509,8 @@
         squares = [blank for _ in range(y_groups)]
         leasts = [blank + 1e30 for _ in range(y_groups)]
         mosts = [blank - 1e30 for _ in range(y_groups)]
-        for z in range(planes):
-            for t in range(blocks // 2):
+        for t in range(blocks // 2):
+            for z in range(planes):
                 depths = [dz for dz in range(3) if 0 <= z + dz - 1 < planes]
 
                 def cells(dz, dy, which):

time: 52.9 us -> 52.8 us (level)
  no operation moved by 1% of the time
where the time goes in v11:
time: 52.8 us; the launch traced here: 52.5 us
  blocking collectives  26.3 us (50%)
  Pallas kernels  12.7 us (24%)
  starting transfers between devices  11.5 us (22%)
  waiting for transfers between devices  1.17 us (2%)
  between operations  0.74 us (1%)
    all_to_all x1, blocking collectives, per_device(): rows = lax.all_to_all(row, ('sy', 'sz'), 0, 0, tiled=True)  19.1 us
    all_gather x1, blocking collectives, per_device(): gathered = lax.all_gather(jnp.concatenate(loads, axis=0), 'sy', axis=0)  7.19 us
    ppermute x3, starting transfers between devices, per_device(): lax.ppermute(load, 'sz', [(i, i ^ k) for i in range(z_groups)])  4.45 us
    ppermute x1, starting transfers between devices, per_device(): z_first = lax.ppermute(z_first, 'sz', pair_first)  3.12 us
    pallas_call x1, Pallas kernels, per_device(): pl.pallas_call(third_kernel(fine_cells, coarse_cells, load_rows, third_ro...  3.08 us
    pallas_call x1, Pallas kernels, per_device(): pl.pallas_call(fourth_kernel(coarse_cells), out_shape=(near_shape((chan_o...  2.1 us
    ppermute x1, starting transfers between devices, per_device(): lax.ppermute(peaks, 'sample', [(i, (i + k) % samples) for i in range(samp...  1.49 us
    pallas_call x1, Pallas kernels, per_device(): pl.pallas_call(matrix_kernel, out_shape=(near_shape((3 * channels, 9 * ch...  1.47 us
  transfers between devices with their start and end apart: 11, of which 3 were waited for; matrix products, arithmetic and copies ran while one was open for 0% of the time, Pallas kernels for 11%

profile of v11, /device:TPU:0, one launch (start us, length us, event | category | flops | bytes accessed | tf_op | source)
XLA Modules:
  0.0 52.5 jit_solution(8321608422782392311)
XLA Ops:
  0.6 1.0 %slabs.1 = (bf16[32,2,8,128]{3,2,1,0:T(8,128)(2,1)S(1)}, bf16[32,2,8,128]{3,2,1,0:T(8,128)(2,1)S(1)}) custom-call(bf16[1,32,4,8,128]{4,3,2,1,0:T(8,128)(2,1)} %vol_ref.3), custom_call_target="tpu_custom_call" | custom-call | tf_op jit(solution)/shard_map/slabs/pallas_call | solution.py:748
  1.6 3.1 %collective-permute-start = (bf16[32,2,8,128]{3,2,1,0:T(8,128)(2,1)S(1)}, bf16[32,2,8,128]{3,2,1,0:T(8,128)(2,1)S(1)}, u32[]{:S(2)}, u32[]{:S(2)}) collective-permute-start(bf16[32,2,8,128]{3,2,1,0:T(8,128)(2,1)S(1)} %get-tuple-element.33), channel_id=1, source_target_pairs={{0,1},{1,0},{2,3},{3,2},{4,5},{5,4},{6,7},{7,6},{8,9},{9,8},{10,11... | collective-permute-start | bytes 393224 | tf_op jit(solution)/shard_map/ppermute | solution.py:795
  4.7 0.7 %collective-permute-start.1 = (bf16[32,2,8,128]{3,2,1,0:T(8,128)(2,1)S(1)}, bf16[32,2,8,128]{3,2,1,0:T(8,128)(2,1)S(1)}, u32[]{:S(2)}, u32[]{:S(2)}) collective-permute-start(bf16[32,2,8,128]{3,2,1,0:T(8,128)(2,1)S(1)} %get-tuple-element.34), channel_id=1, source_target_pairs={{0,0},{1,2},{2,1},{3,3},{4,4},{5,6},{6,5},{7,7},{8,8},{9,10},{10,9... | collective-permute-start | bytes 393224 | tf_op jit(solution)/shard_map/ppermute | solution.py:796
  5.4 1.2 %prep.1 = (bf16[4,8,32,128]{3,2,1,0:T(8,128)(2,1)S(1)}, f32[1,128]{1,0:T(1,128)S(1)}) custom-call(bf16[1,32,4,8,128]{4,3,2,1,0:T(8,128)(2,1)} %vol_ref.3, f32[4,16]{1,0:T(4,128)} %hist_ref.3), custom_call_target="tpu_custom_call" | custom-call | tf_op jit(solution)/shard_map/prep/pallas_call | solution.py:759
  6.5 1.5 %matrices.1 = (bf16[96,288]{1,0:T(8,128)(2,1)S(1)}, bf16[96,288]{1,0:T(8,128)(2,1)S(1)}, bf16[64,256]{1,0:T(8,128)(2,1)S(1)}, bf16[144,192]{1,0:T(8,128)(2,1)S(1...) custom-call(f32[1,128]{1,0:T(1,128)S(1)} %get-tuple-element.35.peak_ref, bf16[27,32,32]{2,1,0:T(8,128)(2,1)} %first_ref.1, ...), custom_call_target="tpu_custom_call" | custom-call | tf_op jit(solution)/shard_map/matrices/pallas_call | solution.py:768
  8.0 0.2 collective-permute-done.got_first_ref
  8.2 0.0 collective-permute-done.1.got_second_ref
  8.2 0.2 deep.1
  8.4 0.1 collective-permute-start.2
  8.5 0.7 %collective-permute-start.3 = (bf16[8,2,32,128]{3,2,1,0:T(8,128)(2,1)S(1)}, bf16[8,2,32,128]{3,2,1,0:T(8,128)(2,1)S(1)}, u32[]{:S(2)}, u32[]{:S(2)}) collective-permute-start(bf16[8,2,32,128]{3,2,1,0:T(8,128)(2,1)S(1)} %get-tuple-element.43), channel_id=1, source_target_pairs={{0,0},{4,8},{8,4},{12,12},{1,1},{5,9},{9,5},{13,13},{2,2},{6,10},{... | collective-permute-start | bytes 393224 | tf_op jit(solution)/shard_map/ppermute | solution.py:811
  9.2 0.9 %first_inner.1 = (bf16[8,8,32,128]{3,2,1,0:T(8,128)(2,1)S(1)}, f32[6,6,32,128]{3,2,1,0:T(8,128)S(1)}, f32[2,32,128]{2,1,0:T(8,128)S(1)}) custom-call(bf16[4,8,32,128]{3,2,1,0:T(8,128)(2,1)S(1)} %get-tuple-element.32.cells_ref.own_ref, bf16[2,8,32,128]{3,2,1,0:T(8,128)(2,1)S(1)} %get-tuple-element.37.got_first_ref, ...), custom_call_target="tpu_custom_call" | custom-call | tf_op jit(solution)/shard_map/first_inner/pallas_call | solution.py:812
  10.1 0.0 collective-permute-done.2.got_first_ref
  10.1 0.0 collective-permute-done.3.got_second_ref
  10.1 0.7 %first_outer.1 = (f32[6,4,32,128]{3,2,1,0:T(8,128)S(1)}, f32[16,1,128]{2,1,0:T(1,128)S(1)}) custom-call(bf16[8,8,32,128]{3,2,1,0:T(8,128)(2,1)S(1)} %get-tuple-element.41.deep_ref, bf16[8,2,32,128]{3,2,1,0:T(8,128)(2,1)S(1)} %collective-permute-done.2.got_first_ref, bf16[8,2,32,128]{3,2,1,0:T(8,128)(2,1)S(1)} %collective-permute-done.3.got_second_ref, ...), custom_call_target="tpu_custom_call" | custom-call | tf_op jit(solution)/shard_map/first_outer/pallas_call | solution.py:821
  10.8 19.1 %all_to_all.5.rows_ref = f32[16,1,128]{2,1,0:T(1,128)S(1)} all-to-all(f32[16,1,128]{2,1,0:T(1,128)S(1)} %get-tuple-element.46), channel_id=1, replica_groups=mesh['sample'=2,'sy'=4,'sz'=4] {'sy','sz'}, dimensions={0} | all-to-all | bytes 16384 | tf_op jit(solution)/shard_map/all_to_all | solution.py:830
  30.0 1.4 %second.1 = (f32[4,8,32,128]{3,2,1,0:T(8,128)S(1)}, bf16[72,256]{1,0:T(8,128)(2,1)S(1)}) custom-call(f32[6,6,32,128]{3,2,1,0:T(8,128)S(1)} %get-tuple-element.40.inner_ref, f32[6,4,32,128]{3,2,1,0:T(8,128)S(1)} %get-tuple-element.45.outer_ref, f32[16,1,128]{2,1,0:T(1,128)S(1)} %all_to_all.5.rows_ref, bf16[96,288]{1,0:T(8,128)(2,1)S(1)} %get-tuple-element.47.weight_ref, ...), custom_call_target="tpu_custom_call" | custom-call | tf_op jit(solution)/shard_map/second/pallas_call | solution.py:831
  31.4 0.7 %collective-permute-start.6 = (bf16[72,256]{1,0:T(8,128)(2,1)S(1)}, bf16[72,256]{1,0:T(8,128)(2,1)S(1)}, u32[]{:S(2)}, u32[]{:S(2)}) collective-permute-start(bf16[72,256]{1,0:T(8,128)(2,1)S(1)} %get-tuple-element.49), channel_id=1, source_target_pairs={{0,3},{1,2},{2,1},{3,0},{4,7},{5,6},{6,5},{7,4},{8,11},{9,10},{10,... | collective-permute-start | bytes 110600 | tf_op jit(solution)/shard_map/ppermute | solution.py:846
  32.1 1.4 %collective-permute-start.5 = (bf16[72,256]{1,0:T(8,128)(2,1)S(1)}, bf16[72,256]{1,0:T(8,128)(2,1)S(1)}, u32[]{:S(2)}, u32[]{:S(2)}) collective-permute-start(bf16[72,256]{1,0:T(8,128)(2,1)S(1)} %get-tuple-element.49), channel_id=1, source_target_pairs={{0,2},{1,3},{2,0},{3,1},{4,6},{5,7},{6,4},{7,5},{8,10},{9,11},{10,... | collective-permute-start | bytes 110600 | tf_op jit(solution)/shard_map/ppermute | solution.py:846
  33.5 2.4 %collective-permute-start.4 = (bf16[72,256]{1,0:T(8,128)(2,1)S(1)}, bf16[72,256]{1,0:T(8,128)(2,1)S(1)}, u32[]{:S(2)}, u32[]{:S(2)}) collective-permute-start(bf16[72,256]{1,0:T(8,128)(2,1)S(1)} %get-tuple-element.49), channel_id=1, source_target_pairs={{0,1},{1,0},{2,3},{3,2},{4,5},{5,4},{6,7},{7,6},{8,9},{9,8},{10,11... | collective-permute-start | bytes 110600 | tf_op jit(solution)/shard_map/ppermute | solution.py:846
  35.9 0.0 collective-permute-start.9
  35.9 0.6 %collective-permute-start.8 = (bf16[64,256]{1,0:T(8,128)(2,1)S(1)}, bf16[64,256]{1,0:T(8,128)(2,1)S(1)}, u32[]{:S(2)}, u32[]{:S(2)}) collective-permute-start(bf16[64,256]{1,0:T(8,128)(2,1)S(1)} %get-tuple-element.50.refs_2_), channel_id=1, source_target_pairs={{0,8},{4,12},{8,0},{12,4},{1,9},{5,13},{9,1},{13,5},{2,10},{6,14},... | collective-permute-start | bytes 98312 | tf_op jit(solution)/shard_map/ppermute | solution.py:793
  36.5 0.8 %collective-permute-done.6 = bf16[72,256]{1,0:T(8,128)(2,1)S(1)} collective-permute-done((bf16[72,256]{1,0:T(8,128)(2,1)S(1)}, bf16[72,256]{1,0:T(8,128)(2,1)S(1)}, u32[]{:S(2)}, u32[]{:S(2)}) %collective-permute-start.6) | collective-permute-done | bytes 36896 | tf_op jit(solution)/shard_map/ppermute | solution.py:846
  37.3 0.5 collective-permute-start.7
  37.7 0.0 collective-permute-done.5
  37.8 0.1 collective-permute-done.4
  37.9 7.2 %all-gather = bf16[1152,256]{1,0:T(8,128)(2,1)S(1)} all-gather(bf16[288,256]{1,0:T(8,128)(2,1)S(1)} %pad_maximum_fusion), channel_id=2, replica_groups=mesh['sample'=2,'sy'=4,'sz'=4] {'sy'}, dimensions={0}, use_global_device_ids=true | all-gather | bytes 737280 | tf_op jit(solution)/shard_map/all_gather | solution.py:847
  45.1 0.0 collective-permute-done.9.refs_5_
  45.1 0.0 collective-permute-done.8.refs_4_
  45.1 0.0 collective-permute-done.7.refs_3_
  45.1 3.1 %third.1 = (f32[8,64,1024]{2,1,0:T(8,128)S(1)}, f32[1,4]{1,0:T(1,128)S(1)}, f32[32,128]{1,0:T(8,128)S(1)}, f32[64,128]{1,0:T(8,128)S(1)}) custom-call(bf16[4,288,256]{2,1,0:T(8,128)(2,1)S(1)} %bitcast.2, f32[32,128]{1,0:T(8,128)S(1)} %get-tuple-element.36.param_ref.refs_1_, bf16[64,256]{1,0:T(8,128)(2,1)S(1)} %get-tuple-element.50.refs_2_, ...), custom_call_target="tpu_custom_call" | custom-call | tf_op jit(solution)/shard_map/third/pallas_call | solution.py:848
  48.2 1.5 %collective-permute-start.10 = (f32[1,4]{1,0:T(1,128)S(1)}, f32[1,4]{1,0:T(1,128)S(1)}, u32[]{:S(2)}, u32[]{:S(2)}) collective-permute-start(f32[1,4]{1,0:T(1,128)S(1)} %get-tuple-element.58.refs_1_), channel_id=1, source_target_pairs={{0,16},{16,0},{1,17},{17,1},{2,18},{18,2},{3,19},{19,3},{4,20},{20... | collective-permute-start | bytes 56 | tf_op jit(solution)/shard_map/ppermute | solution.py:866
  49.7 2.1 %fourth.1 = (bf16[16,2,1024]{2,1,0:T(2,128)(2,1)S(1)}, bf16[1,32,4,8,128]{4,3,2,1,0:T(8,128)(2,1)}) custom-call(f32[8,64,1024]{2,1,0:T(8,128)S(1)} %get-tuple-element.51.raw_ref, bf16[144,192]{1,0:T(8,128)(2,1)S(1)} %get-tuple-element.52.weight_ref, f32[32,128]{1,0:T(8,128)S(1)} %get-tuple-element.36.param_ref.refs_1_, ...), custom_call_target="tpu_custom_call" | custom-call | tf_op jit(solution)/shard_map/fourth/pallas_call | solution.py:871
  51.8 0.0 collective-permute-done.10.refs_2_
  51.8 0.6 %final.1 = (bf16[1,16,2,1024]{3,2,1,0:T(2,128)(2,1)}, f32[1,4]{1,0:T(1,128)}) custom-call(bf16[16,2,1024]{2,1,0:T(2,128)(2,1)S(1)} %get-tuple-element.57.refs_0_, f32[1,4]{1,0:T(1,128)S(1)} %get-tuple-element.58.refs_1_, f32[1,4]{1,0:T(1,128)S(1)} %collective-permute-done.10.refs_2_), custom_call_target="tpu_custom_call" | custom-call | tf_op jit(solution)/shard_map/final/pallas_call | solution.py:887
  (1 shorter events, 0.0 us)
Async XLA Ops:
  1.6 6.6 %collective-permute-start = (bf16[32,2,8,128]{3,2,1,0:T(8,128)(2,1)S(1)}, bf16[32,2,8,128]{3,2,1,0:T(8,128)(2,1)S(1)}, u32[]{:S(2)}, u32[]{:S(2)}) collective-permute-start(bf16[32,2,8,128]{3,2,1,0:T(8,128)(2,1)S(1)} %get-tuple-element.33), channel_id=1, source_target_pairs={{0,1},{1,0},{2,3},{3,2},{4,5},{5,4},{6,7},{7,6},{8,9},{9,8},{10,11... | collective-permute-start | bytes 393224 | tf_op jit(solution)/shard_map/ppermute | solution.py:795
  4.7 3.5 %collective-permute-start.1 = (bf16[32,2,8,128]{3,2,1,0:T(8,128)(2,1)S(1)}, bf16[32,2,8,128]{3,2,1,0:T(8,128)(2,1)S(1)}, u32[]{:S(2)}, u32[]{:S(2)}) collective-permute-start(bf16[32,2,8,128]{3,2,1,0:T(8,128)(2,1)S(1)} %get-tuple-element.34), channel_id=1, source_target_pairs={{0,0},{1,2},{2,1},{3,3},{4,4},{5,6},{6,5},{7,7},{8,8},{9,10},{10,9... | collective-permute-start | bytes 393224 | tf_op jit(solution)/shard_map/ppermute | solution.py:796
  8.4 1.7 %collective-permute-start.2 = (bf16[8,2,32,128]{3,2,1,0:T(8,128)(2,1)S(1)}, bf16[8,2,32,128]{3,2,1,0:T(8,128)(2,1)S(1)}, u32[]{:S(2)}, u32[]{:S(2)}) collective-permute-start(bf16[8,2,32,128]{3,2,1,0:T(8,128)(2,1)S(1)} %get-tuple-element.42), channel_id=1, source_target_pairs={{0,4},{4,0},{8,12},{12,8},{1,5},{5,1},{9,13},{13,9},{2,6},{6,2},{1... | collective-permute-start | bytes 393224 | tf_op jit(solution)/shard_map/ppermute | solution.py:810
  8.5 1.6 %collective-permute-start.3 = (bf16[8,2,32,128]{3,2,1,0:T(8,128)(2,1)S(1)}, bf16[8,2,32,128]{3,2,1,0:T(8,128)(2,1)S(1)}, u32[]{:S(2)}, u32[]{:S(2)}) collective-permute-start(bf16[8,2,32,128]{3,2,1,0:T(8,128)(2,1)S(1)} %get-tuple-element.43), channel_id=1, source_target_pairs={{0,0},{4,8},{8,4},{12,12},{1,1},{5,9},{9,5},{13,13},{2,2},{6,10},{... | collective-permute-start | bytes 393224 | tf_op jit(solution)/shard_map/ppermute | solution.py:811
  31.4 5.9 %collective-permute-start.6 = (bf16[72,256]{1,0:T(8,128)(2,1)S(1)}, bf16[72,256]{1,0:T(8,128)(2,1)S(1)}, u32[]{:S(2)}, u32[]{:S(2)}) collective-permute-start(bf16[72,256]{1,0:T(8,128)(2,1)S(1)} %get-tuple-element.49), channel_id=1, source_target_pairs={{0,3},{1,2},{2,1},{3,0},{4,7},{5,6},{6,5},{7,4},{8,11},{9,10},{10,... | collective-permute-start | bytes 110600 | tf_op jit(solution)/shard_map/ppermute | solution.py:846
  32.1 5.7 %collective-permute-start.5 = (bf16[72,256]{1,0:T(8,128)(2,1)S(1)}, bf16[72,256]{1,0:T(8,128)(2,1)S(1)}, u32[]{:S(2)}, u32[]{:S(2)}) collective-permute-start(bf16[72,256]{1,0:T(8,128)(2,1)S(1)} %get-tuple-element.49), channel_id=1, source_target_pairs={{0,2},{1,3},{2,0},{3,1},{4,6},{5,7},{6,4},{7,5},{8,10},{9,11},{10,... | collective-permute-start | bytes 110600 | tf_op jit(solution)/shard_map/ppermute | solution.py:846
  33.5 4.4 %collective-permute-start.4 = (bf16[72,256]{1,0:T(8,128)(2,1)S(1)}, bf16[72,256]{1,0:T(8,128)(2,1)S(1)}, u32[]{:S(2)}, u32[]{:S(2)}) collective-permute-start(bf16[72,256]{1,0:T(8,128)(2,1)S(1)} %get-tuple-element.49), channel_id=1, source_target_pairs={{0,1},{1,0},{2,3},{3,2},{4,5},{5,4},{6,7},{7,6},{8,9},{9,8},{10,11... | collective-permute-start | bytes 110600 | tf_op jit(solution)/shard_map/ppermute | solution.py:846
  35.9 9.2 %collective-permute-start.9 = (bf16[64,256]{1,0:T(8,128)(2,1)S(1)}, bf16[64,256]{1,0:T(8,128)(2,1)S(1)}, u32[]{:S(2)}, u32[]{:S(2)}) collective-permute-start(bf16[64,256]{1,0:T(8,128)(2,1)S(1)} %get-tuple-element.50.refs_2_), channel_id=1, source_target_pairs={{0,12},{4,8},{8,4},{12,0},{1,13},{5,9},{9,5},{13,1},{2,14},{6,10},... | collective-permute-start | bytes 98312 | tf_op jit(solution)/shard_map/ppermute | solution.py:793
  35.9 9.2 %collective-permute-start.8 = (bf16[64,256]{1,0:T(8,128)(2,1)S(1)}, bf16[64,256]{1,0:T(8,128)(2,1)S(1)}, u32[]{:S(2)}, u32[]{:S(2)}) collective-permute-start(bf16[64,256]{1,0:T(8,128)(2,1)S(1)} %get-tuple-element.50.refs_2_), channel_id=1, source_target_pairs={{0,8},{4,12},{8,0},{12,4},{1,9},{5,13},{9,1},{13,5},{2,10},{6,14},... | collective-permute-start | bytes 98312 | tf_op jit(solution)/shard_map/ppermute | solution.py:793
  37.3 7.8 %collective-permute-start.7 = (bf16[64,256]{1,0:T(8,128)(2,1)S(1)}, bf16[64,256]{1,0:T(8,128)(2,1)S(1)}, u32[]{:S(2)}, u32[]{:S(2)}) collective-permute-start(bf16[64,256]{1,0:T(8,128)(2,1)S(1)} %get-tuple-element.50.refs_2_), channel_id=1, source_target_pairs={{0,4},{4,0},{8,12},{12,8},{1,5},{5,1},{9,13},{13,9},{2,6},{6,2},{1... | collective-permute-start | bytes 98312 | tf_op jit(solution)/shard_map/ppermute | solution.py:793
  48.2 3.6 %collective-permute-start.10 = (f32[1,4]{1,0:T(1,128)S(1)}, f32[1,4]{1,0:T(1,128)S(1)}, u32[]{:S(2)}, u32[]{:S(2)}) collective-permute-start(f32[1,4]{1,0:T(1,128)S(1)} %get-tuple-element.58.refs_1_), channel_id=1, source_target_pairs={{0,16},{16,0},{1,17},{17,1},{2,18},{18,2},{3,19},{19,3},{4,20},{20... | collective-permute-start | bytes 56 | tf_op jit(solution)/shard_map/ppermute | solution.py:866

commit v12 on v11

--- a/solution.py
+++ b/solution.py
@@ -14,7 +14,6 @@
 SLAB_PARTS = 4
 KERNEL_BYTES = 24 * 1024 * 1024
 PEAK_AT = 64
-CODE_AT = 66
 GAIN_AT = 80
 SHIFT_AT = 96
 CODE_SPAN = 83.0
@@ -373,7 +372,8 @@
                 pool_ref[zp, yp] = best
                 least = jnp.minimum(least, best)
                 most = jnp.maximum(most, best)
-        most, least = peak_of(most), -peak_of(-least)
+        most = jnp.max(most, axis=1, keepdims=True)
+        least = jnp.min(least, axis=1, keepdims=True)
         center = 0.5 * (most + least)
         reach = jnp.maximum(0.5 * (most - least), 1e-30)
         rate = CODE_SPAN / reach
@@ -394,19 +394,18 @@
         row = row + as_row(jnp.sum(square, axis=1, keepdims=True), channels)
         row = row + at_lane(peak_vol, PEAK_AT)
         row = row + at_lane(peak_of(peak), PEAK_AT + 1)
-        row = row + at_lane(center, CODE_AT)
-        row = row + at_lane(reach / CODE_SPAN, CODE_AT + 1)
         row = row + gain_row_ref[...]
-        high = row.astype(bf16).astype(f32)
-        middle = (row - high).astype(bf16).astype(f32)
-        low = row - high - middle
+        code_row = as_row(center, 0) + as_row(reach / CODE_SPAN, channels)
         level = lax.broadcasted_iota(jnp.int32, (ROWS, LANES), 0)
-        parts = jnp.where(
-            level == 0, high, jnp.where(level == 1, middle, jnp.where(level == 2, low, 0.0))
-        )
         body = (depth // 2) * channels
-        load_ref[body:, 0:LANES] = parts.astype(bf16)
-        load_ref[body:, LANES:] = jnp.zeros((ROWS, load_ref.shape[1] - LANES), bf16)
+        for place, one in ((0, row), (LANES, code_row)):
+            high = one.astype(bf16).astype(f32)
+            middle = (one - high).astype(bf16).astype(f32)
+            low = one - high - middle
+            parts = jnp.where(
+                level == 0, high, jnp.where(level == 1, middle, jnp.where(level == 2, low, 0.0))
+            )
+            load_ref[body:, place : place + LANES] = parts.astype(bf16)
 
     return kernel
 
@@ -471,6 +470,7 @@
 
         peak_pool = jnp.zeros((channels, span), bf16)
         half_groups = y_groups // 2
+        codes = {}
         for s in range(half_groups):
             for k, zp in [(k, zp) for k in range(z_groups) for zp in range(z_own)]:
                 place = (at_z ^ k) * z_own + zp
@@ -478,10 +478,15 @@
                 ends = []
                 both = []
                 for own in (s, s + half_groups):
-                    center = rows[own, k][:, CODE_AT : CODE_AT + 1]
-                    reach = rows[own, k][:, CODE_AT + 1 : CODE_AT + 2]
+                    if zp == 0:
+                        first = k * load_rows + body
+                        code_row = all_ref[own, first : first + ROWS, LANES : 2 * LANES]
+                        code_row = jnp.sum(code_row.astype(f32), axis=0, keepdims=True)
+                        center = column(code_row, channels, 0)
+                        reach = column(code_row, channels, channels)
+                        codes[own, k] = (scale * reach, scale * center + offset)
                     code = jnp.log(all_ref[own, at : at + channels, :].astype(f32))
-                    value = activated(code, scale * reach, scale * center + offset)
+                    value = activated(code, *codes[own, k])
                     peak_pool = jnp.maximum(peak_pool, jnp.abs(value))
                     both.append(bounded(value, bound))
                 for q in range(span // LANES):

time: 52.8 us -> 53.3 us (level)
  Pallas kernels: 12.7 us -> 13.3 us
    pallas_call x1, Pallas kernels: 3.08 us -> 3.71 us  [per_device(): pl.pallas_call(third_kernel(fine_cells, coarse_cells, load_rows, third_ro...]
  transfers between devices with their start and end apart: 11 -> 11, of which waited for: 3 -> 4; matrix products, arithmetic and copies ran while one was open for 0% -> 0% of each run, Pallas kernels for 11% -> 11%
where the time goes in v12:
time: 53.3 us; the launch traced here: 53 us
  blocking collectives  26.3 us (49%)
  Pallas kernels  13.3 us (25%)
  starting transfers between devices  11.5 us (22%)
  waiting for transfers between devices  1.2 us (2%)
  between operations  0.73 us (1%)
    all_to_all x1, blocking collectives, per_device(): rows = lax.all_to_all(row, ('sy', 'sz'), 0, 0, tiled=True)  19.1 us
    all_gather x1, blocking collectives, per_device(): gathered = lax.all_gather(jnp.concatenate(loads, axis=0), 'sy', axis=0)  7.19 us
    ppermute x3, starting transfers between devices, per_device(): lax.ppermute(load, 'sz', [(i, i ^ k) for i in range(z_groups)])  4.45 us
    pallas_call x1, Pallas kernels, per_device(): pl.pallas_call(third_kernel(fine_cells, coarse_cells, load_rows, third_ro...  3.71 us
    ppermute x1, starting transfers between devices, per_device(): z_first = lax.ppermute(z_first, 'sz', pair_first)  3.12 us
    pallas_call x1, Pallas kernels, per_device(): pl.pallas_call(fourth_kernel(coarse_cells), out_shape=(near_shape((chan_o...  2.1 us
    pallas_call x1, Pallas kernels, per_device(): pl.pallas_call(matrix_kernel, out_shape=(near_shape((3 * channels, 9 * ch...  1.47 us
    ppermute x1, starting transfers between devices, per_device(): lax.ppermute(peaks, 'sample', [(i, (i + k) % samples) for i in range(samp...  1.44 us
  transfers between devices with their start and end apart: 11, of which 4 were waited for; matrix products, arithmetic and copies ran while one was open for 0% of the time, Pallas kernels for 11%

profile of v12, /device:TPU:0, one launch (start us, length us, event | category | flops | bytes accessed | tf_op | source)
XLA Modules:
  0.0 53.0 jit_solution(10935883686001714768)
XLA Ops:
  0.6 1.0 %slabs.1 = (bf16[32,2,8,128]{3,2,1,0:T(8,128)(2,1)S(1)}, bf16[32,2,8,128]{3,2,1,0:T(8,128)(2,1)S(1)}) custom-call(bf16[1,32,4,8,128]{4,3,2,1,0:T(8,128)(2,1)} %vol_ref.3), custom_call_target="tpu_custom_call" | custom-call | tf_op jit(solution)/shard_map/slabs/pallas_call | solution.py:753
  1.6 3.1 %collective-permute-start = (bf16[32,2,8,128]{3,2,1,0:T(8,128)(2,1)S(1)}, bf16[32,2,8,128]{3,2,1,0:T(8,128)(2,1)S(1)}, u32[]{:S(2)}, u32[]{:S(2)}) collective-permute-start(bf16[32,2,8,128]{3,2,1,0:T(8,128)(2,1)S(1)} %get-tuple-element.33), channel_id=1, source_target_pairs={{0,1},{1,0},{2,3},{3,2},{4,5},{5,4},{6,7},{7,6},{8,9},{9,8},{10,11... | collective-permute-start | bytes 393224 | tf_op jit(solution)/shard_map/ppermute | solution.py:800
  4.7 0.7 %collective-permute-start.1 = (bf16[32,2,8,128]{3,2,1,0:T(8,128)(2,1)S(1)}, bf16[32,2,8,128]{3,2,1,0:T(8,128)(2,1)S(1)}, u32[]{:S(2)}, u32[]{:S(2)}) collective-permute-start(bf16[32,2,8,128]{3,2,1,0:T(8,128)(2,1)S(1)} %get-tuple-element.34), channel_id=1, source_target_pairs={{0,0},{1,2},{2,1},{3,3},{4,4},{5,6},{6,5},{7,7},{8,8},{9,10},{10,9... | collective-permute-start | bytes 393224 | tf_op jit(solution)/shard_map/ppermute | solution.py:801
  5.4 1.2 %prep.1 = (bf16[4,8,32,128]{3,2,1,0:T(8,128)(2,1)S(1)}, f32[1,128]{1,0:T(1,128)S(1)}) custom-call(bf16[1,32,4,8,128]{4,3,2,1,0:T(8,128)(2,1)} %vol_ref.3, f32[4,16]{1,0:T(4,128)} %hist_ref.3), custom_call_target="tpu_custom_call" | custom-call | tf_op jit(solution)/shard_map/prep/pallas_call | solution.py:764
  6.5 1.5 %matrices.1 = (bf16[96,288]{1,0:T(8,128)(2,1)S(1)}, bf16[96,288]{1,0:T(8,128)(2,1)S(1)}, bf16[64,256]{1,0:T(8,128)(2,1)S(1)}, bf16[144,192]{1,0:T(8,128)(2,1)S(1...) custom-call(f32[1,128]{1,0:T(1,128)S(1)} %get-tuple-element.35.peak_ref, bf16[27,32,32]{2,1,0:T(8,128)(2,1)} %first_ref.1, ...), custom_call_target="tpu_custom_call" | custom-call | tf_op jit(solution)/shard_map/matrices/pallas_call | solution.py:773
  8.0 0.2 collective-permute-done.got_first_ref
  8.2 0.0 collective-permute-done.1.got_second_ref
  8.2 0.2 deep.1
  8.4 0.1 collective-permute-start.2
  8.5 0.7 %collective-permute-start.3 = (bf16[8,2,32,128]{3,2,1,0:T(8,128)(2,1)S(1)}, bf16[8,2,32,128]{3,2,1,0:T(8,128)(2,1)S(1)}, u32[]{:S(2)}, u32[]{:S(2)}) collective-permute-start(bf16[8,2,32,128]{3,2,1,0:T(8,128)(2,1)S(1)} %get-tuple-element.43), channel_id=1, source_target_pairs={{0,0},{4,8},{8,4},{12,12},{1,1},{5,9},{9,5},{13,13},{2,2},{6,10},{... | collective-permute-start | bytes 393224 | tf_op jit(solution)/shard_map/ppermute | solution.py:816
  9.2 0.9 %first_inner.1 = (bf16[8,8,32,128]{3,2,1,0:T(8,128)(2,1)S(1)}, f32[6,6,32,128]{3,2,1,0:T(8,128)S(1)}, f32[2,32,128]{2,1,0:T(8,128)S(1)}) custom-call(bf16[4,8,32,128]{3,2,1,0:T(8,128)(2,1)S(1)} %get-tuple-element.32.cells_ref.own_ref, bf16[2,8,32,128]{3,2,1,0:T(8,128)(2,1)S(1)} %get-tuple-element.37.got_first_ref, ...), custom_call_target="tpu_custom_call" | custom-call | tf_op jit(solution)/shard_map/first_inner/pallas_call | solution.py:817
  10.1 0.0 collective-permute-done.2.got_first_ref
  10.1 0.0 collective-permute-done.3.got_second_ref
  10.1 0.7 %first_outer.1 = (f32[6,4,32,128]{3,2,1,0:T(8,128)S(1)}, f32[16,1,128]{2,1,0:T(1,128)S(1)}) custom-call(bf16[8,8,32,128]{3,2,1,0:T(8,128)(2,1)S(1)} %get-tuple-element.41.deep_ref, bf16[8,2,32,128]{3,2,1,0:T(8,128)(2,1)S(1)} %collective-permute-done.2.got_first_ref, bf16[8,2,32,128]{3,2,1,0:T(8,128)(2,1)S(1)} %collective-permute-done.3.got_second_ref, ...), custom_call_target="tpu_custom_call" | custom-call | tf_op jit(solution)/shard_map/first_outer/pallas_call | solution.py:826
  10.8 19.1 %all_to_all.5.rows_ref = f32[16,1,128]{2,1,0:T(1,128)S(1)} all-to-all(f32[16,1,128]{2,1,0:T(1,128)S(1)} %get-tuple-element.46), channel_id=1, replica_groups=mesh['sample'=2,'sy'=4,'sz'=4] {'sy','sz'}, dimensions={0} | all-to-all | bytes 16384 | tf_op jit(solution)/shard_map/all_to_all | solution.py:835
  30.0 1.4 %second.1 = (f32[4,8,32,128]{3,2,1,0:T(8,128)S(1)}, bf16[72,256]{1,0:T(8,128)(2,1)S(1)}) custom-call(f32[6,6,32,128]{3,2,1,0:T(8,128)S(1)} %get-tuple-element.40.inner_ref, f32[6,4,32,128]{3,2,1,0:T(8,128)S(1)} %get-tuple-element.45.outer_ref, f32[16,1,128]{2,1,0:T(1,128)S(1)} %all_to_all.5.rows_ref, bf16[96,288]{1,0:T(8,128)(2,1)S(1)} %get-tuple-element.47.weight_ref, ...), custom_call_target="tpu_custom_call" | custom-call | tf_op jit(solution)/shard_map/second/pallas_call | solution.py:836
  31.4 0.7 %collective-permute-start.6 = (bf16[72,256]{1,0:T(8,128)(2,1)S(1)}, bf16[72,256]{1,0:T(8,128)(2,1)S(1)}, u32[]{:S(2)}, u32[]{:S(2)}) collective-permute-start(bf16[72,256]{1,0:T(8,128)(2,1)S(1)} %get-tuple-element.49), channel_id=1, source_target_pairs={{0,3},{1,2},{2,1},{3,0},{4,7},{5,6},{6,5},{7,4},{8,11},{9,10},{10,... | collective-permute-start | bytes 110600 | tf_op jit(solution)/shard_map/ppermute | solution.py:851
  32.1 1.4 %collective-permute-start.5 = (bf16[72,256]{1,0:T(8,128)(2,1)S(1)}, bf16[72,256]{1,0:T(8,128)(2,1)S(1)}, u32[]{:S(2)}, u32[]{:S(2)}) collective-permute-start(bf16[72,256]{1,0:T(8,128)(2,1)S(1)} %get-tuple-element.49), channel_id=1, source_target_pairs={{0,2},{1,3},{2,0},{3,1},{4,6},{5,7},{6,4},{7,5},{8,10},{9,11},{10,... | collective-permute-start | bytes 110600 | tf_op jit(solution)/shard_map/ppermute | solution.py:851
  33.5 2.4 %collective-permute-start.4 = (bf16[72,256]{1,0:T(8,128)(2,1)S(1)}, bf16[72,256]{1,0:T(8,128)(2,1)S(1)}, u32[]{:S(2)}, u32[]{:S(2)}) collective-permute-start(bf16[72,256]{1,0:T(8,128)(2,1)S(1)} %get-tuple-element.49), channel_id=1, source_target_pairs={{0,1},{1,0},{2,3},{3,2},{4,5},{5,4},{6,7},{7,6},{8,9},{9,8},{10,11... | collective-permute-start | bytes 110600 | tf_op jit(solution)/shard_map/ppermute | solution.py:851
  35.8 0.0 collective-permute-start.9
  35.8 0.6 %collective-permute-start.8 = (bf16[64,256]{1,0:T(8,128)(2,1)S(1)}, bf16[64,256]{1,0:T(8,128)(2,1)S(1)}, u32[]{:S(2)}, u32[]{:S(2)}) collective-permute-start(bf16[64,256]{1,0:T(8,128)(2,1)S(1)} %get-tuple-element.50.refs_2_), channel_id=1, source_target_pairs={{0,8},{4,12},{8,0},{12,4},{1,9},{5,13},{9,1},{13,5},{2,10},{6,14},... | collective-permute-start | bytes 98312 | tf_op jit(solution)/shard_map/ppermute | solution.py:798
  36.5 0.8 %collective-permute-done.6 = bf16[72,256]{1,0:T(8,128)(2,1)S(1)} collective-permute-done((bf16[72,256]{1,0:T(8,128)(2,1)S(1)}, bf16[72,256]{1,0:T(8,128)(2,1)S(1)}, u32[]{:S(2)}, u32[]{:S(2)}) %collective-permute-start.6) | collective-permute-done | bytes 36896 | tf_op jit(solution)/shard_map/ppermute | solution.py:851
  37.3 0.4 collective-permute-start.7
  37.7 0.1 collective-permute-done.5
  37.8 0.1 collective-permute-done.4
  37.9 7.2 %all-gather = bf16[1152,256]{1,0:T(8,128)(2,1)S(1)} all-gather(bf16[288,256]{1,0:T(8,128)(2,1)S(1)} %pad_maximum_fusion), channel_id=2, replica_groups=mesh['sample'=2,'sy'=4,'sz'=4] {'sy'}, dimensions={0}, use_global_device_ids=true | all-gather | bytes 737280 | tf_op jit(solution)/shard_map/all_gather | solution.py:852
  45.1 0.0 collective-permute-done.9.refs_5_
  45.1 0.0 collective-permute-done.8.refs_4_
  45.1 0.0 collective-permute-done.7.refs_3_
  45.1 3.7 %third.1 = (f32[8,64,1024]{2,1,0:T(8,128)S(1)}, f32[1,4]{1,0:T(1,128)S(1)}, f32[32,128]{1,0:T(8,128)S(1)}, f32[64,128]{1,0:T(8,128)S(1)}) custom-call(bf16[4,288,256]{2,1,0:T(8,128)(2,1)S(1)} %bitcast.2, f32[32,128]{1,0:T(8,128)S(1)} %get-tuple-element.36.param_ref.refs_1_, bf16[64,256]{1,0:T(8,128)(2,1)S(1)} %get-tuple-element.50.refs_2_, ...), custom_call_target="tpu_custom_call" | custom-call | tf_op jit(solution)/shard_map/third/pallas_call | solution.py:853
  48.8 1.4 %collective-permute-start.10 = (f32[1,4]{1,0:T(1,128)S(1)}, f32[1,4]{1,0:T(1,128)S(1)}, u32[]{:S(2)}, u32[]{:S(2)}) collective-permute-start(f32[1,4]{1,0:T(1,128)S(1)} %get-tuple-element.58.refs_1_), channel_id=1, source_target_pairs={{0,16},{16,0},{1,17},{17,1},{2,18},{18,2},{3,19},{19,3},{4,20},{20... | collective-permute-start | bytes 56 | tf_op jit(solution)/shard_map/ppermute | solution.py:871
  50.2 2.1 %fourth.1 = (bf16[16,2,1024]{2,1,0:T(2,128)(2,1)S(1)}, bf16[1,32,4,8,128]{4,3,2,1,0:T(8,128)(2,1)}) custom-call(f32[8,64,1024]{2,1,0:T(8,128)S(1)} %get-tuple-element.51.raw_ref, bf16[144,192]{1,0:T(8,128)(2,1)S(1)} %get-tuple-element.52.weight_ref, f32[32,128]{1,0:T(8,128)S(1)} %get-tuple-element.36.param_ref.refs_1_, ...), custom_call_target="tpu_custom_call" | custom-call | tf_op jit(solution)/shard_map/fourth/pallas_call | solution.py:876
  52.4 0.0 collective-permute-done.10.refs_2_
  52.4 0.6 %final.1 = (bf16[1,16,2,1024]{3,2,1,0:T(2,128)(2,1)}, f32[1,4]{1,0:T(1,128)}) custom-call(bf16[16,2,1024]{2,1,0:T(2,128)(2,1)S(1)} %get-tuple-element.57.refs_0_, f32[1,4]{1,0:T(1,128)S(1)} %get-tuple-element.58.refs_1_, f32[1,4]{1,0:T(1,128)S(1)} %collective-permute-done.10.refs_2_), custom_call_target="tpu_custom_call" | custom-call | tf_op jit(solution)/shard_map/final/pallas_call | solution.py:892
  (1 shorter events, 0.0 us)
Async XLA Ops:
  1.6 6.6 %collective-permute-start = (bf16[32,2,8,128]{3,2,1,0:T(8,128)(2,1)S(1)}, bf16[32,2,8,128]{3,2,1,0:T(8,128)(2,1)S(1)}, u32[]{:S(2)}, u32[]{:S(2)}) collective-permute-start(bf16[32,2,8,128]{3,2,1,0:T(8,128)(2,1)S(1)} %get-tuple-element.33), channel_id=1, source_target_pairs={{0,1},{1,0},{2,3},{3,2},{4,5},{5,4},{6,7},{7,6},{8,9},{9,8},{10,11... | collective-permute-start | bytes 393224 | tf_op jit(solution)/shard_map/ppermute | solution.py:800
  4.7 3.5 %collective-permute-start.1 = (bf16[32,2,8,128]{3,2,1,0:T(8,128)(2,1)S(1)}, bf16[32,2,8,128]{3,2,1,0:T(8,128)(2,1)S(1)}, u32[]{:S(2)}, u32[]{:S(2)}) collective-permute-start(bf16[32,2,8,128]{3,2,1,0:T(8,128)(2,1)S(1)} %get-tuple-element.34), channel_id=1, source_target_pairs={{0,0},{1,2},{2,1},{3,3},{4,4},{5,6},{6,5},{7,7},{8,8},{9,10},{10,9... | collective-permute-start | bytes 393224 | tf_op jit(solution)/shard_map/ppermute | solution.py:801
  8.4 1.7 %collective-permute-start.2 = (bf16[8,2,32,128]{3,2,1,0:T(8,128)(2,1)S(1)}, bf16[8,2,32,128]{3,2,1,0:T(8,128)(2,1)S(1)}, u32[]{:S(2)}, u32[]{:S(2)}) collective-permute-start(bf16[8,2,32,128]{3,2,1,0:T(8,128)(2,1)S(1)} %get-tuple-element.42), channel_id=1, source_target_pairs={{0,4},{4,0},{8,12},{12,8},{1,5},{5,1},{9,13},{13,9},{2,6},{6,2},{1... | collective-permute-start | bytes 393224 | tf_op jit(solution)/shard_map/ppermute | solution.py:815
  8.5 1.6 %collective-permute-start.3 = (bf16[8,2,32,128]{3,2,1,0:T(8,128)(2,1)S(1)}, bf16[8,2,32,128]{3,2,1,0:T(8,128)(2,1)S(1)}, u32[]{:S(2)}, u32[]{:S(2)}) collective-permute-start(bf16[8,2,32,128]{3,2,1,0:T(8,128)(2,1)S(1)} %get-tuple-element.43), channel_id=1, source_target_pairs={{0,0},{4,8},{8,4},{12,12},{1,1},{5,9},{9,5},{13,13},{2,2},{6,10},{... | collective-permute-start | bytes 393224 | tf_op jit(solution)/shard_map/ppermute | solution.py:816
  31.4 5.9 %collective-permute-start.6 = (bf16[72,256]{1,0:T(8,128)(2,1)S(1)}, bf16[72,256]{1,0:T(8,128)(2,1)S(1)}, u32[]{:S(2)}, u32[]{:S(2)}) collective-permute-start(bf16[72,256]{1,0:T(8,128)(2,1)S(1)} %get-tuple-element.49), channel_id=1, source_target_pairs={{0,3},{1,2},{2,1},{3,0},{4,7},{5,6},{6,5},{7,4},{8,11},{9,10},{10,... | collective-permute-start | bytes 110600 | tf_op jit(solution)/shard_map/ppermute | solution.py:851
  32.1 5.7 %collective-permute-start.5 = (bf16[72,256]{1,0:T(8,128)(2,1)S(1)}, bf16[72,256]{1,0:T(8,128)(2,1)S(1)}, u32[]{:S(2)}, u32[]{:S(2)}) collective-permute-start(bf16[72,256]{1,0:T(8,128)(2,1)S(1)} %get-tuple-element.49), channel_id=1, source_target_pairs={{0,2},{1,3},{2,0},{3,1},{4,6},{5,7},{6,4},{7,5},{8,10},{9,11},{10,... | collective-permute-start | bytes 110600 | tf_op jit(solution)/shard_map/ppermute | solution.py:851
  33.5 4.4 %collective-permute-start.4 = (bf16[72,256]{1,0:T(8,128)(2,1)S(1)}, bf16[72,256]{1,0:T(8,128)(2,1)S(1)}, u32[]{:S(2)}, u32[]{:S(2)}) collective-permute-start(bf16[72,256]{1,0:T(8,128)(2,1)S(1)} %get-tuple-element.49), channel_id=1, source_target_pairs={{0,1},{1,0},{2,3},{3,2},{4,5},{5,4},{6,7},{7,6},{8,9},{9,8},{10,11... | collective-permute-start | bytes 110600 | tf_op jit(solution)/shard_map/ppermute | solution.py:851
  35.8 9.2 %collective-permute-start.9 = (bf16[64,256]{1,0:T(8,128)(2,1)S(1)}, bf16[64,256]{1,0:T(8,128)(2,1)S(1)}, u32[]{:S(2)}, u32[]{:S(2)}) collective-permute-start(bf16[64,256]{1,0:T(8,128)(2,1)S(1)} %get-tuple-element.50.refs_2_), channel_id=1, source_target_pairs={{0,12},{4,8},{8,4},{12,0},{1,13},{5,9},{9,5},{13,1},{2,14},{6,10},... | collective-permute-start | bytes 98312 | tf_op jit(solution)/shard_map/ppermute | solution.py:798
  35.8 9.2 %collective-permute-start.8 = (bf16[64,256]{1,0:T(8,128)(2,1)S(1)}, bf16[64,256]{1,0:T(8,128)(2,1)S(1)}, u32[]{:S(2)}, u32[]{:S(2)}) collective-permute-start(bf16[64,256]{1,0:T(8,128)(2,1)S(1)} %get-tuple-element.50.refs_2_), channel_id=1, source_target_pairs={{0,8},{4,12},{8,0},{12,4},{1,9},{5,13},{9,1},{13,5},{2,10},{6,14},... | collective-permute-start | bytes 98312 | tf_op jit(solution)/shard_map/ppermute | solution.py:798
  37.3 7.8 %collective-permute-start.7 = (bf16[64,256]{1,0:T(8,128)(2,1)S(1)}, bf16[64,256]{1,0:T(8,128)(2,1)S(1)}, u32[]{:S(2)}, u32[]{:S(2)}) collective-permute-start(bf16[64,256]{1,0:T(8,128)(2,1)S(1)} %get-tuple-element.50.refs_2_), channel_id=1, source_target_pairs={{0,4},{4,0},{8,12},{12,8},{1,5},{5,1},{9,13},{13,9},{2,6},{6,2},{1... | collective-permute-start | bytes 98312 | tf_op jit(solution)/shard_map/ppermute | solution.py:798
  48.8 3.6 %collective-permute-start.10 = (f32[1,4]{1,0:T(1,128)S(1)}, f32[1,4]{1,0:T(1,128)S(1)}, u32[]{:S(2)}, u32[]{:S(2)}) collective-permute-start(f32[1,4]{1,0:T(1,128)S(1)} %get-tuple-element.58.refs_1_), channel_id=1, source_target_pairs={{0,16},{16,0},{1,17},{17,1},{2,18},{18,2},{3,19},{19,3},{4,20},{20... | collective-permute-start | bytes 56 | tf_op jit(solution)/shard_map/ppermute | solution.py:871
